TPU v7x, 8 devices: a whole 2x2x1 slice. The times are simulated.
8 devices in a mesh: dp: 1 (over z), tp: 8 (over y, x, core).
Axes of the slice: x: 2, y: 2, z: 1, core: 2. Of those that a mesh axis runs over, the one named last changes fastest.
Arguments:
- ids: int32 [4, 256], P('dp')
- emb: bfloat16 [65536, 3072], P('tp')
- g: bfloat16 [3072], replicated
- w: bfloat16 [3072, 5120], P(None, 'tp')
- du: bfloat16 [4, 256, 5120], P('dp', None, 'tp')
- dres: bfloat16 [4, 256, 3072], P('dp', 'tp')
Outputs:
- output 1: bfloat16 [4, 256, 5120], P('dp', None, 'tp')
- output 2: bfloat16 [4, 256, 3072], P('dp', 'tp')
- output 3: float32 [65536, 3072], P(('dp', 'tp'))
- output 4: float32 [3072, 5120], P(None, ('dp', 'tp'))
- output 5: float32 [3072], P('dp')
All inputs are finite; a program needn't handle non-finite values.
Results may differ from a plain program's by a relative error of at most 0.00621165.
Values are sent between devices in bfloat16 or wider.
A program may use at most 1 GiB of HBM per device.

v0:
```python
import functools

import jax
import jax.numpy as jnp
from jax import lax
from jax.experimental import pallas as pl
from jax.experimental.pallas import tpu as pltpu
from jax.sharding import PartitionSpec as P

EPS = 1e-6
ANY = pl.BlockSpec(memory_space=pl.ANY)
VMEM = pl.BlockSpec(memory_space=pltpu.VMEM)
SMEM = pl.BlockSpec(memory_space=pltpu.SMEM)
ZR = 128
BLK = 128
LOOKUP_SHARE, NORM_SHARE = 40, 12


def zero_fill(de, z, sem, first, last):
    z[...] = jnp.zeros_like(z)

    def copy(i):
        return pltpu.make_async_copy(z, de.at[pl.ds(pl.multiple_of(i * ZR, ZR), ZR)], sem)

    def start():
        pl.loop(first, last)(lambda i: copy(i).start())

    def wait():
        pl.loop(first, last)(lambda i: copy(i).wait())

    return start, wait


def pdn_kernel(js, kc_ref, du_ref, w_ref, mine_ref, theirs_ref):
    k, c = kc_ref[0], kc_ref[1]
    mb, t, _ = du_ref.shape
    tc = t // 4
    hd = w_ref.shape[0] // 2
    wc = 512
    for i, j in enumerate(js):
        z = pl.multiple_of(jnp.bitwise_xor(c, j) * tc, tc)
        rows = jnp.concatenate([du_ref[m, pl.ds(z, tc), :] for m in range(mb)], axis=0)
        for out, half in ((theirs_ref, 1 - k), (mine_ref, k)):
            for n in range(hd // wc):
                wv = w_ref[pl.ds(pl.multiple_of(half * hd + n * wc, wc), wc), :]
                v = lax.dot_general(rows, wv, (((1,), (1,)), ((), ())), preferred_element_type=jnp.float32)
                out[i, :, :, n * wc:(n + 1) * wc] = v.astype(jnp.bfloat16).reshape(mb, tc, wc)


def lookup_kernel(kc_ref, loc_ref, tgt_ref, emb, mine_ref, theirs_ref, de, buf, sem, z, zsem):
    k, c = kc_ref[0], kc_ref[1]
    vl, d = emb.shape
    nj, mb, tc, hd = mine_ref.shape
    n = nj * mb * tc
    step = 64
    start, wait = zero_fill(de, z, zsem, 0, LOOKUP_SHARE)

    @pl.loop(0, 2 * n // step)
    def _(i):
        buf[pl.ds(pl.multiple_of(i * step, step), step), :] = jnp.zeros((step, d), buf.dtype)

    def copy(t, l):
        src = emb.at[pl.ds(pl.multiple_of((l >> 1) * 2, 2), 2)]
        return pltpu.make_async_copy(src, buf.at[pl.ds(pl.multiple_of(t * 2, 2), 2)], sem)

    def issue(i, cnt):
        for q in range(8):
            t = i * 8 + q
            l = loc_ref[t]
            own = (l >= 0) & (l < vl)

            @pl.when(own)
            def _():
                copy(t, l).start()

            cnt = cnt + own.astype(jnp.int32)
        return cnt

    cnt = lax.fori_loop(0, n // 8, issue, jnp.int32(0))
    start()

    @pl.loop(0, cnt)
    def _(i):
        copy(0, 0).wait()

    for j in range(nj):
        zc = jnp.bitwise_xor(c, j)

        @pl.loop(0, mb)
        def _(m):
            t0 = m * (nj * tc) + zc * tc
            tgt = tgt_ref[pl.ds(pl.multiple_of(t0, tc), tc), :]
            sel = (lax.broadcasted_iota(jnp.int32, (tc, 2 * tc), 1) == tgt).astype(jnp.bfloat16)
            rows = pl.ds(pl.multiple_of(2 * t0, 2 * tc), 2 * tc)
            for out, half in ((theirs_ref, 1 - k), (mine_ref, k)):
                v = buf[rows, pl.ds(pl.multiple_of(half * hd, 128), hd)]
                out[j, m] = jnp.dot(sel, v, preferred_element_type=jnp.float32).astype(jnp.bfloat16)

    wait()


def pull(me, blocks, buf, sem):
    hb, tl = blocks[0].shape[:2]
    copies = []
    for i, b in enumerate(blocks):
        j, h = i // 2, i % 2
        s = pl.multiple_of(jnp.bitwise_xor(me, j) * tl, tl)
        copies.append(pltpu.make_async_copy(b, buf.at[h * hb:(h + 1) * hb, pl.ds(s, tl), :], sem.at[i]))
    for c in copies:
        c.start()
    return copies


def norm_kernel(me_ref, g_ref, w_ref, *refs):
    blocks, (de_in, n_ref, u_ref, de, sem, z, zsem) = refs[:16], refs[16:]
    del de_in
    mb, t, _ = n_ref.shape
    start, wait = zero_fill(de, z, zsem, LOOKUP_SHARE, LOOKUP_SHARE + NORM_SHARE)
    copies = pull(me_ref[0], blocks, n_ref, sem)
    start()
    for c in copies:
        c.wait()
    gf = g_ref[...].astype(jnp.float32)
    rows = 32

    @pl.loop(0, mb)
    def _(m):
        @pl.loop(0, t // rows)
        def _(r):
            at = (m, pl.ds(pl.multiple_of(r * rows, rows), rows), slice(None))
            xf = n_ref[at].astype(jnp.float32)
            rs = lax.rsqrt(jnp.mean(xf * xf, axis=-1, keepdims=True) + EPS)
            n_ref[at] = (xf * rs * gf).astype(jnp.bfloat16)

        u_ref[m] = jnp.dot(n_ref[m], w_ref[...], preferred_element_type=jnp.float32).astype(jnp.bfloat16)

    wait()


def dw_kernel(n_ref, du_ref, de_in, dw_ref, de, z, zsem):
    del de_in
    mb, _, d = n_ref.shape
    start, wait = zero_fill(de, z, zsem, LOOKUP_SHARE + NORM_SHARE, de.shape[0] // ZR)
    start()
    dc = 512

    @pl.loop(0, d // dc)
    def _(i):
        c = pl.ds(pl.multiple_of(i * dc, dc), dc)
        acc = jnp.zeros((dc, du_ref.shape[2]), jnp.float32)
        for m in range(mb):
            acc += lax.dot_general(n_ref[m, :, c], du_ref[m], (((0,), (0,)), ((), ())), preferred_element_type=jnp.float32)
        dw_ref[c, :] = acc

    wait()


def scatter_kernel(me_ref, rows_ref, cnt_ref, slot_ref, *refs):
    blocks, (de_in, de, buf, stage, sem, out_sem) = refs[:16], refs[16:]
    del de_in
    mb, t, d = buf.shape
    for c in pull(me_ref[0], blocks, buf, sem):
        c.wait()
    cnt = cnt_ref[0]
    cc = 512

    def copy(q, r):
        return pltpu.make_async_copy(stage.at[pl.ds(q, 1)], de.at[pl.ds(r, 1)], out_sem)

    @pl.loop(0, (cnt + BLK - 1) // BLK)
    def _(b):
        base = b * BLK
        ids = lax.broadcasted_iota(jnp.int32, (BLK, mb * t), 0) + base
        oh = (ids == slot_ref[...]).astype(jnp.bfloat16)
        for i in range(d // cc):
            acc = jnp.zeros((BLK, cc), jnp.float32)
            for m in range(mb):
                acc += jnp.dot(oh[:, m * t:(m + 1) * t], buf[m, :, i * cc:(i + 1) * cc], preferred_element_type=jnp.float32)
            stage[:, i * cc:(i + 1) * cc] = acc
        n = jnp.minimum(cnt - base, BLK)
        pl.loop(0, n)(lambda q: copy(q, rows_ref[base + q]).start())
        pl.loop(0, n)(lambda q: copy(q, rows_ref[base + q]).wait())


def solution(mesh):
    groups = mesh.shape["tp"]

    def swap(v, bit):
        return lax.ppermute(v, "tp", [(i, i ^ bit) for i in range(groups)])

    def local(ids, emb, g, w, du, dres):
        r = lax.axis_index("tp")
        mb, t = ids.shape
        vl, d = emb.shape
        f = w.shape[1]
        tl = t // groups
        hd = d // 2
        tc = t // 4
        k, c = r & 1, r >> 1
        gf = g.astype(jnp.float32)
        me = r.reshape(1)
        kc = jnp.stack([k, c]).astype(jnp.int32)
        de_shape = jax.ShapeDtypeStruct((vl, d), jnp.float32)
        zero_scratch = [pltpu.VMEM((ZR, d), jnp.float32), pltpu.SemaphoreType.DMA]

        def half_shape(nj):
            return jax.ShapeDtypeStruct((nj, mb, tc, hd), jnp.bfloat16)

        def pdn(js):
            mine, theirs = pl.pallas_call(
                functools.partial(pdn_kernel, js),
                out_shape=(half_shape(len(js)),) * 2,
                in_specs=[SMEM, VMEM, VMEM],
                out_specs=(VMEM, VMEM),
                cost_estimate=pl.CostEstimate(flops=5_000_000 * len(js), bytes_accessed=8_000_000, transcendentals=0),
                compiler_params=pltpu.CompilerParams(vmem_limit_bytes=40 * 2**20),
            )(kc, du, w)
            got = swap(theirs, 1)
            return {j: (mine[i], got[i]) for i, j in enumerate(js)}

        def reduce_to_home(pairs, dt):
            def part(j, h):
                a, b = pairs[j]
                return a[:, h * tl:(h + 1) * tl].astype(dt) + b[:, h * tl:(h + 1) * tl].astype(dt)

            dx_ = swap(part(3, 0), 2)
            dy_ = swap(part(3, 1), 4)
            ex = swap(part(1, 0), 2)
            ey = swap(part(2, 1), 4)
            pairs = dict(pairs)
            pairs[2], dx_ = lax.optimization_barrier((pairs[2], dx_))
            pairs[1], dy_ = lax.optimization_barrier((pairs[1], dy_))
            fy = swap(part(2, 0) + dx_, 4)
            fx = swap(part(1, 1) + dy_, 2)
            pairs[0], ex, ey = lax.optimization_barrier((pairs[0], ex, ey))
            s0 = part(0, 0) + ex + fy
            s1 = part(0, 1) + ey + fx
            keep = jnp.where(k == 0, s0, s1)
            give = jnp.where(k == 0, s1, s0)
            other = swap(give, 1)
            return jnp.where(k == 0, jnp.concatenate([keep, other], -1), jnp.concatenate([other, keep], -1))

        def gather_all(v):
            h = v.shape[0] // 2
            own = (v[:h], v[h:])
            x1, y0 = swap(own[1], 2), swap(own[0], 4)
            x0, y1 = swap(own[0], 2), swap(own[1], 4)
            d1, d0 = swap(x1, 4), swap(y0, 2)
            out = {0: own, 2: (x0, x1), 4: (y0, y1), 6: (d0, d1)}
            for j in (0, 2, 4, 6):
                out[j + 1] = tuple(swap(b, 1) for b in out[j])
            return [b for j in range(8) for b in out[j]]

        flat = ids.reshape(-1)
        n = flat.shape[0]
        loc = flat - r * vl
        own = (loc >= 0) & (loc < vl)
        pairs = pdn((3,))
        pairs.update(pdn((1, 2, 0)))
        tgt = jnp.where(own, 2 * (jnp.arange(n) % tc) + (loc & 1), -1).astype(jnp.int32)
        mine, theirs, de = pl.pallas_call(
            lookup_kernel,
            out_shape=(half_shape(4), half_shape(4), de_shape),
            in_specs=[SMEM, SMEM, VMEM, ANY],
            out_specs=(VMEM, VMEM, ANY),
            scratch_shapes=[pltpu.VMEM((2 * n, d), jnp.bfloat16), pltpu.SemaphoreType.DMA] + zero_scratch,
            cost_estimate=pl.CostEstimate(flops=40_000_000, bytes_accessed=60_000_000, transcendentals=0),
            compiler_params=pltpu.CompilerParams(vmem_limit_bytes=40 * 2**20),
            name="lookup",
        )(kc, loc, tgt.reshape(n, 1), emb)
        got = swap(theirs, 1)
        xpairs = {j: (mine[j], got[j]) for j in range(4)}

        dn = reduce_to_home(pairs, jnp.float32)
        x = reduce_to_home(xpairs, jnp.bfloat16)
        xs = gather_all(x)

        nn, u, de = pl.pallas_call(
            norm_kernel,
            out_shape=(jax.ShapeDtypeStruct((mb, t, d), jnp.bfloat16), jax.ShapeDtypeStruct((mb, t, f), jnp.bfloat16), de_shape),
            in_specs=[SMEM, VMEM, VMEM] + [ANY] * 17,
            out_specs=(VMEM, VMEM, ANY),
            scratch_shapes=[pltpu.SemaphoreType.DMA((16,))] + zero_scratch,
            input_output_aliases={19: 2},
            cost_estimate=pl.CostEstimate(flops=30_000_000, bytes_accessed=40_000_000, transcendentals=0),
            compiler_params=pltpu.CompilerParams(vmem_limit_bytes=40 * 2**20),
            name="norm",
        )(me, g.reshape(1, d), w, *xs, de)
        dw, de = pl.pallas_call(
            dw_kernel,
            out_shape=(jax.ShapeDtypeStruct((d, f), jnp.float32), de_shape),
            in_specs=[VMEM, VMEM, ANY],
            out_specs=(VMEM, ANY),
            scratch_shapes=zero_scratch,
            input_output_aliases={2: 1},
            cost_estimate=pl.CostEstimate(flops=30_000_000, bytes_accessed=40_000_000, transcendentals=0),
            compiler_params=pltpu.CompilerParams(vmem_limit_bytes=40 * 2**20),
            name="dw",
        )(nn, du, de)

        xf = x.astype(jnp.float32)
        rs = lax.rsqrt(jnp.mean(xf * xf, axis=-1, keepdims=True) + EPS)
        nh = xf * rs
        gdn = gf * dn
        dxn = rs * (gdn - nh * jnp.mean(nh * gdn, axis=-1, keepdims=True))
        dx = (dres.astype(jnp.float32) + dxn).astype(jnp.bfloat16)
        dg = jnp.sum(dn * nh, axis=(0, 1))
        dxs = gather_all(dx)
        for bit in (1, 2, 4):
            dg = dg + swap(dg, bit)

        i0 = lax.broadcasted_iota(jnp.int32, (n, n), 0)
        i1 = lax.broadcasted_iota(jnp.int32, (n, n), 1)
        same = flat[:, None] == flat[None, :]
        first = jnp.min(jnp.where(same, i0, n), axis=0)
        lead = own & (first == jnp.arange(n))
        pos = jnp.sum(jnp.where(lead[:, None] & (i0 < i1), 1, 0), axis=0)
        pos_of_first = jnp.sum(jnp.where((i0 == first[None, :]), pos[:, None], 0), axis=0)
        slot = jnp.where(own, pos_of_first, -1).astype(jnp.int32)
        rows = jnp.sum(jnp.where(lead[:, None] & (pos[:, None] == i1), loc[:, None], 0), axis=0).astype(jnp.int32)
        cnt = jnp.sum(lead.astype(jnp.int32)).reshape(1)

        de = pl.pallas_call(
            scatter_kernel,
            out_shape=de_shape,
            in_specs=[SMEM, SMEM, SMEM, VMEM] + [ANY] * 17,
            out_specs=ANY,
            scratch_shapes=[
                pltpu.VMEM((mb, t, d), jnp.bfloat16),
                pltpu.VMEM((BLK, d), jnp.float32),
                pltpu.SemaphoreType.DMA((16,)),
                pltpu.SemaphoreType.DMA,
            ],
            input_output_aliases={20: 0},
            name="put_rows",
        )(me, rows, cnt, slot.reshape(1, n), *dxs, de)
        return u, x, de, dw, dg

    return jax.shard_map(
        local,
        mesh=mesh,
        in_specs=(P("dp", None), P("tp", None), P(None), P(None, "tp"), P("dp", None, "tp"), P("dp", "tp", None)),
        out_specs=(P("dp", None, "tp"), P("dp", "tp", None), P(("dp", "tp"), None), P(None, ("dp", "tp")), P("dp")),
        check_vma=False,
    )
```

profile of v0, /device:TPU:0, one launch (start us, length us, event | category | flops | bytes accessed | tf_op | source)
XLA Modules:
  0.0 250.1 jit_solution(7667310702339152492)
XLA Ops:
  0.7 2.1 copy-done
  2.8 1.3 copy-done.2
  4.1 2.2 shard_map.102
  7.2 5.2 %shard_map.101 = (bf16[3,4,64,1536]{3,2,1,0:T(8,128)(2,1)S(1)}, bf16[3,4,64,1536]{3,2,1,0:T(8,128)(2,1)}) custom-call(s32[2]{0:T(128)S(1)} %pad_add_fusion.kc_ref, bf16[4,256,640]{2,1,0:T(8,128)(2,1)S(1)} %copy-done.2, bf16[3072,640]{1,0:T(8,128)(2,1)S(1)} %copy-done), custom_call_target="tpu_custom_call" | custom-call | flops 15000000 | bytes 8000000 | tf_op jit(solution)/shard_map/pallas_call | solution.py:210
  16.3 32.9 %lookup.1 = (bf16[4,4,64,1536]{3,2,1,0:T(8,128)(2,1)S(1)}, bf16[4,4,64,1536]{3,2,1,0:T(8,128)(2,1)}, f32[8192,3072]{1,0:T(8,128)}) custom-call(s32[2]{0:T(128)S(1)} %pad_add_fusion.kc_ref, s32[1024]{0:T(1024)S(1)} %get-tuple-element.78.loc_ref, s32[1024,1]{1,0:T(8,128)S(1)} %fusion.14.tgt_ref, bf16[8192,3072]{1,0:T(8,128)(2,1)} %emb.1), custom_call_target="tpu_custom_call" | custom-call | flops 40000000 | bytes 60000000 | tf_op jit(solution)/shard_map/lookup/pallas_call | solution.py:261
  49.7 1.7 slice_bitcast_fusion.12
  51.5 2.6 %convert_add_fusion = (f32[4,32,1536]{2,1,0:T(8,128)}, f32[4,32,1536]{2,1,0:T(8,128)}) fusion(bf16[4,64,1536]{2,1,0:T(8,128)(2,1)} %bitcast.20, bf16[4,64,1536]{2,1,0:T(8,128)(2,1)S(1)} %bitcast.51), kind=kLoop, calls=%fused_computation.31 | loop fusion | flops 1179648 | bytes 3145728 | tf_op jit(solution)/shard_map/add | solution.py:224
  54.0 2.5 collective-permute-start.26
  56.5 1.5 collective-permute-start.28
  58.1 1.3 slice_bitcast_fusion.8
  59.4 1.8 slice_bitcast_fusion.1
  61.2 13.8 %collective-permute-done.26 = f32[4,32,1536]{2,1,0:T(8,128)} collective-permute-done((f32[4,32,1536]{2,1,0:T(8,128)}, f32[4,32,1536]{2,1,0:T(8,128)}, u32[]{:S(2)}, u32[]{:S(2)}) %collective-permute-start.26) | collective-permute-done | bytes 786464 | tf_op jit(solution)/shard_map/ppermute | solution.py:189
  75.0 1.5 collective-permute-done.28
  77.1 1.8 collective-permute-start.24
  78.8 1.3 add_add_fusion.2
  80.1 2.1 slice_bitcast_fusion.5
  84.5 1.5 collective-permute-start.1
  86.1 19.9 %collective-permute-done.5 = bf16[4,32,1536]{2,1,0:T(8,128)(2,1)S(1)} collective-permute-done((bf16[4,32,1536]{2,1,0:T(8,128)(2,1)S(1)}, bf16[4,32,1536]{2,1,0:T(8,128)(2,1)S(1)}, u32[]{:S(2)}, u32[]{:S(2)}) %collective-permute-start.5) | collective-permute-done | bytes 393248 | tf_op jit(solution)/shard_map/ppermute | solution.py:189
  105.9 1.7 collective-permute-start.3
  107.7 7.5 %collective-permute-done.3 = bf16[4,32,1536]{2,1,0:T(8,128)(2,1)S(1)} collective-permute-done((bf16[4,32,1536]{2,1,0:T(8,128)(2,1)S(1)}, bf16[4,32,1536]{2,1,0:T(8,128)(2,1)S(1)}, u32[]{:S(2)}, u32[]{:S(2)}) %collective-permute-start.3) | collective-permute-done | bytes 393248 | tf_op jit(solution)/shard_map/ppermute | solution.py:189
  115.2 2.1 collective-permute-start.6
  117.4 1.5 collective-permute-start.4
  119.0 1.3 add_add_fusion
  120.8 6.4 %collective-permute-done.6 = bf16[4,32,1536]{2,1,0:T(8,128)(2,1)S(1)} collective-permute-done((bf16[4,32,1536]{2,1,0:T(8,128)(2,1)S(1)}, bf16[4,32,1536]{2,1,0:T(8,128)(2,1)S(1)}, u32[]{:S(2)}, u32[]{:S(2)}) %collective-permute-start.6) | collective-permute-done | bytes 393248 | tf_op jit(solution)/shard_map/ppermute | solution.py:189
  127.3 2.1 collective-permute-done.4
  129.7 8.9 %collective-permute-done.27 = f32[4,32,1536]{2,1,0:T(8,128)S(1)} collective-permute-done((f32[4,32,1536]{2,1,0:T(8,128)S(1)}, f32[4,32,1536]{2,1,0:T(8,128)S(1)}, u32[]{:S(2)}, u32[]{:S(2)}) %collective-permute-start.27) | collective-permute-done | bytes 786464 | tf_op jit(solution)/shard_map/ppermute | solution.py:189
  140.1 1.6 collective-permute-start.14
  141.7 1.5 collective-permute-start.10
  145.9 1.6 collective-permute-start.46
  148.1 13.5 %collective-permute-done.46 = f32[3072]{0:T(1024)S(1)} collective-permute-done((f32[3072]{0:T(1024)S(1)}, f32[3072]{0:T(1024)S(1)}, u32[]{:S(2)}, u32[]{:S(2)}) %collective-permute-start.46) | collective-permute-done | bytes 12320 | tf_op jit(solution)/shard_map/ppermute | solution.py:189
  162.1 3.2 %collective-permute-done.47 = f32[3072]{0:T(1024)S(1)} collective-permute-done((f32[3072]{0:T(1024)S(1)}, f32[3072]{0:T(1024)S(1)}, u32[]{:S(2)}, u32[]{:S(2)}) %collective-permute-start.47) | collective-permute-done | bytes 12320 | tf_op jit(solution)/shard_map/ppermute | solution.py:189
  166.3 1.6 collective-permute-start.34
  168.3 1.6 collective-permute-start.38
  169.9 7.9 %collective-permute-done.37.refs_8_ = bf16[2,32,3072]{2,1,0:T(8,128)(2,1)S(1)} collective-permute-done((bf16[2,32,3072]{2,1,0:T(8,128)(2,1)S(1)}, bf16[2,32,3072]{2,1,0:T(8,128)(2,1)S(1)}, u32[]{:S(2)}, u32[]{:S(2)}) %collective-permute-start.37) | collective-permute-done | bytes 393248 | tf_op jit(solution)/shard_map/ppermute | solution.py:189
  178.2 1.6 collective-permute-start.18
  179.8 6.9 %collective-permute-done.33.refs_4_ = bf16[2,32,3072]{2,1,0:T(8,128)(2,1)S(1)} collective-permute-done((bf16[2,32,3072]{2,1,0:T(8,128)(2,1)S(1)}, bf16[2,32,3072]{2,1,0:T(8,128)(2,1)S(1)}, u32[]{:S(2)}, u32[]{:S(2)}) %collective-permute-start.33) | collective-permute-done | bytes 393248 | tf_op jit(solution)/shard_map/ppermute | solution.py:189
  186.7 1.6 collective-permute-start.19
  188.8 5.0 %collective-permute-done.18.refs_12_ = bf16[2,32,3072]{2,1,0:T(8,128)(2,1)S(1)} collective-permute-done((bf16[2,32,3072]{2,1,0:T(8,128)(2,1)S(1)}, bf16[2,32,3072]{2,1,0:T(8,128)(2,1)S(1)}, u32[]{:S(2)}, u32[]{:S(2)}) %collective-permute-start.18) | collective-permute-done | bytes 393248 | tf_op jit(solution)/shard_map/ppermute | solution.py:189
  193.9 1.5 collective-permute-done.19.refs_13_
  195.4 1.6 collective-permute-start.41
  196.9 1.5 collective-permute-start.42
  199.2 6.2 %collective-permute-done.41.refs_12_ = bf16[2,32,3072]{2,1,0:T(8,128)(2,1)S(1)} collective-permute-done((bf16[2,32,3072]{2,1,0:T(8,128)(2,1)S(1)}, bf16[2,32,3072]{2,1,0:T(8,128)(2,1)S(1)}, u32[]{:S(2)}, u32[]{:S(2)}) %collective-permute-start.41) | collective-permute-done | bytes 393248 | tf_op jit(solution)/shard_map/ppermute | solution.py:189
  205.4 1.3 collective-permute-done.42.refs_13_
  207.7 2.2 select_reduce_fusion
  211.1 15.6 %norm.1 = (bf16[4,256,3072]{2,1,0:T(8,128)(2,1)}, bf16[4,256,640]{2,1,0:T(8,128)(2,1)}, f32[8192,3072]{1,0:T(8,128)}) custom-call(s32[1]{0:T(128)} %bitcast.me_ref, bf16[1,3072]{1,0:T(2,128)(2,1)S(1)} %reshape.152.g_ref, bf16[3072,640]{1,0:T(8,128)(2,1)S(1)} %copy-done.1, ...), custom_call_target="tpu_custom_call", output_to_operand_aliasing={{2}: (19, {})} | custom-call | flops 30000000 | bytes 40000000 | tf_op jit(solution)/shard_map/norm/pallas_call | solution.py:278
  226.9 2.8 %copy-done.4 = bf16[4,256,3072]{2,1,0:T(8,128)(2,1)S(1)} copy-done((bf16[4,256,3072]{2,1,0:T(8,128)(2,1)S(1)}, bf16[4,256,3072]{2,1,0:T(8,128)(2,1)}, u32[]{:S(2)}) %copy-start.4) | copy-done | bytes 6291480
  229.7 9.8 %dw.1 = (f32[3072,640]{1,0:T(8,128)}, f32[8192,3072]{1,0:T(8,128)}) custom-call(bf16[4,256,3072]{2,1,0:T(8,128)(2,1)S(1)} %copy-done.4, bf16[4,256,640]{2,1,0:T(8,128)(2,1)S(1)} %copy-done.3, f32[8192,3072]{1,0:T(8,128)} %get-tuple-element.66.de_in), custom_call_target="tpu_custom_call", output_to_operand_aliasing={{1}: (2, {})} | custom-call | flops 30000000 | bytes 40000000 | tf_op jit(solution)/shard_map/dw/pallas_call | solution.py:289
  241.0 9.0 %put_rows.1 = f32[8192,3072]{1,0:T(8,128)} custom-call(s32[1]{0:T(128)} %bitcast.me_ref, s32[1024]{0:T(1024)} %get-tuple-element.72.rows_ref, s32[1]{0:T(128)} %bitcast.11.cnt_ref, s32[1,1024]{1,0:T(1,128)} %broadcast_select_fusion.4.slot_ref, bf16[2,32,3072]{2,1,0:T(8,128)(2,1)} %copy-done.13, ...), custom_call_target="tpu_custom_call", output_to_operand_aliasing={{}: (20, {})} | custom-call | tf_op jit(solution)/shard_map/put_rows/pallas_call | solution.py:323
  (161 shorter events, 21.2 us)
Async XLA Ops:
  6.4 45.1 %collective-permute-start.25 = (bf16[1,4,64,1536]{3,2,1,0:T(8,128)(2,1)}, bf16[1,4,64,1536]{3,2,1,0:T(8,128)(2,1)}, u32[]{:S(2)}, u32[]{:S(2)}) collective-permute-start(bf16[1,4,64,1536]{3,2,1,0:T(8,128)(2,1)} %get-tuple-element.57), channel_id=1, source_target_pairs={{0,1},{1,0},{2,3},{3,2},{4,5},{5,4},{6,7},{7,6}} | collective-permute-start | bytes 2359304 | tf_op jit(solution)/shard_map/ppermute | solution.py:189
  12.4 46.9 %collective-permute-start.22 = (bf16[3,4,64,1536]{3,2,1,0:T(8,128)(2,1)}, bf16[3,4,64,1536]{3,2,1,0:T(8,128)(2,1)}, u32[]{:S(2)}, u32[]{:S(2)}) collective-permute-start(bf16[3,4,64,1536]{3,2,1,0:T(8,128)(2,1)} %get-tuple-element.52), channel_id=1, source_target_pairs={{0,1},{1,0},{2,3},{3,2},{4,5},{5,4},{6,7},{7,6}} | collective-permute-start | bytes 7077896 | tf_op jit(solution)/shard_map/ppermute | solution.py:189
  49.2 30.9 %collective-permute-start = (bf16[4,4,64,1536]{3,2,1,0:T(8,128)(2,1)}, bf16[4,4,64,1536]{3,2,1,0:T(8,128)(2,1)}, u32[]{:S(2)}, u32[]{:S(2)}) collective-permute-start(bf16[4,4,64,1536]{3,2,1,0:T(8,128)(2,1)} %get-tuple-element.38), channel_id=1, source_target_pairs={{0,1},{1,0},{2,3},{3,2},{4,5},{5,4},{6,7},{7,6}} | collective-permute-start | bytes 9437192 | tf_op jit(solution)/shard_map/ppermute | solution.py:189
  54.0 21.0 %collective-permute-start.26 = (f32[4,32,1536]{2,1,0:T(8,128)}, f32[4,32,1536]{2,1,0:T(8,128)}, u32[]{:S(2)}, u32[]{:S(2)}) collective-permute-start(f32[4,32,1536]{2,1,0:T(8,128)} %get-tuple-element.99), channel_id=1, source_target_pairs={{0,2},{1,3},{2,0},{3,1},{4,6},{5,7},{6,4},{7,5}} | collective-permute-start | bytes 2359304 | tf_op jit(solution)/shard_map/ppermute | solution.py:189
  56.5 20.0 %collective-permute-start.28 = (f32[4,32,1536]{2,1,0:T(8,128)}, f32[4,32,1536]{2,1,0:T(8,128)}, u32[]{:S(2)}, u32[]{:S(2)}) collective-permute-start(f32[4,32,1536]{2,1,0:T(8,128)} %get-tuple-element.98), channel_id=1, source_target_pairs={{0,4},{1,5},{2,6},{3,7},{4,0},{5,1},{6,2},{7,3}} | collective-permute-start | bytes 2359304 | tf_op jit(solution)/shard_map/ppermute | solution.py:189
  76.6 40.8 %collective-permute-start.23 = (f32[4,32,1536]{2,1,0:T(8,128)S(1)}, f32[4,32,1536]{2,1,0:T(8,128)S(1)}, u32[]{:S(2)}, u32[]{:S(2)}) collective-permute-start(f32[4,32,1536]{2,1,0:T(8,128)S(1)} %convert_add_fusion.3), channel_id=1, source_target_pairs={{0,2},{1,3},{2,0},{3,1},{4,6},{5,7},{6,4},{7,5}} | collective-permute-start | bytes 2359304 | tf_op jit(solution)/shard_map/ppermute | solution.py:189
  77.1 43.2 %collective-permute-start.24 = (f32[4,32,1536]{2,1,0:T(8,128)S(1)}, f32[4,32,1536]{2,1,0:T(8,128)S(1)}, u32[]{:S(2)}, u32[]{:S(2)}) collective-permute-start(f32[4,32,1536]{2,1,0:T(8,128)S(1)} %convert_add_fusion.2), channel_id=1, source_target_pairs={{0,4},{1,5},{2,6},{3,7},{4,0},{5,1},{6,2},{7,3}} | collective-permute-start | bytes 2359304 | tf_op jit(solution)/shard_map/ppermute | solution.py:189
  82.4 23.6 %collective-permute-start.5 = (bf16[4,32,1536]{2,1,0:T(8,128)(2,1)S(1)}, bf16[4,32,1536]{2,1,0:T(8,128)(2,1)S(1)}, u32[]{:S(2)}, u32[]{:S(2)}) collective-permute-start(bf16[4,32,1536]{2,1,0:T(8,128)(2,1)S(1)} %get-tuple-element.100), channel_id=1, source_target_pairs={{0,4},{1,5},{2,6},{3,7},{4,0},{5,1},{6,2},{7,3}} | collective-permute-start | bytes 1179656 | tf_op jit(solution)/shard_map/ppermute | solution.py:189
  83.4 37.3 %collective-permute-start.2 = (bf16[4,32,1536]{2,1,0:T(8,128)(2,1)S(1)}, bf16[4,32,1536]{2,1,0:T(8,128)(2,1)S(1)}, u32[]{:S(2)}, u32[]{:S(2)}) collective-permute-start(bf16[4,32,1536]{2,1,0:T(8,128)(2,1)S(1)} %slice_add_fusion.2), channel_id=1, source_target_pairs={{0,4},{1,5},{2,6},{3,7},{4,0},{5,1},{6,2},{7,3}} | collective-permute-start | bytes 1179656 | tf_op jit(solution)/shard_map/ppermute | solution.py:189
  84.5 36.3 %collective-permute-start.1 = (bf16[4,32,1536]{2,1,0:T(8,128)(2,1)S(1)}, bf16[4,32,1536]{2,1,0:T(8,128)(2,1)S(1)}, u32[]{:S(2)}, u32[]{:S(2)}) collective-permute-start(bf16[4,32,1536]{2,1,0:T(8,128)(2,1)S(1)} %slice_add_fusion.3), channel_id=1, source_target_pairs={{0,2},{1,3},{2,0},{3,1},{4,6},{5,7},{6,4},{7,5}} | collective-permute-start | bytes 1179656 | tf_op jit(solution)/shard_map/ppermute | solution.py:189
  105.9 9.3 %collective-permute-start.3 = (bf16[4,32,1536]{2,1,0:T(8,128)(2,1)S(1)}, bf16[4,32,1536]{2,1,0:T(8,128)(2,1)S(1)}, u32[]{:S(2)}, u32[]{:S(2)}) collective-permute-start(bf16[4,32,1536]{2,1,0:T(8,128)(2,1)S(1)} %get-tuple-element.101), channel_id=1, source_target_pairs={{0,2},{1,3},{2,0},{3,1},{4,6},{5,7},{6,4},{7,5}} | collective-permute-start | bytes 1179656 | tf_op jit(solution)/shard_map/ppermute | solution.py:189
  115.2 12.1 %collective-permute-start.6 = (bf16[4,32,1536]{2,1,0:T(8,128)(2,1)S(1)}, bf16[4,32,1536]{2,1,0:T(8,128)(2,1)S(1)}, u32[]{:S(2)}, u32[]{:S(2)}) collective-permute-start(bf16[4,32,1536]{2,1,0:T(8,128)(2,1)S(1)} %add_add_fusion.4), channel_id=1, source_target_pairs={{0,2},{1,3},{2,0},{3,1},{4,6},{5,7},{6,4},{7,5}} | collective-permute-start | bytes 1179656 | tf_op jit(solution)/shard_map/ppermute | solution.py:189
  117.4 12.0 %collective-permute-start.4 = (bf16[4,32,1536]{2,1,0:T(8,128)(2,1)S(1)}, bf16[4,32,1536]{2,1,0:T(8,128)(2,1)S(1)}, u32[]{:S(2)}, u32[]{:S(2)}) collective-permute-start(bf16[4,32,1536]{2,1,0:T(8,128)(2,1)S(1)} %add_add_fusion.6), channel_id=1, source_target_pairs={{0,4},{1,5},{2,6},{3,7},{4,0},{5,1},{6,2},{7,3}} | collective-permute-start | bytes 1179656 | tf_op jit(solution)/shard_map/ppermute | solution.py:189
  120.3 18.3 %collective-permute-start.27 = (f32[4,32,1536]{2,1,0:T(8,128)S(1)}, f32[4,32,1536]{2,1,0:T(8,128)S(1)}, u32[]{:S(2)}, u32[]{:S(2)}) collective-permute-start(f32[4,32,1536]{2,1,0:T(8,128)S(1)} %add_add_fusion.2), channel_id=1, source_target_pairs={{0,4},{1,5},{2,6},{3,7},{4,0},{5,1},{6,2},{7,3}} | collective-permute-start | bytes 2359304 | tf_op jit(solution)/shard_map/ppermute | solution.py:189
  120.8 18.3 %collective-permute-start.29 = (f32[4,32,1536]{2,1,0:T(8,128)S(1)}, f32[4,32,1536]{2,1,0:T(8,128)S(1)}, u32[]{:S(2)}, u32[]{:S(2)}) collective-permute-start(f32[4,32,1536]{2,1,0:T(8,128)S(1)} %add_add_fusion), channel_id=1, source_target_pairs={{0,2},{1,3},{2,0},{3,1},{4,6},{5,7},{6,4},{7,5}} | collective-permute-start | bytes 2359304 | tf_op jit(solution)/shard_map/ppermute | solution.py:189
  129.7 10.0 %collective-permute-start.7 = (bf16[4,32,1536]{2,1,0:T(8,128)(2,1)S(1)}, bf16[4,32,1536]{2,1,0:T(8,128)(2,1)S(1)}, u32[]{:S(2)}, u32[]{:S(2)}) collective-permute-start(bf16[4,32,1536]{2,1,0:T(8,128)(2,1)S(1)} %broadcast_select_fusion.2), channel_id=1, source_target_pairs={{0,1},{1,0},{2,3},{3,2},{4,5},{5,4},{6,7},{7,6}} | collective-permute-start | bytes 1179656 | tf_op jit(solution)/shard_map/ppermute | solution.py:189
  139.6 4.5 %collective-permute-start.30 = (f32[4,32,1536]{2,1,0:T(8,128)S(1)}, f32[4,32,1536]{2,1,0:T(8,128)S(1)}, u32[]{:S(2)}, u32[]{:S(2)}) collective-permute-start(f32[4,32,1536]{2,1,0:T(8,128)S(1)} %get-tuple-element.82), channel_id=1, source_target_pairs={{0,1},{1,0},{2,3},{3,2},{4,5},{5,4},{6,7},{7,6}} | collective-permute-start | bytes 2359304 | tf_op jit(solution)/shard_map/ppermute | solution.py:189
  140.1 25.2 %collective-permute-start.14 = (bf16[2,32,3072]{2,1,0:T(8,128)(2,1)S(1)}, bf16[2,32,3072]{2,1,0:T(8,128)(2,1)S(1)}, u32[]{:S(2)}, u32[]{:S(2)}) collective-permute-start(bf16[2,32,3072]{2,1,0:T(8,128)(2,1)S(1)} %get-tuple-element.105.refs_0_), channel_id=1, source_target_pairs={{0,4},{1,5},{2,6},{3,7},{4,0},{5,1},{6,2},{7,3}} | collective-permute-start | bytes 1179656 | tf_op jit(solution)/shard_map/ppermute | solution.py:189
  141.7 24.6 %collective-permute-start.10 = (bf16[2,32,3072]{2,1,0:T(8,128)(2,1)S(1)}, bf16[2,32,3072]{2,1,0:T(8,128)(2,1)S(1)}, u32[]{:S(2)}, u32[]{:S(2)}) collective-permute-start(bf16[2,32,3072]{2,1,0:T(8,128)(2,1)S(1)} %get-tuple-element.105.refs_0_), channel_id=1, source_target_pairs={{0,2},{1,3},{2,0},{3,1},{4,6},{5,7},{6,4},{7,5}} | collective-permute-start | bytes 1179656 | tf_op jit(solution)/shard_map/ppermute | solution.py:189
  143.2 22.6 %collective-permute-start.11 = (bf16[2,32,3072]{2,1,0:T(8,128)(2,1)S(1)}, bf16[2,32,3072]{2,1,0:T(8,128)(2,1)S(1)}, u32[]{:S(2)}, u32[]{:S(2)}) collective-permute-start(bf16[2,32,3072]{2,1,0:T(8,128)(2,1)S(1)} %get-tuple-element.104.refs_1_), channel_id=1, source_target_pairs={{0,2},{1,3},{2,0},{3,1},{4,6},{5,7},{6,4},{7,5}} | collective-permute-start | bytes 1179656 | tf_op jit(solution)/shard_map/ppermute | solution.py:189
  143.7 24.1 %collective-permute-start.15 = (bf16[2,32,3072]{2,1,0:T(8,128)(2,1)S(1)}, bf16[2,32,3072]{2,1,0:T(8,128)(2,1)S(1)}, u32[]{:S(2)}, u32[]{:S(2)}) collective-permute-start(bf16[2,32,3072]{2,1,0:T(8,128)(2,1)S(1)} %get-tuple-element.104.refs_1_), channel_id=1, source_target_pairs={{0,4},{1,5},{2,6},{3,7},{4,0},{5,1},{6,2},{7,3}} | collective-permute-start | bytes 1179656 | tf_op jit(solution)/shard_map/ppermute | solution.py:189
  144.7 1.2 collective-permute-start.45
  145.9 15.7 %collective-permute-start.46 = (f32[3072]{0:T(1024)S(1)}, f32[3072]{0:T(1024)S(1)}, u32[]{:S(2)}, u32[]{:S(2)}) collective-permute-start(f32[3072]{0:T(1024)S(1)} %add.164), channel_id=1, source_target_pairs={{0,2},{1,3},{2,0},{3,1},{4,6},{5,7},{6,4},{7,5}} | collective-permute-start | bytes 36872 | tf_op jit(solution)/shard_map/ppermute | solution.py:189
  161.6 3.7 %collective-permute-start.47 = (f32[3072]{0:T(1024)S(1)}, f32[3072]{0:T(1024)S(1)}, u32[]{:S(2)}, u32[]{:S(2)}) collective-permute-start(f32[3072]{0:T(1024)S(1)} %add.165), channel_id=1, source_target_pairs={{0,4},{1,5},{2,6},{3,7},{4,0},{5,1},{6,2},{7,3}} | collective-permute-start | bytes 36872 | tf_op jit(solution)/shard_map/ppermute | solution.py:189
  165.3 3.0 %collective-permute-start.8 = (bf16[2,32,3072]{2,1,0:T(8,128)(2,1)S(1)}, bf16[2,32,3072]{2,1,0:T(8,128)(2,1)S(1)}, u32[]{:S(2)}, u32[]{:S(2)}) collective-permute-start(bf16[2,32,3072]{2,1,0:T(8,128)(2,1)S(1)} %get-tuple-element.105.refs_0_), channel_id=1, source_target_pairs={{0,1},{1,0},{2,3},{3,2},{4,5},{5,4},{6,7},{7,6}} | collective-permute-start | bytes 1179656 | tf_op jit(solution)/shard_map/ppermute | solution.py:189
  165.3 4.6 %collective-permute-start.9 = (bf16[2,32,3072]{2,1,0:T(8,128)(2,1)S(1)}, bf16[2,32,3072]{2,1,0:T(8,128)(2,1)S(1)}, u32[]{:S(2)}, u32[]{:S(2)}) collective-permute-start(bf16[2,32,3072]{2,1,0:T(8,128)(2,1)S(1)} %get-tuple-element.104.refs_1_), channel_id=1, source_target_pairs={{0,1},{1,0},{2,3},{3,2},{4,5},{5,4},{6,7},{7,6}} | collective-permute-start | bytes 1179656 | tf_op jit(solution)/shard_map/ppermute | solution.py:189
  165.8 12.0 %collective-permute-start.37 = (bf16[2,32,3072]{2,1,0:T(8,128)(2,1)S(1)}, bf16[2,32,3072]{2,1,0:T(8,128)(2,1)S(1)}, u32[]{:S(2)}, u32[]{:S(2)}) collective-permute-start(bf16[2,32,3072]{2,1,0:T(8,128)(2,1)S(1)} %get-tuple-element.103.refs_0_), channel_id=1, source_target_pairs={{0,4},{1,5},{2,6},{3,7},{4,0},{5,1},{6,2},{7,3}} | collective-permute-start | bytes 1179656 | tf_op jit(solution)/shard_map/ppermute | solution.py:189
  166.3 12.0 %collective-permute-start.34 = (bf16[2,32,3072]{2,1,0:T(8,128)(2,1)S(1)}, bf16[2,32,3072]{2,1,0:T(8,128)(2,1)S(1)}, u32[]{:S(2)}, u32[]{:S(2)}) collective-permute-start(bf16[2,32,3072]{2,1,0:T(8,128)(2,1)S(1)} %get-tuple-element.102.refs_1_), channel_id=1, source_target_pairs={{0,2},{1,3},{2,0},{3,1},{4,6},{5,7},{6,4},{7,5}} | collective-permute-start | bytes 1179656 | tf_op jit(solution)/shard_map/ppermute | solution.py:189
  167.8 18.8 %collective-permute-start.33 = (bf16[2,32,3072]{2,1,0:T(8,128)(2,1)S(1)}, bf16[2,32,3072]{2,1,0:T(8,128)(2,1)S(1)}, u32[]{:S(2)}, u32[]{:S(2)}) collective-permute-start(bf16[2,32,3072]{2,1,0:T(8,128)(2,1)S(1)} %get-tuple-element.103.refs_0_), channel_id=1, source_target_pairs={{0,2},{1,3},{2,0},{3,1},{4,6},{5,7},{6,4},{7,5}} | collective-permute-start | bytes 1179656 | tf_op jit(solution)/shard_map/ppermute | solution.py:189
  168.3 20.0 %collective-permute-start.38 = (bf16[2,32,3072]{2,1,0:T(8,128)(2,1)S(1)}, bf16[2,32,3072]{2,1,0:T(8,128)(2,1)S(1)}, u32[]{:S(2)}, u32[]{:S(2)}) collective-permute-start(bf16[2,32,3072]{2,1,0:T(8,128)(2,1)S(1)} %get-tuple-element.102.refs_1_), channel_id=1, source_target_pairs={{0,4},{1,5},{2,6},{3,7},{4,0},{5,1},{6,2},{7,3}} | collective-permute-start | bytes 1179656 | tf_op jit(solution)/shard_map/ppermute | solution.py:189
  169.9 18.4 %collective-permute-start.31 = (bf16[2,32,3072]{2,1,0:T(8,128)(2,1)S(1)}, bf16[2,32,3072]{2,1,0:T(8,128)(2,1)S(1)}, u32[]{:S(2)}, u32[]{:S(2)}) collective-permute-start(bf16[2,32,3072]{2,1,0:T(8,128)(2,1)S(1)} %get-tuple-element.103.refs_0_), channel_id=1, source_target_pairs={{0,1},{1,0},{2,3},{3,2},{4,5},{5,4},{6,7},{7,6}} | collective-permute-start | bytes 1179656 | tf_op jit(solution)/shard_map/ppermute | solution.py:189
  177.8 11.0 %collective-permute-start.32 = (bf16[2,32,3072]{2,1,0:T(8,128)(2,1)S(1)}, bf16[2,32,3072]{2,1,0:T(8,128)(2,1)S(1)}, u32[]{:S(2)}, u32[]{:S(2)}) collective-permute-start(bf16[2,32,3072]{2,1,0:T(8,128)(2,1)S(1)} %get-tuple-element.102.refs_1_), channel_id=1, source_target_pairs={{0,1},{1,0},{2,3},{3,2},{4,5},{5,4},{6,7},{7,6}} | collective-permute-start | bytes 1179656 | tf_op jit(solution)/shard_map/ppermute | solution.py:189
  178.2 15.6 %collective-permute-start.18 = (bf16[2,32,3072]{2,1,0:T(8,128)(2,1)S(1)}, bf16[2,32,3072]{2,1,0:T(8,128)(2,1)S(1)}, u32[]{:S(2)}, u32[]{:S(2)}) collective-permute-start(bf16[2,32,3072]{2,1,0:T(8,128)(2,1)S(1)} %collective-permute-done.14.refs_8_), channel_id=1, source_target_pairs={{0,2},{1,3},{2,0},{3,1},{4,6},{5,7},{6,4},{7,5}} | collective-permute-start | bytes 1179656 | tf_op jit(solution)/shard_map/ppermute | solution.py:189
  186.7 8.7 %collective-permute-start.19 = (bf16[2,32,3072]{2,1,0:T(8,128)(2,1)S(1)}, bf16[2,32,3072]{2,1,0:T(8,128)(2,1)S(1)}, u32[]{:S(2)}, u32[]{:S(2)}) collective-permute-start(bf16[2,32,3072]{2,1,0:T(8,128)(2,1)S(1)} %collective-permute-done.11.refs_5_), channel_id=1, source_target_pairs={{0,4},{1,5},{2,6},{3,7},{4,0},{5,1},{6,2},{7,3}} | collective-permute-start | bytes 1179656 | tf_op jit(solution)/shard_map/ppermute | solution.py:189
  188.3 8.6 %collective-permute-start.12 = (bf16[2,32,3072]{2,1,0:T(8,128)(2,1)S(1)}, bf16[2,32,3072]{2,1,0:T(8,128)(2,1)S(1)}, u32[]{:S(2)}, u32[]{:S(2)}) collective-permute-start(bf16[2,32,3072]{2,1,0:T(8,128)(2,1)S(1)} %collective-permute-done.10.refs_4_), channel_id=1, source_target_pairs={{0,1},{1,0},{2,3},{3,2},{4,5},{5,4},{6,7},{7,6}} | collective-permute-start | bytes 1179656 | tf_op jit(solution)/shard_map/ppermute | solution.py:189
  188.3 10.1 %collective-permute-start.13 = (bf16[2,32,3072]{2,1,0:T(8,128)(2,1)S(1)}, bf16[2,32,3072]{2,1,0:T(8,128)(2,1)S(1)}, u32[]{:S(2)}, u32[]{:S(2)}) collective-permute-start(bf16[2,32,3072]{2,1,0:T(8,128)(2,1)S(1)} %collective-permute-done.11.refs_5_), channel_id=1, source_target_pairs={{0,1},{1,0},{2,3},{3,2},{4,5},{5,4},{6,7},{7,6}} | collective-permute-start | bytes 1179656 | tf_op jit(solution)/shard_map/ppermute | solution.py:189
  188.8 9.7 %collective-permute-start.16 = (bf16[2,32,3072]{2,1,0:T(8,128)(2,1)S(1)}, bf16[2,32,3072]{2,1,0:T(8,128)(2,1)S(1)}, u32[]{:S(2)}, u32[]{:S(2)}) collective-permute-start(bf16[2,32,3072]{2,1,0:T(8,128)(2,1)S(1)} %collective-permute-done.14.refs_8_), channel_id=1, source_target_pairs={{0,1},{1,0},{2,3},{3,2},{4,5},{5,4},{6,7},{7,6}} | collective-permute-start | bytes 1179656 | tf_op jit(solution)/shard_map/ppermute | solution.py:189
  193.9 5.1 %collective-permute-start.17 = (bf16[2,32,3072]{2,1,0:T(8,128)(2,1)S(1)}, bf16[2,32,3072]{2,1,0:T(8,128)(2,1)S(1)}, u32[]{:S(2)}, u32[]{:S(2)}) collective-permute-start(bf16[2,32,3072]{2,1,0:T(8,128)(2,1)S(1)} %collective-permute-done.15.refs_9_), channel_id=1, source_target_pairs={{0,1},{1,0},{2,3},{3,2},{4,5},{5,4},{6,7},{7,6}} | collective-permute-start | bytes 1179656 | tf_op jit(solution)/shard_map/ppermute | solution.py:189
  195.4 10.1 %collective-permute-start.41 = (bf16[2,32,3072]{2,1,0:T(8,128)(2,1)S(1)}, bf16[2,32,3072]{2,1,0:T(8,128)(2,1)S(1)}, u32[]{:S(2)}, u32[]{:S(2)}) collective-permute-start(bf16[2,32,3072]{2,1,0:T(8,128)(2,1)S(1)} %collective-permute-done.37.refs_8_), channel_id=1, source_target_pairs={{0,2},{1,3},{2,0},{3,1},{4,6},{5,7},{6,4},{7,5}} | collective-permute-start | bytes 1179656 | tf_op jit(solution)/shard_map/ppermute | solution.py:189
  196.9 9.8 %collective-permute-start.42 = (bf16[2,32,3072]{2,1,0:T(8,128)(2,1)S(1)}, bf16[2,32,3072]{2,1,0:T(8,128)(2,1)S(1)}, u32[]{:S(2)}, u32[]{:S(2)}) collective-permute-start(bf16[2,32,3072]{2,1,0:T(8,128)(2,1)S(1)} %collective-permute-done.34.refs_5_), channel_id=1, source_target_pairs={{0,4},{1,5},{2,6},{3,7},{4,0},{5,1},{6,2},{7,3}} | collective-permute-start | bytes 1179656 | tf_op jit(solution)/shard_map/ppermute | solution.py:189
  198.5 8.3 %collective-permute-start.35 = (bf16[2,32,3072]{2,1,0:T(8,128)(2,1)S(1)}, bf16[2,32,3072]{2,1,0:T(8,128)(2,1)S(1)}, u32[]{:S(2)}, u32[]{:S(2)}) collective-permute-start(bf16[2,32,3072]{2,1,0:T(8,128)(2,1)S(1)} %collective-permute-done.33.refs_4_), channel_id=1, source_target_pairs={{0,1},{1,0},{2,3},{3,2},{4,5},{5,4},{6,7},{7,6}} | collective-permute-start | bytes 1179656 | tf_op jit(solution)/shard_map/ppermute | solution.py:189
  198.5 8.8 %collective-permute-start.20 = (bf16[2,32,3072]{2,1,0:T(8,128)(2,1)S(1)}, bf16[2,32,3072]{2,1,0:T(8,128)(2,1)S(1)}, u32[]{:S(2)}, u32[]{:S(2)}) collective-permute-start(bf16[2,32,3072]{2,1,0:T(8,128)(2,1)S(1)} %collective-permute-done.18.refs_12_), channel_id=1, source_target_pairs={{0,1},{1,0},{2,3},{3,2},{4,5},{5,4},{6,7},{7,6}} | collective-permute-start | bytes 1179656 | tf_op jit(solution)/shard_map/ppermute | solution.py:189
  199.0 8.3 %collective-permute-start.21 = (bf16[2,32,3072]{2,1,0:T(8,128)(2,1)S(1)}, bf16[2,32,3072]{2,1,0:T(8,128)(2,1)S(1)}, u32[]{:S(2)}, u32[]{:S(2)}) collective-permute-start(bf16[2,32,3072]{2,1,0:T(8,128)(2,1)S(1)} %collective-permute-done.19.refs_13_), channel_id=1, source_target_pairs={{0,1},{1,0},{2,3},{3,2},{4,5},{5,4},{6,7},{7,6}} | collective-permute-start | bytes 1179656 | tf_op jit(solution)/shard_map/ppermute | solution.py:189
  205.4 34.1 %collective-permute-start.36 = (bf16[2,32,3072]{2,1,0:T(8,128)(2,1)S(1)}, bf16[2,32,3072]{2,1,0:T(8,128)(2,1)S(1)}, u32[]{:S(2)}, u32[]{:S(2)}) collective-permute-start(bf16[2,32,3072]{2,1,0:T(8,128)(2,1)S(1)} %collective-permute-done.34.refs_5_), channel_id=1, source_target_pairs={{0,1},{1,0},{2,3},{3,2},{4,5},{5,4},{6,7},{7,6}} | collective-permute-start | bytes 1179656 | tf_op jit(solution)/shard_map/ppermute | solution.py:189
  206.7 32.8 %collective-permute-start.39 = (bf16[2,32,3072]{2,1,0:T(8,128)(2,1)S(1)}, bf16[2,32,3072]{2,1,0:T(8,128)(2,1)S(1)}, u32[]{:S(2)}, u32[]{:S(2)}) collective-permute-start(bf16[2,32,3072]{2,1,0:T(8,128)(2,1)S(1)} %collective-permute-done.37.refs_8_), channel_id=1, source_target_pairs={{0,1},{1,0},{2,3},{3,2},{4,5},{5,4},{6,7},{7,6}} | collective-permute-start | bytes 1179656 | tf_op jit(solution)/shard_map/ppermute | solution.py:189
  206.7 32.8 %collective-permute-start.40 = (bf16[2,32,3072]{2,1,0:T(8,128)(2,1)S(1)}, bf16[2,32,3072]{2,1,0:T(8,128)(2,1)S(1)}, u32[]{:S(2)}, u32[]{:S(2)}) collective-permute-start(bf16[2,32,3072]{2,1,0:T(8,128)(2,1)S(1)} %collective-permute-done.38.refs_9_), channel_id=1, source_target_pairs={{0,1},{1,0},{2,3},{3,2},{4,5},{5,4},{6,7},{7,6}} | collective-permute-start | bytes 1179656 | tf_op jit(solution)/shard_map/ppermute | solution.py:189
  207.2 32.3 %collective-permute-start.43 = (bf16[2,32,3072]{2,1,0:T(8,128)(2,1)S(1)}, bf16[2,32,3072]{2,1,0:T(8,128)(2,1)S(1)}, u32[]{:S(2)}, u32[]{:S(2)}) collective-permute-start(bf16[2,32,3072]{2,1,0:T(8,128)(2,1)S(1)} %collective-permute-done.41.refs_12_), channel_id=1, source_target_pairs={{0,1},{1,0},{2,3},{3,2},{4,5},{5,4},{6,7},{7,6}} | collective-permute-start | bytes 1179656 | tf_op jit(solution)/shard_map/ppermute | solution.py:189
  207.3 32.3 %collective-permute-start.44 = (bf16[2,32,3072]{2,1,0:T(8,128)(2,1)S(1)}, bf16[2,32,3072]{2,1,0:T(8,128)(2,1)S(1)}, u32[]{:S(2)}, u32[]{:S(2)}) collective-permute-start(bf16[2,32,3072]{2,1,0:T(8,128)(2,1)S(1)} %collective-permute-done.42.refs_13_), channel_id=1, source_target_pairs={{0,1},{1,0},{2,3},{3,2},{4,5},{5,4},{6,7},{7,6}} | collective-permute-start | bytes 1179656 | tf_op jit(solution)/shard_map/ppermute | solution.py:189
  (32 other events, 649.6 us)
where the time goes:
time: 251 us; the launch traced here: 250 us
  waiting for transfers between devices  108 us (43%)
  Pallas kernels  74.8 us (30%)
  starting transfers between devices  35.4 us (14%)
  local copies, waits for them, and re-layouts  16.9 us (7%)
  other arithmetic  14 us (6%)
    ppermute x48, waiting for transfers between devices, swap(): return lax.ppermute(v, 'tp', [(i, i ^ bit) for i in range(groups)])  108 us
    ppermute x48, starting transfers between devices, swap(): return lax.ppermute(v, 'tp', [(i, i ^ bit) for i in range(groups)])  35.4 us
    pallas_call x1, Pallas kernels, local(): pl.pallas_call(lookup_kernel, out_shape=(half_shape(4), half_shape(4), de...  32.9 us
    pallas_call x1, Pallas kernels, local(): pl.pallas_call(norm_kernel, out_shape=(jax.ShapeDtypeStruct((mb, t, d), j...  15.6 us
    pallas_call x1, Pallas kernels, local(): pl.pallas_call(dw_kernel, out_shape=(jax.ShapeDtypeStruct((d, f), jnp.flo...  9.8 us
    unnamed x69, local copies, waits for them, and re-layouts  9.77 us
    pallas_call x1, Pallas kernels, local(): pl.pallas_call(scatter_kernel, out_shape=de_shape, in_specs=[SMEM, SMEM,...  8.99 us
    pallas_call x2, Pallas kernels, pdn(): pl.pallas_call(functools.partial(pdn_kernel, js), out_shape=(half_shape(l...  7.46 us
  transfers between devices with their start and end apart: 48, of which 18 were waited for; matrix products, arithmetic and copies ran while one was open for 9% of the time, Pallas kernels for 25%

commit v1 on v0

--- a/solution.py
+++ b/solution.py
@@ -12,17 +12,18 @@
 VMEM = pl.BlockSpec(memory_space=pltpu.VMEM)
 SMEM = pl.BlockSpec(memory_space=pltpu.SMEM)
 ZR = 128
-BLK = 128
-LOOKUP_SHARE, NORM_SHARE = 40, 12
+BLK = 256
+LOOKUP_EARLY, LOOKUP_SHARE, NORM_SHARE = 14, 28, 20
 
 
 def zero_fill(de, z, sem, first, last):
-    z[...] = jnp.zeros_like(z)
 
     def copy(i):
         return pltpu.make_async_copy(z, de.at[pl.ds(pl.multiple_of(i * ZR, ZR), ZR)], sem)
 
-    def start():
+    def start(clear=True):
+        if clear:
+            z[...] = jnp.zeros_like(z)
         pl.loop(first, last)(lambda i: copy(i).start())
 
     def wait():
@@ -53,7 +54,9 @@
     nj, mb, tc, hd = mine_ref.shape
     n = nj * mb * tc
     step = 64
-    start, wait = zero_fill(de, z, zsem, 0, LOOKUP_SHARE)
+    start, wait = zero_fill(de, z, zsem, 0, LOOKUP_EARLY)
+    late_start, late_wait = zero_fill(de, z, zsem, LOOKUP_EARLY, LOOKUP_SHARE)
+    start()
 
     @pl.loop(0, 2 * n // step)
     def _(i):
@@ -77,11 +80,12 @@
         return cnt
 
     cnt = lax.fori_loop(0, n // 8, issue, jnp.int32(0))
-    start()
 
     @pl.loop(0, cnt)
     def _(i):
         copy(0, 0).wait()
+
+    late_start(False)
 
     for j in range(nj):
         zc = jnp.bitwise_xor(c, j)
@@ -97,6 +101,7 @@
                 out[j, m] = jnp.dot(sel, v, preferred_element_type=jnp.float32).astype(jnp.bfloat16)
 
     wait()
+    late_wait()
 
 
 def pull(me, blocks, buf, sem):
@@ -111,12 +116,25 @@
     return copies
 
 
-def norm_kernel(me_ref, g_ref, w_ref, *refs):
+def pull_halves(k, c, blocks, buf, sem):
+    tl, hd = blocks[0].shape[1:]
+    copies = []
+    for i, b in enumerate(blocks):
+        j, h, q = i // 4, (i // 2) % 2, i % 2
+        s = pl.multiple_of((2 * jnp.bitwise_xor(c, j) + h) * tl, tl)
+        o = pl.multiple_of(jnp.bitwise_xor(k, q) * hd, 128)
+        copies.append(pltpu.make_async_copy(b, buf.at[:, pl.ds(s, tl), pl.ds(o, hd)], sem.at[i]))
+    for c in copies:
+        c.start()
+    return copies
+
+
+def norm_kernel(kc_ref, g_ref, w_ref, *refs):
     blocks, (de_in, n_ref, u_ref, de, sem, z, zsem) = refs[:16], refs[16:]
     del de_in
     mb, t, _ = n_ref.shape
     start, wait = zero_fill(de, z, zsem, LOOKUP_SHARE, LOOKUP_SHARE + NORM_SHARE)
-    copies = pull(me_ref[0], blocks, n_ref, sem)
+    copies = pull_halves(kc_ref[0], kc_ref[1], blocks, n_ref, sem)
     start()
     for c in copies:
         c.wait()
@@ -233,23 +251,24 @@
             fy = swap(part(2, 0) + dx_, 4)
             fx = swap(part(1, 1) + dy_, 2)
             pairs[0], ex, ey = lax.optimization_barrier((pairs[0], ex, ey))
-            s0 = part(0, 0) + ex + fy
-            s1 = part(0, 1) + ey + fx
+            return part(0, 0) + ex + fy, part(0, 1) + ey + fx
+
+        def to_rows(mine, other):
+            return jnp.where(k == 0, jnp.concatenate([mine, other], -1), jnp.concatenate([other, mine], -1))
+
+        def go_home(s0, s1):
             keep = jnp.where(k == 0, s0, s1)
             give = jnp.where(k == 0, s1, s0)
-            other = swap(give, 1)
-            return jnp.where(k == 0, jnp.concatenate([keep, other], -1), jnp.concatenate([other, keep], -1))
-
-        def gather_all(v):
-            h = v.shape[0] // 2
-            own = (v[:h], v[h:])
+            return to_rows(keep, swap(give, 1))
+
+        def gather_all(own):
             x1, y0 = swap(own[1], 2), swap(own[0], 4)
             x0, y1 = swap(own[0], 2), swap(own[1], 4)
             d1, d0 = swap(x1, 4), swap(y0, 2)
             out = {0: own, 2: (x0, x1), 4: (y0, y1), 6: (d0, d1)}
             for j in (0, 2, 4, 6):
                 out[j + 1] = tuple(swap(b, 1) for b in out[j])
-            return [b for j in range(8) for b in out[j]]
+            return out
 
         flat = ids.reshape(-1)
         n = flat.shape[0]
@@ -271,9 +290,22 @@
         got = swap(theirs, 1)
         xpairs = {j: (mine[j], got[j]) for j in range(4)}
 
-        dn = reduce_to_home(pairs, jnp.float32)
-        x = reduce_to_home(xpairs, jnp.bfloat16)
-        xs = gather_all(x)
+        dn = go_home(*reduce_to_home(pairs, jnp.float32))
+        i0 = lax.broadcasted_iota(jnp.int32, (n, n), 0)
+        i1 = lax.broadcasted_iota(jnp.int32, (n, n), 1)
+        same = flat[:, None] == flat[None, :]
+        first = jnp.min(jnp.where(same, i0, n), axis=0)
+        lead = own & (first == jnp.arange(n))
+        pos = jnp.sum(jnp.where(lead[:, None] & (i0 < i1), 1, 0), axis=0)
+        pos_of_first = jnp.sum(jnp.where((i0 == first[None, :]), pos[:, None], 0), axis=0)
+        slot = jnp.where(own, pos_of_first, -1).astype(jnp.int32)
+        rows = jnp.sum(jnp.where(lead[:, None] & (pos[:, None] == i1), loc[:, None], 0), axis=0).astype(jnp.int32)
+        cnt = jnp.sum(lead.astype(jnp.int32)).reshape(1)
+        x0, x1 = reduce_to_home(xpairs, jnp.bfloat16)
+        x0, x1, slot, rows, cnt = lax.optimization_barrier((x0, x1, slot, rows, cnt))
+        xo = gather_all((x0, x1))
+        xs = [xo[2 * j + q][h] for j in range(4) for h in range(2) for q in range(2)]
+        x = to_rows(jnp.where(k == 0, x0, x1), jnp.where(k == 0, xo[1][0], xo[1][1]))
 
         nn, u, de = pl.pallas_call(
             norm_kernel,
@@ -285,7 +317,7 @@
             cost_estimate=pl.CostEstimate(flops=30_000_000, bytes_accessed=40_000_000, transcendentals=0),
             compiler_params=pltpu.CompilerParams(vmem_limit_bytes=40 * 2**20),
             name="norm",
-        )(me, g.reshape(1, d), w, *xs, de)
+        )(kc, g.reshape(1, d), w, *xs, de)
         dw, de = pl.pallas_call(
             dw_kernel,
             out_shape=(jax.ShapeDtypeStruct((d, f), jnp.float32), de_shape),
@@ -305,20 +337,10 @@
         dxn = rs * (gdn - nh * jnp.mean(nh * gdn, axis=-1, keepdims=True))
         dx = (dres.astype(jnp.float32) + dxn).astype(jnp.bfloat16)
         dg = jnp.sum(dn * nh, axis=(0, 1))
-        dxs = gather_all(dx)
+        dxo = gather_all((dx[:mb // 2], dx[mb // 2:]))
+        dxs = [b for j in range(8) for b in dxo[j]]
         for bit in (1, 2, 4):
             dg = dg + swap(dg, bit)
-
-        i0 = lax.broadcasted_iota(jnp.int32, (n, n), 0)
-        i1 = lax.broadcasted_iota(jnp.int32, (n, n), 1)
-        same = flat[:, None] == flat[None, :]
-        first = jnp.min(jnp.where(same, i0, n), axis=0)
-        lead = own & (first == jnp.arange(n))
-        pos = jnp.sum(jnp.where(lead[:, None] & (i0 < i1), 1, 0), axis=0)
-        pos_of_first = jnp.sum(jnp.where((i0 == first[None, :]), pos[:, None], 0), axis=0)
-        slot = jnp.where(own, pos_of_first, -1).astype(jnp.int32)
-        rows = jnp.sum(jnp.where(lead[:, None] & (pos[:, None] == i1), loc[:, None], 0), axis=0).astype(jnp.int32)
-        cnt = jnp.sum(lead.astype(jnp.int32)).reshape(1)
 
         de = pl.pallas_call(
             scatter_kernel,

time: 251 us -> 238 us (0.948)
  Pallas kernels: 74.8 us -> 64.6 us
    pallas_call x1, Pallas kernels: 32.9 us -> 21.8 us  [local(): pl.pallas_call(lookup_kernel, out_shape=(half_shape(4), half_shape(4), de...]
    ppermute x48 -> x47, waiting for transfers between devices: 108 us -> 110 us  [swap(): return lax.ppermute(v, 'tp', [(i, i ^ bit) for i in range(groups)])]
    ppermute x48 -> x47, starting transfers between devices: 35.4 us -> 33.9 us  [swap(): return lax.ppermute(v, 'tp', [(i, i ^ bit) for i in range(groups)])]
    unnamed x69 -> x63, local copies, waits for them, and re-layouts: 9.77 us -> 9.05 us
  transfers between devices with their start and end apart: 48 -> 47, of which waited for: 18 -> 16; matrix products, arithmetic and copies ran while one was open for 9% -> 8% of each run, Pallas kernels for 25% -> 23%
where the time goes in v1:
time: 238 us; the launch traced here: 237 us
  waiting for transfers between devices  110 us (46%)
  Pallas kernels  64.6 us (27%)
  starting transfers between devices  33.9 us (14%)
  local copies, waits for them, and re-layouts  15.7 us (7%)
  other arithmetic  11.7 us (5%)
    ppermute x47, waiting for transfers between devices, swap(): return lax.ppermute(v, 'tp', [(i, i ^ bit) for i in range(groups)])  110 us
    ppermute x47, starting transfers between devices, swap(): return lax.ppermute(v, 'tp', [(i, i ^ bit) for i in range(groups)])  33.9 us
    pallas_call x1, Pallas kernels, local(): pl.pallas_call(lookup_kernel, out_shape=(half_shape(4), half_shape(4), de...  21.8 us
    pallas_call x1, Pallas kernels, local(): pl.pallas_call(norm_kernel, out_shape=(jax.ShapeDtypeStruct((mb, t, d), j...  15.1 us
    pallas_call x1, Pallas kernels, local(): pl.pallas_call(dw_kernel, out_shape=(jax.ShapeDtypeStruct((d, f), jnp.flo...  11.7 us
    unnamed x63, local copies, waits for them, and re-layouts  9.05 us
    pallas_call x1, Pallas kernels, local(): pl.pallas_call(scatter_kernel, out_shape=de_shape, in_specs=[SMEM, SMEM,...  8.52 us
    pallas_call x2, Pallas kernels, pdn(): pl.pallas_call(functools.partial(pdn_kernel, js), out_shape=(half_shape(l...  7.45 us
  transfers between devices with their start and end apart: 47, of which 16 were waited for; matrix products, arithmetic and copies ran while one was open for 8% of the time, Pallas kernels for 23%

profile of v1, /device:TPU:0, one launch (start us, length us, event | category | flops | bytes accessed | tf_op | source)
XLA Modules:
  0.0 237.4 jit_solution(14436307132744008319)
XLA Ops:
  0.7 2.1 copy-done
  2.8 1.3 copy-done.2
  4.1 2.2 shard_map.102
  7.2 5.2 %shard_map.101 = (bf16[3,4,64,1536]{3,2,1,0:T(8,128)(2,1)S(1)}, bf16[3,4,64,1536]{3,2,1,0:T(8,128)(2,1)}) custom-call(s32[2]{0:T(128)S(1)} %pad_add_fusion.kc_ref, bf16[4,256,640]{2,1,0:T(8,128)(2,1)S(1)} %copy-done.2, bf16[3072,640]{1,0:T(8,128)(2,1)S(1)} %copy-done), custom_call_target="tpu_custom_call" | custom-call | flops 15000000 | bytes 8000000 | tf_op jit(solution)/shard_map/pallas_call | solution.py:228
  13.8 1.0 copy.22
  15.1 1.2 fusion.14.tgt_ref
  16.3 21.8 %lookup.1 = (bf16[4,4,64,1536]{3,2,1,0:T(8,128)(2,1)S(1)}, bf16[4,4,64,1536]{3,2,1,0:T(8,128)(2,1)}, f32[8192,3072]{1,0:T(8,128)}) custom-call(s32[2]{0:T(128)S(1)} %pad_add_fusion.kc_ref, s32[1024]{0:T(1024)S(1)} %get-tuple-element.89.loc_ref, s32[1024,1]{1,0:T(8,128)S(1)} %fusion.14.tgt_ref, bf16[8192,3072]{1,0:T(8,128)(2,1)} %emb.1), custom_call_target="tpu_custom_call" | custom-call | flops 40000000 | bytes 60000000 | tf_op jit(solution)/shard_map/lookup/pallas_call | solution.py:280
  38.7 1.5 slice_bitcast_fusion.8
  40.5 1.2 slice_bitcast_fusion.12
  41.7 2.5 %convert_add_fusion = (f32[4,32,1536]{2,1,0:T(8,128)}, f32[4,32,1536]{2,1,0:T(8,128)}) fusion(bf16[4,64,1536]{2,1,0:T(8,128)(2,1)} %bitcast.20, bf16[4,64,1536]{2,1,0:T(8,128)(2,1)S(1)} %bitcast.48), kind=kLoop, calls=%fused_computation.31 | loop fusion | flops 1179648 | bytes 3145728 | tf_op jit(solution)/shard_map/add | solution.py:242
  44.2 2.4 %collective-permute-start.25 = (f32[4,32,1536]{2,1,0:T(8,128)}, f32[4,32,1536]{2,1,0:T(8,128)S(1)}, u32[]{:S(2)}, u32[]{:S(2)}) collective-permute-start(f32[4,32,1536]{2,1,0:T(8,128)} %get-tuple-element.107), channel_id=1, source_target_pairs={{0,2},{1,3},{2,0},{3,1},{4,6},{5,7},{6,4},{7,5}} | collective-permute-start | bytes 2359304 | tf_op jit(solution)/shard_map/ppermute | solution.py:207
  46.6 2.2 select_reduce_fusion
  50.4 1.8 slice_bitcast_fusion.1
  52.2 12.8 %collective-permute-done.25 = f32[4,32,1536]{2,1,0:T(8,128)S(1)} collective-permute-done((f32[4,32,1536]{2,1,0:T(8,128)}, f32[4,32,1536]{2,1,0:T(8,128)S(1)}, u32[]{:S(2)}, u32[]{:S(2)}) %collective-permute-start.25) | collective-permute-done | bytes 786464 | tf_op jit(solution)/shard_map/ppermute | solution.py:207
  65.1 1.8 collective-permute-start.22
  67.0 1.0 collective-permute-start.23
  68.2 1.0 collective-permute-start.26
  69.7 15.9 %collective-permute-done.22 = f32[4,32,1536]{2,1,0:T(8,128)S(1)} collective-permute-done((f32[4,32,1536]{2,1,0:T(8,128)S(1)}, f32[4,32,1536]{2,1,0:T(8,128)S(1)}, u32[]{:S(2)}, u32[]{:S(2)}) %collective-permute-start.22) | collective-permute-done | bytes 786464 | tf_op jit(solution)/shard_map/ppermute | solution.py:207
  85.6 1.9 collective-permute-done.23
  87.4 2.1 slice_bitcast_fusion.5
  90.0 1.5 collective-permute-start.2
  91.5 1.3 collective-permute-start.1
  92.8 18.0 %collective-permute-done.3 = bf16[4,32,1536]{2,1,0:T(8,128)(2,1)S(1)} collective-permute-done((bf16[4,32,1536]{2,1,0:T(8,128)(2,1)S(1)}, bf16[4,32,1536]{2,1,0:T(8,128)(2,1)S(1)}, u32[]{:S(2)}, u32[]{:S(2)}) %collective-permute-start.3) | collective-permute-done | bytes 393248 | tf_op jit(solution)/shard_map/ppermute | solution.py:207
  110.8 1.5 collective-permute-start.5
  112.4 7.8 %collective-permute-done.5 = bf16[4,32,1536]{2,1,0:T(8,128)(2,1)S(1)} collective-permute-done((bf16[4,32,1536]{2,1,0:T(8,128)(2,1)S(1)}, bf16[4,32,1536]{2,1,0:T(8,128)(2,1)S(1)}, u32[]{:S(2)}, u32[]{:S(2)}) %collective-permute-start.5) | collective-permute-done | bytes 393248 | tf_op jit(solution)/shard_map/ppermute | solution.py:207
  120.1 1.5 collective-permute-start.4
  121.7 1.3 collective-permute-start.6
  123.5 4.8 %collective-permute-done.4 = bf16[4,32,1536]{2,1,0:T(8,128)(2,1)S(1)} collective-permute-done((bf16[4,32,1536]{2,1,0:T(8,128)(2,1)S(1)}, bf16[4,32,1536]{2,1,0:T(8,128)(2,1)S(1)}, u32[]{:S(2)}, u32[]{:S(2)}) %collective-permute-start.4) | collective-permute-done | bytes 393248 | tf_op jit(solution)/shard_map/ppermute | solution.py:207
  128.3 1.2 collective-permute-done.6
  130.5 1.7 collective-permute-start.11
  132.7 1.3 collective-permute-start.15
  135.1 6.6 %collective-permute-done.13.refs_8_ = bf16[4,32,1536]{2,1,0:T(8,128)(2,1)S(1)} collective-permute-done((bf16[4,32,1536]{2,1,0:T(8,128)(2,1)S(1)}, bf16[4,32,1536]{2,1,0:T(8,128)(2,1)S(1)}, u32[]{:S(2)}, u32[]{:S(2)}) %collective-permute-start.13) | collective-permute-done | bytes 393248 | tf_op jit(solution)/shard_map/ppermute | solution.py:207
  141.7 1.3 collective-permute-start.17
  144.0 1.2 collective-permute-start.45
  145.9 13.1 %collective-permute-done.45 = f32[3072]{0:T(1024)S(1)} collective-permute-done((f32[3072]{0:T(1024)S(1)}, f32[3072]{0:T(1024)S(1)}, u32[]{:S(2)}, u32[]{:S(2)}) %collective-permute-start.45) | collective-permute-done | bytes 12320 | tf_op jit(solution)/shard_map/ppermute | solution.py:207
  159.0 1.5 collective-permute-start.46
  161.0 1.6 collective-permute-done.46
  163.2 1.5 collective-permute-start.36
  164.6 1.3 collective-permute-start.33
  167.2 7.9 %collective-permute-done.36.refs_8_ = bf16[2,32,3072]{2,1,0:T(8,128)(2,1)S(1)} collective-permute-done((bf16[2,32,3072]{2,1,0:T(8,128)(2,1)S(1)}, bf16[2,32,3072]{2,1,0:T(8,128)(2,1)S(1)}, u32[]{:S(2)}, u32[]{:S(2)}) %collective-permute-start.36) | collective-permute-done | bytes 393248 | tf_op jit(solution)/shard_map/ppermute | solution.py:207
  175.2 1.5 collective-permute-done.33.refs_5_
  176.6 7.2 %collective-permute-done.32.refs_4_ = bf16[2,32,3072]{2,1,0:T(8,128)(2,1)S(1)} collective-permute-done((bf16[2,32,3072]{2,1,0:T(8,128)(2,1)S(1)}, bf16[2,32,3072]{2,1,0:T(8,128)(2,1)S(1)}, u32[]{:S(2)}, u32[]{:S(2)}) %collective-permute-start.32) | collective-permute-done | bytes 393248 | tf_op jit(solution)/shard_map/ppermute | solution.py:207
  183.9 1.3 collective-permute-start.40
  186.7 8.6 %collective-permute-done.40.refs_12_ = bf16[2,32,3072]{2,1,0:T(8,128)(2,1)S(1)} collective-permute-done((bf16[2,32,3072]{2,1,0:T(8,128)(2,1)S(1)}, bf16[2,32,3072]{2,1,0:T(8,128)(2,1)S(1)}, u32[]{:S(2)}, u32[]{:S(2)}) %collective-permute-start.40) | collective-permute-done | bytes 393248 | tf_op jit(solution)/shard_map/ppermute | solution.py:207
  197.5 15.1 %norm.1 = (bf16[4,256,3072]{2,1,0:T(8,128)(2,1)}, bf16[4,256,640]{2,1,0:T(8,128)(2,1)}, f32[8192,3072]{1,0:T(8,128)}) custom-call(s32[2]{0:T(128)S(1)} %pad_add_fusion.kc_ref, bf16[1,3072]{1,0:T(2,128)(2,1)S(1)} %reshape.120.g_ref, bf16[3072,640]{1,0:T(8,128)(2,1)S(1)} %copy-done.1, ...), custom_call_target="tpu_custom_call", output_to_operand_aliasing={{2}: (19, {})} | custom-call | flops 30000000 | bytes 40000000 | tf_op jit(solution)/shard_map/norm/pallas_call | solution.py:310
  212.8 2.8 %copy-done.4 = bf16[4,256,3072]{2,1,0:T(8,128)(2,1)S(1)} copy-done((bf16[4,256,3072]{2,1,0:T(8,128)(2,1)S(1)}, bf16[4,256,3072]{2,1,0:T(8,128)(2,1)}, u32[]{:S(2)}) %copy-start.4) | copy-done | bytes 6291480
  215.5 11.7 %dw.1 = (f32[3072,640]{1,0:T(8,128)}, f32[8192,3072]{1,0:T(8,128)}) custom-call(bf16[4,256,3072]{2,1,0:T(8,128)(2,1)S(1)} %copy-done.4, bf16[4,256,640]{2,1,0:T(8,128)(2,1)S(1)} %copy-done.3, f32[8192,3072]{1,0:T(8,128)} %get-tuple-element.76.de_in), custom_call_target="tpu_custom_call", output_to_operand_aliasing={{1}: (2, {})} | custom-call | flops 30000000 | bytes 40000000 | tf_op jit(solution)/shard_map/dw/pallas_call | solution.py:321
  228.7 8.5 %put_rows.1 = f32[8192,3072]{1,0:T(8,128)} custom-call(s32[1]{0:T(128)} %bitcast.11.me_ref, s32[1024]{0:T(1024)} %get-tuple-element.58.rows_ref, s32[1]{0:T(128)} %bitcast.10.cnt_ref, s32[1,1024]{1,0:T(1,128)} %bitcast.51, bf16[2,32,3072]{2,1,0:T(8,128)(2,1)} %copy-done.11, bf16[2,32,3072]{2,1,0:T(8,128)(2,1)} %copy-done.10, ...), custom_call_target="tpu_custom_call", output_to_operand_aliasing={{}: (20, {})} | custom-call | tf_op jit(solution)/shard_map/put_rows/pallas_call | solution.py:345
  (153 shorter events, 18.6 us)
Async XLA Ops:
  6.4 35.3 %collective-permute-start.24 = (bf16[1,4,64,1536]{3,2,1,0:T(8,128)(2,1)}, bf16[1,4,64,1536]{3,2,1,0:T(8,128)(2,1)}, u32[]{:S(2)}, u32[]{:S(2)}) collective-permute-start(bf16[1,4,64,1536]{3,2,1,0:T(8,128)(2,1)} %get-tuple-element.67), channel_id=1, source_target_pairs={{0,1},{1,0},{2,3},{3,2},{4,5},{5,4},{6,7},{7,6}} | collective-permute-start | bytes 2359304 | tf_op jit(solution)/shard_map/ppermute | solution.py:207
  12.4 38.0 %collective-permute-start.21 = (bf16[3,4,64,1536]{3,2,1,0:T(8,128)(2,1)}, bf16[3,4,64,1536]{3,2,1,0:T(8,128)(2,1)}, u32[]{:S(2)}, u32[]{:S(2)}) collective-permute-start(bf16[3,4,64,1536]{3,2,1,0:T(8,128)(2,1)} %get-tuple-element.62), channel_id=1, source_target_pairs={{0,1},{1,0},{2,3},{3,2},{4,5},{5,4},{6,7},{7,6}} | collective-permute-start | bytes 7077896 | tf_op jit(solution)/shard_map/ppermute | solution.py:207
  38.1 49.3 %collective-permute-start = (bf16[4,4,64,1536]{3,2,1,0:T(8,128)(2,1)}, bf16[4,4,64,1536]{3,2,1,0:T(8,128)(2,1)}, u32[]{:S(2)}, u32[]{:S(2)}) collective-permute-start(bf16[4,4,64,1536]{3,2,1,0:T(8,128)(2,1)} %get-tuple-element.43), channel_id=1, source_target_pairs={{0,1},{1,0},{2,3},{3,2},{4,5},{5,4},{6,7},{7,6}} | collective-permute-start | bytes 9437192 | tf_op jit(solution)/shard_map/ppermute | solution.py:207
  44.2 20.8 %collective-permute-start.25 = (f32[4,32,1536]{2,1,0:T(8,128)}, f32[4,32,1536]{2,1,0:T(8,128)S(1)}, u32[]{:S(2)}, u32[]{:S(2)}) collective-permute-start(f32[4,32,1536]{2,1,0:T(8,128)} %get-tuple-element.107), channel_id=1, source_target_pairs={{0,2},{1,3},{2,0},{3,1},{4,6},{5,7},{6,4},{7,5}} | collective-permute-start | bytes 2359304 | tf_op jit(solution)/shard_map/ppermute | solution.py:207
  49.4 20.2 %collective-permute-start.27 = (f32[4,32,1536]{2,1,0:T(8,128)}, f32[4,32,1536]{2,1,0:T(8,128)S(1)}, u32[]{:S(2)}, u32[]{:S(2)}) collective-permute-start(f32[4,32,1536]{2,1,0:T(8,128)} %get-tuple-element.106), channel_id=1, source_target_pairs={{0,4},{1,5},{2,6},{3,7},{4,0},{5,1},{6,2},{7,3}} | collective-permute-start | bytes 2359304 | tf_op jit(solution)/shard_map/ppermute | solution.py:207
  65.1 20.4 %collective-permute-start.22 = (f32[4,32,1536]{2,1,0:T(8,128)S(1)}, f32[4,32,1536]{2,1,0:T(8,128)S(1)}, u32[]{:S(2)}, u32[]{:S(2)}) collective-permute-start(f32[4,32,1536]{2,1,0:T(8,128)S(1)} %convert_add_fusion.3), channel_id=1, source_target_pairs={{0,2},{1,3},{2,0},{3,1},{4,6},{5,7},{6,4},{7,5}} | collective-permute-start | bytes 2359304 | tf_op jit(solution)/shard_map/ppermute | solution.py:207
  67.0 20.4 %collective-permute-start.23 = (f32[4,32,1536]{2,1,0:T(8,128)S(1)}, f32[4,32,1536]{2,1,0:T(8,128)S(1)}, u32[]{:S(2)}, u32[]{:S(2)}) collective-permute-start(f32[4,32,1536]{2,1,0:T(8,128)S(1)} %convert_add_fusion.2), channel_id=1, source_target_pairs={{0,4},{1,5},{2,6},{3,7},{4,0},{5,1},{6,2},{7,3}} | collective-permute-start | bytes 2359304 | tf_op jit(solution)/shard_map/ppermute | solution.py:207
  68.2 53.5 %collective-permute-start.26 = (f32[4,32,1536]{2,1,0:T(8,128)S(1)}, f32[4,32,1536]{2,1,0:T(8,128)S(1)}, u32[]{:S(2)}, u32[]{:S(2)}) collective-permute-start(f32[4,32,1536]{2,1,0:T(8,128)S(1)} %add_add_fusion.2), channel_id=1, source_target_pairs={{0,4},{1,5},{2,6},{3,7},{4,0},{5,1},{6,2},{7,3}} | collective-permute-start | bytes 2359304 | tf_op jit(solution)/shard_map/ppermute | solution.py:207
  69.7 53.3 %collective-permute-start.28 = (f32[4,32,1536]{2,1,0:T(8,128)S(1)}, f32[4,32,1536]{2,1,0:T(8,128)S(1)}, u32[]{:S(2)}, u32[]{:S(2)}) collective-permute-start(f32[4,32,1536]{2,1,0:T(8,128)S(1)} %add_add_fusion), channel_id=1, source_target_pairs={{0,2},{1,3},{2,0},{3,1},{4,6},{5,7},{6,4},{7,5}} | collective-permute-start | bytes 2359304 | tf_op jit(solution)/shard_map/ppermute | solution.py:207
  89.7 21.2 %collective-permute-start.3 = (bf16[4,32,1536]{2,1,0:T(8,128)(2,1)S(1)}, bf16[4,32,1536]{2,1,0:T(8,128)(2,1)S(1)}, u32[]{:S(2)}, u32[]{:S(2)}) collective-permute-start(bf16[4,32,1536]{2,1,0:T(8,128)(2,1)S(1)} %get-tuple-element.111), channel_id=1, source_target_pairs={{0,2},{1,3},{2,0},{3,1},{4,6},{5,7},{6,4},{7,5}} | collective-permute-start | bytes 1179656 | tf_op jit(solution)/shard_map/ppermute | solution.py:207
  90.0 33.5 %collective-permute-start.2 = (bf16[4,32,1536]{2,1,0:T(8,128)(2,1)S(1)}, bf16[4,32,1536]{2,1,0:T(8,128)(2,1)S(1)}, u32[]{:S(2)}, u32[]{:S(2)}) collective-permute-start(bf16[4,32,1536]{2,1,0:T(8,128)(2,1)S(1)} %slice_add_fusion.2), channel_id=1, source_target_pairs={{0,4},{1,5},{2,6},{3,7},{4,0},{5,1},{6,2},{7,3}} | collective-permute-start | bytes 1179656 | tf_op jit(solution)/shard_map/ppermute | solution.py:207
  91.5 32.0 %collective-permute-start.1 = (bf16[4,32,1536]{2,1,0:T(8,128)(2,1)S(1)}, bf16[4,32,1536]{2,1,0:T(8,128)(2,1)S(1)}, u32[]{:S(2)}, u32[]{:S(2)}) collective-permute-start(bf16[4,32,1536]{2,1,0:T(8,128)(2,1)S(1)} %slice_add_fusion.3), channel_id=1, source_target_pairs={{0,2},{1,3},{2,0},{3,1},{4,6},{5,7},{6,4},{7,5}} | collective-permute-start | bytes 1179656 | tf_op jit(solution)/shard_map/ppermute | solution.py:207
  110.8 9.3 %collective-permute-start.5 = (bf16[4,32,1536]{2,1,0:T(8,128)(2,1)S(1)}, bf16[4,32,1536]{2,1,0:T(8,128)(2,1)S(1)}, u32[]{:S(2)}, u32[]{:S(2)}) collective-permute-start(bf16[4,32,1536]{2,1,0:T(8,128)(2,1)S(1)} %get-tuple-element.110), channel_id=1, source_target_pairs={{0,4},{1,5},{2,6},{3,7},{4,0},{5,1},{6,2},{7,3}} | collective-permute-start | bytes 1179656 | tf_op jit(solution)/shard_map/ppermute | solution.py:207
  120.1 8.2 %collective-permute-start.4 = (bf16[4,32,1536]{2,1,0:T(8,128)(2,1)S(1)}, bf16[4,32,1536]{2,1,0:T(8,128)(2,1)S(1)}, u32[]{:S(2)}, u32[]{:S(2)}) collective-permute-start(bf16[4,32,1536]{2,1,0:T(8,128)(2,1)S(1)} %add_add_fusion.6), channel_id=1, source_target_pairs={{0,4},{1,5},{2,6},{3,7},{4,0},{5,1},{6,2},{7,3}} | collective-permute-start | bytes 1179656 | tf_op jit(solution)/shard_map/ppermute | solution.py:207
  121.7 7.8 %collective-permute-start.6 = (bf16[4,32,1536]{2,1,0:T(8,128)(2,1)S(1)}, bf16[4,32,1536]{2,1,0:T(8,128)(2,1)S(1)}, u32[]{:S(2)}, u32[]{:S(2)}) collective-permute-start(bf16[4,32,1536]{2,1,0:T(8,128)(2,1)S(1)} %add_add_fusion.4), channel_id=1, source_target_pairs={{0,2},{1,3},{2,0},{3,1},{4,6},{5,7},{6,4},{7,5}} | collective-permute-start | bytes 1179656 | tf_op jit(solution)/shard_map/ppermute | solution.py:207
  123.5 11.0 %collective-permute-start.29 = (f32[4,32,1536]{2,1,0:T(8,128)S(1)}, f32[4,32,1536]{2,1,0:T(8,128)S(1)}, u32[]{:S(2)}, u32[]{:S(2)}) collective-permute-start(f32[4,32,1536]{2,1,0:T(8,128)S(1)} %get-tuple-element.90), channel_id=1, source_target_pairs={{0,1},{1,0},{2,3},{3,2},{4,5},{5,4},{6,7},{7,6}} | collective-permute-start | bytes 2359304 | tf_op jit(solution)/shard_map/ppermute | solution.py:207
  129.7 2.6 %collective-permute-start.7 = (bf16[4,32,1536]{2,1,0:T(8,128)(2,1)S(1)}, bf16[4,32,1536]{2,1,0:T(8,128)(2,1)S(1)}, u32[]{:S(2)}, u32[]{:S(2)}) collective-permute-start(bf16[4,32,1536]{2,1,0:T(8,128)(2,1)S(1)} %get-tuple-element.54.refs_0_), channel_id=1, source_target_pairs={{0,1},{1,0},{2,3},{3,2},{4,5},{5,4},{6,7},{7,6}} | collective-permute-start | bytes 1179656 | tf_op jit(solution)/shard_map/ppermute | solution.py:207
  129.7 12.0 %collective-permute-start.13 = (bf16[4,32,1536]{2,1,0:T(8,128)(2,1)S(1)}, bf16[4,32,1536]{2,1,0:T(8,128)(2,1)S(1)}, u32[]{:S(2)}, u32[]{:S(2)}) collective-permute-start(bf16[4,32,1536]{2,1,0:T(8,128)(2,1)S(1)} %get-tuple-element.54.refs_0_), channel_id=1, source_target_pairs={{0,4},{1,5},{2,6},{3,7},{4,0},{5,1},{6,2},{7,3}} | collective-permute-start | bytes 1179656 | tf_op jit(solution)/shard_map/ppermute | solution.py:207
  130.3 2.4 %collective-permute-start.8 = (bf16[4,32,1536]{2,1,0:T(8,128)(2,1)S(1)}, bf16[4,32,1536]{2,1,0:T(8,128)(2,1)S(1)}, u32[]{:S(2)}, u32[]{:S(2)}) collective-permute-start(bf16[4,32,1536]{2,1,0:T(8,128)(2,1)S(1)} %get-tuple-element.55.refs_2_), channel_id=1, source_target_pairs={{0,1},{1,0},{2,3},{3,2},{4,5},{5,4},{6,7},{7,6}} | collective-permute-start | bytes 1179656 | tf_op jit(solution)/shard_map/ppermute | solution.py:207
  130.5 12.5 %collective-permute-start.11 = (bf16[4,32,1536]{2,1,0:T(8,128)(2,1)S(1)}, bf16[4,32,1536]{2,1,0:T(8,128)(2,1)S(1)}, u32[]{:S(2)}, u32[]{:S(2)}) collective-permute-start(bf16[4,32,1536]{2,1,0:T(8,128)(2,1)S(1)} %get-tuple-element.55.refs_2_), channel_id=1, source_target_pairs={{0,2},{1,3},{2,0},{3,1},{4,6},{5,7},{6,4},{7,5}} | collective-permute-start | bytes 1179656 | tf_op jit(solution)/shard_map/ppermute | solution.py:207
  132.3 28.2 %collective-permute-start.9 = (bf16[4,32,1536]{2,1,0:T(8,128)(2,1)S(1)}, bf16[4,32,1536]{2,1,0:T(8,128)(2,1)S(1)}, u32[]{:S(2)}, u32[]{:S(2)}) collective-permute-start(bf16[4,32,1536]{2,1,0:T(8,128)(2,1)S(1)} %get-tuple-element.54.refs_0_), channel_id=1, source_target_pairs={{0,2},{1,3},{2,0},{3,1},{4,6},{5,7},{6,4},{7,5}} | collective-permute-start | bytes 1179656 | tf_op jit(solution)/shard_map/ppermute | solution.py:207
  132.7 27.8 %collective-permute-start.15 = (bf16[4,32,1536]{2,1,0:T(8,128)(2,1)S(1)}, bf16[4,32,1536]{2,1,0:T(8,128)(2,1)S(1)}, u32[]{:S(2)}, u32[]{:S(2)}) collective-permute-start(bf16[4,32,1536]{2,1,0:T(8,128)(2,1)S(1)} %get-tuple-element.55.refs_2_), channel_id=1, source_target_pairs={{0,4},{1,5},{2,6},{3,7},{4,0},{5,1},{6,2},{7,3}} | collective-permute-start | bytes 1179656 | tf_op jit(solution)/shard_map/ppermute | solution.py:207
  135.1 9.0 %collective-permute-start.44 = (f32[3072]{0:T(1024)S(1)}, f32[3072]{0:T(1024)S(1)}, u32[]{:S(2)}, u32[]{:S(2)}) collective-permute-start(f32[3072]{0:T(1024)S(1)} %get-tuple-element.79), channel_id=1, source_target_pairs={{0,1},{1,0},{2,3},{3,2},{4,5},{5,4},{6,7},{7,6}} | collective-permute-start | bytes 36872 | tf_op jit(solution)/shard_map/ppermute | solution.py:207
  141.7 20.9 %collective-permute-start.17 = (bf16[4,32,1536]{2,1,0:T(8,128)(2,1)S(1)}, bf16[4,32,1536]{2,1,0:T(8,128)(2,1)S(1)}, u32[]{:S(2)}, u32[]{:S(2)}) collective-permute-start(bf16[4,32,1536]{2,1,0:T(8,128)(2,1)S(1)} %collective-permute-done.13.refs_8_), channel_id=1, source_target_pairs={{0,2},{1,3},{2,0},{3,1},{4,6},{5,7},{6,4},{7,5}} | collective-permute-start | bytes 1179656 | tf_op jit(solution)/shard_map/ppermute | solution.py:207
  143.0 20.1 %collective-permute-start.19 = (bf16[4,32,1536]{2,1,0:T(8,128)(2,1)S(1)}, bf16[4,32,1536]{2,1,0:T(8,128)(2,1)S(1)}, u32[]{:S(2)}, u32[]{:S(2)}) collective-permute-start(bf16[4,32,1536]{2,1,0:T(8,128)(2,1)S(1)} %collective-permute-done.11.refs_6_), channel_id=1, source_target_pairs={{0,4},{1,5},{2,6},{3,7},{4,0},{5,1},{6,2},{7,3}} | collective-permute-start | bytes 1179656 | tf_op jit(solution)/shard_map/ppermute | solution.py:207
  144.0 14.9 %collective-permute-start.45 = (f32[3072]{0:T(1024)S(1)}, f32[3072]{0:T(1024)S(1)}, u32[]{:S(2)}, u32[]{:S(2)}) collective-permute-start(f32[3072]{0:T(1024)S(1)} %add.164), channel_id=1, source_target_pairs={{0,2},{1,3},{2,0},{3,1},{4,6},{5,7},{6,4},{7,5}} | collective-permute-start | bytes 36872 | tf_op jit(solution)/shard_map/ppermute | solution.py:207
  145.3 52.3 %copy-start.1 = (bf16[3072,640]{1,0:T(8,128)(2,1)S(1)}, bf16[3072,640]{1,0:T(8,128)(2,1)}, u32[]{:S(2)}) copy-start(bf16[3072,640]{1,0:T(8,128)(2,1)} %w_ref.5) | copy-start | bytes 11796484
  159.0 3.7 %collective-permute-start.46 = (f32[3072]{0:T(1024)S(1)}, f32[3072]{0:T(1024)S(1)}, u32[]{:S(2)}, u32[]{:S(2)}) collective-permute-start(f32[3072]{0:T(1024)S(1)} %add.165), channel_id=1, source_target_pairs={{0,4},{1,5},{2,6},{3,7},{4,0},{5,1},{6,2},{7,3}} | collective-permute-start | bytes 36872 | tf_op jit(solution)/shard_map/ppermute | solution.py:207
  160.5 4.1 %collective-permute-start.10 = (bf16[4,32,1536]{2,1,0:T(8,128)(2,1)S(1)}, bf16[4,32,1536]{2,1,0:T(8,128)(2,1)S(1)}, u32[]{:S(2)}, u32[]{:S(2)}) collective-permute-start(bf16[4,32,1536]{2,1,0:T(8,128)(2,1)S(1)} %collective-permute-done.9.refs_4_), channel_id=1, source_target_pairs={{0,1},{1,0},{2,3},{3,2},{4,5},{5,4},{6,7},{7,6}} | collective-permute-start | bytes 1179656 | tf_op jit(solution)/shard_map/ppermute | solution.py:207
  160.6 5.4 %collective-permute-start.12 = (bf16[4,32,1536]{2,1,0:T(8,128)(2,1)S(1)}, bf16[4,32,1536]{2,1,0:T(8,128)(2,1)S(1)}, u32[]{:S(2)}, u32[]{:S(2)}) collective-permute-start(bf16[4,32,1536]{2,1,0:T(8,128)(2,1)S(1)} %collective-permute-done.11.refs_6_), channel_id=1, source_target_pairs={{0,1},{1,0},{2,3},{3,2},{4,5},{5,4},{6,7},{7,6}} | collective-permute-start | bytes 1179656 | tf_op jit(solution)/shard_map/ppermute | solution.py:207
  162.7 4.0 %collective-permute-start.14 = (bf16[4,32,1536]{2,1,0:T(8,128)(2,1)S(1)}, bf16[4,32,1536]{2,1,0:T(8,128)(2,1)S(1)}, u32[]{:S(2)}, u32[]{:S(2)}) collective-permute-start(bf16[4,32,1536]{2,1,0:T(8,128)(2,1)S(1)} %collective-permute-done.13.refs_8_), channel_id=1, source_target_pairs={{0,1},{1,0},{2,3},{3,2},{4,5},{5,4},{6,7},{7,6}} | collective-permute-start | bytes 1179656 | tf_op jit(solution)/shard_map/ppermute | solution.py:207
  162.7 4.6 %collective-permute-start.16 = (bf16[4,32,1536]{2,1,0:T(8,128)(2,1)S(1)}, bf16[4,32,1536]{2,1,0:T(8,128)(2,1)S(1)}, u32[]{:S(2)}, u32[]{:S(2)}) collective-permute-start(bf16[4,32,1536]{2,1,0:T(8,128)(2,1)S(1)} %collective-permute-done.15.refs_10_), channel_id=1, source_target_pairs={{0,1},{1,0},{2,3},{3,2},{4,5},{5,4},{6,7},{7,6}} | collective-permute-start | bytes 1179656 | tf_op jit(solution)/shard_map/ppermute | solution.py:207
  163.2 12.0 %collective-permute-start.36 = (bf16[2,32,3072]{2,1,0:T(8,128)(2,1)S(1)}, bf16[2,32,3072]{2,1,0:T(8,128)(2,1)S(1)}, u32[]{:S(2)}, u32[]{:S(2)}) collective-permute-start(bf16[2,32,3072]{2,1,0:T(8,128)(2,1)S(1)} %get-tuple-element.113.refs_0_), channel_id=1, source_target_pairs={{0,4},{1,5},{2,6},{3,7},{4,0},{5,1},{6,2},{7,3}} | collective-permute-start | bytes 1179656 | tf_op jit(solution)/shard_map/ppermute | solution.py:207
  164.6 12.0 %collective-permute-start.33 = (bf16[2,32,3072]{2,1,0:T(8,128)(2,1)S(1)}, bf16[2,32,3072]{2,1,0:T(8,128)(2,1)S(1)}, u32[]{:S(2)}, u32[]{:S(2)}) collective-permute-start(bf16[2,32,3072]{2,1,0:T(8,128)(2,1)S(1)} %get-tuple-element.112.refs_1_), channel_id=1, source_target_pairs={{0,2},{1,3},{2,0},{3,1},{4,6},{5,7},{6,4},{7,5}} | collective-permute-start | bytes 1179656 | tf_op jit(solution)/shard_map/ppermute | solution.py:207
  165.9 17.9 %collective-permute-start.32 = (bf16[2,32,3072]{2,1,0:T(8,128)(2,1)S(1)}, bf16[2,32,3072]{2,1,0:T(8,128)(2,1)S(1)}, u32[]{:S(2)}, u32[]{:S(2)}) collective-permute-start(bf16[2,32,3072]{2,1,0:T(8,128)(2,1)S(1)} %get-tuple-element.113.refs_0_), channel_id=1, source_target_pairs={{0,2},{1,3},{2,0},{3,1},{4,6},{5,7},{6,4},{7,5}} | collective-permute-start | bytes 1179656 | tf_op jit(solution)/shard_map/ppermute | solution.py:207
  166.7 17.2 %collective-permute-start.37 = (bf16[2,32,3072]{2,1,0:T(8,128)(2,1)S(1)}, bf16[2,32,3072]{2,1,0:T(8,128)(2,1)S(1)}, u32[]{:S(2)}, u32[]{:S(2)}) collective-permute-start(bf16[2,32,3072]{2,1,0:T(8,128)(2,1)S(1)} %get-tuple-element.112.refs_1_), channel_id=1, source_target_pairs={{0,4},{1,5},{2,6},{3,7},{4,0},{5,1},{6,2},{7,3}} | collective-permute-start | bytes 1179656 | tf_op jit(solution)/shard_map/ppermute | solution.py:207
  167.2 17.9 %collective-permute-start.30 = (bf16[2,32,3072]{2,1,0:T(8,128)(2,1)S(1)}, bf16[2,32,3072]{2,1,0:T(8,128)(2,1)S(1)}, u32[]{:S(2)}, u32[]{:S(2)}) collective-permute-start(bf16[2,32,3072]{2,1,0:T(8,128)(2,1)S(1)} %get-tuple-element.113.refs_0_), channel_id=1, source_target_pairs={{0,1},{1,0},{2,3},{3,2},{4,5},{5,4},{6,7},{7,6}} | collective-permute-start | bytes 1179656 | tf_op jit(solution)/shard_map/ppermute | solution.py:207
  175.2 11.0 %collective-permute-start.31 = (bf16[2,32,3072]{2,1,0:T(8,128)(2,1)S(1)}, bf16[2,32,3072]{2,1,0:T(8,128)(2,1)S(1)}, u32[]{:S(2)}, u32[]{:S(2)}) collective-permute-start(bf16[2,32,3072]{2,1,0:T(8,128)(2,1)S(1)} %get-tuple-element.112.refs_1_), channel_id=1, source_target_pairs={{0,1},{1,0},{2,3},{3,2},{4,5},{5,4},{6,7},{7,6}} | collective-permute-start | bytes 1179656 | tf_op jit(solution)/shard_map/ppermute | solution.py:207
  176.6 9.6 %collective-permute-start.18 = (bf16[4,32,1536]{2,1,0:T(8,128)(2,1)S(1)}, bf16[4,32,1536]{2,1,0:T(8,128)(2,1)S(1)}, u32[]{:S(2)}, u32[]{:S(2)}) collective-permute-start(bf16[4,32,1536]{2,1,0:T(8,128)(2,1)S(1)} %collective-permute-done.17.refs_12_), channel_id=1, source_target_pairs={{0,1},{1,0},{2,3},{3,2},{4,5},{5,4},{6,7},{7,6}} | collective-permute-start | bytes 1179656 | tf_op jit(solution)/shard_map/ppermute | solution.py:207
  183.8 2.9 %collective-permute-start.20 = (bf16[4,32,1536]{2,1,0:T(8,128)(2,1)S(1)}, bf16[4,32,1536]{2,1,0:T(8,128)(2,1)S(1)}, u32[]{:S(2)}, u32[]{:S(2)}) collective-permute-start(bf16[4,32,1536]{2,1,0:T(8,128)(2,1)S(1)} %collective-permute-done.19.refs_14_), channel_id=1, source_target_pairs={{0,1},{1,0},{2,3},{3,2},{4,5},{5,4},{6,7},{7,6}} | collective-permute-start | bytes 1179656 | tf_op jit(solution)/shard_map/ppermute | solution.py:207
  183.9 11.5 %collective-permute-start.40 = (bf16[2,32,3072]{2,1,0:T(8,128)(2,1)S(1)}, bf16[2,32,3072]{2,1,0:T(8,128)(2,1)S(1)}, u32[]{:S(2)}, u32[]{:S(2)}) collective-permute-start(bf16[2,32,3072]{2,1,0:T(8,128)(2,1)S(1)} %collective-permute-done.36.refs_8_), channel_id=1, source_target_pairs={{0,2},{1,3},{2,0},{3,1},{4,6},{5,7},{6,4},{7,5}} | collective-permute-start | bytes 1179656 | tf_op jit(solution)/shard_map/ppermute | solution.py:207
  185.2 11.2 %collective-permute-start.41 = (bf16[2,32,3072]{2,1,0:T(8,128)(2,1)S(1)}, bf16[2,32,3072]{2,1,0:T(8,128)(2,1)S(1)}, u32[]{:S(2)}, u32[]{:S(2)}) collective-permute-start(bf16[2,32,3072]{2,1,0:T(8,128)(2,1)S(1)} %collective-permute-done.33.refs_5_), channel_id=1, source_target_pairs={{0,4},{1,5},{2,6},{3,7},{4,0},{5,1},{6,2},{7,3}} | collective-permute-start | bytes 1179656 | tf_op jit(solution)/shard_map/ppermute | solution.py:207
  186.2 10.2 %collective-permute-start.34 = (bf16[2,32,3072]{2,1,0:T(8,128)(2,1)S(1)}, bf16[2,32,3072]{2,1,0:T(8,128)(2,1)S(1)}, u32[]{:S(2)}, u32[]{:S(2)}) collective-permute-start(bf16[2,32,3072]{2,1,0:T(8,128)(2,1)S(1)} %collective-permute-done.32.refs_4_), channel_id=1, source_target_pairs={{0,1},{1,0},{2,3},{3,2},{4,5},{5,4},{6,7},{7,6}} | collective-permute-start | bytes 1179656 | tf_op jit(solution)/shard_map/ppermute | solution.py:207
  186.2 41.0 %collective-permute-start.35 = (bf16[2,32,3072]{2,1,0:T(8,128)(2,1)S(1)}, bf16[2,32,3072]{2,1,0:T(8,128)(2,1)S(1)}, u32[]{:S(2)}, u32[]{:S(2)}) collective-permute-start(bf16[2,32,3072]{2,1,0:T(8,128)(2,1)S(1)} %collective-permute-done.33.refs_5_), channel_id=1, source_target_pairs={{0,1},{1,0},{2,3},{3,2},{4,5},{5,4},{6,7},{7,6}} | collective-permute-start | bytes 1179656 | tf_op jit(solution)/shard_map/ppermute | solution.py:207
  186.7 40.5 %collective-permute-start.38 = (bf16[2,32,3072]{2,1,0:T(8,128)(2,1)S(1)}, bf16[2,32,3072]{2,1,0:T(8,128)(2,1)S(1)}, u32[]{:S(2)}, u32[]{:S(2)}) collective-permute-start(bf16[2,32,3072]{2,1,0:T(8,128)(2,1)S(1)} %collective-permute-done.36.refs_8_), channel_id=1, source_target_pairs={{0,1},{1,0},{2,3},{3,2},{4,5},{5,4},{6,7},{7,6}} | collective-permute-start | bytes 1179656 | tf_op jit(solution)/shard_map/ppermute | solution.py:207
  195.4 31.9 %collective-permute-start.39 = (bf16[2,32,3072]{2,1,0:T(8,128)(2,1)S(1)}, bf16[2,32,3072]{2,1,0:T(8,128)(2,1)S(1)}, u32[]{:S(2)}, u32[]{:S(2)}) collective-permute-start(bf16[2,32,3072]{2,1,0:T(8,128)(2,1)S(1)} %collective-permute-done.37.refs_9_), channel_id=1, source_target_pairs={{0,1},{1,0},{2,3},{3,2},{4,5},{5,4},{6,7},{7,6}} | collective-permute-start | bytes 1179656 | tf_op jit(solution)/shard_map/ppermute | solution.py:207
  196.4 30.9 %collective-permute-start.42 = (bf16[2,32,3072]{2,1,0:T(8,128)(2,1)S(1)}, bf16[2,32,3072]{2,1,0:T(8,128)(2,1)S(1)}, u32[]{:S(2)}, u32[]{:S(2)}) collective-permute-start(bf16[2,32,3072]{2,1,0:T(8,128)(2,1)S(1)} %collective-permute-done.40.refs_12_), channel_id=1, source_target_pairs={{0,1},{1,0},{2,3},{3,2},{4,5},{5,4},{6,7},{7,6}} | collective-permute-start | bytes 1179656 | tf_op jit(solution)/shard_map/ppermute | solution.py:207
  196.4 30.9 %collective-permute-start.43 = (bf16[2,32,3072]{2,1,0:T(8,128)(2,1)S(1)}, bf16[2,32,3072]{2,1,0:T(8,128)(2,1)S(1)}, u32[]{:S(2)}, u32[]{:S(2)}) collective-permute-start(bf16[2,32,3072]{2,1,0:T(8,128)(2,1)S(1)} %collective-permute-done.41.refs_13_), channel_id=1, source_target_pairs={{0,1},{1,0},{2,3},{3,2},{4,5},{5,4},{6,7},{7,6}} | collective-permute-start | bytes 1179656 | tf_op jit(solution)/shard_map/ppermute | solution.py:207
  (28 other events, 451.1 us)

commit v2 on v1

--- a/solution.py
+++ b/solution.py
@@ -13,7 +13,7 @@
 SMEM = pl.BlockSpec(memory_space=pltpu.SMEM)
 ZR = 128
 BLK = 256
-LOOKUP_EARLY, LOOKUP_SHARE, NORM_SHARE = 14, 28, 20
+LOOKUP_EARLY, LOOKUP_SHARE, NORM_SHARE = 14, 28, 5
 
 
 def zero_fill(de, z, sem, first, last):
@@ -32,20 +32,20 @@
     return start, wait
 
 
-def pdn_kernel(js, kc_ref, du_ref, w_ref, mine_ref, theirs_ref):
-    k, c = kc_ref[0], kc_ref[1]
+def pdn_kernel(js, c_ref, du_ref, w_ref, *outs):
+    c = c_ref[0]
     mb, t, _ = du_ref.shape
-    tc = t // 4
-    hd = w_ref.shape[0] // 2
-    wc = 512
+    tc, wc = t // 4, 512
+    tl = tc // 2
     for i, j in enumerate(js):
         z = pl.multiple_of(jnp.bitwise_xor(c, j) * tc, tc)
         rows = jnp.concatenate([du_ref[m, pl.ds(z, tc), :] for m in range(mb)], axis=0)
-        for out, half in ((theirs_ref, 1 - k), (mine_ref, k)):
-            for n in range(hd // wc):
-                wv = w_ref[pl.ds(pl.multiple_of(half * hd + n * wc, wc), wc), :]
-                v = lax.dot_general(rows, wv, (((1,), (1,)), ((), ())), preferred_element_type=jnp.float32)
-                out[i, :, :, n * wc:(n + 1) * wc] = v.astype(jnp.bfloat16).reshape(mb, tc, wc)
+        for n in range(w_ref.shape[0] // wc):
+            cols = slice(n * wc, (n + 1) * wc)
+            v = lax.dot_general(rows, w_ref[cols, :], (((1,), (1,)), ((), ())), preferred_element_type=jnp.float32)
+            v = v.astype(jnp.bfloat16).reshape(mb, tc, wc)
+            for h in range(2):
+                outs[2 * i + h][:, :, cols] = v[:, h * tl:(h + 1) * tl]
 
 
 def lookup_kernel(kc_ref, loc_ref, tgt_ref, emb, mine_ref, theirs_ref, de, buf, sem, z, zsem):
@@ -104,61 +104,39 @@
     late_wait()
 
 
-def pull(me, blocks, buf, sem):
-    hb, tl = blocks[0].shape[:2]
-    copies = []
-    for i, b in enumerate(blocks):
-        j, h = i // 2, i % 2
-        s = pl.multiple_of(jnp.bitwise_xor(me, j) * tl, tl)
-        copies.append(pltpu.make_async_copy(b, buf.at[h * hb:(h + 1) * hb, pl.ds(s, tl), :], sem.at[i]))
-    for c in copies:
-        c.start()
-    return copies
-
-
-def pull_halves(k, c, blocks, buf, sem):
+def norm_kernel(j, kc_ref, g_ref, w_ref, *refs):
+    blocks, (n_ref, u_ref, de, stage, sem, z, zsem) = refs[:4], refs[-7:]
+    k = kc_ref[0]
+    mb, tc, d = n_ref.shape
     tl, hd = blocks[0].shape[1:]
-    copies = []
-    for i, b in enumerate(blocks):
-        j, h, q = i // 4, (i // 2) % 2, i % 2
-        s = pl.multiple_of((2 * jnp.bitwise_xor(c, j) + h) * tl, tl)
-        o = pl.multiple_of(jnp.bitwise_xor(k, q) * hd, 128)
-        copies.append(pltpu.make_async_copy(b, buf.at[:, pl.ds(s, tl), pl.ds(o, hd)], sem.at[i]))
-    for c in copies:
-        c.start()
-    return copies
-
-
-def norm_kernel(kc_ref, g_ref, w_ref, *refs):
-    blocks, (de_in, n_ref, u_ref, de, sem, z, zsem) = refs[:16], refs[16:]
-    del de_in
-    mb, t, _ = n_ref.shape
-    start, wait = zero_fill(de, z, zsem, LOOKUP_SHARE, LOOKUP_SHARE + NORM_SHARE)
-    copies = pull_halves(kc_ref[0], kc_ref[1], blocks, n_ref, sem)
+    first = LOOKUP_SHARE + j * NORM_SHARE
+    start, wait = zero_fill(de, z, zsem, first, first + NORM_SHARE)
     start()
-    for c in copies:
-        c.wait()
-    gf = g_ref[...].astype(jnp.float32)
-    rows = 32
+    at = [pl.ds(pl.multiple_of(jnp.bitwise_xor(k, q) * hd, 128), hd) for q in range(2)]
+    gf = [g_ref[:, at[q]].astype(jnp.float32) for q in range(2)]
 
     @pl.loop(0, mb)
     def _(m):
-        @pl.loop(0, t // rows)
-        def _(r):
-            at = (m, pl.ds(pl.multiple_of(r * rows, rows), rows), slice(None))
-            xf = n_ref[at].astype(jnp.float32)
-            rs = lax.rsqrt(jnp.mean(xf * xf, axis=-1, keepdims=True) + EPS)
-            n_ref[at] = (xf * rs * gf).astype(jnp.bfloat16)
-
-        u_ref[m] = jnp.dot(n_ref[m], w_ref[...], preferred_element_type=jnp.float32).astype(jnp.bfloat16)
-
+        for h in range(2):
+            xf = [blocks[2 * h + q][m].astype(jnp.float32) for q in range(2)]
+            total = sum(jnp.sum(v * v, axis=-1, keepdims=True) for v in xf)
+            rs = lax.rsqrt(total * (1.0 / d) + EPS)
+            for q in range(2):
+                n_ref[m, h * tl:(h + 1) * tl, at[q]] = (xf[q] * rs * gf[q]).astype(jnp.bfloat16)
+
+    v = jnp.dot(n_ref[...].reshape(mb * tc, d), w_ref[...], preferred_element_type=jnp.float32)
+    stage[...] = v.astype(jnp.bfloat16).reshape(stage.shape)
+    rows = pl.ds(pl.multiple_of(jnp.bitwise_xor(kc_ref[1], j) * tc, tc), tc)
+    copy = pltpu.make_async_copy(stage, u_ref.at[:, rows, :], sem)
+    copy.start()
+    copy.wait()
     wait()
 
 
-def dw_kernel(n_ref, du_ref, de_in, dw_ref, de, z, zsem):
-    del de_in
-    mb, _, d = n_ref.shape
-    start, wait = zero_fill(de, z, zsem, LOOKUP_SHARE + NORM_SHARE, de.shape[0] // ZR)
+def dw_kernel(c_ref, du_ref, *refs):
+    ns, (dw_ref, de, z, zsem) = refs[:4], refs[-4:]
+    mb, tc, d = ns[0].shape
+    start, wait = zero_fill(de, z, zsem, LOOKUP_SHARE + 4 * NORM_SHARE, de.shape[0] // ZR)
     start()
     dc = 512
 
@@ -166,19 +144,24 @@
     def _(i):
         c = pl.ds(pl.multiple_of(i * dc, dc), dc)
         acc = jnp.zeros((dc, du_ref.shape[2]), jnp.float32)
-        for m in range(mb):
-            acc += lax.dot_general(n_ref[m, :, c], du_ref[m], (((0,), (0,)), ((), ())), preferred_element_type=jnp.float32)
+        for j, n_ref in enumerate(ns):
+            rows = pl.ds(pl.multiple_of(jnp.bitwise_xor(c_ref[0], j) * tc, tc), tc)
+            left = jnp.concatenate([n_ref[m, :, c] for m in range(mb)], axis=0)
+            right = jnp.concatenate([du_ref[m, rows, :] for m in range(mb)], axis=0)
+            acc += lax.dot_general(left, right, (((0,), (0,)), ((), ())), preferred_element_type=jnp.float32)
         dw_ref[c, :] = acc
 
     wait()
 
 
 def scatter_kernel(me_ref, rows_ref, cnt_ref, slot_ref, *refs):
-    blocks, (de_in, de, buf, stage, sem, out_sem) = refs[:16], refs[16:]
-    del de_in
+    blocks, (de, buf, stage, out_sem) = refs[:16], refs[-4:]
     mb, t, d = buf.shape
-    for c in pull(me_ref[0], blocks, buf, sem):
-        c.wait()
+    hb, tl = blocks[0].shape[:2]
+    for i, b in enumerate(blocks):
+        at = pl.ds(pl.multiple_of(jnp.bitwise_xor(me_ref[0], i // 2) * tl, tl), tl)
+        for m in range(hb):
+            buf[(i % 2) * hb + m, at, :] = b[m]
     cnt = cnt_ref[0]
     cc = 512
 
@@ -225,16 +208,21 @@
             return jax.ShapeDtypeStruct((nj, mb, tc, hd), jnp.bfloat16)
 
         def pdn(js):
-            mine, theirs = pl.pallas_call(
+            out = pl.pallas_call(
                 functools.partial(pdn_kernel, js),
-                out_shape=(half_shape(len(js)),) * 2,
+                out_shape=(jax.ShapeDtypeStruct((mb, tl, d), jnp.bfloat16),) * (2 * len(js)),
                 in_specs=[SMEM, VMEM, VMEM],
-                out_specs=(VMEM, VMEM),
+                out_specs=(VMEM,) * (2 * len(js)),
                 cost_estimate=pl.CostEstimate(flops=5_000_000 * len(js), bytes_accessed=8_000_000, transcendentals=0),
                 compiler_params=pltpu.CompilerParams(vmem_limit_bytes=40 * 2**20),
-            )(kc, du, w)
-            got = swap(theirs, 1)
-            return {j: (mine[i], got[i]) for i, j in enumerate(js)}
+            )(c.reshape(1), du, w)
+            return {j: out[2 * i:2 * i + 2] for i, j in enumerate(js)}
+
+        def pick(a, b):
+            return jnp.where(k == 0, a, b)
+
+        def f32(v):
+            return v.astype(jnp.float32)
 
         def reduce_to_home(pairs, dt):
             def part(j, h):
@@ -256,11 +244,6 @@
         def to_rows(mine, other):
             return jnp.where(k == 0, jnp.concatenate([mine, other], -1), jnp.concatenate([other, mine], -1))
 
-        def go_home(s0, s1):
-            keep = jnp.where(k == 0, s0, s1)
-            give = jnp.where(k == 0, s1, s0)
-            return to_rows(keep, swap(give, 1))
-
         def gather_all(own):
             x1, y0 = swap(own[1], 2), swap(own[0], 4)
             x0, y1 = swap(own[0], 2), swap(own[1], 4)
@@ -274,9 +257,29 @@
         n = flat.shape[0]
         loc = flat - r * vl
         own = (loc >= 0) & (loc < vl)
-        pairs = pdn((3,))
-        pairs.update(pdn((1, 2, 0)))
+        part = pdn((3,))
+        part.update(pdn((1, 2)))
+        part.update(pdn((0,)))
+        d0, d1 = swap(part[3][0], 2), swap(part[3][1], 4)
+        ex, ey = swap(part[1][0], 2), swap(part[2][1], 4)
         tgt = jnp.where(own, 2 * (jnp.arange(n) % tc) + (loc & 1), -1).astype(jnp.int32)
+        i0 = lax.broadcasted_iota(jnp.int32, (n, n), 0)
+        i1 = lax.broadcasted_iota(jnp.int32, (n, n), 1)
+        same = flat[:, None] == flat[None, :]
+        first = jnp.min(jnp.where(same, i0, n), axis=0)
+        lead = own & (first == jnp.arange(n))
+        pos = jnp.sum(jnp.where(lead[:, None] & (i0 < i1), 1, 0), axis=0)
+        pos_of_first = jnp.sum(jnp.where((i0 == first[None, :]), pos[:, None], 0), axis=0)
+        slot = jnp.where(own, pos_of_first, -1).astype(jnp.int32)
+        rows = jnp.sum(jnp.where(lead[:, None] & (pos[:, None] == i1), loc[:, None], 0), axis=0).astype(jnp.int32)
+        cnt = jnp.sum(lead.astype(jnp.int32)).reshape(1)
+        d0, d1, loc, tgt, slot, rows, cnt = lax.optimization_barrier((d0, d1, loc, tgt, slot, rows, cnt))
+        ty, tx = f32(part[2][0]) + f32(d0), f32(part[1][1]) + f32(d1)
+        gy = swap(pick(ty[..., hd:], ty[..., :hd]), 1)
+        gx = swap(pick(tx[..., hd:], tx[..., :hd]), 1)
+        fy = swap(pick(ty[..., :hd], ty[..., hd:]) + gy, 4)
+        fx = swap(pick(tx[..., :hd], tx[..., hd:]) + gx, 2)
+
         mine, theirs, de = pl.pallas_call(
             lookup_kernel,
             out_shape=(half_shape(4), half_shape(4), de_shape),
@@ -290,45 +293,42 @@
         got = swap(theirs, 1)
         xpairs = {j: (mine[j], got[j]) for j in range(4)}
 
-        dn = go_home(*reduce_to_home(pairs, jnp.float32))
-        i0 = lax.broadcasted_iota(jnp.int32, (n, n), 0)
-        i1 = lax.broadcasted_iota(jnp.int32, (n, n), 1)
-        same = flat[:, None] == flat[None, :]
-        first = jnp.min(jnp.where(same, i0, n), axis=0)
-        lead = own & (first == jnp.arange(n))
-        pos = jnp.sum(jnp.where(lead[:, None] & (i0 < i1), 1, 0), axis=0)
-        pos_of_first = jnp.sum(jnp.where((i0 == first[None, :]), pos[:, None], 0), axis=0)
-        slot = jnp.where(own, pos_of_first, -1).astype(jnp.int32)
-        rows = jnp.sum(jnp.where(lead[:, None] & (pos[:, None] == i1), loc[:, None], 0), axis=0).astype(jnp.int32)
-        cnt = jnp.sum(lead.astype(jnp.int32)).reshape(1)
+        def widen(v):
+            o = jnp.zeros_like(v)
+            return to_rows(v, o)
+
+        v0 = f32(part[0][0]) + f32(ex) + widen(fy)
+        v1 = f32(part[0][1]) + f32(ey) + widen(fx)
+        dn = pick(v0, v1) + swap(pick(v1, v0), 1)
         x0, x1 = reduce_to_home(xpairs, jnp.bfloat16)
-        x0, x1, slot, rows, cnt = lax.optimization_barrier((x0, x1, slot, rows, cnt))
         xo = gather_all((x0, x1))
-        xs = [xo[2 * j + q][h] for j in range(4) for h in range(2) for q in range(2)]
         x = to_rows(jnp.where(k == 0, x0, x1), jnp.where(k == 0, xo[1][0], xo[1][1]))
 
-        nn, u, de = pl.pallas_call(
-            norm_kernel,
-            out_shape=(jax.ShapeDtypeStruct((mb, t, d), jnp.bfloat16), jax.ShapeDtypeStruct((mb, t, f), jnp.bfloat16), de_shape),
-            in_specs=[SMEM, VMEM, VMEM] + [ANY] * 17,
-            out_specs=(VMEM, VMEM, ANY),
-            scratch_shapes=[pltpu.SemaphoreType.DMA((16,))] + zero_scratch,
-            input_output_aliases={19: 2},
-            cost_estimate=pl.CostEstimate(flops=30_000_000, bytes_accessed=40_000_000, transcendentals=0),
-            compiler_params=pltpu.CompilerParams(vmem_limit_bytes=40 * 2**20),
-            name="norm",
-        )(kc, g.reshape(1, d), w, *xs, de)
+        ns, u = [], None
+        for j in range(4):
+            more = (de,) if u is None else (u, de)
+            nj, u, de = pl.pallas_call(
+                functools.partial(norm_kernel, j),
+                out_shape=(jax.ShapeDtypeStruct((mb, tc, d), jnp.bfloat16), jax.ShapeDtypeStruct((mb, t, f), jnp.bfloat16), de_shape),
+                in_specs=[SMEM] + [VMEM] * 6 + [ANY] * len(more),
+                out_specs=(VMEM, ANY, ANY),
+                scratch_shapes=[pltpu.VMEM((mb, tc, f), jnp.bfloat16), pltpu.SemaphoreType.DMA] + zero_scratch,
+                input_output_aliases={7 + i: 3 - len(more) + i for i in range(len(more))},
+                cost_estimate=pl.CostEstimate(flops=8_000_000, bytes_accessed=12_000_000, transcendentals=0),
+                compiler_params=pltpu.CompilerParams(vmem_limit_bytes=40 * 2**20),
+            )(kc, g.reshape(1, d), w, *(xo[2 * j + q][h] for h in range(2) for q in range(2)), *more)
+            ns.append(nj)
         dw, de = pl.pallas_call(
             dw_kernel,
             out_shape=(jax.ShapeDtypeStruct((d, f), jnp.float32), de_shape),
-            in_specs=[VMEM, VMEM, ANY],
+            in_specs=[SMEM] + [VMEM] * 5 + [ANY],
             out_specs=(VMEM, ANY),
             scratch_shapes=zero_scratch,
-            input_output_aliases={2: 1},
+            input_output_aliases={6: 1},
             cost_estimate=pl.CostEstimate(flops=30_000_000, bytes_accessed=40_000_000, transcendentals=0),
             compiler_params=pltpu.CompilerParams(vmem_limit_bytes=40 * 2**20),
             name="dw",
-        )(nn, du, de)
+        )(c.reshape(1), du, *ns, de)
 
         xf = x.astype(jnp.float32)
         rs = lax.rsqrt(jnp.mean(xf * xf, axis=-1, keepdims=True) + EPS)
@@ -345,15 +345,15 @@
         de = pl.pallas_call(
             scatter_kernel,
             out_shape=de_shape,
-            in_specs=[SMEM, SMEM, SMEM, VMEM] + [ANY] * 17,
+            in_specs=[SMEM, SMEM, SMEM, VMEM] + [VMEM] * 16 + [ANY],
             out_specs=ANY,
             scratch_shapes=[
                 pltpu.VMEM((mb, t, d), jnp.bfloat16),
                 pltpu.VMEM((BLK, d), jnp.float32),
-                pltpu.SemaphoreType.DMA((16,)),
                 pltpu.SemaphoreType.DMA,
             ],
             input_output_aliases={20: 0},
+            compiler_params=pltpu.CompilerParams(vmem_limit_bytes=40 * 2**20),
             name="put_rows",
         )(me, rows, cnt, slot.reshape(1, n), *dxs, de)
         return u, x, de, dw, dg

time: 238 us -> 208 us (0.87)
  waiting for transfers between devices: 110 us -> 92.3 us
  starting transfers between devices: 33.9 us -> 28 us
  local copies, waits for them, and re-layouts: 15.7 us -> 10.3 us
    ppermute x47, waiting for transfers between devices: 110 us -> 92.3 us  [swap(): return lax.ppermute(v, 'tp', [(i, i ^ bit) for i in range(groups)])]
    ppermute x47, starting transfers between devices: 33.9 us -> 28 us  [swap(): return lax.ppermute(v, 'tp', [(i, i ^ bit) for i in range(groups)])]
    squeeze x2 -> x0, local copies, waits for them, and re-layouts: 3.26 us -> none  [pdn(): return {j: (mine[i], got[i]) for i, j in enumerate(js)}]
    squeeze x2, local copies, waits for them, and re-layouts: 3.3 us -> 0.56 us  [local(): xpairs = {j: (mine[j], got[j]) for j in range(4)}]
    add x6 -> x3, other arithmetic: 2.89 us -> 0.17 us  [part(): a[:, h * tl:(h + 1) * tl].astype(dt) + b[:, h * tl:(h + 1) * tl].astype(dt)]
    add x1 -> x4, other arithmetic: 0.22 us -> 2.87 us  [the longest x2 2.63 us: local(): ty, tx = (f32(part[2][0]) + f32(d0), f32(part[1][1]) + f32(d1))]
    pallas_call x3 -> x7, Pallas kernels: 22.5 us -> 23.2 us  [the longest x4 15.6 us: local(): pl.pallas_call(functools.partial(norm_kernel, j), out_shape=(jax.ShapeDty...]
    unnamed x63 -> x51, local copies, waits for them, and re-layouts: 9.05 us -> 9.47 us
  transfers between devices with their start and end apart: 47 -> 47, of which waited for: 16 -> 20; matrix products, arithmetic and copies ran while one was open for 8% -> 7% of each run, Pallas kernels for 23% -> 25%
where the time goes in v2:
time: 208 us; the launch traced here: 207 us
  waiting for transfers between devices  92.3 us (44%)
  Pallas kernels  62.4 us (30%)
  starting transfers between devices  28 us (13%)
  other arithmetic  13.1 us (6%)
  local copies, waits for them, and re-layouts  10.3 us (5%)
    ppermute x47, waiting for transfers between devices, swap(): return lax.ppermute(v, 'tp', [(i, i ^ bit) for i in range(groups)])  92.3 us
    ppermute x47, starting transfers between devices, swap(): return lax.ppermute(v, 'tp', [(i, i ^ bit) for i in range(groups)])  28 us
    pallas_call x1, Pallas kernels, local(): pl.pallas_call(lookup_kernel, out_shape=(half_shape(4), half_shape(4), de...  20.2 us
    pallas_call x4, Pallas kernels, local(): pl.pallas_call(functools.partial(norm_kernel, j), out_shape=(jax.ShapeDty...  15.6 us
    pallas_call x1, Pallas kernels, local(): pl.pallas_call(dw_kernel, out_shape=(jax.ShapeDtypeStruct((d, f), jnp.flo...  11.7 us
    unnamed x51, local copies, waits for them, and re-layouts  9.47 us
    pallas_call x3, Pallas kernels, pdn(): pl.pallas_call(functools.partial(pdn_kernel, js), out_shape=(jax.ShapeDty...  7.57 us
    pallas_call x1, Pallas kernels, local(): pl.pallas_call(scatter_kernel, out_shape=de_shape, in_specs=[SMEM, SMEM,...  7.38 us
  transfers between devices with their start and end apart: 47, of which 20 were waited for; matrix products, arithmetic and copies ran while one was open for 7% of the time, Pallas kernels for 25%

profile of v2, /device:TPU:0, one launch (start us, length us, event | category | flops | bytes accessed | tf_op | source)
XLA Modules:
  0.0 207.5 jit_solution(4223283990470942937)
XLA Ops:
  0.6 2.1 %copy-done = bf16[3072,640]{1,0:T(8,128)(2,1)S(1)} copy-done((bf16[3072,640]{1,0:T(8,128)(2,1)S(1)}, bf16[3072,640]{1,0:T(8,128)(2,1)}, u32[]{:S(2)}) %copy-start) | copy-done | bytes 3932184
  2.8 1.3 copy-done.3
  4.1 2.6 %shard_map.101 = (bf16[4,32,3072]{2,1,0:T(8,128)(2,1)}, bf16[4,32,3072]{2,1,0:T(8,128)(2,1)}) custom-call(s32[1]{0:T(128)} %bitcast.1.c_ref, bf16[4,256,640]{2,1,0:T(8,128)(2,1)S(1)} %copy-done.3, bf16[3072,640]{1,0:T(8,128)(2,1)S(1)} %copy-done), custom_call_target="tpu_custom_call" | custom-call | flops 5000000 | bytes 8000000 | tf_op jit(solution)/shard_map/pallas_call | solution.py:211
  6.6 3.3 %collective-permute-start = (bf16[4,32,3072]{2,1,0:T(8,128)(2,1)}, bf16[4,32,3072]{2,1,0:T(8,128)(2,1)}, u32[]{:S(2)}, u32[]{:S(2)}) collective-permute-start(bf16[4,32,3072]{2,1,0:T(8,128)(2,1)} %get-tuple-element.47), channel_id=1, source_target_pairs={{0,2},{1,3},{2,0},{3,1},{4,6},{5,7},{6,4},{7,5}} | collective-permute-start | bytes 2359304 | tf_op jit(solution)/shard_map/ppermute | solution.py:190
  9.9 1.5 collective-permute-start.1
  11.5 3.6 %shard_map.107 = (bf16[4,32,3072]{2,1,0:T(8,128)(2,1)}, bf16[4,32,3072]{2,1,0:T(8,128)(2,1)S(1)}, bf16[4,32,3072]{2,1,0:T(8,128)(2,1)S(1)}, bf16[4,32,3072]{2,1,0:T(8,128)(2,1)}) custom-call(s32[1]{0:T(128)} %bitcast.1.c_ref, bf16[4,256,640]{2,1,0:T(8,128)(2,1)S(1)} %copy-done.3, bf16[3072,640]{1,0:T(8,128)(2,1)S(1)} %copy-done), custom_call_target="tpu_custom_call" | custom-call | flops 10000000 | bytes 8000000 | tf_op jit(solution)/shard_map/pallas_call | solution.py:211
  17.4 2.1 %copy-done.1 = bf16[3072,640]{1,0:T(8,128)(2,1)S(1)} copy-done((bf16[3072,640]{1,0:T(8,128)(2,1)S(1)}, bf16[3072,640]{1,0:T(8,128)(2,1)}, u32[]{:S(2)}) %copy-start.1) | copy-done | bytes 3932184
  19.5 1.4 shard_map.106
  22.6 1.6 select_reduce_fusion
  24.2 4.4 %collective-permute-done = bf16[4,32,3072]{2,1,0:T(8,128)(2,1)} collective-permute-done((bf16[4,32,3072]{2,1,0:T(8,128)(2,1)}, bf16[4,32,3072]{2,1,0:T(8,128)(2,1)}, u32[]{:S(2)}, u32[]{:S(2)}) %collective-permute-start) | collective-permute-done | bytes 786464 | tf_op jit(solution)/shard_map/ppermute | solution.py:190
  28.6 2.0 collective-permute-done.1
  30.9 20.2 %lookup.1 = (bf16[4,4,64,1536]{3,2,1,0:T(8,128)(2,1)S(1)}, bf16[4,4,64,1536]{3,2,1,0:T(8,128)(2,1)S(1)}, f32[8192,3072]{1,0:T(8,128)}) custom-call(s32[2]{0:T(128)S(1)} %pad_add_fusion.kc_ref, s32[1024]{0:T(1024)S(1)} %get-tuple-element.49.loc_ref, s32[1024,1]{1,0:T(8,128)S(1)} %copy.21.tgt_ref, bf16[8192,3072]{1,0:T(8,128)(2,1)} %emb.1), custom_call_target="tpu_custom_call" | custom-call | flops 40000000 | bytes 60000000 | tf_op jit(solution)/shard_map/lookup/pallas_call | solution.py:283
  51.1 1.3 convert_add_fusion.1
  53.6 1.3 convert_add_fusion
  55.8 2.1 %collective-permute-done.24 = f32[4,32,1536]{2,1,0:T(8,128)S(1)} collective-permute-done((f32[4,32,1536]{2,1,0:T(8,128)S(1)}, f32[4,32,1536]{2,1,0:T(8,128)S(1)}, u32[]{:S(2)}, u32[]{:S(2)}) %collective-permute-start.24) | collective-permute-done | bytes 786464 | tf_op jit(solution)/shard_map/ppermute | solution.py:190
  58.0 1.2 collective-permute-start.25
  60.1 1.0 collective-permute-start.10
  61.2 9.5 %collective-permute-done.5 = bf16[4,32,1536]{2,1,0:T(8,128)(2,1)S(1)} collective-permute-done((bf16[4,32,1536]{2,1,0:T(8,128)(2,1)S(1)}, bf16[4,32,1536]{2,1,0:T(8,128)(2,1)S(1)}, u32[]{:S(2)}, u32[]{:S(2)}) %collective-permute-start.5) | collective-permute-done | bytes 393248 | tf_op jit(solution)/shard_map/ppermute | solution.py:190
  71.0 15.0 %collective-permute-done.10 = bf16[4,32,1536]{2,1,0:T(8,128)(2,1)S(1)} collective-permute-done((bf16[4,32,1536]{2,1,0:T(8,128)(2,1)S(1)}, bf16[4,32,1536]{2,1,0:T(8,128)(2,1)S(1)}, u32[]{:S(2)}, u32[]{:S(2)}) %collective-permute-start.10) | collective-permute-done | bytes 393248 | tf_op jit(solution)/shard_map/ppermute | solution.py:190
  86.1 1.2 collective-permute-start.4
  88.3 2.0 collective-permute-start.11
  90.3 2.0 broadcast_select_fusion
  92.4 5.7 %collective-permute-done.4 = bf16[4,32,1536]{2,1,0:T(8,128)(2,1)S(1)} collective-permute-done((bf16[4,32,1536]{2,1,0:T(8,128)(2,1)S(1)}, bf16[4,32,1536]{2,1,0:T(8,128)(2,1)S(1)}, u32[]{:S(2)}, u32[]{:S(2)}) %collective-permute-start.4) | collective-permute-done | bytes 393248 | tf_op jit(solution)/shard_map/ppermute | solution.py:190
  98.0 1.4 collective-permute-done.3
  99.4 5.4 %collective-permute-done.6 = bf16[4,32,1536]{2,1,0:T(8,128)(2,1)S(1)} collective-permute-done((bf16[4,32,1536]{2,1,0:T(8,128)(2,1)S(1)}, bf16[4,32,1536]{2,1,0:T(8,128)(2,1)S(1)}, u32[]{:S(2)}, u32[]{:S(2)}) %collective-permute-start.6) | collective-permute-done | bytes 393248 | tf_op jit(solution)/shard_map/ppermute | solution.py:190
  104.8 1.3 collective-permute-done.11
  107.1 1.7 collective-permute-start.12
  108.9 1.5 collective-permute-start.7
  111.3 2.8 %fusion.10 = (f32[3072]{0:T(1024)S(1)}, f32[4,32]{1,0:T(4,128)S(1)}, f32[4,32,3072]{2,1,0:T(8,128)S(1)}) fusion(bf16[4,32,3072]{2,1,0:T(8,128)(2,1)S(1)} %get-tuple-element.95, f32[4,32]{1,0:T(4,128)S(1)} %add_rsqrt_fusion, f32[3072]{0:T(1024)S(1)} %convert_element_type.43, f32[4,32,3072]{2,1,0:T(8,128)S(1)} %collective-permute-done.29, ...), kind=kLoop, calls=%fused_computation.19 | loop fusion | flops 7467904 | bytes 8676353 | tf_op jit(solution)/shard_map/reduce_sum | solution.py:339
  114.1 1.2 collective-permute-done.44
  116.1 2.7 %collective-permute-done.18.refs_0_ = bf16[4,32,1536]{2,1,0:T(8,128)(2,1)S(1)} collective-permute-done((bf16[4,32,1536]{2,1,0:T(8,128)(2,1)S(1)}, bf16[4,32,1536]{2,1,0:T(8,128)(2,1)S(1)}, u32[]{:S(2)}, u32[]{:S(2)}) %collective-permute-start.18) | collective-permute-done | bytes 393248 | tf_op jit(solution)/shard_map/ppermute | solution.py:190
  118.8 7.6 %collective-permute-done.12.refs_2_ = bf16[4,32,1536]{2,1,0:T(8,128)(2,1)S(1)} collective-permute-done((bf16[4,32,1536]{2,1,0:T(8,128)(2,1)S(1)}, bf16[4,32,1536]{2,1,0:T(8,128)(2,1)S(1)}, u32[]{:S(2)}, u32[]{:S(2)}) %collective-permute-start.12) | collective-permute-done | bytes 393248 | tf_op jit(solution)/shard_map/ppermute | solution.py:190
  126.6 1.5 collective-permute-start.46
  128.6 1.6 collective-permute-done.46
  130.3 1.5 collective-permute-start.13
  132.6 1.7 collective-permute-start.33
  134.6 7.6 %collective-permute-done.13.refs_2_ = bf16[4,32,1536]{2,1,0:T(8,128)(2,1)S(1)} collective-permute-done((bf16[4,32,1536]{2,1,0:T(8,128)(2,1)S(1)}, bf16[4,32,1536]{2,1,0:T(8,128)(2,1)S(1)}, u32[]{:S(2)}, u32[]{:S(2)}) %collective-permute-start.13) | collective-permute-done | bytes 393248 | tf_op jit(solution)/shard_map/ppermute | solution.py:190
  142.3 1.5 collective-permute-start.37
  144.5 6.3 %collective-permute-done.36.refs_8_ = bf16[2,32,3072]{2,1,0:T(8,128)(2,1)} collective-permute-done((bf16[2,32,3072]{2,1,0:T(8,128)(2,1)S(1)}, bf16[2,32,3072]{2,1,0:T(8,128)(2,1)}, u32[]{:S(2)}, u32[]{:S(2)}) %collective-permute-start.36) | collective-permute-done | bytes 393248 | tf_op jit(solution)/shard_map/ppermute | solution.py:190
  150.8 1.5 collective-permute-done.33.refs_5_
  152.2 6.3 %collective-permute-done.32.refs_4_ = bf16[2,32,3072]{2,1,0:T(8,128)(2,1)S(1)} collective-permute-done((bf16[2,32,3072]{2,1,0:T(8,128)(2,1)S(1)}, bf16[2,32,3072]{2,1,0:T(8,128)(2,1)S(1)}, u32[]{:S(2)}, u32[]{:S(2)}) %collective-permute-start.32) | collective-permute-done | bytes 393248 | tf_op jit(solution)/shard_map/ppermute | solution.py:190
  160.8 9.6 %collective-permute-done.40.refs_12_ = bf16[2,32,3072]{2,1,0:T(8,128)(2,1)} collective-permute-done((bf16[2,32,3072]{2,1,0:T(8,128)(2,1)}, bf16[2,32,3072]{2,1,0:T(8,128)(2,1)}, u32[]{:S(2)}, u32[]{:S(2)}) %collective-permute-start.40) | collective-permute-done | bytes 393248 | tf_op jit(solution)/shard_map/ppermute | solution.py:190
  171.8 3.9 %shard_map.102 = (bf16[4,64,3072]{2,1,0:T(8,128)(2,1)S(1)}, bf16[4,256,640]{2,1,0:T(8,128)(2,1)}, f32[8192,3072]{1,0:T(8,128)}) custom-call(s32[2]{0:T(128)S(1)} %pad_add_fusion.kc_ref, bf16[1,3072]{1,0:T(2,128)(2,1)S(1)} %reshape.72.g_ref, bf16[3072,640]{1,0:T(8,128)(2,1)S(1)} %copy-done.2, ...), custom_call_target="tpu_custom_call", output_to_operand_aliasing={{2}: (7, {})} | custom-call | flops 8000000 | bytes 12000000 | tf_op jit(solution)/shard_map/pallas_call | solution.py:310
  176.3 3.9 %shard_map.103 = (bf16[4,64,3072]{2,1,0:T(8,128)(2,1)S(1)}, bf16[4,256,640]{2,1,0:T(8,128)(2,1)}, f32[8192,3072]{1,0:T(8,128)}) custom-call(s32[2]{0:T(128)S(1)} %pad_add_fusion.kc_ref, bf16[1,3072]{1,0:T(2,128)(2,1)S(1)} %reshape.72.g_ref, bf16[3072,640]{1,0:T(8,128)(2,1)S(1)} %copy-done.2, ...), custom_call_target="tpu_custom_call", output_to_operand_aliasing={{1}: (7, {}), {2}: (8, {})} | custom-call | flops 8000000 | bytes 12000000 | tf_op jit(solution)/shard_map/pallas_call | solution.py:310
  180.2 3.9 %shard_map.104 = (bf16[4,64,3072]{2,1,0:T(8,128)(2,1)S(1)}, bf16[4,256,640]{2,1,0:T(8,128)(2,1)}, f32[8192,3072]{1,0:T(8,128)}) custom-call(s32[2]{0:T(128)S(1)} %pad_add_fusion.kc_ref, bf16[1,3072]{1,0:T(2,128)(2,1)S(1)} %reshape.72.g_ref, bf16[3072,640]{1,0:T(8,128)(2,1)S(1)} %copy-done.2, ...), custom_call_target="tpu_custom_call", output_to_operand_aliasing={{1}: (7, {}), {2}: (8, {})} | custom-call | flops 8000000 | bytes 12000000 | tf_op jit(solution)/shard_map/pallas_call | solution.py:310
  184.1 3.9 %shard_map.105 = (bf16[4,64,3072]{2,1,0:T(8,128)(2,1)S(1)}, bf16[4,256,640]{2,1,0:T(8,128)(2,1)}, f32[8192,3072]{1,0:T(8,128)}) custom-call(s32[2]{0:T(128)S(1)} %pad_add_fusion.kc_ref, bf16[1,3072]{1,0:T(2,128)(2,1)S(1)} %reshape.72.g_ref, bf16[3072,640]{1,0:T(8,128)(2,1)S(1)} %copy-done.2, ...), custom_call_target="tpu_custom_call", output_to_operand_aliasing={{1}: (7, {}), {2}: (8, {})} | custom-call | flops 8000000 | bytes 12000000 | tf_op jit(solution)/shard_map/pallas_call | solution.py:310
  188.1 11.7 %dw.1 = (f32[3072,640]{1,0:T(8,128)}, f32[8192,3072]{1,0:T(8,128)}) custom-call(s32[1]{0:T(128)} %bitcast.1.c_ref, bf16[4,256,640]{2,1,0:T(8,128)(2,1)S(1)} %copy-done.4, bf16[4,64,3072]{2,1,0:T(8,128)(2,1)S(1)} %get-tuple-element.82.refs_0_, bf16[4,64,3072]{2,1,0:T(8,128)(2,1)S(1)} %get-tuple-element.83.refs_1_, ...), custom_call_target="tpu_custom_call", output_to_operand_aliasing={{1}: (6, {})} | custom-call | flops 30000000 | bytes 40000000 | tf_op jit(solution)/shard_map/dw/pallas_call | solution.py:321
  199.9 7.4 %put_rows.1 = f32[8192,3072]{1,0:T(8,128)} custom-call(s32[1]{0:T(128)} %bitcast.12.me_ref, s32[1024]{0:T(1024)S(1)} %get-tuple-element.71.rows_ref, s32[1]{0:T(128)} %bitcast.2.cnt_ref, s32[1,1024]{1,0:T(1,128)S(1)} %bitcast.24, bf16[2,32,3072]{2,1,0:T(8,128)(2,1)S(1)} %copy-done.8, ...), custom_call_target="tpu_custom_call", output_to_operand_aliasing={{}: (20, {})} | custom-call | tf_op jit(solution)/shard_map/put_rows/pallas_call | solution.py:345
  (143 shorter events, 18.3 us)
Async XLA Ops:
  6.6 22.0 %collective-permute-start = (bf16[4,32,3072]{2,1,0:T(8,128)(2,1)}, bf16[4,32,3072]{2,1,0:T(8,128)(2,1)}, u32[]{:S(2)}, u32[]{:S(2)}) collective-permute-start(bf16[4,32,3072]{2,1,0:T(8,128)(2,1)} %get-tuple-element.47), channel_id=1, source_target_pairs={{0,2},{1,3},{2,0},{3,1},{4,6},{5,7},{6,4},{7,5}} | collective-permute-start | bytes 2359304 | tf_op jit(solution)/shard_map/ppermute | solution.py:190
  9.9 20.7 %collective-permute-start.1 = (bf16[4,32,3072]{2,1,0:T(8,128)(2,1)}, bf16[4,32,3072]{2,1,0:T(8,128)(2,1)}, u32[]{:S(2)}, u32[]{:S(2)}) collective-permute-start(bf16[4,32,3072]{2,1,0:T(8,128)(2,1)} %get-tuple-element.48), channel_id=1, source_target_pairs={{0,4},{1,5},{2,6},{3,7},{4,0},{5,1},{6,2},{7,3}} | collective-permute-start | bytes 2359304 | tf_op jit(solution)/shard_map/ppermute | solution.py:190
  16.9 70.5 %collective-permute-start.23 = (bf16[4,32,3072]{2,1,0:T(8,128)(2,1)}, bf16[4,32,3072]{2,1,0:T(8,128)(2,1)}, u32[]{:S(2)}, u32[]{:S(2)}) collective-permute-start(bf16[4,32,3072]{2,1,0:T(8,128)(2,1)} %get-tuple-element.75), channel_id=1, source_target_pairs={{0,2},{1,3},{2,0},{3,1},{4,6},{5,7},{6,4},{7,5}} | collective-permute-start | bytes 2359304 | tf_op jit(solution)/shard_map/ppermute | solution.py:190
  17.4 70.4 %collective-permute-start.26 = (bf16[4,32,3072]{2,1,0:T(8,128)(2,1)}, bf16[4,32,3072]{2,1,0:T(8,128)(2,1)}, u32[]{:S(2)}, u32[]{:S(2)}) collective-permute-start(bf16[4,32,3072]{2,1,0:T(8,128)(2,1)} %get-tuple-element.79), channel_id=1, source_target_pairs={{0,4},{1,5},{2,6},{3,7},{4,0},{5,1},{6,2},{7,3}} | collective-permute-start | bytes 2359304 | tf_op jit(solution)/shard_map/ppermute | solution.py:190
  51.1 8.3 %collective-permute-start.2 = (bf16[4,4,64,1536]{3,2,1,0:T(8,128)(2,1)S(1)}, bf16[4,4,64,1536]{3,2,1,0:T(8,128)(2,1)S(1)}, u32[]{:S(2)}, u32[]{:S(2)}) collective-permute-start(bf16[4,4,64,1536]{3,2,1,0:T(8,128)(2,1)S(1)} %get-tuple-element.52), channel_id=1, source_target_pairs={{0,1},{1,0},{2,3},{3,2},{4,5},{5,4},{6,7},{7,6}} | collective-permute-start | bytes 9437192 | tf_op jit(solution)/shard_map/ppermute | solution.py:190
  52.6 5.3 %collective-permute-start.24 = (f32[4,32,1536]{2,1,0:T(8,128)S(1)}, f32[4,32,1536]{2,1,0:T(8,128)S(1)}, u32[]{:S(2)}, u32[]{:S(2)}) collective-permute-start(f32[4,32,1536]{2,1,0:T(8,128)S(1)} %slice_select_fusion.1), channel_id=1, source_target_pairs={{0,1},{1,0},{2,3},{3,2},{4,5},{5,4},{6,7},{7,6}} | collective-permute-start | bytes 2359304 | tf_op jit(solution)/shard_map/ppermute | solution.py:190
  55.0 4.2 %collective-permute-start.27 = (f32[4,32,1536]{2,1,0:T(8,128)S(1)}, f32[4,32,1536]{2,1,0:T(8,128)S(1)}, u32[]{:S(2)}, u32[]{:S(2)}) collective-permute-start(f32[4,32,1536]{2,1,0:T(8,128)S(1)} %slice_select_fusion), channel_id=1, source_target_pairs={{0,1},{1,0},{2,3},{3,2},{4,5},{5,4},{6,7},{7,6}} | collective-permute-start | bytes 2359304 | tf_op jit(solution)/shard_map/ppermute | solution.py:190
  58.0 30.3 %collective-permute-start.25 = (f32[4,32,1536]{2,1,0:T(8,128)S(1)}, f32[4,32,1536]{2,1,0:T(8,128)S(1)}, u32[]{:S(2)}, u32[]{:S(2)}) collective-permute-start(f32[4,32,1536]{2,1,0:T(8,128)S(1)} %select_add_fusion.4), channel_id=1, source_target_pairs={{0,4},{1,5},{2,6},{3,7},{4,0},{5,1},{6,2},{7,3}} | collective-permute-start | bytes 2359304 | tf_op jit(solution)/shard_map/ppermute | solution.py:190
  59.8 10.9 %collective-permute-start.5 = (bf16[4,32,1536]{2,1,0:T(8,128)(2,1)S(1)}, bf16[4,32,1536]{2,1,0:T(8,128)(2,1)S(1)}, u32[]{:S(2)}, u32[]{:S(2)}) collective-permute-start(bf16[4,32,1536]{2,1,0:T(8,128)(2,1)S(1)} %get-tuple-element.109), channel_id=1, source_target_pairs={{0,2},{1,3},{2,0},{3,1},{4,6},{5,7},{6,4},{7,5}} | collective-permute-start | bytes 1179656 | tf_op jit(solution)/shard_map/ppermute | solution.py:190
  60.1 25.9 %collective-permute-start.10 = (bf16[4,32,1536]{2,1,0:T(8,128)(2,1)S(1)}, bf16[4,32,1536]{2,1,0:T(8,128)(2,1)S(1)}, u32[]{:S(2)}, u32[]{:S(2)}) collective-permute-start(bf16[4,32,1536]{2,1,0:T(8,128)(2,1)S(1)} %get-tuple-element.110), channel_id=1, source_target_pairs={{0,4},{1,5},{2,6},{3,7},{4,0},{5,1},{6,2},{7,3}} | collective-permute-start | bytes 1179656 | tf_op jit(solution)/shard_map/ppermute | solution.py:190
  70.7 19.6 %collective-permute-start.28 = (f32[4,32,1536]{2,1,0:T(8,128)S(1)}, f32[4,32,1536]{2,1,0:T(8,128)S(1)}, u32[]{:S(2)}, u32[]{:S(2)}) collective-permute-start(f32[4,32,1536]{2,1,0:T(8,128)S(1)} %select_add_fusion.3), channel_id=1, source_target_pairs={{0,2},{1,3},{2,0},{3,1},{4,6},{5,7},{6,4},{7,5}} | collective-permute-start | bytes 2359304 | tf_op jit(solution)/shard_map/ppermute | solution.py:190
  86.1 12.0 %collective-permute-start.4 = (bf16[4,32,1536]{2,1,0:T(8,128)(2,1)S(1)}, bf16[4,32,1536]{2,1,0:T(8,128)(2,1)S(1)}, u32[]{:S(2)}, u32[]{:S(2)}) collective-permute-start(bf16[4,32,1536]{2,1,0:T(8,128)(2,1)S(1)} %slice_add_fusion.2), channel_id=1, source_target_pairs={{0,4},{1,5},{2,6},{3,7},{4,0},{5,1},{6,2},{7,3}} | collective-permute-start | bytes 1179656 | tf_op jit(solution)/shard_map/ppermute | solution.py:190
  87.4 12.0 %collective-permute-start.3 = (bf16[4,32,1536]{2,1,0:T(8,128)(2,1)S(1)}, bf16[4,32,1536]{2,1,0:T(8,128)(2,1)S(1)}, u32[]{:S(2)}, u32[]{:S(2)}) collective-permute-start(bf16[4,32,1536]{2,1,0:T(8,128)(2,1)S(1)} %slice_add_fusion.3), channel_id=1, source_target_pairs={{0,2},{1,3},{2,0},{3,1},{4,6},{5,7},{6,4},{7,5}} | collective-permute-start | bytes 1179656 | tf_op jit(solution)/shard_map/ppermute | solution.py:190
  87.8 17.0 %collective-permute-start.6 = (bf16[4,32,1536]{2,1,0:T(8,128)(2,1)S(1)}, bf16[4,32,1536]{2,1,0:T(8,128)(2,1)S(1)}, u32[]{:S(2)}, u32[]{:S(2)}) collective-permute-start(bf16[4,32,1536]{2,1,0:T(8,128)(2,1)S(1)} %add_add_fusion.2), channel_id=1, source_target_pairs={{0,4},{1,5},{2,6},{3,7},{4,0},{5,1},{6,2},{7,3}} | collective-permute-start | bytes 1179656 | tf_op jit(solution)/shard_map/ppermute | solution.py:190
  88.3 17.8 %collective-permute-start.11 = (bf16[4,32,1536]{2,1,0:T(8,128)(2,1)S(1)}, bf16[4,32,1536]{2,1,0:T(8,128)(2,1)S(1)}, u32[]{:S(2)}, u32[]{:S(2)}) collective-permute-start(bf16[4,32,1536]{2,1,0:T(8,128)(2,1)S(1)} %add_add_fusion), channel_id=1, source_target_pairs={{0,2},{1,3},{2,0},{3,1},{4,6},{5,7},{6,4},{7,5}} | collective-permute-start | bytes 1179656 | tf_op jit(solution)/shard_map/ppermute | solution.py:190
  92.3 19.0 %collective-permute-start.29 = (f32[4,32,3072]{2,1,0:T(8,128)S(1)}, f32[4,32,3072]{2,1,0:T(8,128)S(1)}, u32[]{:S(2)}, u32[]{:S(2)}) collective-permute-start(f32[4,32,3072]{2,1,0:T(8,128)S(1)} %broadcast_select_fusion), channel_id=1, source_target_pairs={{0,1},{1,0},{2,3},{3,2},{4,5},{5,4},{6,7},{7,6}} | collective-permute-start | bytes 4718600 | tf_op jit(solution)/shard_map/ppermute | solution.py:190
  106.3 2.6 %collective-permute-start.21 = (bf16[4,32,1536]{2,1,0:T(8,128)(2,1)S(1)}, bf16[4,32,1536]{2,1,0:T(8,128)(2,1)S(1)}, u32[]{:S(2)}, u32[]{:S(2)}) collective-permute-start(bf16[4,32,1536]{2,1,0:T(8,128)(2,1)S(1)} %get-tuple-element.98.refs_0_), channel_id=1, source_target_pairs={{0,1},{1,0},{2,3},{3,2},{4,5},{5,4},{6,7},{7,6}} | collective-permute-start | bytes 1179656 | tf_op jit(solution)/shard_map/ppermute | solution.py:190
  106.3 4.0 %collective-permute-start.22 = (bf16[4,32,1536]{2,1,0:T(8,128)(2,1)S(1)}, bf16[4,32,1536]{2,1,0:T(8,128)(2,1)S(1)}, u32[]{:S(2)}, u32[]{:S(2)}) collective-permute-start(bf16[4,32,1536]{2,1,0:T(8,128)(2,1)S(1)} %get-tuple-element.97.refs_2_), channel_id=1, source_target_pairs={{0,1},{1,0},{2,3},{3,2},{4,5},{5,4},{6,7},{7,6}} | collective-permute-start | bytes 1179656 | tf_op jit(solution)/shard_map/ppermute | solution.py:190
  106.8 12.0 %collective-permute-start.18 = (bf16[4,32,1536]{2,1,0:T(8,128)(2,1)S(1)}, bf16[4,32,1536]{2,1,0:T(8,128)(2,1)S(1)}, u32[]{:S(2)}, u32[]{:S(2)}) collective-permute-start(bf16[4,32,1536]{2,1,0:T(8,128)(2,1)S(1)} %get-tuple-element.98.refs_0_), channel_id=1, source_target_pairs={{0,2},{1,3},{2,0},{3,1},{4,6},{5,7},{6,4},{7,5}} | collective-permute-start | bytes 1179656 | tf_op jit(solution)/shard_map/ppermute | solution.py:190
  107.1 19.3 %collective-permute-start.12 = (bf16[4,32,1536]{2,1,0:T(8,128)(2,1)S(1)}, bf16[4,32,1536]{2,1,0:T(8,128)(2,1)S(1)}, u32[]{:S(2)}, u32[]{:S(2)}) collective-permute-start(bf16[4,32,1536]{2,1,0:T(8,128)(2,1)S(1)} %get-tuple-element.97.refs_2_), channel_id=1, source_target_pairs={{0,2},{1,3},{2,0},{3,1},{4,6},{5,7},{6,4},{7,5}} | collective-permute-start | bytes 1179656 | tf_op jit(solution)/shard_map/ppermute | solution.py:190
  108.9 19.2 %collective-permute-start.7 = (bf16[4,32,1536]{2,1,0:T(8,128)(2,1)S(1)}, bf16[4,32,1536]{2,1,0:T(8,128)(2,1)S(1)}, u32[]{:S(2)}, u32[]{:S(2)}) collective-permute-start(bf16[4,32,1536]{2,1,0:T(8,128)(2,1)S(1)} %get-tuple-element.98.refs_0_), channel_id=1, source_target_pairs={{0,4},{1,5},{2,6},{3,7},{4,0},{5,1},{6,2},{7,3}} | collective-permute-start | bytes 1179656 | tf_op jit(solution)/shard_map/ppermute | solution.py:190
  110.3 17.9 %collective-permute-start.16 = (bf16[4,32,1536]{2,1,0:T(8,128)(2,1)S(1)}, bf16[4,32,1536]{2,1,0:T(8,128)(2,1)S(1)}, u32[]{:S(2)}, u32[]{:S(2)}) collective-permute-start(bf16[4,32,1536]{2,1,0:T(8,128)(2,1)S(1)} %get-tuple-element.97.refs_2_), channel_id=1, source_target_pairs={{0,4},{1,5},{2,6},{3,7},{4,0},{5,1},{6,2},{7,3}} | collective-permute-start | bytes 1179656 | tf_op jit(solution)/shard_map/ppermute | solution.py:190
  114.1 1.2 collective-permute-start.44
  115.3 11.3 %collective-permute-start.45 = (f32[3072]{0:T(1024)S(1)}, f32[3072]{0:T(1024)S(1)}, u32[]{:S(2)}, u32[]{:S(2)}) collective-permute-start(f32[3072]{0:T(1024)S(1)} %add.138), channel_id=1, source_target_pairs={{0,2},{1,3},{2,0},{3,1},{4,6},{5,7},{6,4},{7,5}} | collective-permute-start | bytes 36872 | tf_op jit(solution)/shard_map/ppermute | solution.py:190
  115.6 56.2 %copy-start.2 = (bf16[3072,640]{1,0:T(8,128)(2,1)S(1)}, bf16[3072,640]{1,0:T(8,128)(2,1)}, u32[]{:S(2)}) copy-start(bf16[3072,640]{1,0:T(8,128)(2,1)} %w_ref.13) | copy-start | bytes 11796484
  118.8 12.9 %collective-permute-start.19 = (bf16[4,32,1536]{2,1,0:T(8,128)(2,1)S(1)}, bf16[4,32,1536]{2,1,0:T(8,128)(2,1)S(1)}, u32[]{:S(2)}, u32[]{:S(2)}) collective-permute-start(bf16[4,32,1536]{2,1,0:T(8,128)(2,1)S(1)} %collective-permute-done.18.refs_0_), channel_id=1, source_target_pairs={{0,1},{1,0},{2,3},{3,2},{4,5},{5,4},{6,7},{7,6}} | collective-permute-start | bytes 1179656 | tf_op jit(solution)/shard_map/ppermute | solution.py:190
  126.4 5.6 %collective-permute-start.20 = (bf16[4,32,1536]{2,1,0:T(8,128)(2,1)S(1)}, bf16[4,32,1536]{2,1,0:T(8,128)(2,1)S(1)}, u32[]{:S(2)}, u32[]{:S(2)}) collective-permute-start(bf16[4,32,1536]{2,1,0:T(8,128)(2,1)S(1)} %collective-permute-done.12.refs_2_), channel_id=1, source_target_pairs={{0,1},{1,0},{2,3},{3,2},{4,5},{5,4},{6,7},{7,6}} | collective-permute-start | bytes 1179656 | tf_op jit(solution)/shard_map/ppermute | solution.py:190
  126.6 3.7 %collective-permute-start.46 = (f32[3072]{0:T(1024)S(1)}, f32[3072]{0:T(1024)S(1)}, u32[]{:S(2)}, u32[]{:S(2)}) collective-permute-start(f32[3072]{0:T(1024)S(1)} %add.139), channel_id=1, source_target_pairs={{0,4},{1,5},{2,6},{3,7},{4,0},{5,1},{6,2},{7,3}} | collective-permute-start | bytes 36872 | tf_op jit(solution)/shard_map/ppermute | solution.py:190
  128.1 4.5 %collective-permute-start.15 = (bf16[4,32,1536]{2,1,0:T(8,128)(2,1)S(1)}, bf16[4,32,1536]{2,1,0:T(8,128)(2,1)S(1)}, u32[]{:S(2)}, u32[]{:S(2)}) collective-permute-start(bf16[4,32,1536]{2,1,0:T(8,128)(2,1)S(1)} %collective-permute-done.7.refs_0_), channel_id=1, source_target_pairs={{0,1},{1,0},{2,3},{3,2},{4,5},{5,4},{6,7},{7,6}} | collective-permute-start | bytes 1179656 | tf_op jit(solution)/shard_map/ppermute | solution.py:190
  128.2 6.1 %collective-permute-start.17 = (bf16[4,32,1536]{2,1,0:T(8,128)(2,1)S(1)}, bf16[4,32,1536]{2,1,0:T(8,128)(2,1)S(1)}, u32[]{:S(2)}, u32[]{:S(2)}) collective-permute-start(bf16[4,32,1536]{2,1,0:T(8,128)(2,1)S(1)} %collective-permute-done.16.refs_2_), channel_id=1, source_target_pairs={{0,1},{1,0},{2,3},{3,2},{4,5},{5,4},{6,7},{7,6}} | collective-permute-start | bytes 1179656 | tf_op jit(solution)/shard_map/ppermute | solution.py:190
  130.3 12.0 %collective-permute-start.13 = (bf16[4,32,1536]{2,1,0:T(8,128)(2,1)S(1)}, bf16[4,32,1536]{2,1,0:T(8,128)(2,1)S(1)}, u32[]{:S(2)}, u32[]{:S(2)}) collective-permute-start(bf16[4,32,1536]{2,1,0:T(8,128)(2,1)S(1)} %collective-permute-done.12.refs_2_), channel_id=1, source_target_pairs={{0,4},{1,5},{2,6},{3,7},{4,0},{5,1},{6,2},{7,3}} | collective-permute-start | bytes 1179656 | tf_op jit(solution)/shard_map/ppermute | solution.py:190
  131.7 12.0 %collective-permute-start.8 = (bf16[4,32,1536]{2,1,0:T(8,128)(2,1)S(1)}, bf16[4,32,1536]{2,1,0:T(8,128)(2,1)S(1)}, u32[]{:S(2)}, u32[]{:S(2)}) collective-permute-start(bf16[4,32,1536]{2,1,0:T(8,128)(2,1)S(1)} %collective-permute-done.7.refs_0_), channel_id=1, source_target_pairs={{0,2},{1,3},{2,0},{3,1},{4,6},{5,7},{6,4},{7,5}} | collective-permute-start | bytes 1179656 | tf_op jit(solution)/shard_map/ppermute | solution.py:190
  132.1 18.7 %collective-permute-start.36 = (bf16[2,32,3072]{2,1,0:T(8,128)(2,1)S(1)}, bf16[2,32,3072]{2,1,0:T(8,128)(2,1)}, u32[]{:S(2)}, u32[]{:S(2)}) collective-permute-start(bf16[2,32,3072]{2,1,0:T(8,128)(2,1)S(1)} %get-tuple-element.112.refs_0_), channel_id=1, source_target_pairs={{0,4},{1,5},{2,6},{3,7},{4,0},{5,1},{6,2},{7,3}} | collective-permute-start | bytes 1179656 | tf_op jit(solution)/shard_map/ppermute | solution.py:190
  132.6 19.7 %collective-permute-start.33 = (bf16[2,32,3072]{2,1,0:T(8,128)(2,1)S(1)}, bf16[2,32,3072]{2,1,0:T(8,128)(2,1)}, u32[]{:S(2)}, u32[]{:S(2)}) collective-permute-start(bf16[2,32,3072]{2,1,0:T(8,128)(2,1)S(1)} %get-tuple-element.111.refs_1_), channel_id=1, source_target_pairs={{0,2},{1,3},{2,0},{3,1},{4,6},{5,7},{6,4},{7,5}} | collective-permute-start | bytes 1179656 | tf_op jit(solution)/shard_map/ppermute | solution.py:190
  134.3 24.2 %collective-permute-start.32 = (bf16[2,32,3072]{2,1,0:T(8,128)(2,1)S(1)}, bf16[2,32,3072]{2,1,0:T(8,128)(2,1)S(1)}, u32[]{:S(2)}, u32[]{:S(2)}) collective-permute-start(bf16[2,32,3072]{2,1,0:T(8,128)(2,1)S(1)} %get-tuple-element.112.refs_0_), channel_id=1, source_target_pairs={{0,2},{1,3},{2,0},{3,1},{4,6},{5,7},{6,4},{7,5}} | collective-permute-start | bytes 1179656 | tf_op jit(solution)/shard_map/ppermute | solution.py:190
  142.3 16.3 %collective-permute-start.37 = (bf16[2,32,3072]{2,1,0:T(8,128)(2,1)S(1)}, bf16[2,32,3072]{2,1,0:T(8,128)(2,1)}, u32[]{:S(2)}, u32[]{:S(2)}) collective-permute-start(bf16[2,32,3072]{2,1,0:T(8,128)(2,1)S(1)} %get-tuple-element.111.refs_1_), channel_id=1, source_target_pairs={{0,4},{1,5},{2,6},{3,7},{4,0},{5,1},{6,2},{7,3}} | collective-permute-start | bytes 1179656 | tf_op jit(solution)/shard_map/ppermute | solution.py:190
  143.7 15.2 %collective-permute-start.30 = (bf16[2,32,3072]{2,1,0:T(8,128)(2,1)S(1)}, bf16[2,32,3072]{2,1,0:T(8,128)(2,1)S(1)}, u32[]{:S(2)}, u32[]{:S(2)}) collective-permute-start(bf16[2,32,3072]{2,1,0:T(8,128)(2,1)S(1)} %get-tuple-element.112.refs_0_), channel_id=1, source_target_pairs={{0,1},{1,0},{2,3},{3,2},{4,5},{5,4},{6,7},{7,6}} | collective-permute-start | bytes 1179656 | tf_op jit(solution)/shard_map/ppermute | solution.py:190
  150.8 9.4 %collective-permute-start.31 = (bf16[2,32,3072]{2,1,0:T(8,128)(2,1)S(1)}, bf16[2,32,3072]{2,1,0:T(8,128)(2,1)S(1)}, u32[]{:S(2)}, u32[]{:S(2)}) collective-permute-start(bf16[2,32,3072]{2,1,0:T(8,128)(2,1)S(1)} %get-tuple-element.111.refs_1_), channel_id=1, source_target_pairs={{0,1},{1,0},{2,3},{3,2},{4,5},{5,4},{6,7},{7,6}} | collective-permute-start | bytes 1179656 | tf_op jit(solution)/shard_map/ppermute | solution.py:190
  152.2 8.0 %collective-permute-start.14 = (bf16[4,32,1536]{2,1,0:T(8,128)(2,1)S(1)}, bf16[4,32,1536]{2,1,0:T(8,128)(2,1)S(1)}, u32[]{:S(2)}, u32[]{:S(2)}) collective-permute-start(bf16[4,32,1536]{2,1,0:T(8,128)(2,1)S(1)} %collective-permute-done.13.refs_2_), channel_id=1, source_target_pairs={{0,1},{1,0},{2,3},{3,2},{4,5},{5,4},{6,7},{7,6}} | collective-permute-start | bytes 1179656 | tf_op jit(solution)/shard_map/ppermute | solution.py:190
  158.6 2.2 %collective-permute-start.9 = (bf16[4,32,1536]{2,1,0:T(8,128)(2,1)S(1)}, bf16[4,32,1536]{2,1,0:T(8,128)(2,1)S(1)}, u32[]{:S(2)}, u32[]{:S(2)}) collective-permute-start(bf16[4,32,1536]{2,1,0:T(8,128)(2,1)S(1)} %collective-permute-done.8.refs_0_), channel_id=1, source_target_pairs={{0,1},{1,0},{2,3},{3,2},{4,5},{5,4},{6,7},{7,6}} | collective-permute-start | bytes 1179656 | tf_op jit(solution)/shard_map/ppermute | solution.py:190
  158.6 11.8 %collective-permute-start.40 = (bf16[2,32,3072]{2,1,0:T(8,128)(2,1)}, bf16[2,32,3072]{2,1,0:T(8,128)(2,1)}, u32[]{:S(2)}, u32[]{:S(2)}) collective-permute-start(bf16[2,32,3072]{2,1,0:T(8,128)(2,1)} %collective-permute-done.36.refs_8_), channel_id=1, source_target_pairs={{0,2},{1,3},{2,0},{3,1},{4,6},{5,7},{6,4},{7,5}} | collective-permute-start | bytes 1179656 | tf_op jit(solution)/shard_map/ppermute | solution.py:190
  159.7 11.5 %collective-permute-start.41 = (bf16[2,32,3072]{2,1,0:T(8,128)(2,1)}, bf16[2,32,3072]{2,1,0:T(8,128)(2,1)}, u32[]{:S(2)}, u32[]{:S(2)}) collective-permute-start(bf16[2,32,3072]{2,1,0:T(8,128)(2,1)} %collective-permute-done.33.refs_5_), channel_id=1, source_target_pairs={{0,4},{1,5},{2,6},{3,7},{4,0},{5,1},{6,2},{7,3}} | collective-permute-start | bytes 1179656 | tf_op jit(solution)/shard_map/ppermute | solution.py:190
  160.2 11.0 %collective-permute-start.34 = (bf16[2,32,3072]{2,1,0:T(8,128)(2,1)S(1)}, bf16[2,32,3072]{2,1,0:T(8,128)(2,1)S(1)}, u32[]{:S(2)}, u32[]{:S(2)}) collective-permute-start(bf16[2,32,3072]{2,1,0:T(8,128)(2,1)S(1)} %collective-permute-done.32.refs_4_), channel_id=1, source_target_pairs={{0,1},{1,0},{2,3},{3,2},{4,5},{5,4},{6,7},{7,6}} | collective-permute-start | bytes 1179656 | tf_op jit(solution)/shard_map/ppermute | solution.py:190
  160.2 39.6 %collective-permute-start.35 = (bf16[2,32,3072]{2,1,0:T(8,128)(2,1)}, bf16[2,32,3072]{2,1,0:T(8,128)(2,1)}, u32[]{:S(2)}, u32[]{:S(2)}) collective-permute-start(bf16[2,32,3072]{2,1,0:T(8,128)(2,1)} %collective-permute-done.33.refs_5_), channel_id=1, source_target_pairs={{0,1},{1,0},{2,3},{3,2},{4,5},{5,4},{6,7},{7,6}} | collective-permute-start | bytes 1179656 | tf_op jit(solution)/shard_map/ppermute | solution.py:190
  160.7 39.1 %collective-permute-start.38 = (bf16[2,32,3072]{2,1,0:T(8,128)(2,1)}, bf16[2,32,3072]{2,1,0:T(8,128)(2,1)}, u32[]{:S(2)}, u32[]{:S(2)}) collective-permute-start(bf16[2,32,3072]{2,1,0:T(8,128)(2,1)} %collective-permute-done.36.refs_8_), channel_id=1, source_target_pairs={{0,1},{1,0},{2,3},{3,2},{4,5},{5,4},{6,7},{7,6}} | collective-permute-start | bytes 1179656 | tf_op jit(solution)/shard_map/ppermute | solution.py:190
  170.4 29.4 %collective-permute-start.39 = (bf16[2,32,3072]{2,1,0:T(8,128)(2,1)}, bf16[2,32,3072]{2,1,0:T(8,128)(2,1)}, u32[]{:S(2)}, u32[]{:S(2)}) collective-permute-start(bf16[2,32,3072]{2,1,0:T(8,128)(2,1)} %collective-permute-done.37.refs_9_), channel_id=1, source_target_pairs={{0,1},{1,0},{2,3},{3,2},{4,5},{5,4},{6,7},{7,6}} | collective-permute-start | bytes 1179656 | tf_op jit(solution)/shard_map/ppermute | solution.py:190
  171.2 28.6 %collective-permute-start.42 = (bf16[2,32,3072]{2,1,0:T(8,128)(2,1)}, bf16[2,32,3072]{2,1,0:T(8,128)(2,1)}, u32[]{:S(2)}, u32[]{:S(2)}) collective-permute-start(bf16[2,32,3072]{2,1,0:T(8,128)(2,1)} %collective-permute-done.40.refs_12_), channel_id=1, source_target_pairs={{0,1},{1,0},{2,3},{3,2},{4,5},{5,4},{6,7},{7,6}} | collective-permute-start | bytes 1179656 | tf_op jit(solution)/shard_map/ppermute | solution.py:190
  171.2 28.6 %collective-permute-start.43 = (bf16[2,32,3072]{2,1,0:T(8,128)(2,1)}, bf16[2,32,3072]{2,1,0:T(8,128)(2,1)}, u32[]{:S(2)}, u32[]{:S(2)}) collective-permute-start(bf16[2,32,3072]{2,1,0:T(8,128)(2,1)} %collective-permute-done.41.refs_13_), channel_id=1, source_target_pairs={{0,1},{1,0},{2,3},{3,2},{4,5},{5,4},{6,7},{7,6}} | collective-permute-start | bytes 1179656 | tf_op jit(solution)/shard_map/ppermute | solution.py:190
  (24 other events, 210.7 us)

commit v3 on v2

--- a/solution.py
+++ b/solution.py
@@ -11,6 +11,7 @@
 ANY = pl.BlockSpec(memory_space=pl.ANY)
 VMEM = pl.BlockSpec(memory_space=pltpu.VMEM)
 SMEM = pl.BlockSpec(memory_space=pltpu.SMEM)
+HBM = pl.BlockSpec(memory_space=pltpu.HBM)
 ZR = 128
 BLK = 256
 LOOKUP_EARLY, LOOKUP_SHARE, NORM_SHARE = 14, 28, 5
@@ -30,6 +31,29 @@
         pl.loop(first, last)(lambda i: copy(i).wait())
 
     return start, wait
+
+
+def pdn_first_kernel(j, c_ref, du_hbm, w_hbm, h0, h1, du_ref, w_ref, sem, wsem):
+    c = c_ref[0]
+    mb, tc, _ = du_ref.shape
+    tl = tc // 2
+    wc = 512
+    steps = w_hbm.shape[0] // wc
+    z = pl.multiple_of(jnp.bitwise_xor(c, j) * tc, tc)
+    rows_in = pltpu.make_async_copy(du_hbm.at[:, pl.ds(z, tc), :], du_ref, sem)
+    rows_in.start()
+    loads = [pltpu.make_async_copy(w_hbm.at[pl.ds(n * wc, wc)], w_ref.at[pl.ds(n * wc, wc)], wsem.at[n]) for n in range(steps)]
+    for cp in loads:
+        cp.start()
+    rows_in.wait()
+    rows = du_ref[...].reshape(mb * tc, du_ref.shape[2])
+    for n in range(steps):
+        loads[n].wait()
+        cols = slice(n * wc, (n + 1) * wc)
+        v = lax.dot_general(rows, w_ref[cols, :], (((1,), (1,)), ((), ())), preferred_element_type=jnp.float32)
+        v = v.astype(jnp.bfloat16).reshape(mb, tc, wc)
+        h0[:, :, cols] = v[:, :tl]
+        h1[:, :, cols] = v[:, tl:]
 
 
 def pdn_kernel(js, c_ref, du_ref, w_ref, *outs):
@@ -48,7 +72,7 @@
                 outs[2 * i + h][:, :, cols] = v[:, h * tl:(h + 1) * tl]
 
 
-def lookup_kernel(kc_ref, loc_ref, tgt_ref, emb, mine_ref, theirs_ref, de, buf, sem, z, zsem):
+def lookup_kernel(kc_ref, loc_ref, tgt_ref, emb, mine_ref, far_ref, near_ref, de, buf, sem, z, zsem):
     k, c = kc_ref[0], kc_ref[1]
     vl, d = emb.shape
     nj, mb, tc, hd = mine_ref.shape
@@ -88,6 +112,7 @@
     late_start(False)
 
     for j in range(nj):
+        theirs = far_ref.at[0] if j == 3 else near_ref.at[j]
         zc = jnp.bitwise_xor(c, j)
 
         @pl.loop(0, mb)
@@ -96,9 +121,9 @@
             tgt = tgt_ref[pl.ds(pl.multiple_of(t0, tc), tc), :]
             sel = (lax.broadcasted_iota(jnp.int32, (tc, 2 * tc), 1) == tgt).astype(jnp.bfloat16)
             rows = pl.ds(pl.multiple_of(2 * t0, 2 * tc), 2 * tc)
-            for out, half in ((theirs_ref, 1 - k), (mine_ref, k)):
+            for out, half in ((theirs, 1 - k), (mine_ref.at[j], k)):
                 v = buf[rows, pl.ds(pl.multiple_of(half * hd, 128), hd)]
-                out[j, m] = jnp.dot(sel, v, preferred_element_type=jnp.float32).astype(jnp.bfloat16)
+                out[m] = jnp.dot(sel, v, preferred_element_type=jnp.float32).astype(jnp.bfloat16)
 
     wait()
     late_wait()
@@ -134,23 +159,26 @@
 
 
 def dw_kernel(c_ref, du_ref, *refs):
-    ns, (dw_ref, de, z, zsem) = refs[:4], refs[-4:]
+    ns, (dw, de, stage, sem, z, zsem) = refs[:4], refs[-6:]
     mb, tc, d = ns[0].shape
     start, wait = zero_fill(de, z, zsem, LOOKUP_SHARE + 4 * NORM_SHARE, de.shape[0] // ZR)
     start()
-    dc = 512
-
-    @pl.loop(0, d // dc)
-    def _(i):
-        c = pl.ds(pl.multiple_of(i * dc, dc), dc)
-        acc = jnp.zeros((dc, du_ref.shape[2]), jnp.float32)
+    dc = stage.shape[1]
+    copies = []
+    for i in range(d // dc):
+        acc = jnp.zeros(stage.shape[1:], jnp.float32)
         for j, n_ref in enumerate(ns):
             rows = pl.ds(pl.multiple_of(jnp.bitwise_xor(c_ref[0], j) * tc, tc), tc)
-            left = jnp.concatenate([n_ref[m, :, c] for m in range(mb)], axis=0)
+            left = jnp.concatenate([n_ref[m, :, i * dc:(i + 1) * dc] for m in range(mb)], axis=0)
             right = jnp.concatenate([du_ref[m, rows, :] for m in range(mb)], axis=0)
             acc += lax.dot_general(left, right, (((0,), (0,)), ((), ())), preferred_element_type=jnp.float32)
-        dw_ref[c, :] = acc
-
+        if i >= 2:
+            copies[i - 2].wait()
+        stage[i % 2] = acc
+        copies.append(pltpu.make_async_copy(stage.at[i % 2], dw.at[pl.ds(i * dc, dc)], sem.at[i % 2]))
+        copies[i].start()
+    for cp in copies[-2:]:
+        cp.wait()
     wait()
 
 
@@ -257,7 +285,21 @@
         n = flat.shape[0]
         loc = flat - r * vl
         own = (loc >= 0) & (loc < vl)
-        part = pdn((3,))
+        part = {3: pl.pallas_call(
+            functools.partial(pdn_first_kernel, 3),
+            out_shape=(jax.ShapeDtypeStruct((mb, tl, d), jnp.bfloat16),) * 2,
+            in_specs=[SMEM, HBM, HBM],
+            out_specs=(VMEM, VMEM),
+            scratch_shapes=[
+                pltpu.VMEM((mb, tc, f), jnp.bfloat16),
+                pltpu.VMEM((d, f), jnp.bfloat16),
+                pltpu.SemaphoreType.DMA,
+                pltpu.SemaphoreType.DMA((6,)),
+            ],
+            cost_estimate=pl.CostEstimate(flops=5_000_000, bytes_accessed=8_000_000, transcendentals=0),
+            compiler_params=pltpu.CompilerParams(vmem_limit_bytes=63 * 2**20),
+            name="pdn_a",
+        )(c.reshape(1), du, w)}
         part.update(pdn((1, 2)))
         part.update(pdn((0,)))
         d0, d1 = swap(part[3][0], 2), swap(part[3][1], 4)
@@ -280,18 +322,18 @@
         fy = swap(pick(ty[..., :hd], ty[..., hd:]) + gy, 4)
         fx = swap(pick(tx[..., :hd], tx[..., hd:]) + gx, 2)
 
-        mine, theirs, de = pl.pallas_call(
+        mine, far, near, de = pl.pallas_call(
             lookup_kernel,
-            out_shape=(half_shape(4), half_shape(4), de_shape),
+            out_shape=(half_shape(4), half_shape(1), half_shape(3), de_shape),
             in_specs=[SMEM, SMEM, VMEM, ANY],
-            out_specs=(VMEM, VMEM, ANY),
+            out_specs=(VMEM, VMEM, VMEM, ANY),
             scratch_shapes=[pltpu.VMEM((2 * n, d), jnp.bfloat16), pltpu.SemaphoreType.DMA] + zero_scratch,
             cost_estimate=pl.CostEstimate(flops=40_000_000, bytes_accessed=60_000_000, transcendentals=0),
             compiler_params=pltpu.CompilerParams(vmem_limit_bytes=40 * 2**20),
             name="lookup",
         )(kc, loc, tgt.reshape(n, 1), emb)
-        got = swap(theirs, 1)
-        xpairs = {j: (mine[j], got[j]) for j in range(4)}
+        far, near = swap(far, 1), swap(near, 1)
+        xpairs = {j: (mine[j], far[0] if j == 3 else near[j]) for j in range(4)}
 
         def widen(v):
             o = jnp.zeros_like(v)
@@ -322,8 +364,8 @@
             dw_kernel,
             out_shape=(jax.ShapeDtypeStruct((d, f), jnp.float32), de_shape),
             in_specs=[SMEM] + [VMEM] * 5 + [ANY],
-            out_specs=(VMEM, ANY),
-            scratch_shapes=zero_scratch,
+            out_specs=(ANY, ANY),
+            scratch_shapes=[pltpu.VMEM((2, 512, f), jnp.float32), pltpu.SemaphoreType.DMA((2,))] + zero_scratch,
             input_output_aliases={6: 1},
             cost_estimate=pl.CostEstimate(flops=30_000_000, bytes_accessed=40_000_000, transcendentals=0),
             compiler_params=pltpu.CompilerParams(vmem_limit_bytes=40 * 2**20),

time: 208 us -> 210 us (level)
  waiting for transfers between devices: 92.3 us -> 84.5 us
  Pallas kernels: 62.4 us -> 69.5 us
    ppermute x47 -> x48, waiting for transfers between devices: 92.3 us -> 84.5 us  [swap(): return lax.ppermute(v, 'tp', [(i, i ^ bit) for i in range(groups)])]
    pallas_call x1 -> x2, Pallas kernels: 20.2 us -> 25.8 us  [the longest x1 20.2 us: local(): pl.pallas_call(lookup_kernel, out_shape=(half_shape(4), half_shape(1), ha...]
    pallas_call x1, Pallas kernels: 11.7 us -> 15.7 us  [local(): pl.pallas_call(dw_kernel, out_shape=(jax.ShapeDtypeStruct((d, f), jnp.flo...]
    pallas_call x3 -> x2, Pallas kernels: 7.57 us -> 5.02 us  [pdn(): pl.pallas_call(functools.partial(pdn_kernel, js), out_shape=(jax.ShapeDty...]
    ppermute x47 -> x48, starting transfers between devices: 28 us -> 29.4 us  [swap(): return lax.ppermute(v, 'tp', [(i, i ^ bit) for i in range(groups)])]
  transfers between devices with their start and end apart: 47 -> 48, of which waited for: 20 -> 21; matrix products, arithmetic and copies ran while one was open for 7% -> 7% of each run, Pallas kernels for 25% -> 27%
where the time goes in v3:
time: 210 us; the launch traced here: 209 us
  waiting for transfers between devices  84.5 us (40%)
  Pallas kernels  69.5 us (33%)
  starting transfers between devices  29.4 us (14%)
  other arithmetic  13.1 us (6%)
  local copies, waits for them, and re-layouts  11 us (5%)
    ppermute x48, waiting for transfers between devices, swap(): return lax.ppermute(v, 'tp', [(i, i ^ bit) for i in range(groups)])  84.5 us
    ppermute x48, starting transfers between devices, swap(): return lax.ppermute(v, 'tp', [(i, i ^ bit) for i in range(groups)])  29.4 us
    pallas_call x1, Pallas kernels, local(): pl.pallas_call(lookup_kernel, out_shape=(half_shape(4), half_shape(1), ha...  20.2 us
    pallas_call x1, Pallas kernels, local(): pl.pallas_call(dw_kernel, out_shape=(jax.ShapeDtypeStruct((d, f), jnp.flo...  15.7 us
    pallas_call x4, Pallas kernels, local(): pl.pallas_call(functools.partial(norm_kernel, j), out_shape=(jax.ShapeDty...  15.6 us
    unnamed x51, local copies, waits for them, and re-layouts  10.2 us
    pallas_call x1, Pallas kernels, local(): pl.pallas_call(scatter_kernel, out_shape=de_shape, in_specs=[SMEM, SMEM,...  7.38 us
    pallas_call x1, Pallas kernels, local(): pl.pallas_call(functools.partial(pdn_first_kernel, 3), out_shape=(jax.Sha...  5.59 us
  transfers between devices with their start and end apart: 48, of which 21 were waited for; matrix products, arithmetic and copies ran while one was open for 7% of the time, Pallas kernels for 27%

profile of v3, /device:TPU:0, one launch (start us, length us, event | category | flops | bytes accessed | tf_op | source)
XLA Modules:
  0.0 209.0 jit_solution(3062381336466206330)
XLA Ops:
  0.6 5.6 %pdn_a.1 = (bf16[4,32,3072]{2,1,0:T(8,128)(2,1)}, bf16[4,32,3072]{2,1,0:T(8,128)(2,1)}) custom-call(s32[1]{0:T(128)} %bitcast.1.c_ref, bf16[4,256,640]{2,1,0:T(8,128)(2,1)} %du_ref.5, bf16[3072,640]{1,0:T(8,128)(2,1)} %w_ref.11), custom_call_target="tpu_custom_call" | custom-call | flops 5000000 | bytes 8000000 | tf_op jit(solution)/shard_map/pdn_a/pallas_call | solution.py:288
  6.2 3.3 %collective-permute-start = (bf16[4,32,3072]{2,1,0:T(8,128)(2,1)}, bf16[4,32,3072]{2,1,0:T(8,128)(2,1)}, u32[]{:S(2)}, u32[]{:S(2)}) collective-permute-start(bf16[4,32,3072]{2,1,0:T(8,128)(2,1)} %get-tuple-element.48), channel_id=1, source_target_pairs={{0,2},{1,3},{2,0},{3,1},{4,6},{5,7},{6,4},{7,5}} | collective-permute-start | bytes 2359304 | tf_op jit(solution)/shard_map/ppermute | solution.py:218
  9.6 1.5 collective-permute-start.1
  11.1 2.1 %copy-done = bf16[3072,640]{1,0:T(8,128)(2,1)S(1)} copy-done((bf16[3072,640]{1,0:T(8,128)(2,1)S(1)}, bf16[3072,640]{1,0:T(8,128)(2,1)}, u32[]{:S(2)}) %copy-start) | copy-done | bytes 3932184
  13.2 1.3 copy-done.3
  14.5 3.6 %shard_map.106 = (bf16[4,32,3072]{2,1,0:T(8,128)(2,1)}, bf16[4,32,3072]{2,1,0:T(8,128)(2,1)S(1)}, bf16[4,32,3072]{2,1,0:T(8,128)(2,1)S(1)}, bf16[4,32,3072]{2,1,0:T(8,128)(2,1)}) custom-call(s32[1]{0:T(128)} %bitcast.1.c_ref, bf16[4,256,640]{2,1,0:T(8,128)(2,1)S(1)} %copy-done.3, bf16[3072,640]{1,0:T(8,128)(2,1)S(1)} %copy-done), custom_call_target="tpu_custom_call" | custom-call | flops 10000000 | bytes 8000000 | tf_op jit(solution)/shard_map/pallas_call | solution.py:239
  20.5 2.1 %copy-done.1 = bf16[3072,640]{1,0:T(8,128)(2,1)S(1)} copy-done((bf16[3072,640]{1,0:T(8,128)(2,1)S(1)}, bf16[3072,640]{1,0:T(8,128)(2,1)}, u32[]{:S(2)}) %copy-start.1) | copy-done | bytes 3932184
  22.6 1.4 shard_map.105
  25.7 1.6 select_reduce_fusion
  28.3 2.0 collective-permute-done.1
  30.5 20.2 %lookup.1 = (bf16[4,4,64,1536]{3,2,1,0:T(8,128)(2,1)S(1)}, bf16[1,4,64,1536]{3,2,1,0:T(8,128)(2,1)S(1)}, bf16[3,4,64,1536]{3,2,1,0:T(8,128)(2,1)S(1)}, f32[8192,3072]{1,0:T(8,128)}) custom-call(s32[2]{0:T(128)S(1)} %pad_add_fusion.kc_ref, s32[1024]{0:T(1024)S(1)} %get-tuple-element.50.loc_ref, s32[1024,1]{1,0:T(8,128)S(1)} %copy.21.tgt_ref, ...), custom_call_target="tpu_custom_call" | custom-call | flops 40000000 | bytes 60000000 | tf_op jit(solution)/shard_map/lookup/pallas_call | solution.py:325
  51.8 1.3 convert_add_fusion.1
  54.3 1.3 convert_add_fusion
  55.8 2.0 collective-permute-done.25
  58.9 1.2 collective-permute-start.11
  61.4 7.6 %collective-permute-done.6 = bf16[4,32,1536]{2,1,0:T(8,128)(2,1)S(1)} collective-permute-done((bf16[4,32,1536]{2,1,0:T(8,128)(2,1)S(1)}, bf16[4,32,1536]{2,1,0:T(8,128)(2,1)S(1)}, u32[]{:S(2)}, u32[]{:S(2)}) %collective-permute-start.6) | collective-permute-done | bytes 393248 | tf_op jit(solution)/shard_map/ppermute | solution.py:218
  69.4 1.5 collective-permute-done.11
  70.9 1.2 collective-permute-start.7
  73.1 1.1 collective-permute-start.3
  74.2 13.6 %collective-permute-done.26 = f32[4,32,1536]{2,1,0:T(8,128)S(1)} collective-permute-done((f32[4,32,1536]{2,1,0:T(8,128)S(1)}, f32[4,32,1536]{2,1,0:T(8,128)S(1)}, u32[]{:S(2)}, u32[]{:S(2)}) %collective-permute-start.26) | collective-permute-done | bytes 786464 | tf_op jit(solution)/shard_map/ppermute | solution.py:218
  87.8 1.1 collective-permute-start.12
  89.4 2.0 broadcast_select_fusion
  91.4 12.4 %collective-permute-done.4 = bf16[4,32,1536]{2,1,0:T(8,128)(2,1)S(1)} collective-permute-done((bf16[4,32,1536]{2,1,0:T(8,128)(2,1)S(1)}, bf16[4,32,1536]{2,1,0:T(8,128)(2,1)S(1)}, u32[]{:S(2)}, u32[]{:S(2)}) %collective-permute-start.4) | collective-permute-done | bytes 393248 | tf_op jit(solution)/shard_map/ppermute | solution.py:218
  105.8 1.5 collective-permute-start.13
  107.3 1.2 collective-permute-start.8
  109.7 2.7 %fusion.10 = (f32[3072]{0:T(1024)S(1)}, f32[4,32]{1,0:T(4,128)S(1)}, f32[4,32,3072]{2,1,0:T(8,128)S(1)}) fusion(bf16[4,32,3072]{2,1,0:T(8,128)(2,1)S(1)} %get-tuple-element.97, f32[4,32]{1,0:T(4,128)S(1)} %add_rsqrt_fusion, f32[3072]{0:T(1024)S(1)} %convert_element_type.43, f32[4,32,3072]{2,1,0:T(8,128)S(1)} %collective-permute-done.30, ...), kind=kLoop, calls=%fused_computation.19 | loop fusion | flops 7467904 | bytes 8676353 | tf_op jit(solution)/shard_map/reduce_sum | solution.py:381
  112.5 1.2 collective-permute-done.45
  114.7 2.5 %collective-permute-done.19.refs_0_ = bf16[4,32,1536]{2,1,0:T(8,128)(2,1)S(1)} collective-permute-done((bf16[4,32,1536]{2,1,0:T(8,128)(2,1)S(1)}, bf16[4,32,1536]{2,1,0:T(8,128)(2,1)S(1)}, u32[]{:S(2)}, u32[]{:S(2)}) %collective-permute-start.19) | collective-permute-done | bytes 393248 | tf_op jit(solution)/shard_map/ppermute | solution.py:218
  117.3 7.6 %collective-permute-done.13.refs_2_ = bf16[4,32,1536]{2,1,0:T(8,128)(2,1)S(1)} collective-permute-done((bf16[4,32,1536]{2,1,0:T(8,128)(2,1)S(1)}, bf16[4,32,1536]{2,1,0:T(8,128)(2,1)S(1)}, u32[]{:S(2)}, u32[]{:S(2)}) %collective-permute-start.13) | collective-permute-done | bytes 393248 | tf_op jit(solution)/shard_map/ppermute | solution.py:218
  125.0 1.2 collective-permute-start.47
  126.8 1.9 collective-permute-done.47
  129.3 1.0 collective-permute-start.14
  130.3 1.0 collective-permute-start.37
  131.3 1.5 collective-permute-start.34
  133.3 7.4 %collective-permute-done.9.refs_0_ = bf16[4,32,1536]{2,1,0:T(8,128)(2,1)S(1)} collective-permute-done((bf16[4,32,1536]{2,1,0:T(8,128)(2,1)S(1)}, bf16[4,32,1536]{2,1,0:T(8,128)(2,1)S(1)}, u32[]{:S(2)}, u32[]{:S(2)}) %collective-permute-start.9) | collective-permute-done | bytes 393248 | tf_op jit(solution)/shard_map/ppermute | solution.py:218
  140.7 1.2 collective-permute-start.38
  142.7 7.1 %collective-permute-done.37.refs_8_ = bf16[2,32,3072]{2,1,0:T(8,128)(2,1)} collective-permute-done((bf16[2,32,3072]{2,1,0:T(8,128)(2,1)S(1)}, bf16[2,32,3072]{2,1,0:T(8,128)(2,1)}, u32[]{:S(2)}, u32[]{:S(2)}) %collective-permute-start.37) | collective-permute-done | bytes 393248 | tf_op jit(solution)/shard_map/ppermute | solution.py:218
  150.3 5.5 %collective-permute-done.33.refs_4_ = bf16[2,32,3072]{2,1,0:T(8,128)(2,1)S(1)} collective-permute-done((bf16[2,32,3072]{2,1,0:T(8,128)(2,1)S(1)}, bf16[2,32,3072]{2,1,0:T(8,128)(2,1)S(1)}, u32[]{:S(2)}, u32[]{:S(2)}) %collective-permute-start.33) | collective-permute-done | bytes 393248 | tf_op jit(solution)/shard_map/ppermute | solution.py:218
  156.2 1.5 collective-permute-start.41
  158.4 1.2 collective-permute-start.42
  160.2 7.5 %collective-permute-done.41.refs_12_ = bf16[2,32,3072]{2,1,0:T(8,128)(2,1)} collective-permute-done((bf16[2,32,3072]{2,1,0:T(8,128)(2,1)}, bf16[2,32,3072]{2,1,0:T(8,128)(2,1)}, u32[]{:S(2)}, u32[]{:S(2)}) %collective-permute-start.41) | collective-permute-done | bytes 393248 | tf_op jit(solution)/shard_map/ppermute | solution.py:218
  167.7 1.0 collective-permute-done.42.refs_13_
  169.2 3.9 %shard_map.101 = (bf16[4,64,3072]{2,1,0:T(8,128)(2,1)S(1)}, bf16[4,256,640]{2,1,0:T(8,128)(2,1)}, f32[8192,3072]{1,0:T(8,128)}) custom-call(s32[2]{0:T(128)S(1)} %pad_add_fusion.kc_ref, bf16[1,3072]{1,0:T(2,128)(2,1)S(1)} %reshape.72.g_ref, bf16[3072,640]{1,0:T(8,128)(2,1)S(1)} %copy-done.2, ...), custom_call_target="tpu_custom_call", output_to_operand_aliasing={{2}: (7, {})} | custom-call | flops 8000000 | bytes 12000000 | tf_op jit(solution)/shard_map/pallas_call | solution.py:352
  173.8 3.9 %shard_map.102 = (bf16[4,64,3072]{2,1,0:T(8,128)(2,1)S(1)}, bf16[4,256,640]{2,1,0:T(8,128)(2,1)}, f32[8192,3072]{1,0:T(8,128)}) custom-call(s32[2]{0:T(128)S(1)} %pad_add_fusion.kc_ref, bf16[1,3072]{1,0:T(2,128)(2,1)S(1)} %reshape.72.g_ref, bf16[3072,640]{1,0:T(8,128)(2,1)S(1)} %copy-done.2, ...), custom_call_target="tpu_custom_call", output_to_operand_aliasing={{1}: (7, {}), {2}: (8, {})} | custom-call | flops 8000000 | bytes 12000000 | tf_op jit(solution)/shard_map/pallas_call | solution.py:352
  177.7 3.9 %shard_map.103 = (bf16[4,64,3072]{2,1,0:T(8,128)(2,1)S(1)}, bf16[4,256,640]{2,1,0:T(8,128)(2,1)}, f32[8192,3072]{1,0:T(8,128)}) custom-call(s32[2]{0:T(128)S(1)} %pad_add_fusion.kc_ref, bf16[1,3072]{1,0:T(2,128)(2,1)S(1)} %reshape.72.g_ref, bf16[3072,640]{1,0:T(8,128)(2,1)S(1)} %copy-done.2, ...), custom_call_target="tpu_custom_call", output_to_operand_aliasing={{1}: (7, {}), {2}: (8, {})} | custom-call | flops 8000000 | bytes 12000000 | tf_op jit(solution)/shard_map/pallas_call | solution.py:352
  181.6 3.9 %shard_map.104 = (bf16[4,64,3072]{2,1,0:T(8,128)(2,1)S(1)}, bf16[4,256,640]{2,1,0:T(8,128)(2,1)}, f32[8192,3072]{1,0:T(8,128)}) custom-call(s32[2]{0:T(128)S(1)} %pad_add_fusion.kc_ref, bf16[1,3072]{1,0:T(2,128)(2,1)S(1)} %reshape.72.g_ref, bf16[3072,640]{1,0:T(8,128)(2,1)S(1)} %copy-done.2, ...), custom_call_target="tpu_custom_call", output_to_operand_aliasing={{1}: (7, {}), {2}: (8, {})} | custom-call | flops 8000000 | bytes 12000000 | tf_op jit(solution)/shard_map/pallas_call | solution.py:352
  185.6 15.7 %dw.1 = (f32[3072,640]{1,0:T(8,128)}, f32[8192,3072]{1,0:T(8,128)}) custom-call(s32[1]{0:T(128)} %bitcast.1.c_ref, bf16[4,256,640]{2,1,0:T(8,128)(2,1)S(1)} %copy-done.4, bf16[4,64,3072]{2,1,0:T(8,128)(2,1)S(1)} %get-tuple-element.84.refs_0_, bf16[4,64,3072]{2,1,0:T(8,128)(2,1)S(1)} %get-tuple-element.85.refs_1_, ...), custom_call_target="tpu_custom_call", output_to_operand_aliasing={{1}: (6, {})} | custom-call | flops 30000000 | bytes 40000000 | tf_op jit(solution)/shard_map/dw/pallas_call | solution.py:363
  201.4 7.4 %put_rows.1 = f32[8192,3072]{1,0:T(8,128)} custom-call(s32[1]{0:T(128)} %bitcast.12.me_ref, s32[1024]{0:T(1024)S(1)} %get-tuple-element.73.rows_ref, s32[1]{0:T(128)} %bitcast.2.cnt_ref, s32[1,1024]{1,0:T(1,128)S(1)} %bitcast.23, bf16[2,32,3072]{2,1,0:T(8,128)(2,1)S(1)} %copy-done.8, ...), custom_call_target="tpu_custom_call", output_to_operand_aliasing={{}: (20, {})} | custom-call | tf_op jit(solution)/shard_map/put_rows/pallas_call | solution.py:387
  (145 shorter events, 22.1 us)
Async XLA Ops:
  6.2 22.0 %collective-permute-start = (bf16[4,32,3072]{2,1,0:T(8,128)(2,1)}, bf16[4,32,3072]{2,1,0:T(8,128)(2,1)}, u32[]{:S(2)}, u32[]{:S(2)}) collective-permute-start(bf16[4,32,3072]{2,1,0:T(8,128)(2,1)} %get-tuple-element.48), channel_id=1, source_target_pairs={{0,2},{1,3},{2,0},{3,1},{4,6},{5,7},{6,4},{7,5}} | collective-permute-start | bytes 2359304 | tf_op jit(solution)/shard_map/ppermute | solution.py:218
  9.6 20.7 %collective-permute-start.1 = (bf16[4,32,3072]{2,1,0:T(8,128)(2,1)}, bf16[4,32,3072]{2,1,0:T(8,128)(2,1)}, u32[]{:S(2)}, u32[]{:S(2)}) collective-permute-start(bf16[4,32,3072]{2,1,0:T(8,128)(2,1)} %get-tuple-element.49), channel_id=1, source_target_pairs={{0,4},{1,5},{2,6},{3,7},{4,0},{5,1},{6,2},{7,3}} | collective-permute-start | bytes 2359304 | tf_op jit(solution)/shard_map/ppermute | solution.py:218
  19.9 52.3 %collective-permute-start.24 = (bf16[4,32,3072]{2,1,0:T(8,128)(2,1)}, bf16[4,32,3072]{2,1,0:T(8,128)(2,1)}, u32[]{:S(2)}, u32[]{:S(2)}) collective-permute-start(bf16[4,32,3072]{2,1,0:T(8,128)(2,1)} %get-tuple-element.77), channel_id=1, source_target_pairs={{0,2},{1,3},{2,0},{3,1},{4,6},{5,7},{6,4},{7,5}} | collective-permute-start | bytes 2359304 | tf_op jit(solution)/shard_map/ppermute | solution.py:218
  20.4 52.6 %collective-permute-start.27 = (bf16[4,32,3072]{2,1,0:T(8,128)(2,1)}, bf16[4,32,3072]{2,1,0:T(8,128)(2,1)}, u32[]{:S(2)}, u32[]{:S(2)}) collective-permute-start(bf16[4,32,3072]{2,1,0:T(8,128)(2,1)} %get-tuple-element.81), channel_id=1, source_target_pairs={{0,4},{1,5},{2,6},{3,7},{4,0},{5,1},{6,2},{7,3}} | collective-permute-start | bytes 2359304 | tf_op jit(solution)/shard_map/ppermute | solution.py:218
  51.0 4.7 %collective-permute-start.5 = (bf16[1,4,64,1536]{3,2,1,0:T(8,128)(2,1)S(1)}, bf16[1,4,64,1536]{3,2,1,0:T(8,128)(2,1)S(1)}, u32[]{:S(2)}, u32[]{:S(2)}) collective-permute-start(bf16[1,4,64,1536]{3,2,1,0:T(8,128)(2,1)S(1)} %get-tuple-element.57), channel_id=1, source_target_pairs={{0,1},{1,0},{2,3},{3,2},{4,5},{5,4},{6,7},{7,6}} | collective-permute-start | bytes 2359304 | tf_op jit(solution)/shard_map/ppermute | solution.py:218
  51.0 9.2 %collective-permute-start.2 = (bf16[3,4,64,1536]{3,2,1,0:T(8,128)(2,1)S(1)}, bf16[3,4,64,1536]{3,2,1,0:T(8,128)(2,1)S(1)}, u32[]{:S(2)}, u32[]{:S(2)}) collective-permute-start(bf16[3,4,64,1536]{3,2,1,0:T(8,128)(2,1)S(1)} %get-tuple-element.53), channel_id=1, source_target_pairs={{0,1},{1,0},{2,3},{3,2},{4,5},{5,4},{6,7},{7,6}} | collective-permute-start | bytes 7077896 | tf_op jit(solution)/shard_map/ppermute | solution.py:218
  53.3 4.5 %collective-permute-start.25 = (f32[4,32,1536]{2,1,0:T(8,128)S(1)}, f32[4,32,1536]{2,1,0:T(8,128)S(1)}, u32[]{:S(2)}, u32[]{:S(2)}) collective-permute-start(f32[4,32,1536]{2,1,0:T(8,128)S(1)} %slice_select_fusion.1), channel_id=1, source_target_pairs={{0,1},{1,0},{2,3},{3,2},{4,5},{5,4},{6,7},{7,6}} | collective-permute-start | bytes 2359304 | tf_op jit(solution)/shard_map/ppermute | solution.py:218
  55.7 3.2 %collective-permute-start.28 = (f32[4,32,1536]{2,1,0:T(8,128)S(1)}, f32[4,32,1536]{2,1,0:T(8,128)S(1)}, u32[]{:S(2)}, u32[]{:S(2)}) collective-permute-start(f32[4,32,1536]{2,1,0:T(8,128)S(1)} %slice_select_fusion), channel_id=1, source_target_pairs={{0,1},{1,0},{2,3},{3,2},{4,5},{5,4},{6,7},{7,6}} | collective-permute-start | bytes 2359304 | tf_op jit(solution)/shard_map/ppermute | solution.py:218
  57.8 11.2 %collective-permute-start.6 = (bf16[4,32,1536]{2,1,0:T(8,128)(2,1)S(1)}, bf16[4,32,1536]{2,1,0:T(8,128)(2,1)S(1)}, u32[]{:S(2)}, u32[]{:S(2)}) collective-permute-start(bf16[4,32,1536]{2,1,0:T(8,128)(2,1)S(1)} %get-tuple-element.110), channel_id=1, source_target_pairs={{0,2},{1,3},{2,0},{3,1},{4,6},{5,7},{6,4},{7,5}} | collective-permute-start | bytes 1179656 | tf_op jit(solution)/shard_map/ppermute | solution.py:218
  58.9 12.0 %collective-permute-start.11 = (bf16[4,32,1536]{2,1,0:T(8,128)(2,1)S(1)}, bf16[4,32,1536]{2,1,0:T(8,128)(2,1)S(1)}, u32[]{:S(2)}, u32[]{:S(2)}) collective-permute-start(bf16[4,32,1536]{2,1,0:T(8,128)(2,1)S(1)} %get-tuple-element.111), channel_id=1, source_target_pairs={{0,4},{1,5},{2,6},{3,7},{4,0},{5,1},{6,2},{7,3}} | collective-permute-start | bytes 1179656 | tf_op jit(solution)/shard_map/ppermute | solution.py:218
  60.3 27.5 %collective-permute-start.26 = (f32[4,32,1536]{2,1,0:T(8,128)S(1)}, f32[4,32,1536]{2,1,0:T(8,128)S(1)}, u32[]{:S(2)}, u32[]{:S(2)}) collective-permute-start(f32[4,32,1536]{2,1,0:T(8,128)S(1)} %select_add_fusion.4), channel_id=1, source_target_pairs={{0,4},{1,5},{2,6},{3,7},{4,0},{5,1},{6,2},{7,3}} | collective-permute-start | bytes 2359304 | tf_op jit(solution)/shard_map/ppermute | solution.py:218
  69.0 20.4 %collective-permute-start.29 = (f32[4,32,1536]{2,1,0:T(8,128)S(1)}, f32[4,32,1536]{2,1,0:T(8,128)S(1)}, u32[]{:S(2)}, u32[]{:S(2)}) collective-permute-start(f32[4,32,1536]{2,1,0:T(8,128)S(1)} %select_add_fusion.3), channel_id=1, source_target_pairs={{0,2},{1,3},{2,0},{3,1},{4,6},{5,7},{6,4},{7,5}} | collective-permute-start | bytes 2359304 | tf_op jit(solution)/shard_map/ppermute | solution.py:218
  70.9 32.9 %collective-permute-start.7 = (bf16[4,32,1536]{2,1,0:T(8,128)(2,1)S(1)}, bf16[4,32,1536]{2,1,0:T(8,128)(2,1)S(1)}, u32[]{:S(2)}, u32[]{:S(2)}) collective-permute-start(bf16[4,32,1536]{2,1,0:T(8,128)(2,1)S(1)} %add_add_fusion.2), channel_id=1, source_target_pairs={{0,4},{1,5},{2,6},{3,7},{4,0},{5,1},{6,2},{7,3}} | collective-permute-start | bytes 1179656 | tf_op jit(solution)/shard_map/ppermute | solution.py:218
  72.3 31.5 %collective-permute-start.4 = (bf16[4,32,1536]{2,1,0:T(8,128)(2,1)S(1)}, bf16[4,32,1536]{2,1,0:T(8,128)(2,1)S(1)}, u32[]{:S(2)}, u32[]{:S(2)}) collective-permute-start(bf16[4,32,1536]{2,1,0:T(8,128)(2,1)S(1)} %slice_add_fusion.2), channel_id=1, source_target_pairs={{0,4},{1,5},{2,6},{3,7},{4,0},{5,1},{6,2},{7,3}} | collective-permute-start | bytes 1179656 | tf_op jit(solution)/shard_map/ppermute | solution.py:218
  73.1 30.7 %collective-permute-start.3 = (bf16[4,32,1536]{2,1,0:T(8,128)(2,1)S(1)}, bf16[4,32,1536]{2,1,0:T(8,128)(2,1)S(1)}, u32[]{:S(2)}, u32[]{:S(2)}) collective-permute-start(bf16[4,32,1536]{2,1,0:T(8,128)(2,1)S(1)} %slice_add_fusion.3), channel_id=1, source_target_pairs={{0,2},{1,3},{2,0},{3,1},{4,6},{5,7},{6,4},{7,5}} | collective-permute-start | bytes 1179656 | tf_op jit(solution)/shard_map/ppermute | solution.py:218
  87.8 16.8 %collective-permute-start.12 = (bf16[4,32,1536]{2,1,0:T(8,128)(2,1)S(1)}, bf16[4,32,1536]{2,1,0:T(8,128)(2,1)S(1)}, u32[]{:S(2)}, u32[]{:S(2)}) collective-permute-start(bf16[4,32,1536]{2,1,0:T(8,128)(2,1)S(1)} %add_add_fusion), channel_id=1, source_target_pairs={{0,2},{1,3},{2,0},{3,1},{4,6},{5,7},{6,4},{7,5}} | collective-permute-start | bytes 1179656 | tf_op jit(solution)/shard_map/ppermute | solution.py:218
  91.4 18.4 %collective-permute-start.30 = (f32[4,32,3072]{2,1,0:T(8,128)S(1)}, f32[4,32,3072]{2,1,0:T(8,128)S(1)}, u32[]{:S(2)}, u32[]{:S(2)}) collective-permute-start(f32[4,32,3072]{2,1,0:T(8,128)S(1)} %broadcast_select_fusion), channel_id=1, source_target_pairs={{0,1},{1,0},{2,3},{3,2},{4,5},{5,4},{6,7},{7,6}} | collective-permute-start | bytes 4718600 | tf_op jit(solution)/shard_map/ppermute | solution.py:218
  104.7 2.6 %collective-permute-start.22 = (bf16[4,32,1536]{2,1,0:T(8,128)(2,1)S(1)}, bf16[4,32,1536]{2,1,0:T(8,128)(2,1)S(1)}, u32[]{:S(2)}, u32[]{:S(2)}) collective-permute-start(bf16[4,32,1536]{2,1,0:T(8,128)(2,1)S(1)} %get-tuple-element.100.refs_0_), channel_id=1, source_target_pairs={{0,1},{1,0},{2,3},{3,2},{4,5},{5,4},{6,7},{7,6}} | collective-permute-start | bytes 1179656 | tf_op jit(solution)/shard_map/ppermute | solution.py:218
  104.8 3.7 %collective-permute-start.23 = (bf16[4,32,1536]{2,1,0:T(8,128)(2,1)S(1)}, bf16[4,32,1536]{2,1,0:T(8,128)(2,1)S(1)}, u32[]{:S(2)}, u32[]{:S(2)}) collective-permute-start(bf16[4,32,1536]{2,1,0:T(8,128)(2,1)S(1)} %get-tuple-element.99.refs_2_), channel_id=1, source_target_pairs={{0,1},{1,0},{2,3},{3,2},{4,5},{5,4},{6,7},{7,6}} | collective-permute-start | bytes 1179656 | tf_op jit(solution)/shard_map/ppermute | solution.py:218
  105.3 12.0 %collective-permute-start.19 = (bf16[4,32,1536]{2,1,0:T(8,128)(2,1)S(1)}, bf16[4,32,1536]{2,1,0:T(8,128)(2,1)S(1)}, u32[]{:S(2)}, u32[]{:S(2)}) collective-permute-start(bf16[4,32,1536]{2,1,0:T(8,128)(2,1)S(1)} %get-tuple-element.100.refs_0_), channel_id=1, source_target_pairs={{0,2},{1,3},{2,0},{3,1},{4,6},{5,7},{6,4},{7,5}} | collective-permute-start | bytes 1179656 | tf_op jit(solution)/shard_map/ppermute | solution.py:218
  105.8 19.1 %collective-permute-start.13 = (bf16[4,32,1536]{2,1,0:T(8,128)(2,1)S(1)}, bf16[4,32,1536]{2,1,0:T(8,128)(2,1)S(1)}, u32[]{:S(2)}, u32[]{:S(2)}) collective-permute-start(bf16[4,32,1536]{2,1,0:T(8,128)(2,1)S(1)} %get-tuple-element.99.refs_2_), channel_id=1, source_target_pairs={{0,2},{1,3},{2,0},{3,1},{4,6},{5,7},{6,4},{7,5}} | collective-permute-start | bytes 1179656 | tf_op jit(solution)/shard_map/ppermute | solution.py:218
  107.3 19.0 %collective-permute-start.8 = (bf16[4,32,1536]{2,1,0:T(8,128)(2,1)S(1)}, bf16[4,32,1536]{2,1,0:T(8,128)(2,1)S(1)}, u32[]{:S(2)}, u32[]{:S(2)}) collective-permute-start(bf16[4,32,1536]{2,1,0:T(8,128)(2,1)S(1)} %get-tuple-element.100.refs_0_), channel_id=1, source_target_pairs={{0,4},{1,5},{2,6},{3,7},{4,0},{5,1},{6,2},{7,3}} | collective-permute-start | bytes 1179656 | tf_op jit(solution)/shard_map/ppermute | solution.py:218
  108.5 17.9 %collective-permute-start.17 = (bf16[4,32,1536]{2,1,0:T(8,128)(2,1)S(1)}, bf16[4,32,1536]{2,1,0:T(8,128)(2,1)S(1)}, u32[]{:S(2)}, u32[]{:S(2)}) collective-permute-start(bf16[4,32,1536]{2,1,0:T(8,128)(2,1)S(1)} %get-tuple-element.99.refs_2_), channel_id=1, source_target_pairs={{0,4},{1,5},{2,6},{3,7},{4,0},{5,1},{6,2},{7,3}} | collective-permute-start | bytes 1179656 | tf_op jit(solution)/shard_map/ppermute | solution.py:218
  112.4 1.2 collective-permute-start.45
  113.7 11.4 %collective-permute-start.46 = (f32[3072]{0:T(1024)S(1)}, f32[3072]{0:T(1024)S(1)}, u32[]{:S(2)}, u32[]{:S(2)}) collective-permute-start(f32[3072]{0:T(1024)S(1)} %add.138), channel_id=1, source_target_pairs={{0,2},{1,3},{2,0},{3,1},{4,6},{5,7},{6,4},{7,5}} | collective-permute-start | bytes 36872 | tf_op jit(solution)/shard_map/ppermute | solution.py:218
  117.3 12.0 %collective-permute-start.20 = (bf16[4,32,1536]{2,1,0:T(8,128)(2,1)S(1)}, bf16[4,32,1536]{2,1,0:T(8,128)(2,1)S(1)}, u32[]{:S(2)}, u32[]{:S(2)}) collective-permute-start(bf16[4,32,1536]{2,1,0:T(8,128)(2,1)S(1)} %collective-permute-done.19.refs_0_), channel_id=1, source_target_pairs={{0,1},{1,0},{2,3},{3,2},{4,5},{5,4},{6,7},{7,6}} | collective-permute-start | bytes 1179656 | tf_op jit(solution)/shard_map/ppermute | solution.py:218
  124.9 5.4 %collective-permute-start.21 = (bf16[4,32,1536]{2,1,0:T(8,128)(2,1)S(1)}, bf16[4,32,1536]{2,1,0:T(8,128)(2,1)S(1)}, u32[]{:S(2)}, u32[]{:S(2)}) collective-permute-start(bf16[4,32,1536]{2,1,0:T(8,128)(2,1)S(1)} %collective-permute-done.13.refs_2_), channel_id=1, source_target_pairs={{0,1},{1,0},{2,3},{3,2},{4,5},{5,4},{6,7},{7,6}} | collective-permute-start | bytes 1179656 | tf_op jit(solution)/shard_map/ppermute | solution.py:218
  125.0 3.7 %collective-permute-start.47 = (f32[3072]{0:T(1024)S(1)}, f32[3072]{0:T(1024)S(1)}, u32[]{:S(2)}, u32[]{:S(2)}) collective-permute-start(f32[3072]{0:T(1024)S(1)} %add.139), channel_id=1, source_target_pairs={{0,4},{1,5},{2,6},{3,7},{4,0},{5,1},{6,2},{7,3}} | collective-permute-start | bytes 36872 | tf_op jit(solution)/shard_map/ppermute | solution.py:218
  126.3 5.0 %collective-permute-start.16 = (bf16[4,32,1536]{2,1,0:T(8,128)(2,1)S(1)}, bf16[4,32,1536]{2,1,0:T(8,128)(2,1)S(1)}, u32[]{:S(2)}, u32[]{:S(2)}) collective-permute-start(bf16[4,32,1536]{2,1,0:T(8,128)(2,1)S(1)} %collective-permute-done.8.refs_0_), channel_id=1, source_target_pairs={{0,1},{1,0},{2,3},{3,2},{4,5},{5,4},{6,7},{7,6}} | collective-permute-start | bytes 1179656 | tf_op jit(solution)/shard_map/ppermute | solution.py:218
  126.4 6.4 %collective-permute-start.18 = (bf16[4,32,1536]{2,1,0:T(8,128)(2,1)S(1)}, bf16[4,32,1536]{2,1,0:T(8,128)(2,1)S(1)}, u32[]{:S(2)}, u32[]{:S(2)}) collective-permute-start(bf16[4,32,1536]{2,1,0:T(8,128)(2,1)S(1)} %collective-permute-done.17.refs_2_), channel_id=1, source_target_pairs={{0,1},{1,0},{2,3},{3,2},{4,5},{5,4},{6,7},{7,6}} | collective-permute-start | bytes 1179656 | tf_op jit(solution)/shard_map/ppermute | solution.py:218
  128.7 12.0 %collective-permute-start.9 = (bf16[4,32,1536]{2,1,0:T(8,128)(2,1)S(1)}, bf16[4,32,1536]{2,1,0:T(8,128)(2,1)S(1)}, u32[]{:S(2)}, u32[]{:S(2)}) collective-permute-start(bf16[4,32,1536]{2,1,0:T(8,128)(2,1)S(1)} %collective-permute-done.8.refs_0_), channel_id=1, source_target_pairs={{0,2},{1,3},{2,0},{3,1},{4,6},{5,7},{6,4},{7,5}} | collective-permute-start | bytes 1179656 | tf_op jit(solution)/shard_map/ppermute | solution.py:218
  129.3 12.7 %collective-permute-start.14 = (bf16[4,32,1536]{2,1,0:T(8,128)(2,1)S(1)}, bf16[4,32,1536]{2,1,0:T(8,128)(2,1)S(1)}, u32[]{:S(2)}, u32[]{:S(2)}) collective-permute-start(bf16[4,32,1536]{2,1,0:T(8,128)(2,1)S(1)} %collective-permute-done.13.refs_2_), channel_id=1, source_target_pairs={{0,4},{1,5},{2,6},{3,7},{4,0},{5,1},{6,2},{7,3}} | collective-permute-start | bytes 1179656 | tf_op jit(solution)/shard_map/ppermute | solution.py:218
  130.3 19.5 %collective-permute-start.37 = (bf16[2,32,3072]{2,1,0:T(8,128)(2,1)S(1)}, bf16[2,32,3072]{2,1,0:T(8,128)(2,1)}, u32[]{:S(2)}, u32[]{:S(2)}) collective-permute-start(bf16[2,32,3072]{2,1,0:T(8,128)(2,1)S(1)} %get-tuple-element.113.refs_0_), channel_id=1, source_target_pairs={{0,4},{1,5},{2,6},{3,7},{4,0},{5,1},{6,2},{7,3}} | collective-permute-start | bytes 1179656 | tf_op jit(solution)/shard_map/ppermute | solution.py:218
  131.3 18.5 %collective-permute-start.34 = (bf16[2,32,3072]{2,1,0:T(8,128)(2,1)S(1)}, bf16[2,32,3072]{2,1,0:T(8,128)(2,1)}, u32[]{:S(2)}, u32[]{:S(2)}) collective-permute-start(bf16[2,32,3072]{2,1,0:T(8,128)(2,1)S(1)} %get-tuple-element.112.refs_1_), channel_id=1, source_target_pairs={{0,2},{1,3},{2,0},{3,1},{4,6},{5,7},{6,4},{7,5}} | collective-permute-start | bytes 1179656 | tf_op jit(solution)/shard_map/ppermute | solution.py:218
  132.8 23.0 %collective-permute-start.33 = (bf16[2,32,3072]{2,1,0:T(8,128)(2,1)S(1)}, bf16[2,32,3072]{2,1,0:T(8,128)(2,1)S(1)}, u32[]{:S(2)}, u32[]{:S(2)}) collective-permute-start(bf16[2,32,3072]{2,1,0:T(8,128)(2,1)S(1)} %get-tuple-element.113.refs_0_), channel_id=1, source_target_pairs={{0,2},{1,3},{2,0},{3,1},{4,6},{5,7},{6,4},{7,5}} | collective-permute-start | bytes 1179656 | tf_op jit(solution)/shard_map/ppermute | solution.py:218
  140.7 15.5 %collective-permute-start.38 = (bf16[2,32,3072]{2,1,0:T(8,128)(2,1)S(1)}, bf16[2,32,3072]{2,1,0:T(8,128)(2,1)}, u32[]{:S(2)}, u32[]{:S(2)}) collective-permute-start(bf16[2,32,3072]{2,1,0:T(8,128)(2,1)S(1)} %get-tuple-element.112.refs_1_), channel_id=1, source_target_pairs={{0,4},{1,5},{2,6},{3,7},{4,0},{5,1},{6,2},{7,3}} | collective-permute-start | bytes 1179656 | tf_op jit(solution)/shard_map/ppermute | solution.py:218
  141.9 15.8 %collective-permute-start.31 = (bf16[2,32,3072]{2,1,0:T(8,128)(2,1)S(1)}, bf16[2,32,3072]{2,1,0:T(8,128)(2,1)S(1)}, u32[]{:S(2)}, u32[]{:S(2)}) collective-permute-start(bf16[2,32,3072]{2,1,0:T(8,128)(2,1)S(1)} %get-tuple-element.113.refs_0_), channel_id=1, source_target_pairs={{0,1},{1,0},{2,3},{3,2},{4,5},{5,4},{6,7},{7,6}} | collective-permute-start | bytes 1179656 | tf_op jit(solution)/shard_map/ppermute | solution.py:218
  149.8 9.9 %collective-permute-start.32 = (bf16[2,32,3072]{2,1,0:T(8,128)(2,1)S(1)}, bf16[2,32,3072]{2,1,0:T(8,128)(2,1)S(1)}, u32[]{:S(2)}, u32[]{:S(2)}) collective-permute-start(bf16[2,32,3072]{2,1,0:T(8,128)(2,1)S(1)} %get-tuple-element.112.refs_1_), channel_id=1, source_target_pairs={{0,1},{1,0},{2,3},{3,2},{4,5},{5,4},{6,7},{7,6}} | collective-permute-start | bytes 1179656 | tf_op jit(solution)/shard_map/ppermute | solution.py:218
  149.8 9.9 %collective-permute-start.10 = (bf16[4,32,1536]{2,1,0:T(8,128)(2,1)S(1)}, bf16[4,32,1536]{2,1,0:T(8,128)(2,1)S(1)}, u32[]{:S(2)}, u32[]{:S(2)}) collective-permute-start(bf16[4,32,1536]{2,1,0:T(8,128)(2,1)S(1)} %collective-permute-done.9.refs_0_), channel_id=1, source_target_pairs={{0,1},{1,0},{2,3},{3,2},{4,5},{5,4},{6,7},{7,6}} | collective-permute-start | bytes 1179656 | tf_op jit(solution)/shard_map/ppermute | solution.py:218
  155.8 4.3 %collective-permute-start.15 = (bf16[4,32,1536]{2,1,0:T(8,128)(2,1)S(1)}, bf16[4,32,1536]{2,1,0:T(8,128)(2,1)S(1)}, u32[]{:S(2)}, u32[]{:S(2)}) collective-permute-start(bf16[4,32,1536]{2,1,0:T(8,128)(2,1)S(1)} %collective-permute-done.14.refs_2_), channel_id=1, source_target_pairs={{0,1},{1,0},{2,3},{3,2},{4,5},{5,4},{6,7},{7,6}} | collective-permute-start | bytes 1179656 | tf_op jit(solution)/shard_map/ppermute | solution.py:218
  156.2 11.5 %collective-permute-start.41 = (bf16[2,32,3072]{2,1,0:T(8,128)(2,1)}, bf16[2,32,3072]{2,1,0:T(8,128)(2,1)}, u32[]{:S(2)}, u32[]{:S(2)}) collective-permute-start(bf16[2,32,3072]{2,1,0:T(8,128)(2,1)} %collective-permute-done.37.refs_8_), channel_id=1, source_target_pairs={{0,2},{1,3},{2,0},{3,1},{4,6},{5,7},{6,4},{7,5}} | collective-permute-start | bytes 1179656 | tf_op jit(solution)/shard_map/ppermute | solution.py:218
  158.4 10.3 %collective-permute-start.42 = (bf16[2,32,3072]{2,1,0:T(8,128)(2,1)}, bf16[2,32,3072]{2,1,0:T(8,128)(2,1)}, u32[]{:S(2)}, u32[]{:S(2)}) collective-permute-start(bf16[2,32,3072]{2,1,0:T(8,128)(2,1)} %collective-permute-done.34.refs_5_), channel_id=1, source_target_pairs={{0,4},{1,5},{2,6},{3,7},{4,0},{5,1},{6,2},{7,3}} | collective-permute-start | bytes 1179656 | tf_op jit(solution)/shard_map/ppermute | solution.py:218
  159.7 9.0 %collective-permute-start.35 = (bf16[2,32,3072]{2,1,0:T(8,128)(2,1)S(1)}, bf16[2,32,3072]{2,1,0:T(8,128)(2,1)S(1)}, u32[]{:S(2)}, u32[]{:S(2)}) collective-permute-start(bf16[2,32,3072]{2,1,0:T(8,128)(2,1)S(1)} %collective-permute-done.33.refs_4_), channel_id=1, source_target_pairs={{0,1},{1,0},{2,3},{3,2},{4,5},{5,4},{6,7},{7,6}} | collective-permute-start | bytes 1179656 | tf_op jit(solution)/shard_map/ppermute | solution.py:218
  159.7 41.6 %collective-permute-start.36 = (bf16[2,32,3072]{2,1,0:T(8,128)(2,1)}, bf16[2,32,3072]{2,1,0:T(8,128)(2,1)}, u32[]{:S(2)}, u32[]{:S(2)}) collective-permute-start(bf16[2,32,3072]{2,1,0:T(8,128)(2,1)} %collective-permute-done.34.refs_5_), channel_id=1, source_target_pairs={{0,1},{1,0},{2,3},{3,2},{4,5},{5,4},{6,7},{7,6}} | collective-permute-start | bytes 1179656 | tf_op jit(solution)/shard_map/ppermute | solution.py:218
  160.2 41.1 %collective-permute-start.39 = (bf16[2,32,3072]{2,1,0:T(8,128)(2,1)}, bf16[2,32,3072]{2,1,0:T(8,128)(2,1)}, u32[]{:S(2)}, u32[]{:S(2)}) collective-permute-start(bf16[2,32,3072]{2,1,0:T(8,128)(2,1)} %collective-permute-done.37.refs_8_), channel_id=1, source_target_pairs={{0,1},{1,0},{2,3},{3,2},{4,5},{5,4},{6,7},{7,6}} | collective-permute-start | bytes 1179656 | tf_op jit(solution)/shard_map/ppermute | solution.py:218
  167.7 33.7 %collective-permute-start.40 = (bf16[2,32,3072]{2,1,0:T(8,128)(2,1)}, bf16[2,32,3072]{2,1,0:T(8,128)(2,1)}, u32[]{:S(2)}, u32[]{:S(2)}) collective-permute-start(bf16[2,32,3072]{2,1,0:T(8,128)(2,1)} %collective-permute-done.38.refs_9_), channel_id=1, source_target_pairs={{0,1},{1,0},{2,3},{3,2},{4,5},{5,4},{6,7},{7,6}} | collective-permute-start | bytes 1179656 | tf_op jit(solution)/shard_map/ppermute | solution.py:218
  168.7 32.6 %collective-permute-start.43 = (bf16[2,32,3072]{2,1,0:T(8,128)(2,1)}, bf16[2,32,3072]{2,1,0:T(8,128)(2,1)}, u32[]{:S(2)}, u32[]{:S(2)}) collective-permute-start(bf16[2,32,3072]{2,1,0:T(8,128)(2,1)} %collective-permute-done.41.refs_12_), channel_id=1, source_target_pairs={{0,1},{1,0},{2,3},{3,2},{4,5},{5,4},{6,7},{7,6}} | collective-permute-start | bytes 1179656 | tf_op jit(solution)/shard_map/ppermute | solution.py:218
  168.7 32.6 %collective-permute-start.44 = (bf16[2,32,3072]{2,1,0:T(8,128)(2,1)}, bf16[2,32,3072]{2,1,0:T(8,128)(2,1)}, u32[]{:S(2)}, u32[]{:S(2)}) collective-permute-start(bf16[2,32,3072]{2,1,0:T(8,128)(2,1)} %collective-permute-done.42.refs_13_), channel_id=1, source_target_pairs={{0,1},{1,0},{2,3},{3,2},{4,5},{5,4},{6,7},{7,6}} | collective-permute-start | bytes 1179656 | tf_op jit(solution)/shard_map/ppermute | solution.py:218
  (25 other events, 261.3 us)

commit v4 on v3

--- a/solution.py
+++ b/solution.py
@@ -14,7 +14,7 @@
 HBM = pl.BlockSpec(memory_space=pltpu.HBM)
 ZR = 128
 BLK = 256
-LOOKUP_EARLY, LOOKUP_SHARE, NORM_SHARE = 14, 28, 5
+LOOKUP_EARLY, LOOKUP_SHARE, NORM_SHARE = 8, 26, 6
 
 
 def zero_fill(de, z, sem, first, last):
@@ -72,9 +72,9 @@
                 outs[2 * i + h][:, :, cols] = v[:, h * tl:(h + 1) * tl]
 
 
-def lookup_kernel(kc_ref, loc_ref, tgt_ref, emb, mine_ref, far_ref, near_ref, de, buf, sem, z, zsem):
+def lookup_kernel(kc_ref, list_ref, cnt_ref, loc_ref, tgt_ref, emb, mine_ref, far_ref, near_ref, de, buf, sem, z, zsem):
     k, c = kc_ref[0], kc_ref[1]
-    vl, d = emb.shape
+    _, d = emb.shape
     nj, mb, tc, hd = mine_ref.shape
     n = nj * mb * tc
     step = 64
@@ -90,20 +90,12 @@
         src = emb.at[pl.ds(pl.multiple_of((l >> 1) * 2, 2), 2)]
         return pltpu.make_async_copy(src, buf.at[pl.ds(pl.multiple_of(t * 2, 2), 2)], sem)
 
-    def issue(i, cnt):
-        for q in range(8):
-            t = i * 8 + q
-            l = loc_ref[t]
-            own = (l >= 0) & (l < vl)
-
-            @pl.when(own)
-            def _():
-                copy(t, l).start()
-
-            cnt = cnt + own.astype(jnp.int32)
-        return cnt
-
-    cnt = lax.fori_loop(0, n // 8, issue, jnp.int32(0))
+    cnt = cnt_ref[0]
+
+    @pl.loop(0, cnt)
+    def _(q):
+        t = list_ref[q]
+        copy(t, loc_ref[t]).start()
 
     @pl.loop(0, cnt)
     def _(i):
@@ -130,10 +122,11 @@
 
 
 def norm_kernel(j, kc_ref, g_ref, w_ref, *refs):
-    blocks, (n_ref, u_ref, de, stage, sem, z, zsem) = refs[:4], refs[-7:]
+    blocks, (nt_ref, u_ref, de, n_ref, stage, sem, z, zsem) = refs[:4], refs[-8:]
     k = kc_ref[0]
-    mb, tc, d = n_ref.shape
-    tl, hd = blocks[0].shape[1:]
+    d = nt_ref.shape[0]
+    mb, tl, hd = blocks[0].shape
+    tc = 2 * tl
     first = LOOKUP_SHARE + j * NORM_SHARE
     start, wait = zero_fill(de, z, zsem, first, first + NORM_SHARE)
     start()
@@ -147,38 +140,56 @@
             total = sum(jnp.sum(v * v, axis=-1, keepdims=True) for v in xf)
             rs = lax.rsqrt(total * (1.0 / d) + EPS)
             for q in range(2):
-                n_ref[m, h * tl:(h + 1) * tl, at[q]] = (xf[q] * rs * gf[q]).astype(jnp.bfloat16)
-
-    v = jnp.dot(n_ref[...].reshape(mb * tc, d), w_ref[...], preferred_element_type=jnp.float32)
+                to = pl.ds(pl.multiple_of(m * tc + h * tl, tl), tl)
+                n_ref[to, at[q]] = (xf[q] * rs * gf[q]).astype(jnp.bfloat16)
+
+    v = jnp.dot(n_ref[...], w_ref[...], preferred_element_type=jnp.float32)
     stage[...] = v.astype(jnp.bfloat16).reshape(stage.shape)
     rows = pl.ds(pl.multiple_of(jnp.bitwise_xor(kc_ref[1], j) * tc, tc), tc)
     copy = pltpu.make_async_copy(stage, u_ref.at[:, rows, :], sem)
     copy.start()
+    wc = 512
+
+    @pl.loop(0, d // wc)
+    def _(i):
+        c = pl.ds(pl.multiple_of(i * wc, wc), wc)
+        nt_ref[c, :] = n_ref[:, c].T
+
     copy.wait()
     wait()
 
 
 def dw_kernel(c_ref, du_ref, *refs):
-    ns, (dw, de, stage, sem, z, zsem) = refs[:4], refs[-6:]
-    mb, tc, d = ns[0].shape
+    ns, (dw, de, right, stage, sem, z, zsem) = refs[:4], refs[-7:]
+    mb, _, _ = du_ref.shape
+    d, kj = ns[0].shape
+    tc = kj // mb
     start, wait = zero_fill(de, z, zsem, LOOKUP_SHARE + 4 * NORM_SHARE, de.shape[0] // ZR)
     start()
+    for j in range(4):
+        rows = pl.ds(pl.multiple_of(jnp.bitwise_xor(c_ref[0], j) * tc, tc), tc)
+        for m in range(mb):
+            right[j * kj + m * tc:j * kj + (m + 1) * tc, :] = du_ref[m, rows, :]
     dc = stage.shape[1]
-    copies = []
-    for i in range(d // dc):
-        acc = jnp.zeros(stage.shape[1:], jnp.float32)
-        for j, n_ref in enumerate(ns):
-            rows = pl.ds(pl.multiple_of(jnp.bitwise_xor(c_ref[0], j) * tc, tc), tc)
-            left = jnp.concatenate([n_ref[m, :, i * dc:(i + 1) * dc] for m in range(mb)], axis=0)
-            right = jnp.concatenate([du_ref[m, rows, :] for m in range(mb)], axis=0)
-            acc += lax.dot_general(left, right, (((0,), (0,)), ((), ())), preferred_element_type=jnp.float32)
-        if i >= 2:
-            copies[i - 2].wait()
-        stage[i % 2] = acc
-        copies.append(pltpu.make_async_copy(stage.at[i % 2], dw.at[pl.ds(i * dc, dc)], sem.at[i % 2]))
-        copies[i].start()
-    for cp in copies[-2:]:
-        cp.wait()
+
+    def copy(i, q):
+        return pltpu.make_async_copy(stage.at[q], dw.at[pl.ds(pl.multiple_of(i * dc, dc), dc)], sem.at[q])
+
+    @pl.loop(0, d // dc)
+    def _(i):
+        q = lax.rem(i, 2)
+
+        @pl.when(i >= 2)
+        def _():
+            copy(i - 2, q).wait()
+
+        c = pl.ds(pl.multiple_of(i * dc, dc), dc)
+        left = jnp.concatenate([n[c, :] for n in ns], axis=1)
+        stage[q] = jnp.dot(left, right[...], preferred_element_type=jnp.float32)
+        copy(i, q).start()
+
+    for q in range(2):
+        copy(d // dc - 2 + q, q).wait()
     wait()
 
 
@@ -298,7 +309,7 @@
             ],
             cost_estimate=pl.CostEstimate(flops=5_000_000, bytes_accessed=8_000_000, transcendentals=0),
             compiler_params=pltpu.CompilerParams(vmem_limit_bytes=63 * 2**20),
-            name="pdn_a",
+            name="pa",
         )(c.reshape(1), du, w)}
         part.update(pdn((1, 2)))
         part.update(pdn((0,)))
@@ -315,7 +326,12 @@
         slot = jnp.where(own, pos_of_first, -1).astype(jnp.int32)
         rows = jnp.sum(jnp.where(lead[:, None] & (pos[:, None] == i1), loc[:, None], 0), axis=0).astype(jnp.int32)
         cnt = jnp.sum(lead.astype(jnp.int32)).reshape(1)
-        d0, d1, loc, tgt, slot, rows, cnt = lax.optimization_barrier((d0, d1, loc, tgt, slot, rows, cnt))
+        n_owned = jnp.sum(own.astype(jnp.int32)).reshape(1)
+        own_pos = jnp.sum(jnp.where(own[:, None] & (i0 < i1), 1, 0), axis=0)
+        owned = jnp.sum(jnp.where(own[:, None] & (own_pos[:, None] == i1), i0, 0), axis=0).astype(jnp.int32)
+        d0, d1, loc, tgt, slot, rows, cnt, owned, n_owned = lax.optimization_barrier(
+            (d0, d1, loc, tgt, slot, rows, cnt, owned, n_owned)
+        )
         ty, tx = f32(part[2][0]) + f32(d0), f32(part[1][1]) + f32(d1)
         gy = swap(pick(ty[..., hd:], ty[..., :hd]), 1)
         gx = swap(pick(tx[..., hd:], tx[..., :hd]), 1)
@@ -325,13 +341,13 @@
         mine, far, near, de = pl.pallas_call(
             lookup_kernel,
             out_shape=(half_shape(4), half_shape(1), half_shape(3), de_shape),
-            in_specs=[SMEM, SMEM, VMEM, ANY],
+            in_specs=[SMEM, SMEM, SMEM, SMEM, VMEM, ANY],
             out_specs=(VMEM, VMEM, VMEM, ANY),
             scratch_shapes=[pltpu.VMEM((2 * n, d), jnp.bfloat16), pltpu.SemaphoreType.DMA] + zero_scratch,
             cost_estimate=pl.CostEstimate(flops=40_000_000, bytes_accessed=60_000_000, transcendentals=0),
             compiler_params=pltpu.CompilerParams(vmem_limit_bytes=40 * 2**20),
-            name="lookup",
-        )(kc, loc, tgt.reshape(n, 1), emb)
+            name="look",
+        )(kc, owned, n_owned, loc, tgt.reshape(n, 1), emb)
         far, near = swap(far, 1), swap(near, 1)
         xpairs = {j: (mine[j], far[0] if j == 3 else near[j]) for j in range(4)}
 
@@ -351,10 +367,14 @@
             more = (de,) if u is None else (u, de)
             nj, u, de = pl.pallas_call(
                 functools.partial(norm_kernel, j),
-                out_shape=(jax.ShapeDtypeStruct((mb, tc, d), jnp.bfloat16), jax.ShapeDtypeStruct((mb, t, f), jnp.bfloat16), de_shape),
+                out_shape=(jax.ShapeDtypeStruct((d, mb * tc), jnp.bfloat16), jax.ShapeDtypeStruct((mb, t, f), jnp.bfloat16), de_shape),
                 in_specs=[SMEM] + [VMEM] * 6 + [ANY] * len(more),
                 out_specs=(VMEM, ANY, ANY),
-                scratch_shapes=[pltpu.VMEM((mb, tc, f), jnp.bfloat16), pltpu.SemaphoreType.DMA] + zero_scratch,
+                scratch_shapes=[
+                    pltpu.VMEM((mb * tc, d), jnp.bfloat16),
+                    pltpu.VMEM((mb, tc, f), jnp.bfloat16),
+                    pltpu.SemaphoreType.DMA,
+                ] + zero_scratch,
                 input_output_aliases={7 + i: 3 - len(more) + i for i in range(len(more))},
                 cost_estimate=pl.CostEstimate(flops=8_000_000, bytes_accessed=12_000_000, transcendentals=0),
                 compiler_params=pltpu.CompilerParams(vmem_limit_bytes=40 * 2**20),
@@ -365,7 +385,11 @@
             out_shape=(jax.ShapeDtypeStruct((d, f), jnp.float32), de_shape),
             in_specs=[SMEM] + [VMEM] * 5 + [ANY],
             out_specs=(ANY, ANY),
-            scratch_shapes=[pltpu.VMEM((2, 512, f), jnp.float32), pltpu.SemaphoreType.DMA((2,))] + zero_scratch,
+            scratch_shapes=[
+                pltpu.VMEM((n, f), jnp.bfloat16),
+                pltpu.VMEM((2, 512, f), jnp.float32),
+                pltpu.SemaphoreType.DMA((2,)),
+            ] + zero_scratch,
             input_output_aliases={6: 1},
             cost_estimate=pl.CostEstimate(flops=30_000_000, bytes_accessed=40_000_000, transcendentals=0),
             compiler_params=pltpu.CompilerParams(vmem_limit_bytes=40 * 2**20),
@@ -396,7 +420,7 @@
             ],
             input_output_aliases={20: 0},
             compiler_params=pltpu.CompilerParams(vmem_limit_bytes=40 * 2**20),
-            name="put_rows",
+            name="put",
         )(me, rows, cnt, slot.reshape(1, n), *dxs, de)
         return u, x, de, dw, dg
 

time: 210 us -> 204 us (0.971)
  Pallas kernels: 69.5 us -> 64 us
    pallas_call x1, Pallas kernels: 20.2 us -> 15.6 us  [local(): pl.pallas_call(lookup_kernel, out_shape=(half_shape(4), half_shape(1), ha...]
    pallas_call x1, Pallas kernels: 15.7 us -> 13 us  [local(): pl.pallas_call(dw_kernel, out_shape=(jax.ShapeDtypeStruct((d, f), jnp.flo...]
  transfers between devices with their start and end apart: 48 -> 48, of which waited for: 21 -> 21; matrix products, arithmetic and copies ran while one was open for 7% -> 7% of each run, Pallas kernels for 27% -> 25%
where the time goes in v4:
time: 204 us; the launch traced here: 203 us
  waiting for transfers between devices  84.7 us (42%)
  Pallas kernels  64 us (31%)
  starting transfers between devices  27.9 us (14%)
  other arithmetic  14.5 us (7%)
  local copies, waits for them, and re-layouts  10.9 us (5%)
    ppermute x48, waiting for transfers between devices, swap(): return lax.ppermute(v, 'tp', [(i, i ^ bit) for i in range(groups)])  84.7 us
    ppermute x48, starting transfers between devices, swap(): return lax.ppermute(v, 'tp', [(i, i ^ bit) for i in range(groups)])  27.9 us
    pallas_call x4, Pallas kernels, local(): pl.pallas_call(functools.partial(norm_kernel, j), out_shape=(jax.ShapeDty...  17.5 us
    pallas_call x1, Pallas kernels, local(): pl.pallas_call(lookup_kernel, out_shape=(half_shape(4), half_shape(1), ha...  15.6 us
    pallas_call x1, Pallas kernels, local(): pl.pallas_call(dw_kernel, out_shape=(jax.ShapeDtypeStruct((d, f), jnp.flo...  13 us
    unnamed x51, local copies, waits for them, and re-layouts  10.2 us
    pallas_call x1, Pallas kernels, local(): pl.pallas_call(scatter_kernel, out_shape=de_shape, in_specs=[SMEM, SMEM,...  7.31 us
    pallas_call x1, Pallas kernels, local(): pl.pallas_call(functools.partial(pdn_first_kernel, 3), out_shape=(jax.Sha...  5.59 us
  transfers between devices with their start and end apart: 48, of which 21 were waited for; matrix products, arithmetic and copies ran while one was open for 7% of the time, Pallas kernels for 25%

profile of v4, /device:TPU:0, one launch (start us, length us, event | category | flops | bytes accessed | tf_op | source)
XLA Modules:
  0.0 203.4 jit_solution(16543850226093672350)
XLA Ops:
  0.6 5.6 %pa.1 = (bf16[4,32,3072]{2,1,0:T(8,128)(2,1)}, bf16[4,32,3072]{2,1,0:T(8,128)(2,1)}) custom-call(s32[1]{0:T(128)} %bitcast.1.c_ref, bf16[4,256,640]{2,1,0:T(8,128)(2,1)} %du_ref.5, bf16[3072,640]{1,0:T(8,128)(2,1)} %w_ref.11), custom_call_target="tpu_custom_call" | custom-call | flops 5000000 | bytes 8000000 | tf_op jit(solution)/shard_map/pa/pallas_call | solution.py:299
  6.2 3.3 %collective-permute-start = (bf16[4,32,3072]{2,1,0:T(8,128)(2,1)}, bf16[4,32,3072]{2,1,0:T(8,128)(2,1)}, u32[]{:S(2)}, u32[]{:S(2)}) collective-permute-start(bf16[4,32,3072]{2,1,0:T(8,128)(2,1)} %get-tuple-element.50), channel_id=1, source_target_pairs={{0,2},{1,3},{2,0},{3,1},{4,6},{5,7},{6,4},{7,5}} | collective-permute-start | bytes 2359304 | tf_op jit(solution)/shard_map/ppermute | solution.py:229
  9.6 1.5 collective-permute-start.1
  11.1 2.1 %copy-done = bf16[3072,640]{1,0:T(8,128)(2,1)S(1)} copy-done((bf16[3072,640]{1,0:T(8,128)(2,1)S(1)}, bf16[3072,640]{1,0:T(8,128)(2,1)}, u32[]{:S(2)}) %copy-start) | copy-done | bytes 3932184
  13.2 1.3 copy-done.3
  14.5 3.6 %shard_map.106 = (bf16[4,32,3072]{2,1,0:T(8,128)(2,1)}, bf16[4,32,3072]{2,1,0:T(8,128)(2,1)S(1)}, bf16[4,32,3072]{2,1,0:T(8,128)(2,1)S(1)}, bf16[4,32,3072]{2,1,0:T(8,128)(2,1)}) custom-call(s32[1]{0:T(128)} %bitcast.1.c_ref, bf16[4,256,640]{2,1,0:T(8,128)(2,1)S(1)} %copy-done.3, bf16[3072,640]{1,0:T(8,128)(2,1)S(1)} %copy-done), custom_call_target="tpu_custom_call" | custom-call | flops 10000000 | bytes 8000000 | tf_op jit(solution)/shard_map/pallas_call | solution.py:250
  18.1 0.9 copy-done.9
  19.0 0.9 copy-done.11
  20.5 2.1 %copy-done.1 = bf16[3072,640]{1,0:T(8,128)(2,1)S(1)} copy-done((bf16[3072,640]{1,0:T(8,128)(2,1)S(1)}, bf16[3072,640]{1,0:T(8,128)(2,1)}, u32[]{:S(2)}) %copy-start.1) | copy-done | bytes 3932184
  22.6 1.4 shard_map.105
  26.0 2.9 %select_reduce_fusion.2 = (s32[1024]{0:T(1024)S(1)}, s32[1024]{0:T(1024)S(1)}, s32[1024]{0:T(1024)S(1)}) fusion(s32[1024]{0:T(1024)S(1)} %get-tuple-element.54.loc_ref, s32[1024]{0:T(1024)S(1)} %select_reduce_fusion.4, pred[1024]{0:T(1024)(128)(4,1)S(1)} %get-tuple-element.107, s32[1024]{0:T(1024)S(1)} %select_reduce_fusion.5, ...), kind=kLoop, calls=%fused_computation.3 | loop fusion | flops 11531264 | bytes 30720 | tf_op jit(solution)/shard_map/reduce_sum | solution.py:327
  28.8 1.4 collective-permute-done.1
  30.5 15.6 %look.1 = (bf16[4,4,64,1536]{3,2,1,0:T(8,128)(2,1)S(1)}, bf16[1,4,64,1536]{3,2,1,0:T(8,128)(2,1)S(1)}, bf16[3,4,64,1536]{3,2,1,0:T(8,128)(2,1)S(1)}, f32[8192,3072]{1,0:T(8,128)}) custom-call(s32[2]{0:T(128)S(1)} %pad_add_fusion.kc_ref, s32[1024]{0:T(1024)S(1)} %get-tuple-element.52.list_ref, s32[1]{0:T(128)} %bitcast.3.cnt_ref, ...), custom_call_target="tpu_custom_call" | custom-call | flops 40000000 | bytes 60000000 | tf_op jit(solution)/shard_map/look/pallas_call | solution.py:341
  47.2 1.3 convert_add_fusion.1
  48.7 1.0 copy-done.10
  49.7 1.3 convert_add_fusion
  51.2 2.0 collective-permute-done.25
  55.0 1.5 collective-permute-start.26
  56.7 7.7 %collective-permute-done.6 = bf16[4,32,1536]{2,1,0:T(8,128)(2,1)S(1)} collective-permute-done((bf16[4,32,1536]{2,1,0:T(8,128)(2,1)S(1)}, bf16[4,32,1536]{2,1,0:T(8,128)(2,1)S(1)}, u32[]{:S(2)}, u32[]{:S(2)}) %collective-permute-start.6) | collective-permute-done | bytes 393248 | tf_op jit(solution)/shard_map/ppermute | solution.py:229
  65.0 1.3 collective-permute-done.11
  67.0 1.5 collective-permute-start.4
  68.5 1.1 collective-permute-start.3
  69.5 13.6 %collective-permute-done.26 = f32[4,32,1536]{2,1,0:T(8,128)S(1)} collective-permute-done((f32[4,32,1536]{2,1,0:T(8,128)S(1)}, f32[4,32,1536]{2,1,0:T(8,128)S(1)}, u32[]{:S(2)}, u32[]{:S(2)}) %collective-permute-start.26) | collective-permute-done | bytes 786464 | tf_op jit(solution)/shard_map/ppermute | solution.py:229
  83.2 1.1 collective-permute-start.12
  84.8 2.0 broadcast_select_fusion
  86.8 12.4 %collective-permute-done.4 = bf16[4,32,1536]{2,1,0:T(8,128)(2,1)S(1)} collective-permute-done((bf16[4,32,1536]{2,1,0:T(8,128)(2,1)S(1)}, bf16[4,32,1536]{2,1,0:T(8,128)(2,1)S(1)}, u32[]{:S(2)}, u32[]{:S(2)}) %collective-permute-start.4) | collective-permute-done | bytes 393248 | tf_op jit(solution)/shard_map/ppermute | solution.py:229
  101.2 1.5 collective-permute-start.13
  103.2 1.5 collective-permute-start.17
  105.1 2.7 %fusion.12 = (f32[3072]{0:T(1024)S(1)}, f32[4,32]{1,0:T(4,128)S(1)}, f32[4,32,3072]{2,1,0:T(8,128)S(1)}) fusion(bf16[4,32,3072]{2,1,0:T(8,128)(2,1)S(1)} %get-tuple-element.103, f32[4,32]{1,0:T(4,128)S(1)} %add_rsqrt_fusion, f32[3072]{0:T(1024)S(1)} %convert_element_type.48, f32[4,32,3072]{2,1,0:T(8,128)S(1)} %collective-permute-done.30, ...), kind=kLoop, calls=%fused_computation.24 | loop fusion | flops 7467904 | bytes 8676353 | tf_op jit(solution)/shard_map/reduce_sum | solution.py:405
  107.8 1.2 collective-permute-done.45
  110.1 2.5 %collective-permute-done.19.refs_0_ = bf16[4,32,1536]{2,1,0:T(8,128)(2,1)S(1)} collective-permute-done((bf16[4,32,1536]{2,1,0:T(8,128)(2,1)S(1)}, bf16[4,32,1536]{2,1,0:T(8,128)(2,1)S(1)}, u32[]{:S(2)}, u32[]{:S(2)}) %collective-permute-start.19) | collective-permute-done | bytes 393248 | tf_op jit(solution)/shard_map/ppermute | solution.py:229
  112.6 7.6 %collective-permute-done.13.refs_2_ = bf16[4,32,1536]{2,1,0:T(8,128)(2,1)S(1)} collective-permute-done((bf16[4,32,1536]{2,1,0:T(8,128)(2,1)S(1)}, bf16[4,32,1536]{2,1,0:T(8,128)(2,1)S(1)}, u32[]{:S(2)}, u32[]{:S(2)}) %collective-permute-start.13) | collective-permute-done | bytes 393248 | tf_op jit(solution)/shard_map/ppermute | solution.py:229
  121.6 2.5 %collective-permute-done.47 = f32[3072]{0:T(1024)S(1)} collective-permute-done((f32[3072]{0:T(1024)S(1)}, f32[3072]{0:T(1024)S(1)}, u32[]{:S(2)}, u32[]{:S(2)}) %collective-permute-start.47) | collective-permute-done | bytes 12320 | tf_op jit(solution)/shard_map/ppermute | solution.py:229
  125.1 1.5 collective-permute-start.37
  126.6 1.5 collective-permute-start.34
  128.7 7.4 %collective-permute-done.9.refs_0_ = bf16[4,32,1536]{2,1,0:T(8,128)(2,1)S(1)} collective-permute-done((bf16[4,32,1536]{2,1,0:T(8,128)(2,1)S(1)}, bf16[4,32,1536]{2,1,0:T(8,128)(2,1)S(1)}, u32[]{:S(2)}, u32[]{:S(2)}) %collective-permute-start.9) | collective-permute-done | bytes 393248 | tf_op jit(solution)/shard_map/ppermute | solution.py:229
  136.6 0.8 copy-done.7
  137.4 7.7 %collective-permute-done.37.refs_8_ = bf16[2,32,3072]{2,1,0:T(8,128)(2,1)} collective-permute-done((bf16[2,32,3072]{2,1,0:T(8,128)(2,1)S(1)}, bf16[2,32,3072]{2,1,0:T(8,128)(2,1)}, u32[]{:S(2)}, u32[]{:S(2)}) %collective-permute-start.37) | collective-permute-done | bytes 393248 | tf_op jit(solution)/shard_map/ppermute | solution.py:229
  145.6 5.5 %collective-permute-done.33.refs_4_ = bf16[2,32,3072]{2,1,0:T(8,128)(2,1)S(1)} collective-permute-done((bf16[2,32,3072]{2,1,0:T(8,128)(2,1)S(1)}, bf16[2,32,3072]{2,1,0:T(8,128)(2,1)S(1)}, u32[]{:S(2)}, u32[]{:S(2)}) %collective-permute-start.33) | collective-permute-done | bytes 393248 | tf_op jit(solution)/shard_map/ppermute | solution.py:229
  151.5 1.5 collective-permute-start.41
  154.9 8.1 %collective-permute-done.41.refs_12_ = bf16[2,32,3072]{2,1,0:T(8,128)(2,1)} collective-permute-done((bf16[2,32,3072]{2,1,0:T(8,128)(2,1)}, bf16[2,32,3072]{2,1,0:T(8,128)(2,1)}, u32[]{:S(2)}, u32[]{:S(2)}) %collective-permute-start.41) | collective-permute-done | bytes 393248 | tf_op jit(solution)/shard_map/ppermute | solution.py:229
  163.0 1.0 collective-permute-done.42.refs_13_
  164.6 4.4 %shard_map.101 = (bf16[3072,256]{1,0:T(8,128)(2,1)S(1)}, bf16[4,256,640]{2,1,0:T(8,128)(2,1)}, f32[8192,3072]{1,0:T(8,128)}) custom-call(s32[2]{0:T(128)S(1)} %pad_add_fusion.kc_ref, bf16[1,3072]{1,0:T(2,128)(2,1)S(1)} %reshape.79.g_ref, bf16[3072,640]{1,0:T(8,128)(2,1)S(1)} %copy-done.2, ...), custom_call_target="tpu_custom_call", output_to_operand_aliasing={{2}: (7, {})} | custom-call | flops 8000000 | bytes 12000000 | tf_op jit(solution)/shard_map/pallas_call | solution.py:368
  169.6 4.4 %shard_map.102 = (bf16[3072,256]{1,0:T(8,128)(2,1)S(1)}, bf16[4,256,640]{2,1,0:T(8,128)(2,1)}, f32[8192,3072]{1,0:T(8,128)}) custom-call(s32[2]{0:T(128)S(1)} %pad_add_fusion.kc_ref, bf16[1,3072]{1,0:T(2,128)(2,1)S(1)} %reshape.79.g_ref, bf16[3072,640]{1,0:T(8,128)(2,1)S(1)} %copy-done.2, ...), custom_call_target="tpu_custom_call", output_to_operand_aliasing={{1}: (7, {}), {2}: (8, {})} | custom-call | flops 8000000 | bytes 12000000 | tf_op jit(solution)/shard_map/pallas_call | solution.py:368
  174.0 4.4 %shard_map.103 = (bf16[3072,256]{1,0:T(8,128)(2,1)S(1)}, bf16[4,256,640]{2,1,0:T(8,128)(2,1)}, f32[8192,3072]{1,0:T(8,128)}) custom-call(s32[2]{0:T(128)S(1)} %pad_add_fusion.kc_ref, bf16[1,3072]{1,0:T(2,128)(2,1)S(1)} %reshape.79.g_ref, bf16[3072,640]{1,0:T(8,128)(2,1)S(1)} %copy-done.2, ...), custom_call_target="tpu_custom_call", output_to_operand_aliasing={{1}: (7, {}), {2}: (8, {})} | custom-call | flops 8000000 | bytes 12000000 | tf_op jit(solution)/shard_map/pallas_call | solution.py:368
  178.4 4.4 %shard_map.104 = (bf16[3072,256]{1,0:T(8,128)(2,1)S(1)}, bf16[4,256,640]{2,1,0:T(8,128)(2,1)}, f32[8192,3072]{1,0:T(8,128)}) custom-call(s32[2]{0:T(128)S(1)} %pad_add_fusion.kc_ref, bf16[1,3072]{1,0:T(2,128)(2,1)S(1)} %reshape.79.g_ref, bf16[3072,640]{1,0:T(8,128)(2,1)S(1)} %copy-done.2, ...), custom_call_target="tpu_custom_call", output_to_operand_aliasing={{1}: (7, {}), {2}: (8, {})} | custom-call | flops 8000000 | bytes 12000000 | tf_op jit(solution)/shard_map/pallas_call | solution.py:368
  182.8 13.0 %dw.1 = (f32[3072,640]{1,0:T(8,128)}, f32[8192,3072]{1,0:T(8,128)}) custom-call(s32[1]{0:T(128)} %bitcast.1.c_ref, bf16[4,256,640]{2,1,0:T(8,128)(2,1)S(1)} %copy-done.4, bf16[3072,256]{1,0:T(8,128)(2,1)S(1)} %get-tuple-element.88.refs_0_, bf16[3072,256]{1,0:T(8,128)(2,1)S(1)} %get-tuple-element.89.refs_1_, ...), custom_call_target="tpu_custom_call", output_to_operand_aliasing={{1}: (6, {})} | custom-call | flops 30000000 | bytes 40000000 | tf_op jit(solution)/shard_map/dw/pallas_call | solution.py:383
  195.9 7.3 %put.1 = f32[8192,3072]{1,0:T(8,128)} custom-call(s32[1]{0:T(128)} %bitcast.13.me_ref, s32[1024]{0:T(1024)S(1)} %get-tuple-element.77.rows_ref, s32[1]{0:T(128)} %bitcast.2.cnt_ref, s32[1,1024]{1,0:T(1,128)S(1)} %bitcast.24, bf16[2,32,3072]{2,1,0:T(8,128)(2,1)S(1)} %copy-done.8, bf16[2,32,3072]{2,1,0:T(8,128)(2,1)S(1)} %copy-done.6, ...), custom_call_target="tpu_custom_call", output_to_operand_aliasing={{}: (20, {})} | custom-call | tf_op jit(solution)/shard_map/put/pallas_call | solution.py:411
  (146 shorter events, 19.5 us)
Async XLA Ops:
  6.2 22.6 %collective-permute-start = (bf16[4,32,3072]{2,1,0:T(8,128)(2,1)}, bf16[4,32,3072]{2,1,0:T(8,128)(2,1)}, u32[]{:S(2)}, u32[]{:S(2)}) collective-permute-start(bf16[4,32,3072]{2,1,0:T(8,128)(2,1)} %get-tuple-element.50), channel_id=1, source_target_pairs={{0,2},{1,3},{2,0},{3,1},{4,6},{5,7},{6,4},{7,5}} | collective-permute-start | bytes 2359304 | tf_op jit(solution)/shard_map/ppermute | solution.py:229
  9.6 20.7 %collective-permute-start.1 = (bf16[4,32,3072]{2,1,0:T(8,128)(2,1)}, bf16[4,32,3072]{2,1,0:T(8,128)(2,1)}, u32[]{:S(2)}, u32[]{:S(2)}) collective-permute-start(bf16[4,32,3072]{2,1,0:T(8,128)(2,1)} %get-tuple-element.51), channel_id=1, source_target_pairs={{0,4},{1,5},{2,6},{3,7},{4,0},{5,1},{6,2},{7,3}} | collective-permute-start | bytes 2359304 | tf_op jit(solution)/shard_map/ppermute | solution.py:229
  19.9 47.1 %collective-permute-start.24 = (bf16[4,32,3072]{2,1,0:T(8,128)(2,1)}, bf16[4,32,3072]{2,1,0:T(8,128)(2,1)}, u32[]{:S(2)}, u32[]{:S(2)}) collective-permute-start(bf16[4,32,3072]{2,1,0:T(8,128)(2,1)} %get-tuple-element.81), channel_id=1, source_target_pairs={{0,2},{1,3},{2,0},{3,1},{4,6},{5,7},{6,4},{7,5}} | collective-permute-start | bytes 2359304 | tf_op jit(solution)/shard_map/ppermute | solution.py:229
  20.4 48.0 %collective-permute-start.27 = (bf16[4,32,3072]{2,1,0:T(8,128)(2,1)}, bf16[4,32,3072]{2,1,0:T(8,128)(2,1)}, u32[]{:S(2)}, u32[]{:S(2)}) collective-permute-start(bf16[4,32,3072]{2,1,0:T(8,128)(2,1)} %get-tuple-element.85), channel_id=1, source_target_pairs={{0,4},{1,5},{2,6},{3,7},{4,0},{5,1},{6,2},{7,3}} | collective-permute-start | bytes 2359304 | tf_op jit(solution)/shard_map/ppermute | solution.py:229
  46.4 4.7 %collective-permute-start.5 = (bf16[1,4,64,1536]{3,2,1,0:T(8,128)(2,1)S(1)}, bf16[1,4,64,1536]{3,2,1,0:T(8,128)(2,1)S(1)}, u32[]{:S(2)}, u32[]{:S(2)}) collective-permute-start(bf16[1,4,64,1536]{3,2,1,0:T(8,128)(2,1)S(1)} %get-tuple-element.61), channel_id=1, source_target_pairs={{0,1},{1,0},{2,3},{3,2},{4,5},{5,4},{6,7},{7,6}} | collective-permute-start | bytes 2359304 | tf_op jit(solution)/shard_map/ppermute | solution.py:229
  46.4 8.6 %collective-permute-start.2 = (bf16[3,4,64,1536]{3,2,1,0:T(8,128)(2,1)S(1)}, bf16[3,4,64,1536]{3,2,1,0:T(8,128)(2,1)S(1)}, u32[]{:S(2)}, u32[]{:S(2)}) collective-permute-start(bf16[3,4,64,1536]{3,2,1,0:T(8,128)(2,1)S(1)} %get-tuple-element.57), channel_id=1, source_target_pairs={{0,1},{1,0},{2,3},{3,2},{4,5},{5,4},{6,7},{7,6}} | collective-permute-start | bytes 7077896 | tf_op jit(solution)/shard_map/ppermute | solution.py:229
  48.7 4.5 %collective-permute-start.25 = (f32[4,32,1536]{2,1,0:T(8,128)S(1)}, f32[4,32,1536]{2,1,0:T(8,128)S(1)}, u32[]{:S(2)}, u32[]{:S(2)}) collective-permute-start(f32[4,32,1536]{2,1,0:T(8,128)S(1)} %slice_select_fusion.1), channel_id=1, source_target_pairs={{0,1},{1,0},{2,3},{3,2},{4,5},{5,4},{6,7},{7,6}} | collective-permute-start | bytes 2359304 | tf_op jit(solution)/shard_map/ppermute | solution.py:229
  51.1 3.2 %collective-permute-start.28 = (f32[4,32,1536]{2,1,0:T(8,128)S(1)}, f32[4,32,1536]{2,1,0:T(8,128)S(1)}, u32[]{:S(2)}, u32[]{:S(2)}) collective-permute-start(f32[4,32,1536]{2,1,0:T(8,128)S(1)} %slice_select_fusion), channel_id=1, source_target_pairs={{0,1},{1,0},{2,3},{3,2},{4,5},{5,4},{6,7},{7,6}} | collective-permute-start | bytes 2359304 | tf_op jit(solution)/shard_map/ppermute | solution.py:229
  53.2 11.2 %collective-permute-start.6 = (bf16[4,32,1536]{2,1,0:T(8,128)(2,1)S(1)}, bf16[4,32,1536]{2,1,0:T(8,128)(2,1)S(1)}, u32[]{:S(2)}, u32[]{:S(2)}) collective-permute-start(bf16[4,32,1536]{2,1,0:T(8,128)(2,1)S(1)} %get-tuple-element.117), channel_id=1, source_target_pairs={{0,2},{1,3},{2,0},{3,1},{4,6},{5,7},{6,4},{7,5}} | collective-permute-start | bytes 1179656 | tf_op jit(solution)/shard_map/ppermute | solution.py:229
  54.3 12.0 %collective-permute-start.11 = (bf16[4,32,1536]{2,1,0:T(8,128)(2,1)S(1)}, bf16[4,32,1536]{2,1,0:T(8,128)(2,1)S(1)}, u32[]{:S(2)}, u32[]{:S(2)}) collective-permute-start(bf16[4,32,1536]{2,1,0:T(8,128)(2,1)S(1)} %get-tuple-element.118), channel_id=1, source_target_pairs={{0,4},{1,5},{2,6},{3,7},{4,0},{5,1},{6,2},{7,3}} | collective-permute-start | bytes 1179656 | tf_op jit(solution)/shard_map/ppermute | solution.py:229
  55.0 28.1 %collective-permute-start.26 = (f32[4,32,1536]{2,1,0:T(8,128)S(1)}, f32[4,32,1536]{2,1,0:T(8,128)S(1)}, u32[]{:S(2)}, u32[]{:S(2)}) collective-permute-start(f32[4,32,1536]{2,1,0:T(8,128)S(1)} %select_add_fusion.4), channel_id=1, source_target_pairs={{0,4},{1,5},{2,6},{3,7},{4,0},{5,1},{6,2},{7,3}} | collective-permute-start | bytes 2359304 | tf_op jit(solution)/shard_map/ppermute | solution.py:229
  64.3 20.4 %collective-permute-start.29 = (f32[4,32,1536]{2,1,0:T(8,128)S(1)}, f32[4,32,1536]{2,1,0:T(8,128)S(1)}, u32[]{:S(2)}, u32[]{:S(2)}) collective-permute-start(f32[4,32,1536]{2,1,0:T(8,128)S(1)} %select_add_fusion.3), channel_id=1, source_target_pairs={{0,2},{1,3},{2,0},{3,1},{4,6},{5,7},{6,4},{7,5}} | collective-permute-start | bytes 2359304 | tf_op jit(solution)/shard_map/ppermute | solution.py:229
  66.3 32.9 %collective-permute-start.7 = (bf16[4,32,1536]{2,1,0:T(8,128)(2,1)S(1)}, bf16[4,32,1536]{2,1,0:T(8,128)(2,1)S(1)}, u32[]{:S(2)}, u32[]{:S(2)}) collective-permute-start(bf16[4,32,1536]{2,1,0:T(8,128)(2,1)S(1)} %add_add_fusion.2), channel_id=1, source_target_pairs={{0,4},{1,5},{2,6},{3,7},{4,0},{5,1},{6,2},{7,3}} | collective-permute-start | bytes 1179656 | tf_op jit(solution)/shard_map/ppermute | solution.py:229
  67.0 32.2 %collective-permute-start.4 = (bf16[4,32,1536]{2,1,0:T(8,128)(2,1)S(1)}, bf16[4,32,1536]{2,1,0:T(8,128)(2,1)S(1)}, u32[]{:S(2)}, u32[]{:S(2)}) collective-permute-start(bf16[4,32,1536]{2,1,0:T(8,128)(2,1)S(1)} %slice_add_fusion.2), channel_id=1, source_target_pairs={{0,4},{1,5},{2,6},{3,7},{4,0},{5,1},{6,2},{7,3}} | collective-permute-start | bytes 1179656 | tf_op jit(solution)/shard_map/ppermute | solution.py:229
  68.5 30.7 %collective-permute-start.3 = (bf16[4,32,1536]{2,1,0:T(8,128)(2,1)S(1)}, bf16[4,32,1536]{2,1,0:T(8,128)(2,1)S(1)}, u32[]{:S(2)}, u32[]{:S(2)}) collective-permute-start(bf16[4,32,1536]{2,1,0:T(8,128)(2,1)S(1)} %slice_add_fusion.3), channel_id=1, source_target_pairs={{0,2},{1,3},{2,0},{3,1},{4,6},{5,7},{6,4},{7,5}} | collective-permute-start | bytes 1179656 | tf_op jit(solution)/shard_map/ppermute | solution.py:229
  83.2 16.8 %collective-permute-start.12 = (bf16[4,32,1536]{2,1,0:T(8,128)(2,1)S(1)}, bf16[4,32,1536]{2,1,0:T(8,128)(2,1)S(1)}, u32[]{:S(2)}, u32[]{:S(2)}) collective-permute-start(bf16[4,32,1536]{2,1,0:T(8,128)(2,1)S(1)} %add_add_fusion), channel_id=1, source_target_pairs={{0,2},{1,3},{2,0},{3,1},{4,6},{5,7},{6,4},{7,5}} | collective-permute-start | bytes 1179656 | tf_op jit(solution)/shard_map/ppermute | solution.py:229
  86.8 18.3 %collective-permute-start.30 = (f32[4,32,3072]{2,1,0:T(8,128)S(1)}, f32[4,32,3072]{2,1,0:T(8,128)S(1)}, u32[]{:S(2)}, u32[]{:S(2)}) collective-permute-start(f32[4,32,3072]{2,1,0:T(8,128)S(1)} %broadcast_select_fusion), channel_id=1, source_target_pairs={{0,1},{1,0},{2,3},{3,2},{4,5},{5,4},{6,7},{7,6}} | collective-permute-start | bytes 4718600 | tf_op jit(solution)/shard_map/ppermute | solution.py:229
  100.1 2.6 %collective-permute-start.22 = (bf16[4,32,1536]{2,1,0:T(8,128)(2,1)S(1)}, bf16[4,32,1536]{2,1,0:T(8,128)(2,1)S(1)}, u32[]{:S(2)}, u32[]{:S(2)}) collective-permute-start(bf16[4,32,1536]{2,1,0:T(8,128)(2,1)S(1)} %get-tuple-element.106.refs_0_), channel_id=1, source_target_pairs={{0,1},{1,0},{2,3},{3,2},{4,5},{5,4},{6,7},{7,6}} | collective-permute-start | bytes 1179656 | tf_op jit(solution)/shard_map/ppermute | solution.py:229
  100.1 3.1 %collective-permute-start.23 = (bf16[4,32,1536]{2,1,0:T(8,128)(2,1)S(1)}, bf16[4,32,1536]{2,1,0:T(8,128)(2,1)S(1)}, u32[]{:S(2)}, u32[]{:S(2)}) collective-permute-start(bf16[4,32,1536]{2,1,0:T(8,128)(2,1)S(1)} %get-tuple-element.105.refs_2_), channel_id=1, source_target_pairs={{0,1},{1,0},{2,3},{3,2},{4,5},{5,4},{6,7},{7,6}} | collective-permute-start | bytes 1179656 | tf_op jit(solution)/shard_map/ppermute | solution.py:229
  100.6 12.0 %collective-permute-start.19 = (bf16[4,32,1536]{2,1,0:T(8,128)(2,1)S(1)}, bf16[4,32,1536]{2,1,0:T(8,128)(2,1)S(1)}, u32[]{:S(2)}, u32[]{:S(2)}) collective-permute-start(bf16[4,32,1536]{2,1,0:T(8,128)(2,1)S(1)} %get-tuple-element.106.refs_0_), channel_id=1, source_target_pairs={{0,2},{1,3},{2,0},{3,1},{4,6},{5,7},{6,4},{7,5}} | collective-permute-start | bytes 1179656 | tf_op jit(solution)/shard_map/ppermute | solution.py:229
  101.2 19.1 %collective-permute-start.13 = (bf16[4,32,1536]{2,1,0:T(8,128)(2,1)S(1)}, bf16[4,32,1536]{2,1,0:T(8,128)(2,1)S(1)}, u32[]{:S(2)}, u32[]{:S(2)}) collective-permute-start(bf16[4,32,1536]{2,1,0:T(8,128)(2,1)S(1)} %get-tuple-element.105.refs_2_), channel_id=1, source_target_pairs={{0,2},{1,3},{2,0},{3,1},{4,6},{5,7},{6,4},{7,5}} | collective-permute-start | bytes 1179656 | tf_op jit(solution)/shard_map/ppermute | solution.py:229
  102.7 18.4 %collective-permute-start.8 = (bf16[4,32,1536]{2,1,0:T(8,128)(2,1)S(1)}, bf16[4,32,1536]{2,1,0:T(8,128)(2,1)S(1)}, u32[]{:S(2)}, u32[]{:S(2)}) collective-permute-start(bf16[4,32,1536]{2,1,0:T(8,128)(2,1)S(1)} %get-tuple-element.106.refs_0_), channel_id=1, source_target_pairs={{0,4},{1,5},{2,6},{3,7},{4,0},{5,1},{6,2},{7,3}} | collective-permute-start | bytes 1179656 | tf_op jit(solution)/shard_map/ppermute | solution.py:229
  103.2 18.3 %collective-permute-start.17 = (bf16[4,32,1536]{2,1,0:T(8,128)(2,1)S(1)}, bf16[4,32,1536]{2,1,0:T(8,128)(2,1)S(1)}, u32[]{:S(2)}, u32[]{:S(2)}) collective-permute-start(bf16[4,32,1536]{2,1,0:T(8,128)(2,1)S(1)} %get-tuple-element.105.refs_2_), channel_id=1, source_target_pairs={{0,4},{1,5},{2,6},{3,7},{4,0},{5,1},{6,2},{7,3}} | collective-permute-start | bytes 1179656 | tf_op jit(solution)/shard_map/ppermute | solution.py:229
  107.8 1.2 collective-permute-start.45
  109.0 11.4 %collective-permute-start.46 = (f32[3072]{0:T(1024)S(1)}, f32[3072]{0:T(1024)S(1)}, u32[]{:S(2)}, u32[]{:S(2)}) collective-permute-start(f32[3072]{0:T(1024)S(1)} %add.138), channel_id=1, source_target_pairs={{0,2},{1,3},{2,0},{3,1},{4,6},{5,7},{6,4},{7,5}} | collective-permute-start | bytes 36872 | tf_op jit(solution)/shard_map/ppermute | solution.py:229
  112.6 12.0 %collective-permute-start.20 = (bf16[4,32,1536]{2,1,0:T(8,128)(2,1)S(1)}, bf16[4,32,1536]{2,1,0:T(8,128)(2,1)S(1)}, u32[]{:S(2)}, u32[]{:S(2)}) collective-permute-start(bf16[4,32,1536]{2,1,0:T(8,128)(2,1)S(1)} %collective-permute-done.19.refs_0_), channel_id=1, source_target_pairs={{0,1},{1,0},{2,3},{3,2},{4,5},{5,4},{6,7},{7,6}} | collective-permute-start | bytes 1179656 | tf_op jit(solution)/shard_map/ppermute | solution.py:229
  120.2 4.9 %collective-permute-start.21 = (bf16[4,32,1536]{2,1,0:T(8,128)(2,1)S(1)}, bf16[4,32,1536]{2,1,0:T(8,128)(2,1)S(1)}, u32[]{:S(2)}, u32[]{:S(2)}) collective-permute-start(bf16[4,32,1536]{2,1,0:T(8,128)(2,1)S(1)} %collective-permute-done.13.refs_2_), channel_id=1, source_target_pairs={{0,1},{1,0},{2,3},{3,2},{4,5},{5,4},{6,7},{7,6}} | collective-permute-start | bytes 1179656 | tf_op jit(solution)/shard_map/ppermute | solution.py:229
  120.4 3.7 %collective-permute-start.47 = (f32[3072]{0:T(1024)S(1)}, f32[3072]{0:T(1024)S(1)}, u32[]{:S(2)}, u32[]{:S(2)}) collective-permute-start(f32[3072]{0:T(1024)S(1)} %add.139), channel_id=1, source_target_pairs={{0,4},{1,5},{2,6},{3,7},{4,0},{5,1},{6,2},{7,3}} | collective-permute-start | bytes 36872 | tf_op jit(solution)/shard_map/ppermute | solution.py:229
  121.0 5.6 %collective-permute-start.16 = (bf16[4,32,1536]{2,1,0:T(8,128)(2,1)S(1)}, bf16[4,32,1536]{2,1,0:T(8,128)(2,1)S(1)}, u32[]{:S(2)}, u32[]{:S(2)}) collective-permute-start(bf16[4,32,1536]{2,1,0:T(8,128)(2,1)S(1)} %collective-permute-done.8.refs_0_), channel_id=1, source_target_pairs={{0,1},{1,0},{2,3},{3,2},{4,5},{5,4},{6,7},{7,6}} | collective-permute-start | bytes 1179656 | tf_op jit(solution)/shard_map/ppermute | solution.py:229
  121.6 6.6 %collective-permute-start.18 = (bf16[4,32,1536]{2,1,0:T(8,128)(2,1)S(1)}, bf16[4,32,1536]{2,1,0:T(8,128)(2,1)S(1)}, u32[]{:S(2)}, u32[]{:S(2)}) collective-permute-start(bf16[4,32,1536]{2,1,0:T(8,128)(2,1)S(1)} %collective-permute-done.17.refs_2_), channel_id=1, source_target_pairs={{0,1},{1,0},{2,3},{3,2},{4,5},{5,4},{6,7},{7,6}} | collective-permute-start | bytes 1179656 | tf_op jit(solution)/shard_map/ppermute | solution.py:229
  124.1 12.0 %collective-permute-start.9 = (bf16[4,32,1536]{2,1,0:T(8,128)(2,1)S(1)}, bf16[4,32,1536]{2,1,0:T(8,128)(2,1)S(1)}, u32[]{:S(2)}, u32[]{:S(2)}) collective-permute-start(bf16[4,32,1536]{2,1,0:T(8,128)(2,1)S(1)} %collective-permute-done.8.refs_0_), channel_id=1, source_target_pairs={{0,2},{1,3},{2,0},{3,1},{4,6},{5,7},{6,4},{7,5}} | collective-permute-start | bytes 1179656 | tf_op jit(solution)/shard_map/ppermute | solution.py:229
  124.6 12.0 %collective-permute-start.14 = (bf16[4,32,1536]{2,1,0:T(8,128)(2,1)S(1)}, bf16[4,32,1536]{2,1,0:T(8,128)(2,1)S(1)}, u32[]{:S(2)}, u32[]{:S(2)}) collective-permute-start(bf16[4,32,1536]{2,1,0:T(8,128)(2,1)S(1)} %collective-permute-done.13.refs_2_), channel_id=1, source_target_pairs={{0,4},{1,5},{2,6},{3,7},{4,0},{5,1},{6,2},{7,3}} | collective-permute-start | bytes 1179656 | tf_op jit(solution)/shard_map/ppermute | solution.py:229
  125.1 20.0 %collective-permute-start.37 = (bf16[2,32,3072]{2,1,0:T(8,128)(2,1)S(1)}, bf16[2,32,3072]{2,1,0:T(8,128)(2,1)}, u32[]{:S(2)}, u32[]{:S(2)}) collective-permute-start(bf16[2,32,3072]{2,1,0:T(8,128)(2,1)S(1)} %get-tuple-element.120.refs_0_), channel_id=1, source_target_pairs={{0,4},{1,5},{2,6},{3,7},{4,0},{5,1},{6,2},{7,3}} | collective-permute-start | bytes 1179656 | tf_op jit(solution)/shard_map/ppermute | solution.py:229
  126.6 18.5 %collective-permute-start.34 = (bf16[2,32,3072]{2,1,0:T(8,128)(2,1)S(1)}, bf16[2,32,3072]{2,1,0:T(8,128)(2,1)}, u32[]{:S(2)}, u32[]{:S(2)}) collective-permute-start(bf16[2,32,3072]{2,1,0:T(8,128)(2,1)S(1)} %get-tuple-element.119.refs_1_), channel_id=1, source_target_pairs={{0,2},{1,3},{2,0},{3,1},{4,6},{5,7},{6,4},{7,5}} | collective-permute-start | bytes 1179656 | tf_op jit(solution)/shard_map/ppermute | solution.py:229
  128.1 23.0 %collective-permute-start.33 = (bf16[2,32,3072]{2,1,0:T(8,128)(2,1)S(1)}, bf16[2,32,3072]{2,1,0:T(8,128)(2,1)S(1)}, u32[]{:S(2)}, u32[]{:S(2)}) collective-permute-start(bf16[2,32,3072]{2,1,0:T(8,128)(2,1)S(1)} %get-tuple-element.120.refs_0_), channel_id=1, source_target_pairs={{0,2},{1,3},{2,0},{3,1},{4,6},{5,7},{6,4},{7,5}} | collective-permute-start | bytes 1179656 | tf_op jit(solution)/shard_map/ppermute | solution.py:229
  136.1 15.5 %collective-permute-start.38 = (bf16[2,32,3072]{2,1,0:T(8,128)(2,1)S(1)}, bf16[2,32,3072]{2,1,0:T(8,128)(2,1)}, u32[]{:S(2)}, u32[]{:S(2)}) collective-permute-start(bf16[2,32,3072]{2,1,0:T(8,128)(2,1)S(1)} %get-tuple-element.119.refs_1_), channel_id=1, source_target_pairs={{0,4},{1,5},{2,6},{3,7},{4,0},{5,1},{6,2},{7,3}} | collective-permute-start | bytes 1179656 | tf_op jit(solution)/shard_map/ppermute | solution.py:229
  136.6 16.4 %collective-permute-start.31 = (bf16[2,32,3072]{2,1,0:T(8,128)(2,1)S(1)}, bf16[2,32,3072]{2,1,0:T(8,128)(2,1)S(1)}, u32[]{:S(2)}, u32[]{:S(2)}) collective-permute-start(bf16[2,32,3072]{2,1,0:T(8,128)(2,1)S(1)} %get-tuple-element.120.refs_0_), channel_id=1, source_target_pairs={{0,1},{1,0},{2,3},{3,2},{4,5},{5,4},{6,7},{7,6}} | collective-permute-start | bytes 1179656 | tf_op jit(solution)/shard_map/ppermute | solution.py:229
  145.1 9.2 %collective-permute-start.32 = (bf16[2,32,3072]{2,1,0:T(8,128)(2,1)S(1)}, bf16[2,32,3072]{2,1,0:T(8,128)(2,1)S(1)}, u32[]{:S(2)}, u32[]{:S(2)}) collective-permute-start(bf16[2,32,3072]{2,1,0:T(8,128)(2,1)S(1)} %get-tuple-element.119.refs_1_), channel_id=1, source_target_pairs={{0,1},{1,0},{2,3},{3,2},{4,5},{5,4},{6,7},{7,6}} | collective-permute-start | bytes 1179656 | tf_op jit(solution)/shard_map/ppermute | solution.py:229
  145.1 9.2 %collective-permute-start.10 = (bf16[4,32,1536]{2,1,0:T(8,128)(2,1)S(1)}, bf16[4,32,1536]{2,1,0:T(8,128)(2,1)S(1)}, u32[]{:S(2)}, u32[]{:S(2)}) collective-permute-start(bf16[4,32,1536]{2,1,0:T(8,128)(2,1)S(1)} %collective-permute-done.9.refs_0_), channel_id=1, source_target_pairs={{0,1},{1,0},{2,3},{3,2},{4,5},{5,4},{6,7},{7,6}} | collective-permute-start | bytes 1179656 | tf_op jit(solution)/shard_map/ppermute | solution.py:229
  151.2 3.7 %collective-permute-start.15 = (bf16[4,32,1536]{2,1,0:T(8,128)(2,1)S(1)}, bf16[4,32,1536]{2,1,0:T(8,128)(2,1)S(1)}, u32[]{:S(2)}, u32[]{:S(2)}) collective-permute-start(bf16[4,32,1536]{2,1,0:T(8,128)(2,1)S(1)} %collective-permute-done.14.refs_2_), channel_id=1, source_target_pairs={{0,1},{1,0},{2,3},{3,2},{4,5},{5,4},{6,7},{7,6}} | collective-permute-start | bytes 1179656 | tf_op jit(solution)/shard_map/ppermute | solution.py:229
  151.5 11.5 %collective-permute-start.41 = (bf16[2,32,3072]{2,1,0:T(8,128)(2,1)}, bf16[2,32,3072]{2,1,0:T(8,128)(2,1)}, u32[]{:S(2)}, u32[]{:S(2)}) collective-permute-start(bf16[2,32,3072]{2,1,0:T(8,128)(2,1)} %collective-permute-done.37.refs_8_), channel_id=1, source_target_pairs={{0,2},{1,3},{2,0},{3,1},{4,6},{5,7},{6,4},{7,5}} | collective-permute-start | bytes 1179656 | tf_op jit(solution)/shard_map/ppermute | solution.py:229
  153.8 10.3 %collective-permute-start.42 = (bf16[2,32,3072]{2,1,0:T(8,128)(2,1)}, bf16[2,32,3072]{2,1,0:T(8,128)(2,1)}, u32[]{:S(2)}, u32[]{:S(2)}) collective-permute-start(bf16[2,32,3072]{2,1,0:T(8,128)(2,1)} %collective-permute-done.34.refs_5_), channel_id=1, source_target_pairs={{0,4},{1,5},{2,6},{3,7},{4,0},{5,1},{6,2},{7,3}} | collective-permute-start | bytes 1179656 | tf_op jit(solution)/shard_map/ppermute | solution.py:229
  154.4 9.7 %collective-permute-start.35 = (bf16[2,32,3072]{2,1,0:T(8,128)(2,1)S(1)}, bf16[2,32,3072]{2,1,0:T(8,128)(2,1)S(1)}, u32[]{:S(2)}, u32[]{:S(2)}) collective-permute-start(bf16[2,32,3072]{2,1,0:T(8,128)(2,1)S(1)} %collective-permute-done.33.refs_4_), channel_id=1, source_target_pairs={{0,1},{1,0},{2,3},{3,2},{4,5},{5,4},{6,7},{7,6}} | collective-permute-start | bytes 1179656 | tf_op jit(solution)/shard_map/ppermute | solution.py:229
  154.4 41.5 %collective-permute-start.36 = (bf16[2,32,3072]{2,1,0:T(8,128)(2,1)}, bf16[2,32,3072]{2,1,0:T(8,128)(2,1)}, u32[]{:S(2)}, u32[]{:S(2)}) collective-permute-start(bf16[2,32,3072]{2,1,0:T(8,128)(2,1)} %collective-permute-done.34.refs_5_), channel_id=1, source_target_pairs={{0,1},{1,0},{2,3},{3,2},{4,5},{5,4},{6,7},{7,6}} | collective-permute-start | bytes 1179656 | tf_op jit(solution)/shard_map/ppermute | solution.py:229
  154.9 41.0 %collective-permute-start.39 = (bf16[2,32,3072]{2,1,0:T(8,128)(2,1)}, bf16[2,32,3072]{2,1,0:T(8,128)(2,1)}, u32[]{:S(2)}, u32[]{:S(2)}) collective-permute-start(bf16[2,32,3072]{2,1,0:T(8,128)(2,1)} %collective-permute-done.37.refs_8_), channel_id=1, source_target_pairs={{0,1},{1,0},{2,3},{3,2},{4,5},{5,4},{6,7},{7,6}} | collective-permute-start | bytes 1179656 | tf_op jit(solution)/shard_map/ppermute | solution.py:229
  163.0 32.8 %collective-permute-start.40 = (bf16[2,32,3072]{2,1,0:T(8,128)(2,1)}, bf16[2,32,3072]{2,1,0:T(8,128)(2,1)}, u32[]{:S(2)}, u32[]{:S(2)}) collective-permute-start(bf16[2,32,3072]{2,1,0:T(8,128)(2,1)} %collective-permute-done.38.refs_9_), channel_id=1, source_target_pairs={{0,1},{1,0},{2,3},{3,2},{4,5},{5,4},{6,7},{7,6}} | collective-permute-start | bytes 1179656 | tf_op jit(solution)/shard_map/ppermute | solution.py:229
  164.0 31.8 %collective-permute-start.43 = (bf16[2,32,3072]{2,1,0:T(8,128)(2,1)}, bf16[2,32,3072]{2,1,0:T(8,128)(2,1)}, u32[]{:S(2)}, u32[]{:S(2)}) collective-permute-start(bf16[2,32,3072]{2,1,0:T(8,128)(2,1)} %collective-permute-done.41.refs_12_), channel_id=1, source_target_pairs={{0,1},{1,0},{2,3},{3,2},{4,5},{5,4},{6,7},{7,6}} | collective-permute-start | bytes 1179656 | tf_op jit(solution)/shard_map/ppermute | solution.py:229
  164.1 31.8 %collective-permute-start.44 = (bf16[2,32,3072]{2,1,0:T(8,128)(2,1)}, bf16[2,32,3072]{2,1,0:T(8,128)(2,1)}, u32[]{:S(2)}, u32[]{:S(2)}) collective-permute-start(bf16[2,32,3072]{2,1,0:T(8,128)(2,1)} %collective-permute-done.42.refs_13_), channel_id=1, source_target_pairs={{0,1},{1,0},{2,3},{3,2},{4,5},{5,4},{6,7},{7,6}} | collective-permute-start | bytes 1179656 | tf_op jit(solution)/shard_map/ppermute | solution.py:229
  (25 other events, 248.2 us)

commit v5 on v4

--- a/solution.py
+++ b/solution.py
@@ -14,7 +14,7 @@
 HBM = pl.BlockSpec(memory_space=pltpu.HBM)
 ZR = 128
 BLK = 256
-LOOKUP_EARLY, LOOKUP_SHARE, NORM_SHARE = 8, 26, 6
+LOOKUP_EARLY, LOOKUP_SHARE, ZERO_A, ZERO_B, NORM_SHARE = 8, 22, 33, 48, 3
 
 
 def zero_fill(de, z, sem, first, last):
@@ -31,6 +31,13 @@
         pl.loop(first, last)(lambda i: copy(i).wait())
 
     return start, wait
+
+
+def zero_kernel(first, last, de_in, de, z, sem):
+    del de_in
+    start, wait = zero_fill(de, z, sem, first, last)
+    start()
+    wait()
 
 
 def pdn_first_kernel(j, c_ref, du_hbm, w_hbm, h0, h1, du_ref, w_ref, sem, wsem):
@@ -127,7 +134,7 @@
     d = nt_ref.shape[0]
     mb, tl, hd = blocks[0].shape
     tc = 2 * tl
-    first = LOOKUP_SHARE + j * NORM_SHARE
+    first = ZERO_B + j * NORM_SHARE
     start, wait = zero_fill(de, z, zsem, first, first + NORM_SHARE)
     start()
     at = [pl.ds(pl.multiple_of(jnp.bitwise_xor(k, q) * hd, 128), hd) for q in range(2)]
@@ -164,7 +171,7 @@
     mb, _, _ = du_ref.shape
     d, kj = ns[0].shape
     tc = kj // mb
-    start, wait = zero_fill(de, z, zsem, LOOKUP_SHARE + 4 * NORM_SHARE, de.shape[0] // ZR)
+    start, wait = zero_fill(de, z, zsem, ZERO_B + 4 * NORM_SHARE, de.shape[0] // ZR)
     start()
     for j in range(4):
         rows = pl.ds(pl.multiple_of(jnp.bitwise_xor(c_ref[0], j) * tc, tc), tc)
@@ -253,7 +260,7 @@
                 in_specs=[SMEM, VMEM, VMEM],
                 out_specs=(VMEM,) * (2 * len(js)),
                 cost_estimate=pl.CostEstimate(flops=5_000_000 * len(js), bytes_accessed=8_000_000, transcendentals=0),
-                compiler_params=pltpu.CompilerParams(vmem_limit_bytes=40 * 2**20),
+                compiler_params=pltpu.CompilerParams(vmem_limit_bytes=20 * 2**20),
             )(c.reshape(1), du, w)
             return {j: out[2 * i:2 * i + 2] for i, j in enumerate(js)}
 
@@ -308,7 +315,7 @@
                 pltpu.SemaphoreType.DMA((6,)),
             ],
             cost_estimate=pl.CostEstimate(flops=5_000_000, bytes_accessed=8_000_000, transcendentals=0),
-            compiler_params=pltpu.CompilerParams(vmem_limit_bytes=63 * 2**20),
+            compiler_params=pltpu.CompilerParams(vmem_limit_bytes=60 * 2**20),
             name="pa",
         )(c.reshape(1), du, w)}
         part.update(pdn((1, 2)))
@@ -345,9 +352,20 @@
             out_specs=(VMEM, VMEM, VMEM, ANY),
             scratch_shapes=[pltpu.VMEM((2 * n, d), jnp.bfloat16), pltpu.SemaphoreType.DMA] + zero_scratch,
             cost_estimate=pl.CostEstimate(flops=40_000_000, bytes_accessed=60_000_000, transcendentals=0),
-            compiler_params=pltpu.CompilerParams(vmem_limit_bytes=40 * 2**20),
+            compiler_params=pltpu.CompilerParams(vmem_limit_bytes=32 * 2**20),
             name="look",
         )(kc, owned, n_owned, loc, tgt.reshape(n, 1), emb)
+        for first, last in ((LOOKUP_SHARE, ZERO_A), (ZERO_A, ZERO_B)):
+            de = pl.pallas_call(
+                functools.partial(zero_kernel, first, last),
+                out_shape=de_shape,
+                in_specs=[ANY],
+                out_specs=ANY,
+                scratch_shapes=zero_scratch,
+                input_output_aliases={0: 0},
+                cost_estimate=pl.CostEstimate(flops=10_000_000, bytes_accessed=20_000_000, transcendentals=0),
+                compiler_params=pltpu.CompilerParams(vmem_limit_bytes=4 * 2**20),
+            )(de)
         far, near = swap(far, 1), swap(near, 1)
         xpairs = {j: (mine[j], far[0] if j == 3 else near[j]) for j in range(4)}
 
@@ -377,7 +395,7 @@
                 ] + zero_scratch,
                 input_output_aliases={7 + i: 3 - len(more) + i for i in range(len(more))},
                 cost_estimate=pl.CostEstimate(flops=8_000_000, bytes_accessed=12_000_000, transcendentals=0),
-                compiler_params=pltpu.CompilerParams(vmem_limit_bytes=40 * 2**20),
+                compiler_params=pltpu.CompilerParams(vmem_limit_bytes=24 * 2**20),
             )(kc, g.reshape(1, d), w, *(xo[2 * j + q][h] for h in range(2) for q in range(2)), *more)
             ns.append(nj)
         dw, de = pl.pallas_call(
@@ -392,7 +410,7 @@
             ] + zero_scratch,
             input_output_aliases={6: 1},
             cost_estimate=pl.CostEstimate(flops=30_000_000, bytes_accessed=40_000_000, transcendentals=0),
-            compiler_params=pltpu.CompilerParams(vmem_limit_bytes=40 * 2**20),
+            compiler_params=pltpu.CompilerParams(vmem_limit_bytes=24 * 2**20),
             name="dw",
         )(c.reshape(1), du, *ns, de)
 
@@ -419,7 +437,7 @@
                 pltpu.SemaphoreType.DMA,
             ],
             input_output_aliases={20: 0},
-            compiler_params=pltpu.CompilerParams(vmem_limit_bytes=40 * 2**20),
+            compiler_params=pltpu.CompilerParams(vmem_limit_bytes=28 * 2**20),
             name="put",
         )(me, rows, cnt, slot.reshape(1, n), *dxs, de)
         return u, x, de, dw, dg

time: 204 us -> 211 us (1.034)
  Pallas kernels: 64 us -> 69.6 us
  local copies, waits for them, and re-layouts: 10.9 us -> 15.5 us
  waiting for transfers between devices: 84.7 us -> 81.8 us
    pallas_call x0 -> x2, Pallas kernels: none -> 14.8 us  [local(): pl.pallas_call(functools.partial(zero_kernel, first, last), out_shape=de_...]
    pallas_call x1, Pallas kernels: 13 us -> 8.29 us  [local(): pl.pallas_call(dw_kernel, out_shape=(jax.ShapeDtypeStruct((d, f), jnp.flo...]
    unnamed x51 -> x85, local copies, waits for them, and re-layouts: 10.2 us -> 14.8 us
    ppermute x48, waiting for transfers between devices: 84.7 us -> 81.8 us  [swap(): return lax.ppermute(v, 'tp', [(i, i ^ bit) for i in range(groups)])]
    pallas_call x4, Pallas kernels: 17.5 us -> 14.7 us  [local(): pl.pallas_call(functools.partial(norm_kernel, j), out_shape=(jax.ShapeDty...]
  transfers between devices with their start and end apart: 48 -> 48, of which waited for: 21 -> 23; matrix products, arithmetic and copies ran while one was open for 7% -> 7% of each run, Pallas kernels for 25% -> 27%
where the time goes in v5:
time: 211 us; the launch traced here: 210 us
  waiting for transfers between devices  81.8 us (39%)
  Pallas kernels  69.6 us (33%)
  starting transfers between devices  27.1 us (13%)
  local copies, waits for them, and re-layouts  15.5 us (7%)
  other arithmetic  14.4 us (7%)
    ppermute x48, waiting for transfers between devices, swap(): return lax.ppermute(v, 'tp', [(i, i ^ bit) for i in range(groups)])  81.8 us
    ppermute x48, starting transfers between devices, swap(): return lax.ppermute(v, 'tp', [(i, i ^ bit) for i in range(groups)])  27.1 us
    unnamed x85, local copies, waits for them, and re-layouts  14.8 us
    pallas_call x2, Pallas kernels, local(): pl.pallas_call(functools.partial(zero_kernel, first, last), out_shape=de_...  14.8 us
    pallas_call x4, Pallas kernels, local(): pl.pallas_call(functools.partial(norm_kernel, j), out_shape=(jax.ShapeDty...  14.7 us
    pallas_call x1, Pallas kernels, local(): pl.pallas_call(lookup_kernel, out_shape=(half_shape(4), half_shape(1), ha...  13.7 us
    pallas_call x1, Pallas kernels, local(): pl.pallas_call(dw_kernel, out_shape=(jax.ShapeDtypeStruct((d, f), jnp.flo...  8.29 us
    pallas_call x1, Pallas kernels, local(): pl.pallas_call(scatter_kernel, out_shape=de_shape, in_specs=[SMEM, SMEM,...  7.45 us
  transfers between devices with their start and end apart: 48, of which 23 were waited for; matrix products, arithmetic and copies ran while one was open for 7% of the time, Pallas kernels for 27%

profile of v5, /device:TPU:0, one launch (start us, length us, event | category | flops | bytes accessed | tf_op | source)
XLA Modules:
  0.0 210.1 jit_solution(10686009991368084443)
XLA Ops:
  0.6 5.7 %pa.1 = (bf16[4,32,3072]{2,1,0:T(8,128)(2,1)}, bf16[4,32,3072]{2,1,0:T(8,128)(2,1)}) custom-call(s32[1]{0:T(128)} %bitcast.1.c_ref, bf16[4,256,640]{2,1,0:T(8,128)(2,1)} %du_ref.5, bf16[3072,640]{1,0:T(8,128)(2,1)} %w_ref.11), custom_call_target="tpu_custom_call" | custom-call | flops 5000000 | bytes 8000000 | tf_op jit(solution)/shard_map/pa/pallas_call | solution.py:306
  6.4 3.3 %collective-permute-start = (bf16[4,32,3072]{2,1,0:T(8,128)(2,1)}, bf16[4,32,3072]{2,1,0:T(8,128)(2,1)}, u32[]{:S(2)}, u32[]{:S(2)}) collective-permute-start(bf16[4,32,3072]{2,1,0:T(8,128)(2,1)} %get-tuple-element.50), channel_id=1, source_target_pairs={{0,2},{1,3},{2,0},{3,1},{4,6},{5,7},{6,4},{7,5}} | collective-permute-start | bytes 2359304 | tf_op jit(solution)/shard_map/ppermute | solution.py:236
  9.7 1.5 collective-permute-start.1
  11.2 1.3 copy-done.3
  12.6 3.6 %shard_map.108 = (bf16[4,32,3072]{2,1,0:T(8,128)(2,1)}, bf16[4,32,3072]{2,1,0:T(8,128)(2,1)S(1)}, bf16[4,32,3072]{2,1,0:T(8,128)(2,1)S(1)}, bf16[4,32,3072]{2,1,0:T(8,128)(2,1)}) custom-call(s32[1]{0:T(128)} %bitcast.1.c_ref, bf16[4,256,640]{2,1,0:T(8,128)(2,1)S(1)} %copy-done.3, bf16[3072,640]{1,0:T(8,128)(2,1)S(1)} %copy-done), custom_call_target="tpu_custom_call" | custom-call | flops 10000000 | bytes 8000000 | tf_op jit(solution)/shard_map/pallas_call | solution.py:257
  18.5 2.1 %copy-done.1 = bf16[3072,640]{1,0:T(8,128)(2,1)S(1)} copy-done((bf16[3072,640]{1,0:T(8,128)(2,1)S(1)}, bf16[3072,640]{1,0:T(8,128)(2,1)}, u32[]{:S(2)}) %copy-start.1) | copy-done | bytes 3932184
  20.6 1.3 copy-done.4
  21.9 1.4 shard_map.107
  25.3 2.9 %select_reduce_fusion.2 = (s32[1024]{0:T(1024)S(1)}, s32[1024]{0:T(1024)S(1)}, s32[1024]{0:T(1024)S(1)}) fusion(s32[1024]{0:T(1024)S(1)} %get-tuple-element.54.loc_ref, s32[1024]{0:T(1024)S(1)} %select_reduce_fusion.4, pred[1024]{0:T(1024)(128)(4,1)S(1)} %get-tuple-element.107, s32[1024]{0:T(1024)S(1)} %select_reduce_fusion.5, ...), kind=kLoop, calls=%fused_computation.3 | loop fusion | flops 11531264 | bytes 30720 | tf_op jit(solution)/shard_map/reduce_sum | solution.py:334
  28.4 2.0 collective-permute-done.1
  30.7 13.7 %look.1 = (bf16[4,4,64,1536]{3,2,1,0:T(8,128)(2,1)S(1)}, bf16[1,4,64,1536]{3,2,1,0:T(8,128)(2,1)S(1)}, bf16[3,4,64,1536]{3,2,1,0:T(8,128)(2,1)S(1)}, f32[8192,3072]{1,0:T(8,128)}) custom-call(s32[2]{0:T(128)S(1)} %pad_add_fusion.kc_ref, s32[1024]{0:T(1024)S(1)} %get-tuple-element.52.list_ref, s32[1]{0:T(128)} %bitcast.3.cnt_ref, ...), custom_call_target="tpu_custom_call" | custom-call | flops 40000000 | bytes 60000000 | tf_op jit(solution)/shard_map/look/pallas_call | solution.py:348
  45.5 1.3 convert_add_fusion.1
  47.0 1.0 copy-done.11
  48.0 1.4 convert_add_fusion
  49.6 1.8 collective-permute-done.25
  51.5 1.0 collective-permute-done.28
  53.2 1.5 collective-permute-start.26
  54.9 7.7 %collective-permute-done.6 = bf16[4,32,1536]{2,1,0:T(8,128)(2,1)S(1)} collective-permute-done((bf16[4,32,1536]{2,1,0:T(8,128)(2,1)S(1)}, bf16[4,32,1536]{2,1,0:T(8,128)(2,1)S(1)}, u32[]{:S(2)}, u32[]{:S(2)}) %collective-permute-start.6) | collective-permute-done | bytes 393248 | tf_op jit(solution)/shard_map/ppermute | solution.py:236
  62.9 1.5 collective-permute-done.11
  65.2 1.5 collective-permute-start.4
  66.7 1.1 collective-permute-start.3
  67.7 13.6 %collective-permute-done.26 = f32[4,32,1536]{2,1,0:T(8,128)S(1)} collective-permute-done((f32[4,32,1536]{2,1,0:T(8,128)S(1)}, f32[4,32,1536]{2,1,0:T(8,128)S(1)}, u32[]{:S(2)}, u32[]{:S(2)}) %collective-permute-start.26) | collective-permute-done | bytes 786464 | tf_op jit(solution)/shard_map/ppermute | solution.py:236
  81.3 1.1 collective-permute-start.12
  83.0 1.8 broadcast_select_fusion
  84.8 12.6 %collective-permute-done.4 = bf16[4,32,1536]{2,1,0:T(8,128)(2,1)S(1)} collective-permute-done((bf16[4,32,1536]{2,1,0:T(8,128)(2,1)S(1)}, bf16[4,32,1536]{2,1,0:T(8,128)(2,1)S(1)}, u32[]{:S(2)}, u32[]{:S(2)}) %collective-permute-start.4) | collective-permute-done | bytes 393248 | tf_op jit(solution)/shard_map/ppermute | solution.py:236
  99.4 1.5 collective-permute-start.13
  101.5 1.5 collective-permute-start.17
  103.3 2.6 %fusion.12 = (f32[3072]{0:T(1024)S(1)}, f32[4,32]{1,0:T(4,128)S(1)}, f32[4,32,3072]{2,1,0:T(8,128)S(1)}) fusion(bf16[4,32,3072]{2,1,0:T(8,128)(2,1)S(1)} %get-tuple-element.103, f32[4,32]{1,0:T(4,128)S(1)} %add_rsqrt_fusion, f32[3072]{0:T(1024)S(1)} %convert_element_type.48, f32[4,32,3072]{2,1,0:T(8,128)S(1)} %collective-permute-done.30, ...), kind=kLoop, calls=%fused_computation.24 | loop fusion | flops 7467904 | bytes 8676353 | tf_op jit(solution)/shard_map/reduce_sum | solution.py:423
  106.0 1.2 collective-permute-done.45
  108.3 2.6 %collective-permute-done.19.refs_0_ = bf16[4,32,1536]{2,1,0:T(8,128)(2,1)S(1)} collective-permute-done((bf16[4,32,1536]{2,1,0:T(8,128)(2,1)S(1)}, bf16[4,32,1536]{2,1,0:T(8,128)(2,1)S(1)}, u32[]{:S(2)}, u32[]{:S(2)}) %collective-permute-start.19) | collective-permute-done | bytes 393248 | tf_op jit(solution)/shard_map/ppermute | solution.py:236
  110.8 7.6 %collective-permute-done.13.refs_2_ = bf16[4,32,1536]{2,1,0:T(8,128)(2,1)S(1)} collective-permute-done((bf16[4,32,1536]{2,1,0:T(8,128)(2,1)S(1)}, bf16[4,32,1536]{2,1,0:T(8,128)(2,1)S(1)}, u32[]{:S(2)}, u32[]{:S(2)}) %collective-permute-start.13) | collective-permute-done | bytes 393248 | tf_op jit(solution)/shard_map/ppermute | solution.py:236
  120.5 1.7 collective-permute-done.47
  124.1 1.6 collective-permute-start.37
  126.4 1.5 collective-permute-start.34
  129.2 5.1 %collective-permute-done.9.refs_0_ = bf16[4,32,1536]{2,1,0:T(8,128)(2,1)S(1)} collective-permute-done((bf16[4,32,1536]{2,1,0:T(8,128)(2,1)S(1)}, bf16[4,32,1536]{2,1,0:T(8,128)(2,1)S(1)}, u32[]{:S(2)}, u32[]{:S(2)}) %collective-permute-start.9) | collective-permute-done | bytes 393248 | tf_op jit(solution)/shard_map/ppermute | solution.py:236
  135.6 8.5 %collective-permute-done.37.refs_8_ = bf16[2,32,3072]{2,1,0:T(8,128)(2,1)} collective-permute-done((bf16[2,32,3072]{2,1,0:T(8,128)(2,1)S(1)}, bf16[2,32,3072]{2,1,0:T(8,128)(2,1)}, u32[]{:S(2)}, u32[]{:S(2)}) %collective-permute-start.37) | collective-permute-done | bytes 393248 | tf_op jit(solution)/shard_map/ppermute | solution.py:236
  145.4 4.0 %collective-permute-done.33.refs_4_ = bf16[2,32,3072]{2,1,0:T(8,128)(2,1)S(1)} collective-permute-done((bf16[2,32,3072]{2,1,0:T(8,128)(2,1)S(1)}, bf16[2,32,3072]{2,1,0:T(8,128)(2,1)S(1)}, u32[]{:S(2)}, u32[]{:S(2)}) %collective-permute-start.33) | collective-permute-done | bytes 393248 | tf_op jit(solution)/shard_map/ppermute | solution.py:236
  150.5 1.5 collective-permute-start.41
  155.4 6.6 %collective-permute-done.41.refs_12_ = bf16[2,32,3072]{2,1,0:T(8,128)(2,1)} collective-permute-done((bf16[2,32,3072]{2,1,0:T(8,128)(2,1)}, bf16[2,32,3072]{2,1,0:T(8,128)(2,1)}, u32[]{:S(2)}, u32[]{:S(2)}) %collective-permute-start.41) | collective-permute-done | bytes 393248 | tf_op jit(solution)/shard_map/ppermute | solution.py:236
  162.0 1.0 collective-permute-done.42.refs_13_
  163.6 6.1 %shard_map.101.de_in = f32[8192,3072]{1,0:T(8,128)} custom-call(f32[8192,3072]{1,0:T(8,128)} %get-tuple-element.69.de_in), custom_call_target="tpu_custom_call", output_to_operand_aliasing={{}: (0, {})} | custom-call | flops 10000000 | bytes 20000000 | tf_op jit(solution)/shard_map/pallas_call | solution.py:359
  169.8 8.6 %shard_map.102.refs_4_ = f32[8192,3072]{1,0:T(8,128)} custom-call(f32[8192,3072]{1,0:T(8,128)} %shard_map.101.de_in), custom_call_target="tpu_custom_call", output_to_operand_aliasing={{}: (0, {})} | custom-call | flops 10000000 | bytes 20000000 | tf_op jit(solution)/shard_map/pallas_call | solution.py:359
  178.4 3.6 %shard_map.103 = (bf16[3072,256]{1,0:T(8,128)(2,1)S(1)}, bf16[4,256,640]{2,1,0:T(8,128)(2,1)}, f32[8192,3072]{1,0:T(8,128)}) custom-call(s32[2]{0:T(128)S(1)} %pad_add_fusion.kc_ref, bf16[1,3072]{1,0:T(2,128)(2,1)S(1)} %reshape.79.g_ref, bf16[3072,640]{1,0:T(8,128)(2,1)S(1)} %copy-done.2, ...), custom_call_target="tpu_custom_call", output_to_operand_aliasing={{2}: (7, {})} | custom-call | flops 8000000 | bytes 12000000 | tf_op jit(solution)/shard_map/pallas_call | solution.py:386
  182.7 3.6 %shard_map.104 = (bf16[3072,256]{1,0:T(8,128)(2,1)S(1)}, bf16[4,256,640]{2,1,0:T(8,128)(2,1)}, f32[8192,3072]{1,0:T(8,128)}) custom-call(s32[2]{0:T(128)S(1)} %pad_add_fusion.kc_ref, bf16[1,3072]{1,0:T(2,128)(2,1)S(1)} %reshape.79.g_ref, bf16[3072,640]{1,0:T(8,128)(2,1)S(1)} %copy-done.2, ...), custom_call_target="tpu_custom_call", output_to_operand_aliasing={{1}: (7, {}), {2}: (8, {})} | custom-call | flops 8000000 | bytes 12000000 | tf_op jit(solution)/shard_map/pallas_call | solution.py:386
  186.4 3.8 %shard_map.105 = (bf16[3072,256]{1,0:T(8,128)(2,1)S(1)}, bf16[4,256,640]{2,1,0:T(8,128)(2,1)}, f32[8192,3072]{1,0:T(8,128)}) custom-call(s32[2]{0:T(128)S(1)} %pad_add_fusion.kc_ref, bf16[1,3072]{1,0:T(2,128)(2,1)S(1)} %reshape.79.g_ref, bf16[3072,640]{1,0:T(8,128)(2,1)S(1)} %copy-done.2, ...), custom_call_target="tpu_custom_call", output_to_operand_aliasing={{1}: (7, {}), {2}: (8, {})} | custom-call | flops 8000000 | bytes 12000000 | tf_op jit(solution)/shard_map/pallas_call | solution.py:386
  190.3 3.6 %shard_map.106 = (bf16[3072,256]{1,0:T(8,128)(2,1)S(1)}, bf16[4,256,640]{2,1,0:T(8,128)(2,1)}, f32[8192,3072]{1,0:T(8,128)}) custom-call(s32[2]{0:T(128)S(1)} %pad_add_fusion.kc_ref, bf16[1,3072]{1,0:T(2,128)(2,1)S(1)} %reshape.79.g_ref, bf16[3072,640]{1,0:T(8,128)(2,1)S(1)} %copy-done.2, ...), custom_call_target="tpu_custom_call", output_to_operand_aliasing={{1}: (7, {}), {2}: (8, {})} | custom-call | flops 8000000 | bytes 12000000 | tf_op jit(solution)/shard_map/pallas_call | solution.py:386
  194.0 8.3 %dw.1 = (f32[3072,640]{1,0:T(8,128)}, f32[8192,3072]{1,0:T(8,128)}) custom-call(s32[1]{0:T(128)} %bitcast.1.c_ref, bf16[4,256,640]{2,1,0:T(8,128)(2,1)S(1)} %copy-done.5, bf16[3072,256]{1,0:T(8,128)(2,1)S(1)} %get-tuple-element.88.refs_0_, bf16[3072,256]{1,0:T(8,128)(2,1)S(1)} %get-tuple-element.89.refs_1_, ...), custom_call_target="tpu_custom_call", output_to_operand_aliasing={{1}: (6, {})} | custom-call | flops 30000000 | bytes 40000000 | tf_op jit(solution)/shard_map/dw/pallas_call | solution.py:401
  202.4 7.4 %put.1 = f32[8192,3072]{1,0:T(8,128)} custom-call(s32[1]{0:T(128)} %bitcast.13.me_ref, s32[1024]{0:T(1024)S(1)} %get-tuple-element.77.rows_ref, s32[1]{0:T(128)} %bitcast.2.cnt_ref, s32[1,1024]{1,0:T(1,128)S(1)} %bitcast.24, bf16[2,32,3072]{2,1,0:T(8,128)(2,1)S(1)} %copy-done.9, bf16[2,32,3072]{2,1,0:T(8,128)(2,1)S(1)} %copy-done.7, ...), custom_call_target="tpu_custom_call", output_to_operand_aliasing={{}: (20, {})} | custom-call | tf_op jit(solution)/shard_map/put/pallas_call | solution.py:429
  (182 shorter events, 27.1 us)
Async XLA Ops:
  6.4 22.0 %collective-permute-start = (bf16[4,32,3072]{2,1,0:T(8,128)(2,1)}, bf16[4,32,3072]{2,1,0:T(8,128)(2,1)}, u32[]{:S(2)}, u32[]{:S(2)}) collective-permute-start(bf16[4,32,3072]{2,1,0:T(8,128)(2,1)} %get-tuple-element.50), channel_id=1, source_target_pairs={{0,2},{1,3},{2,0},{3,1},{4,6},{5,7},{6,4},{7,5}} | collective-permute-start | bytes 2359304 | tf_op jit(solution)/shard_map/ppermute | solution.py:236
  9.7 20.7 %collective-permute-start.1 = (bf16[4,32,3072]{2,1,0:T(8,128)(2,1)}, bf16[4,32,3072]{2,1,0:T(8,128)(2,1)}, u32[]{:S(2)}, u32[]{:S(2)}) collective-permute-start(bf16[4,32,3072]{2,1,0:T(8,128)(2,1)} %get-tuple-element.51), channel_id=1, source_target_pairs={{0,4},{1,5},{2,6},{3,7},{4,0},{5,1},{6,2},{7,3}} | collective-permute-start | bytes 2359304 | tf_op jit(solution)/shard_map/ppermute | solution.py:236
  17.9 47.2 %collective-permute-start.24 = (bf16[4,32,3072]{2,1,0:T(8,128)(2,1)}, bf16[4,32,3072]{2,1,0:T(8,128)(2,1)S(1)}, u32[]{:S(2)}, u32[]{:S(2)}) collective-permute-start(bf16[4,32,3072]{2,1,0:T(8,128)(2,1)} %get-tuple-element.81), channel_id=1, source_target_pairs={{0,2},{1,3},{2,0},{3,1},{4,6},{5,7},{6,4},{7,5}} | collective-permute-start | bytes 2359304 | tf_op jit(solution)/shard_map/ppermute | solution.py:236
  18.5 48.2 %collective-permute-start.27 = (bf16[4,32,3072]{2,1,0:T(8,128)(2,1)}, bf16[4,32,3072]{2,1,0:T(8,128)(2,1)}, u32[]{:S(2)}, u32[]{:S(2)}) collective-permute-start(bf16[4,32,3072]{2,1,0:T(8,128)(2,1)} %get-tuple-element.85), channel_id=1, source_target_pairs={{0,4},{1,5},{2,6},{3,7},{4,0},{5,1},{6,2},{7,3}} | collective-permute-start | bytes 2359304 | tf_op jit(solution)/shard_map/ppermute | solution.py:236
  44.6 4.9 %collective-permute-start.5 = (bf16[1,4,64,1536]{3,2,1,0:T(8,128)(2,1)S(1)}, bf16[1,4,64,1536]{3,2,1,0:T(8,128)(2,1)S(1)}, u32[]{:S(2)}, u32[]{:S(2)}) collective-permute-start(bf16[1,4,64,1536]{3,2,1,0:T(8,128)(2,1)S(1)} %get-tuple-element.61), channel_id=1, source_target_pairs={{0,1},{1,0},{2,3},{3,2},{4,5},{5,4},{6,7},{7,6}} | collective-permute-start | bytes 2359304 | tf_op jit(solution)/shard_map/ppermute | solution.py:236
  44.6 8.6 %collective-permute-start.2 = (bf16[3,4,64,1536]{3,2,1,0:T(8,128)(2,1)S(1)}, bf16[3,4,64,1536]{3,2,1,0:T(8,128)(2,1)S(1)}, u32[]{:S(2)}, u32[]{:S(2)}) collective-permute-start(bf16[3,4,64,1536]{3,2,1,0:T(8,128)(2,1)S(1)} %get-tuple-element.57), channel_id=1, source_target_pairs={{0,1},{1,0},{2,3},{3,2},{4,5},{5,4},{6,7},{7,6}} | collective-permute-start | bytes 7077896 | tf_op jit(solution)/shard_map/ppermute | solution.py:236
  46.9 4.5 %collective-permute-start.25 = (f32[4,32,1536]{2,1,0:T(8,128)S(1)}, f32[4,32,1536]{2,1,0:T(8,128)S(1)}, u32[]{:S(2)}, u32[]{:S(2)}) collective-permute-start(f32[4,32,1536]{2,1,0:T(8,128)S(1)} %slice_select_fusion.1), channel_id=1, source_target_pairs={{0,1},{1,0},{2,3},{3,2},{4,5},{5,4},{6,7},{7,6}} | collective-permute-start | bytes 2359304 | tf_op jit(solution)/shard_map/ppermute | solution.py:236
  49.5 3.1 %collective-permute-start.28 = (f32[4,32,1536]{2,1,0:T(8,128)S(1)}, f32[4,32,1536]{2,1,0:T(8,128)S(1)}, u32[]{:S(2)}, u32[]{:S(2)}) collective-permute-start(f32[4,32,1536]{2,1,0:T(8,128)S(1)} %slice_select_fusion), channel_id=1, source_target_pairs={{0,1},{1,0},{2,3},{3,2},{4,5},{5,4},{6,7},{7,6}} | collective-permute-start | bytes 2359304 | tf_op jit(solution)/shard_map/ppermute | solution.py:236
  51.4 11.2 %collective-permute-start.6 = (bf16[4,32,1536]{2,1,0:T(8,128)(2,1)S(1)}, bf16[4,32,1536]{2,1,0:T(8,128)(2,1)S(1)}, u32[]{:S(2)}, u32[]{:S(2)}) collective-permute-start(bf16[4,32,1536]{2,1,0:T(8,128)(2,1)S(1)} %get-tuple-element.117), channel_id=1, source_target_pairs={{0,2},{1,3},{2,0},{3,1},{4,6},{5,7},{6,4},{7,5}} | collective-permute-start | bytes 1179656 | tf_op jit(solution)/shard_map/ppermute | solution.py:236
  52.5 12.0 %collective-permute-start.11 = (bf16[4,32,1536]{2,1,0:T(8,128)(2,1)S(1)}, bf16[4,32,1536]{2,1,0:T(8,128)(2,1)S(1)}, u32[]{:S(2)}, u32[]{:S(2)}) collective-permute-start(bf16[4,32,1536]{2,1,0:T(8,128)(2,1)S(1)} %get-tuple-element.118), channel_id=1, source_target_pairs={{0,4},{1,5},{2,6},{3,7},{4,0},{5,1},{6,2},{7,3}} | collective-permute-start | bytes 1179656 | tf_op jit(solution)/shard_map/ppermute | solution.py:236
  53.2 28.1 %collective-permute-start.26 = (f32[4,32,1536]{2,1,0:T(8,128)S(1)}, f32[4,32,1536]{2,1,0:T(8,128)S(1)}, u32[]{:S(2)}, u32[]{:S(2)}) collective-permute-start(f32[4,32,1536]{2,1,0:T(8,128)S(1)} %select_add_fusion.4), channel_id=1, source_target_pairs={{0,4},{1,5},{2,6},{3,7},{4,0},{5,1},{6,2},{7,3}} | collective-permute-start | bytes 2359304 | tf_op jit(solution)/shard_map/ppermute | solution.py:236
  62.5 20.4 %collective-permute-start.29 = (f32[4,32,1536]{2,1,0:T(8,128)S(1)}, f32[4,32,1536]{2,1,0:T(8,128)S(1)}, u32[]{:S(2)}, u32[]{:S(2)}) collective-permute-start(f32[4,32,1536]{2,1,0:T(8,128)S(1)} %select_add_fusion.3), channel_id=1, source_target_pairs={{0,2},{1,3},{2,0},{3,1},{4,6},{5,7},{6,4},{7,5}} | collective-permute-start | bytes 2359304 | tf_op jit(solution)/shard_map/ppermute | solution.py:236
  64.5 32.9 %collective-permute-start.7 = (bf16[4,32,1536]{2,1,0:T(8,128)(2,1)S(1)}, bf16[4,32,1536]{2,1,0:T(8,128)(2,1)S(1)}, u32[]{:S(2)}, u32[]{:S(2)}) collective-permute-start(bf16[4,32,1536]{2,1,0:T(8,128)(2,1)S(1)} %add_add_fusion.2), channel_id=1, source_target_pairs={{0,4},{1,5},{2,6},{3,7},{4,0},{5,1},{6,2},{7,3}} | collective-permute-start | bytes 1179656 | tf_op jit(solution)/shard_map/ppermute | solution.py:236
  65.2 32.2 %collective-permute-start.4 = (bf16[4,32,1536]{2,1,0:T(8,128)(2,1)S(1)}, bf16[4,32,1536]{2,1,0:T(8,128)(2,1)S(1)}, u32[]{:S(2)}, u32[]{:S(2)}) collective-permute-start(bf16[4,32,1536]{2,1,0:T(8,128)(2,1)S(1)} %slice_add_fusion.2), channel_id=1, source_target_pairs={{0,4},{1,5},{2,6},{3,7},{4,0},{5,1},{6,2},{7,3}} | collective-permute-start | bytes 1179656 | tf_op jit(solution)/shard_map/ppermute | solution.py:236
  66.7 30.7 %collective-permute-start.3 = (bf16[4,32,1536]{2,1,0:T(8,128)(2,1)S(1)}, bf16[4,32,1536]{2,1,0:T(8,128)(2,1)S(1)}, u32[]{:S(2)}, u32[]{:S(2)}) collective-permute-start(bf16[4,32,1536]{2,1,0:T(8,128)(2,1)S(1)} %slice_add_fusion.3), channel_id=1, source_target_pairs={{0,2},{1,3},{2,0},{3,1},{4,6},{5,7},{6,4},{7,5}} | collective-permute-start | bytes 1179656 | tf_op jit(solution)/shard_map/ppermute | solution.py:236
  81.3 16.8 %collective-permute-start.12 = (bf16[4,32,1536]{2,1,0:T(8,128)(2,1)S(1)}, bf16[4,32,1536]{2,1,0:T(8,128)(2,1)S(1)}, u32[]{:S(2)}, u32[]{:S(2)}) collective-permute-start(bf16[4,32,1536]{2,1,0:T(8,128)(2,1)S(1)} %add_add_fusion), channel_id=1, source_target_pairs={{0,2},{1,3},{2,0},{3,1},{4,6},{5,7},{6,4},{7,5}} | collective-permute-start | bytes 1179656 | tf_op jit(solution)/shard_map/ppermute | solution.py:236
  84.8 18.5 %collective-permute-start.30 = (f32[4,32,3072]{2,1,0:T(8,128)S(1)}, f32[4,32,3072]{2,1,0:T(8,128)S(1)}, u32[]{:S(2)}, u32[]{:S(2)}) collective-permute-start(f32[4,32,3072]{2,1,0:T(8,128)S(1)} %broadcast_select_fusion), channel_id=1, source_target_pairs={{0,1},{1,0},{2,3},{3,2},{4,5},{5,4},{6,7},{7,6}} | collective-permute-start | bytes 4718600 | tf_op jit(solution)/shard_map/ppermute | solution.py:236
  98.3 2.6 %collective-permute-start.22 = (bf16[4,32,1536]{2,1,0:T(8,128)(2,1)S(1)}, bf16[4,32,1536]{2,1,0:T(8,128)(2,1)S(1)}, u32[]{:S(2)}, u32[]{:S(2)}) collective-permute-start(bf16[4,32,1536]{2,1,0:T(8,128)(2,1)S(1)} %get-tuple-element.106.refs_0_), channel_id=1, source_target_pairs={{0,1},{1,0},{2,3},{3,2},{4,5},{5,4},{6,7},{7,6}} | collective-permute-start | bytes 1179656 | tf_op jit(solution)/shard_map/ppermute | solution.py:236
  98.3 3.1 %collective-permute-start.23 = (bf16[4,32,1536]{2,1,0:T(8,128)(2,1)S(1)}, bf16[4,32,1536]{2,1,0:T(8,128)(2,1)S(1)}, u32[]{:S(2)}, u32[]{:S(2)}) collective-permute-start(bf16[4,32,1536]{2,1,0:T(8,128)(2,1)S(1)} %get-tuple-element.105.refs_2_), channel_id=1, source_target_pairs={{0,1},{1,0},{2,3},{3,2},{4,5},{5,4},{6,7},{7,6}} | collective-permute-start | bytes 1179656 | tf_op jit(solution)/shard_map/ppermute | solution.py:236
  98.9 12.0 %collective-permute-start.19 = (bf16[4,32,1536]{2,1,0:T(8,128)(2,1)S(1)}, bf16[4,32,1536]{2,1,0:T(8,128)(2,1)S(1)}, u32[]{:S(2)}, u32[]{:S(2)}) collective-permute-start(bf16[4,32,1536]{2,1,0:T(8,128)(2,1)S(1)} %get-tuple-element.106.refs_0_), channel_id=1, source_target_pairs={{0,2},{1,3},{2,0},{3,1},{4,6},{5,7},{6,4},{7,5}} | collective-permute-start | bytes 1179656 | tf_op jit(solution)/shard_map/ppermute | solution.py:236
  99.4 19.1 %collective-permute-start.13 = (bf16[4,32,1536]{2,1,0:T(8,128)(2,1)S(1)}, bf16[4,32,1536]{2,1,0:T(8,128)(2,1)S(1)}, u32[]{:S(2)}, u32[]{:S(2)}) collective-permute-start(bf16[4,32,1536]{2,1,0:T(8,128)(2,1)S(1)} %get-tuple-element.105.refs_2_), channel_id=1, source_target_pairs={{0,2},{1,3},{2,0},{3,1},{4,6},{5,7},{6,4},{7,5}} | collective-permute-start | bytes 1179656 | tf_op jit(solution)/shard_map/ppermute | solution.py:236
  100.9 18.4 %collective-permute-start.8 = (bf16[4,32,1536]{2,1,0:T(8,128)(2,1)S(1)}, bf16[4,32,1536]{2,1,0:T(8,128)(2,1)S(1)}, u32[]{:S(2)}, u32[]{:S(2)}) collective-permute-start(bf16[4,32,1536]{2,1,0:T(8,128)(2,1)S(1)} %get-tuple-element.106.refs_0_), channel_id=1, source_target_pairs={{0,4},{1,5},{2,6},{3,7},{4,0},{5,1},{6,2},{7,3}} | collective-permute-start | bytes 1179656 | tf_op jit(solution)/shard_map/ppermute | solution.py:236
  101.5 18.4 %collective-permute-start.17 = (bf16[4,32,1536]{2,1,0:T(8,128)(2,1)S(1)}, bf16[4,32,1536]{2,1,0:T(8,128)(2,1)S(1)}, u32[]{:S(2)}, u32[]{:S(2)}) collective-permute-start(bf16[4,32,1536]{2,1,0:T(8,128)(2,1)S(1)} %get-tuple-element.105.refs_2_), channel_id=1, source_target_pairs={{0,4},{1,5},{2,6},{3,7},{4,0},{5,1},{6,2},{7,3}} | collective-permute-start | bytes 1179656 | tf_op jit(solution)/shard_map/ppermute | solution.py:236
  105.9 1.2 collective-permute-start.45
  107.1 11.5 %collective-permute-start.46 = (f32[3072]{0:T(1024)S(1)}, f32[3072]{0:T(1024)S(1)}, u32[]{:S(2)}, u32[]{:S(2)}) collective-permute-start(f32[3072]{0:T(1024)S(1)} %add.138), channel_id=1, source_target_pairs={{0,2},{1,3},{2,0},{3,1},{4,6},{5,7},{6,4},{7,5}} | collective-permute-start | bytes 36872 | tf_op jit(solution)/shard_map/ppermute | solution.py:236
  110.8 12.8 %collective-permute-start.20 = (bf16[4,32,1536]{2,1,0:T(8,128)(2,1)S(1)}, bf16[4,32,1536]{2,1,0:T(8,128)(2,1)S(1)}, u32[]{:S(2)}, u32[]{:S(2)}) collective-permute-start(bf16[4,32,1536]{2,1,0:T(8,128)(2,1)S(1)} %collective-permute-done.19.refs_0_), channel_id=1, source_target_pairs={{0,1},{1,0},{2,3},{3,2},{4,5},{5,4},{6,7},{7,6}} | collective-permute-start | bytes 1179656 | tf_op jit(solution)/shard_map/ppermute | solution.py:236
  118.5 5.6 %collective-permute-start.21 = (bf16[4,32,1536]{2,1,0:T(8,128)(2,1)S(1)}, bf16[4,32,1536]{2,1,0:T(8,128)(2,1)S(1)}, u32[]{:S(2)}, u32[]{:S(2)}) collective-permute-start(bf16[4,32,1536]{2,1,0:T(8,128)(2,1)S(1)} %collective-permute-done.13.refs_2_), channel_id=1, source_target_pairs={{0,1},{1,0},{2,3},{3,2},{4,5},{5,4},{6,7},{7,6}} | collective-permute-start | bytes 1179656 | tf_op jit(solution)/shard_map/ppermute | solution.py:236
  118.6 3.7 %collective-permute-start.47 = (f32[3072]{0:T(1024)S(1)}, f32[3072]{0:T(1024)S(1)}, u32[]{:S(2)}, u32[]{:S(2)}) collective-permute-start(f32[3072]{0:T(1024)S(1)} %add.139), channel_id=1, source_target_pairs={{0,4},{1,5},{2,6},{3,7},{4,0},{5,1},{6,2},{7,3}} | collective-permute-start | bytes 36872 | tf_op jit(solution)/shard_map/ppermute | solution.py:236
  119.3 6.4 %collective-permute-start.16 = (bf16[4,32,1536]{2,1,0:T(8,128)(2,1)S(1)}, bf16[4,32,1536]{2,1,0:T(8,128)(2,1)S(1)}, u32[]{:S(2)}, u32[]{:S(2)}) collective-permute-start(bf16[4,32,1536]{2,1,0:T(8,128)(2,1)S(1)} %collective-permute-done.8.refs_0_), channel_id=1, source_target_pairs={{0,1},{1,0},{2,3},{3,2},{4,5},{5,4},{6,7},{7,6}} | collective-permute-start | bytes 1179656 | tf_op jit(solution)/shard_map/ppermute | solution.py:236
  119.8 8.0 %collective-permute-start.18 = (bf16[4,32,1536]{2,1,0:T(8,128)(2,1)S(1)}, bf16[4,32,1536]{2,1,0:T(8,128)(2,1)S(1)}, u32[]{:S(2)}, u32[]{:S(2)}) collective-permute-start(bf16[4,32,1536]{2,1,0:T(8,128)(2,1)S(1)} %collective-permute-done.17.refs_2_), channel_id=1, source_target_pairs={{0,1},{1,0},{2,3},{3,2},{4,5},{5,4},{6,7},{7,6}} | collective-permute-start | bytes 1179656 | tf_op jit(solution)/shard_map/ppermute | solution.py:236
  122.3 12.0 %collective-permute-start.9 = (bf16[4,32,1536]{2,1,0:T(8,128)(2,1)S(1)}, bf16[4,32,1536]{2,1,0:T(8,128)(2,1)S(1)}, u32[]{:S(2)}, u32[]{:S(2)}) collective-permute-start(bf16[4,32,1536]{2,1,0:T(8,128)(2,1)S(1)} %collective-permute-done.8.refs_0_), channel_id=1, source_target_pairs={{0,2},{1,3},{2,0},{3,1},{4,6},{5,7},{6,4},{7,5}} | collective-permute-start | bytes 1179656 | tf_op jit(solution)/shard_map/ppermute | solution.py:236
  123.6 12.0 %collective-permute-start.14 = (bf16[4,32,1536]{2,1,0:T(8,128)(2,1)S(1)}, bf16[4,32,1536]{2,1,0:T(8,128)(2,1)S(1)}, u32[]{:S(2)}, u32[]{:S(2)}) collective-permute-start(bf16[4,32,1536]{2,1,0:T(8,128)(2,1)S(1)} %collective-permute-done.13.refs_2_), channel_id=1, source_target_pairs={{0,4},{1,5},{2,6},{3,7},{4,0},{5,1},{6,2},{7,3}} | collective-permute-start | bytes 1179656 | tf_op jit(solution)/shard_map/ppermute | solution.py:236
  124.1 20.1 %collective-permute-start.37 = (bf16[2,32,3072]{2,1,0:T(8,128)(2,1)S(1)}, bf16[2,32,3072]{2,1,0:T(8,128)(2,1)}, u32[]{:S(2)}, u32[]{:S(2)}) collective-permute-start(bf16[2,32,3072]{2,1,0:T(8,128)(2,1)S(1)} %get-tuple-element.120.refs_0_), channel_id=1, source_target_pairs={{0,4},{1,5},{2,6},{3,7},{4,0},{5,1},{6,2},{7,3}} | collective-permute-start | bytes 1179656 | tf_op jit(solution)/shard_map/ppermute | solution.py:236
  126.4 17.8 %collective-permute-start.34 = (bf16[2,32,3072]{2,1,0:T(8,128)(2,1)S(1)}, bf16[2,32,3072]{2,1,0:T(8,128)(2,1)}, u32[]{:S(2)}, u32[]{:S(2)}) collective-permute-start(bf16[2,32,3072]{2,1,0:T(8,128)(2,1)S(1)} %get-tuple-element.119.refs_1_), channel_id=1, source_target_pairs={{0,2},{1,3},{2,0},{3,1},{4,6},{5,7},{6,4},{7,5}} | collective-permute-start | bytes 1179656 | tf_op jit(solution)/shard_map/ppermute | solution.py:236
  128.6 20.8 %collective-permute-start.33 = (bf16[2,32,3072]{2,1,0:T(8,128)(2,1)S(1)}, bf16[2,32,3072]{2,1,0:T(8,128)(2,1)S(1)}, u32[]{:S(2)}, u32[]{:S(2)}) collective-permute-start(bf16[2,32,3072]{2,1,0:T(8,128)(2,1)S(1)} %get-tuple-element.120.refs_0_), channel_id=1, source_target_pairs={{0,2},{1,3},{2,0},{3,1},{4,6},{5,7},{6,4},{7,5}} | collective-permute-start | bytes 1179656 | tf_op jit(solution)/shard_map/ppermute | solution.py:236
  134.3 16.2 %collective-permute-start.38 = (bf16[2,32,3072]{2,1,0:T(8,128)(2,1)S(1)}, bf16[2,32,3072]{2,1,0:T(8,128)(2,1)}, u32[]{:S(2)}, u32[]{:S(2)}) collective-permute-start(bf16[2,32,3072]{2,1,0:T(8,128)(2,1)S(1)} %get-tuple-element.119.refs_1_), channel_id=1, source_target_pairs={{0,4},{1,5},{2,6},{3,7},{4,0},{5,1},{6,2},{7,3}} | collective-permute-start | bytes 1179656 | tf_op jit(solution)/shard_map/ppermute | solution.py:236
  135.6 16.4 %collective-permute-start.31 = (bf16[2,32,3072]{2,1,0:T(8,128)(2,1)S(1)}, bf16[2,32,3072]{2,1,0:T(8,128)(2,1)S(1)}, u32[]{:S(2)}, u32[]{:S(2)}) collective-permute-start(bf16[2,32,3072]{2,1,0:T(8,128)(2,1)S(1)} %get-tuple-element.120.refs_0_), channel_id=1, source_target_pairs={{0,1},{1,0},{2,3},{3,2},{4,5},{5,4},{6,7},{7,6}} | collective-permute-start | bytes 1179656 | tf_op jit(solution)/shard_map/ppermute | solution.py:236
  144.1 9.2 %collective-permute-start.32 = (bf16[2,32,3072]{2,1,0:T(8,128)(2,1)S(1)}, bf16[2,32,3072]{2,1,0:T(8,128)(2,1)S(1)}, u32[]{:S(2)}, u32[]{:S(2)}) collective-permute-start(bf16[2,32,3072]{2,1,0:T(8,128)(2,1)S(1)} %get-tuple-element.119.refs_1_), channel_id=1, source_target_pairs={{0,1},{1,0},{2,3},{3,2},{4,5},{5,4},{6,7},{7,6}} | collective-permute-start | bytes 1179656 | tf_op jit(solution)/shard_map/ppermute | solution.py:236
  144.1 10.7 %collective-permute-start.10 = (bf16[4,32,1536]{2,1,0:T(8,128)(2,1)S(1)}, bf16[4,32,1536]{2,1,0:T(8,128)(2,1)S(1)}, u32[]{:S(2)}, u32[]{:S(2)}) collective-permute-start(bf16[4,32,1536]{2,1,0:T(8,128)(2,1)S(1)} %collective-permute-done.9.refs_0_), channel_id=1, source_target_pairs={{0,1},{1,0},{2,3},{3,2},{4,5},{5,4},{6,7},{7,6}} | collective-permute-start | bytes 1179656 | tf_op jit(solution)/shard_map/ppermute | solution.py:236
  149.4 6.0 %collective-permute-start.15 = (bf16[4,32,1536]{2,1,0:T(8,128)(2,1)S(1)}, bf16[4,32,1536]{2,1,0:T(8,128)(2,1)S(1)}, u32[]{:S(2)}, u32[]{:S(2)}) collective-permute-start(bf16[4,32,1536]{2,1,0:T(8,128)(2,1)S(1)} %collective-permute-done.14.refs_2_), channel_id=1, source_target_pairs={{0,1},{1,0},{2,3},{3,2},{4,5},{5,4},{6,7},{7,6}} | collective-permute-start | bytes 1179656 | tf_op jit(solution)/shard_map/ppermute | solution.py:236
  150.5 11.5 %collective-permute-start.41 = (bf16[2,32,3072]{2,1,0:T(8,128)(2,1)}, bf16[2,32,3072]{2,1,0:T(8,128)(2,1)}, u32[]{:S(2)}, u32[]{:S(2)}) collective-permute-start(bf16[2,32,3072]{2,1,0:T(8,128)(2,1)} %collective-permute-done.37.refs_8_), channel_id=1, source_target_pairs={{0,2},{1,3},{2,0},{3,1},{4,6},{5,7},{6,4},{7,5}} | collective-permute-start | bytes 1179656 | tf_op jit(solution)/shard_map/ppermute | solution.py:236
  152.7 10.3 %collective-permute-start.42 = (bf16[2,32,3072]{2,1,0:T(8,128)(2,1)}, bf16[2,32,3072]{2,1,0:T(8,128)(2,1)}, u32[]{:S(2)}, u32[]{:S(2)}) collective-permute-start(bf16[2,32,3072]{2,1,0:T(8,128)(2,1)} %collective-permute-done.34.refs_5_), channel_id=1, source_target_pairs={{0,4},{1,5},{2,6},{3,7},{4,0},{5,1},{6,2},{7,3}} | collective-permute-start | bytes 1179656 | tf_op jit(solution)/shard_map/ppermute | solution.py:236
  154.1 9.0 %collective-permute-start.35 = (bf16[2,32,3072]{2,1,0:T(8,128)(2,1)S(1)}, bf16[2,32,3072]{2,1,0:T(8,128)(2,1)S(1)}, u32[]{:S(2)}, u32[]{:S(2)}) collective-permute-start(bf16[2,32,3072]{2,1,0:T(8,128)(2,1)S(1)} %collective-permute-done.33.refs_4_), channel_id=1, source_target_pairs={{0,1},{1,0},{2,3},{3,2},{4,5},{5,4},{6,7},{7,6}} | collective-permute-start | bytes 1179656 | tf_op jit(solution)/shard_map/ppermute | solution.py:236
  154.9 47.5 %collective-permute-start.36 = (bf16[2,32,3072]{2,1,0:T(8,128)(2,1)}, bf16[2,32,3072]{2,1,0:T(8,128)(2,1)}, u32[]{:S(2)}, u32[]{:S(2)}) collective-permute-start(bf16[2,32,3072]{2,1,0:T(8,128)(2,1)} %collective-permute-done.34.refs_5_), channel_id=1, source_target_pairs={{0,1},{1,0},{2,3},{3,2},{4,5},{5,4},{6,7},{7,6}} | collective-permute-start | bytes 1179656 | tf_op jit(solution)/shard_map/ppermute | solution.py:236
  155.4 47.0 %collective-permute-start.39 = (bf16[2,32,3072]{2,1,0:T(8,128)(2,1)}, bf16[2,32,3072]{2,1,0:T(8,128)(2,1)}, u32[]{:S(2)}, u32[]{:S(2)}) collective-permute-start(bf16[2,32,3072]{2,1,0:T(8,128)(2,1)} %collective-permute-done.37.refs_8_), channel_id=1, source_target_pairs={{0,1},{1,0},{2,3},{3,2},{4,5},{5,4},{6,7},{7,6}} | collective-permute-start | bytes 1179656 | tf_op jit(solution)/shard_map/ppermute | solution.py:236
  162.0 40.3 %collective-permute-start.40 = (bf16[2,32,3072]{2,1,0:T(8,128)(2,1)}, bf16[2,32,3072]{2,1,0:T(8,128)(2,1)}, u32[]{:S(2)}, u32[]{:S(2)}) collective-permute-start(bf16[2,32,3072]{2,1,0:T(8,128)(2,1)} %collective-permute-done.38.refs_9_), channel_id=1, source_target_pairs={{0,1},{1,0},{2,3},{3,2},{4,5},{5,4},{6,7},{7,6}} | collective-permute-start | bytes 1179656 | tf_op jit(solution)/shard_map/ppermute | solution.py:236
  163.0 39.3 %collective-permute-start.43 = (bf16[2,32,3072]{2,1,0:T(8,128)(2,1)}, bf16[2,32,3072]{2,1,0:T(8,128)(2,1)}, u32[]{:S(2)}, u32[]{:S(2)}) collective-permute-start(bf16[2,32,3072]{2,1,0:T(8,128)(2,1)} %collective-permute-done.41.refs_12_), channel_id=1, source_target_pairs={{0,1},{1,0},{2,3},{3,2},{4,5},{5,4},{6,7},{7,6}} | collective-permute-start | bytes 1179656 | tf_op jit(solution)/shard_map/ppermute | solution.py:236
  163.1 39.3 %collective-permute-start.44 = (bf16[2,32,3072]{2,1,0:T(8,128)(2,1)}, bf16[2,32,3072]{2,1,0:T(8,128)(2,1)}, u32[]{:S(2)}, u32[]{:S(2)}) collective-permute-start(bf16[2,32,3072]{2,1,0:T(8,128)(2,1)} %collective-permute-done.42.refs_13_), channel_id=1, source_target_pairs={{0,1},{1,0},{2,3},{3,2},{4,5},{5,4},{6,7},{7,6}} | collective-permute-start | bytes 1179656 | tf_op jit(solution)/shard_map/ppermute | solution.py:236
  (42 other events, 267.8 us)

commit v6 on v5

--- a/solution.py
+++ b/solution.py
@@ -13,8 +13,9 @@
 SMEM = pl.BlockSpec(memory_space=pltpu.SMEM)
 HBM = pl.BlockSpec(memory_space=pltpu.HBM)
 ZR = 128
+CUT = 3
 BLK = 256
-LOOKUP_EARLY, LOOKUP_SHARE, ZERO_A, ZERO_B, NORM_SHARE = 8, 22, 33, 48, 3
+LOOKUP_EARLY, LOOKUP_SHARE, ZERO_A, ZERO_B, NORM_SHARE = 8, 22, 34, 52, 3
 
 
 def zero_fill(de, z, sem, first, last):
@@ -40,16 +41,18 @@
     wait()
 
 
-def pdn_first_kernel(j, c_ref, du_hbm, w_hbm, h0, h1, du_ref, w_ref, sem, wsem):
+def pdn_first_kernel(j, col0, c_ref, du_hbm, w_hbm, h0, h1, du_ref, w_ref, sem, wsem):
     c = c_ref[0]
     mb, tc, _ = du_ref.shape
     tl = tc // 2
     wc = 512
-    steps = w_hbm.shape[0] // wc
+    steps = w_ref.shape[0] // wc
     z = pl.multiple_of(jnp.bitwise_xor(c, j) * tc, tc)
     rows_in = pltpu.make_async_copy(du_hbm.at[:, pl.ds(z, tc), :], du_ref, sem)
     rows_in.start()
-    loads = [pltpu.make_async_copy(w_hbm.at[pl.ds(n * wc, wc)], w_ref.at[pl.ds(n * wc, wc)], wsem.at[n]) for n in range(steps)]
+    loads = [
+        pltpu.make_async_copy(w_hbm.at[pl.ds(col0 + n * wc, wc)], w_ref.at[pl.ds(n * wc, wc)], wsem.at[n]) for n in range(steps)
+    ]
     for cp in loads:
         cp.start()
     rows_in.wait()
@@ -167,12 +170,10 @@
 
 
 def dw_kernel(c_ref, du_ref, *refs):
-    ns, (dw, de, right, stage, sem, z, zsem) = refs[:4], refs[-7:]
+    ns, (dw, right, stage, sem) = refs[:4], refs[-4:]
     mb, _, _ = du_ref.shape
     d, kj = ns[0].shape
     tc = kj // mb
-    start, wait = zero_fill(de, z, zsem, ZERO_B + 4 * NORM_SHARE, de.shape[0] // ZR)
-    start()
     for j in range(4):
         rows = pl.ds(pl.multiple_of(jnp.bitwise_xor(c_ref[0], j) * tc, tc), tc)
         for m in range(mb):
@@ -197,36 +198,41 @@
 
     for q in range(2):
         copy(d // dc - 2 + q, q).wait()
-    wait()
-
-
-def scatter_kernel(me_ref, rows_ref, cnt_ref, slot_ref, *refs):
-    blocks, (de, buf, stage, out_sem) = refs[:16], refs[-4:]
-    mb, t, d = buf.shape
-    hb, tl = blocks[0].shape[:2]
-    for i, b in enumerate(blocks):
-        at = pl.ds(pl.multiple_of(jnp.bitwise_xor(me_ref[0], i // 2) * tl, tl), tl)
-        for m in range(hb):
-            buf[(i % 2) * hb + m, at, :] = b[m]
+
+
+def scatter_kernel(rows_ref, cnt_ref, slot_ref, *refs):
+    blocks, (de, stage, out_sem) = refs[:16], refs[-3:]
+    hb, tl, d = blocks[0].shape
+    kb = hb * tl
     cnt = cnt_ref[0]
     cc = 512
 
-    def copy(q, r):
-        return pltpu.make_async_copy(stage.at[pl.ds(q, 1)], de.at[pl.ds(r, 1)], out_sem)
+    def copy(q, r, size=1):
+        return pltpu.make_async_copy(stage.at[pl.ds(q, size)], de.at[pl.ds(r, size)], out_sem)
 
     @pl.loop(0, (cnt + BLK - 1) // BLK)
     def _(b):
         base = b * BLK
-        ids = lax.broadcasted_iota(jnp.int32, (BLK, mb * t), 0) + base
+        ids = lax.broadcasted_iota(jnp.int32, (BLK, len(blocks) * kb), 0) + base
         oh = (ids == slot_ref[...]).astype(jnp.bfloat16)
         for i in range(d // cc):
-            acc = jnp.zeros((BLK, cc), jnp.float32)
-            for m in range(mb):
-                acc += jnp.dot(oh[:, m * t:(m + 1) * t], buf[m, :, i * cc:(i + 1) * cc], preferred_element_type=jnp.float32)
-            stage[:, i * cc:(i + 1) * cc] = acc
+            cols = slice(i * cc, (i + 1) * cc)
+            right = jnp.concatenate([v[:, :, cols].reshape(kb, cc) for v in blocks], axis=0)
+            stage[:, cols] = jnp.dot(oh, right, preferred_element_type=jnp.float32)
         n = jnp.minimum(cnt - base, BLK)
-        pl.loop(0, n)(lambda q: copy(q, rows_ref[base + q]).start())
-        pl.loop(0, n)(lambda q: copy(q, rows_ref[base + q]).wait())
+        full = n // 8
+
+        @pl.loop(0, full)
+        def _(i):
+            for u in range(8):
+                copy(i * 8 + u, rows_ref[base + i * 8 + u]).start()
+
+        pl.loop(full * 8, n)(lambda q: copy(q, rows_ref[base + q]).start())
+        for bit in range(9):
+
+            @pl.when((n >> bit) & 1 == 1)
+            def _():
+                copy(0, 0, 1 << bit).wait()
 
 
 def solution(mesh):
@@ -245,7 +251,6 @@
         tc = t // 4
         k, c = r & 1, r >> 1
         gf = g.astype(jnp.float32)
-        me = r.reshape(1)
         kc = jnp.stack([k, c]).astype(jnp.int32)
         de_shape = jax.ShapeDtypeStruct((vl, d), jnp.float32)
         zero_scratch = [pltpu.VMEM((ZR, d), jnp.float32), pltpu.SemaphoreType.DMA]
@@ -303,35 +308,46 @@
         n = flat.shape[0]
         loc = flat - r * vl
         own = (loc >= 0) & (loc < vl)
-        part = {3: pl.pallas_call(
-            functools.partial(pdn_first_kernel, 3),
-            out_shape=(jax.ShapeDtypeStruct((mb, tl, d), jnp.bfloat16),) * 2,
-            in_specs=[SMEM, HBM, HBM],
-            out_specs=(VMEM, VMEM),
-            scratch_shapes=[
-                pltpu.VMEM((mb, tc, f), jnp.bfloat16),
-                pltpu.VMEM((d, f), jnp.bfloat16),
-                pltpu.SemaphoreType.DMA,
-                pltpu.SemaphoreType.DMA((6,)),
-            ],
-            cost_estimate=pl.CostEstimate(flops=5_000_000, bytes_accessed=8_000_000, transcendentals=0),
-            compiler_params=pltpu.CompilerParams(vmem_limit_bytes=60 * 2**20),
-            name="pa",
-        )(c.reshape(1), du, w)}
+        diag = []
+        for q in range(2):
+            diag.append(pl.pallas_call(
+                functools.partial(pdn_first_kernel, 3, q * hd),
+                out_shape=(jax.ShapeDtypeStruct((mb, tl, hd), jnp.bfloat16),) * 2,
+                in_specs=[SMEM, HBM, HBM],
+                out_specs=(VMEM, VMEM),
+                scratch_shapes=[
+                    pltpu.VMEM((mb, tc, f), jnp.bfloat16),
+                    pltpu.VMEM((hd, f), jnp.bfloat16),
+                    pltpu.SemaphoreType.DMA,
+                    pltpu.SemaphoreType.DMA((3,)),
+                ],
+                cost_estimate=pl.CostEstimate(flops=3_000_000, bytes_accessed=4_000_000, transcendentals=0),
+                compiler_params=pltpu.CompilerParams(vmem_limit_bytes=60 * 2**20),
+            )(c.reshape(1), du, w))
+        part = {}
         part.update(pdn((1, 2)))
         part.update(pdn((0,)))
-        d0, d1 = swap(part[3][0], 2), swap(part[3][1], 4)
+        d0, d1 = ([swap(diag[q][h], bit) for q in range(2)] for h, bit in ((0, 2), (1, 4)))
         ex, ey = swap(part[1][0], 2), swap(part[2][1], 4)
         tgt = jnp.where(own, 2 * (jnp.arange(n) % tc) + (loc & 1), -1).astype(jnp.int32)
         i0 = lax.broadcasted_iota(jnp.int32, (n, n), 0)
         i1 = lax.broadcasted_iota(jnp.int32, (n, n), 1)
-        same = flat[:, None] == flat[None, :]
-        first = jnp.min(jnp.where(same, i0, n), axis=0)
-        lead = own & (first == jnp.arange(n))
+
+        def by_piece(v):
+            v = v.reshape(mb, 2, 2, 2, tl)
+            for ax, bit in ((1, 4), (2, 2), (3, 1)):
+                v = jnp.where((r & bit) > 0, jnp.flip(v, ax), v)
+            return v.reshape(2, mb // 2, groups, tl).transpose(2, 0, 1, 3).reshape(-1)
+
+        flat_p = by_piece(ids)
+        loc_p = flat_p - r * vl
+        own_p = (loc_p >= 0) & (loc_p < vl)
+        first = jnp.min(jnp.where(flat_p[:, None] == flat_p[None, :], i0, n), axis=0)
+        lead = own_p & (first == jnp.arange(n))
         pos = jnp.sum(jnp.where(lead[:, None] & (i0 < i1), 1, 0), axis=0)
         pos_of_first = jnp.sum(jnp.where((i0 == first[None, :]), pos[:, None], 0), axis=0)
-        slot = jnp.where(own, pos_of_first, -1).astype(jnp.int32)
-        rows = jnp.sum(jnp.where(lead[:, None] & (pos[:, None] == i1), loc[:, None], 0), axis=0).astype(jnp.int32)
+        slot = jnp.where(own_p, pos_of_first, -1).astype(jnp.int32)
+        rows = jnp.sum(jnp.where(lead[:, None] & (pos[:, None] == i1), loc_p[:, None], 0), axis=0).astype(jnp.int32)
         cnt = jnp.sum(lead.astype(jnp.int32)).reshape(1)
         n_owned = jnp.sum(own.astype(jnp.int32)).reshape(1)
         own_pos = jnp.sum(jnp.where(own[:, None] & (i0 < i1), 1, 0), axis=0)
@@ -339,11 +355,14 @@
         d0, d1, loc, tgt, slot, rows, cnt, owned, n_owned = lax.optimization_barrier(
             (d0, d1, loc, tgt, slot, rows, cnt, owned, n_owned)
         )
-        ty, tx = f32(part[2][0]) + f32(d0), f32(part[1][1]) + f32(d1)
-        gy = swap(pick(ty[..., hd:], ty[..., :hd]), 1)
-        gx = swap(pick(tx[..., hd:], tx[..., :hd]), 1)
-        fy = swap(pick(ty[..., :hd], ty[..., hd:]) + gy, 4)
-        fx = swap(pick(tx[..., :hd], tx[..., hd:]) + gx, 2)
+
+        def relay(mine, far, bit):
+            left, right = f32(mine[..., :hd]) + f32(far[0]), f32(mine[..., hd:]) + f32(far[1])
+            got = swap(pick(right, left), 1)
+            v = pick(left, right) + got
+            return swap(v[:CUT], bit), v[CUT:]
+
+        (fy, ly), (fx, lx) = relay(part[2][0], d0, 4), relay(part[1][1], d1, 2)
 
         mine, far, near, de = pl.pallas_call(
             lookup_kernel,
@@ -369,13 +388,16 @@
         far, near = swap(far, 1), swap(near, 1)
         xpairs = {j: (mine[j], far[0] if j == 3 else near[j]) for j in range(4)}
 
+        ly, lx = swap(ly, 4), swap(lx, 2)
+
         def widen(v):
-            o = jnp.zeros_like(v)
-            return to_rows(v, o)
-
-        v0 = f32(part[0][0]) + f32(ex) + widen(fy)
-        v1 = f32(part[0][1]) + f32(ey) + widen(fx)
-        dn = pick(v0, v1) + swap(pick(v1, v0), 1)
+            return to_rows(v, jnp.zeros_like(v))
+
+        ex, ey, fy, fx, ly, lx = lax.optimization_barrier((ex, ey, fy, fx, ly, lx))
+        v0 = f32(part[0][0]) + f32(ex) + widen(jnp.concatenate([fy, ly], axis=0))
+        v1 = f32(part[0][1]) + f32(ey) + widen(jnp.concatenate([fx, lx], axis=0))
+        keep, give = pick(v0, v1), pick(v1, v0)
+        dn = keep + swap(give, 1)
         x0, x1 = reduce_to_home(xpairs, jnp.bfloat16)
         xo = gather_all((x0, x1))
         x = to_rows(jnp.where(k == 0, x0, x1), jnp.where(k == 0, xo[1][0], xo[1][1]))
@@ -398,21 +420,20 @@
                 compiler_params=pltpu.CompilerParams(vmem_limit_bytes=24 * 2**20),
             )(kc, g.reshape(1, d), w, *(xo[2 * j + q][h] for h in range(2) for q in range(2)), *more)
             ns.append(nj)
-        dw, de = pl.pallas_call(
+        dw = pl.pallas_call(
             dw_kernel,
-            out_shape=(jax.ShapeDtypeStruct((d, f), jnp.float32), de_shape),
-            in_specs=[SMEM] + [VMEM] * 5 + [ANY],
-            out_specs=(ANY, ANY),
+            out_shape=jax.ShapeDtypeStruct((d, f), jnp.float32),
+            in_specs=[SMEM] + [VMEM] * 5,
+            out_specs=ANY,
             scratch_shapes=[
                 pltpu.VMEM((n, f), jnp.bfloat16),
                 pltpu.VMEM((2, 512, f), jnp.float32),
                 pltpu.SemaphoreType.DMA((2,)),
-            ] + zero_scratch,
-            input_output_aliases={6: 1},
+            ],
             cost_estimate=pl.CostEstimate(flops=30_000_000, bytes_accessed=40_000_000, transcendentals=0),
             compiler_params=pltpu.CompilerParams(vmem_limit_bytes=24 * 2**20),
             name="dw",
-        )(c.reshape(1), du, *ns, de)
+        )(c.reshape(1), du, *ns)
 
         xf = x.astype(jnp.float32)
         rs = lax.rsqrt(jnp.mean(xf * xf, axis=-1, keepdims=True) + EPS)
@@ -429,17 +450,16 @@
         de = pl.pallas_call(
             scatter_kernel,
             out_shape=de_shape,
-            in_specs=[SMEM, SMEM, SMEM, VMEM] + [VMEM] * 16 + [ANY],
+            in_specs=[SMEM, SMEM, VMEM] + [VMEM] * 16 + [ANY],
             out_specs=ANY,
             scratch_shapes=[
-                pltpu.VMEM((mb, t, d), jnp.bfloat16),
                 pltpu.VMEM((BLK, d), jnp.float32),
                 pltpu.SemaphoreType.DMA,
             ],
-            input_output_aliases={20: 0},
+            input_output_aliases={19: 0},
             compiler_params=pltpu.CompilerParams(vmem_limit_bytes=28 * 2**20),
             name="put",
-        )(me, rows, cnt, slot.reshape(1, n), *dxs, de)
+        )(rows, cnt, slot.reshape(1, n), *dxs, de)
         return u, x, de, dw, dg
 
     return jax.shard_map(

time: 211 us -> 214 us (1.014)
  starting transfers between devices: 27.1 us -> 34.7 us
  local copies, waits for them, and re-layouts: 15.5 us -> 9.52 us
  other arithmetic: 14.4 us -> 17.2 us
    ppermute x48 -> x52, starting transfers between devices: 27.1 us -> 34.7 us  [swap(): return lax.ppermute(v, 'tp', [(i, i ^ bit) for i in range(groups)])]
    unnamed x85 -> x99, local copies, waits for them, and re-layouts: 14.8 us -> 8.49 us
    select_n x3, other arithmetic: 1.99 us -> 4.14 us  [pick(): return jnp.where(k == 0, a, b)]
    ppermute x48 -> x52, waiting for transfers between devices: 81.8 us -> 79.9 us  [swap(): return lax.ppermute(v, 'tp', [(i, i ^ bit) for i in range(groups)])]
    pallas_call x2 -> x3, Pallas kernels: 14 us -> 14.2 us  [the longest x1 7.22 us: local(): pl.pallas_call(dw_kernel, out_shape=jax.ShapeDtypeStruct((d, f), jnp.floa...]
  transfers between devices with their start and end apart: 48 -> 52, of which waited for: 23 -> 17; matrix products, arithmetic and copies ran while one was open for 7% -> 8% of each run, Pallas kernels for 27% -> 28%
where the time goes in v6:
time: 214 us
  waiting for transfers between devices  79.9 us (37%)
  Pallas kernels  70.6 us (33%)
  starting transfers between devices  34.7 us (16%)
  other arithmetic  17.2 us (8%)
  local copies, waits for them, and re-layouts  9.52 us (4%)
    ppermute x52, waiting for transfers between devices, swap(): return lax.ppermute(v, 'tp', [(i, i ^ bit) for i in range(groups)])  79.9 us
    ppermute x52, starting transfers between devices, swap(): return lax.ppermute(v, 'tp', [(i, i ^ bit) for i in range(groups)])  34.7 us
    pallas_call x2, Pallas kernels, local(): pl.pallas_call(functools.partial(zero_kernel, first, last), out_shape=de_...  16.7 us
    pallas_call x4, Pallas kernels, local(): pl.pallas_call(functools.partial(norm_kernel, j), out_shape=(jax.ShapeDty...  14.7 us
    pallas_call x1, Pallas kernels, local(): pl.pallas_call(lookup_kernel, out_shape=(half_shape(4), half_shape(1), ha...  13.8 us
    unnamed x99, local copies, waits for them, and re-layouts  8.49 us
    pallas_call x1, Pallas kernels, local(): pl.pallas_call(dw_kernel, out_shape=jax.ShapeDtypeStruct((d, f), jnp.floa...  7.22 us
    pallas_call x2, Pallas kernels, local(): pl.pallas_call(functools.partial(pdn_first_kernel, 3, q * hd), out_shape=...  7.01 us
  transfers between devices with their start and end apart: 52, of which 17 were waited for; matrix products, arithmetic and copies ran while one was open for 8% of the time, Pallas kernels for 28%

profile of v6, /device:TPU:0, one launch (start us, length us, event | category | flops | bytes accessed | tf_op | source)
XLA Modules:
  0.0 213.7 jit_solution(16752808228210136799)
XLA Ops:
  0.6 3.5 %shard_map.101 = (bf16[4,32,1536]{2,1,0:T(8,128)(2,1)}, bf16[4,32,1536]{2,1,0:T(8,128)(2,1)}) custom-call(s32[1]{0:T(128)} %bitcast.1.c_ref, bf16[4,256,640]{2,1,0:T(8,128)(2,1)} %du_ref.5, bf16[3072,640]{1,0:T(8,128)(2,1)} %w_ref.11), custom_call_target="tpu_custom_call" | custom-call | flops 3000000 | bytes 4000000 | tf_op jit(solution)/shard_map/pallas_call | solution.py:313
  4.2 3.3 %collective-permute-start = (bf16[4,32,1536]{2,1,0:T(8,128)(2,1)}, bf16[4,32,1536]{2,1,0:T(8,128)(2,1)S(1)}, u32[]{:S(2)}, u32[]{:S(2)}) collective-permute-start(bf16[4,32,1536]{2,1,0:T(8,128)(2,1)} %get-tuple-element.58), channel_id=1, source_target_pairs={{0,2},{1,3},{2,0},{3,1},{4,6},{5,7},{6,4},{7,5}} | collective-permute-start | bytes 1179656 | tf_op jit(solution)/shard_map/ppermute | solution.py:242
  7.5 3.5 %shard_map.102 = (bf16[4,32,1536]{2,1,0:T(8,128)(2,1)}, bf16[4,32,1536]{2,1,0:T(8,128)(2,1)}) custom-call(s32[1]{0:T(128)} %bitcast.1.c_ref, bf16[4,256,640]{2,1,0:T(8,128)(2,1)} %du_ref.5, bf16[3072,640]{1,0:T(8,128)(2,1)} %w_ref.11), custom_call_target="tpu_custom_call" | custom-call | flops 3000000 | bytes 4000000 | tf_op jit(solution)/shard_map/pallas_call | solution.py:313
  11.2 1.9 collective-permute-start.2
  15.2 2.9 %select_reduce_fusion.2 = (s32[1024]{0:T(1024)S(1)}, s32[1024]{0:T(1024)S(1)}, s32[1024]{0:T(1024)S(1)}) fusion(s32[1024]{0:T(1024)S(1)} %get-tuple-element.123, s32[1024]{0:T(1024)S(1)} %select_reduce_fusion.4, pred[1024]{0:T(1024)(128)(4,1)S(1)} %get-tuple-element.121, s32[1024]{0:T(1024)S(1)} %select_reduce_fusion.5, s32[1024]{0:T(1024)S(1)} %select_reduce_fusion.1, ...), kind=kLoop, calls=%fused_computation.3 | loop fusion | flops 11531264 | bytes 30720 | tf_op jit(solution)/shard_map/reduce_sum | solution.py:350
  18.3 2.1 copy-done
  20.4 3.5 %shard_map.110 = (bf16[4,32,3072]{2,1,0:T(8,128)(2,1)}, bf16[4,32,3072]{2,1,0:T(8,128)(2,1)S(1)}, bf16[4,32,3072]{2,1,0:T(8,128)(2,1)S(1)}, bf16[4,32,3072]{2,1,0:T(8,128)(2,1)}) custom-call(s32[1]{0:T(128)} %bitcast.1.c_ref, bf16[4,256,640]{2,1,0:T(8,128)(2,1)S(1)} %copy-done.2, bf16[3072,640]{1,0:T(8,128)(2,1)S(1)} %copy-done), custom_call_target="tpu_custom_call" | custom-call | flops 10000000 | bytes 8000000 | tf_op jit(solution)/shard_map/pallas_call | solution.py:262
  25.3 5.0 %collective-permute-done.3 = bf16[4,32,1536]{2,1,0:T(8,128)(2,1)S(1)} collective-permute-done((bf16[4,32,1536]{2,1,0:T(8,128)(2,1)}, bf16[4,32,1536]{2,1,0:T(8,128)(2,1)S(1)}, u32[]{:S(2)}, u32[]{:S(2)}) %collective-permute-start.3) | collective-permute-done | bytes 393248 | tf_op jit(solution)/shard_map/ppermute | solution.py:242
  31.3 1.1 fusion.15
  33.0 1.5 collective-permute-start.26
  34.5 1.5 collective-permute-start.27
  36.0 1.4 shard_map.109
  37.8 13.8 %look.1 = (bf16[4,4,64,1536]{3,2,1,0:T(8,128)(2,1)S(1)}, bf16[1,4,64,1536]{3,2,1,0:T(8,128)(2,1)S(1)}, bf16[3,4,64,1536]{3,2,1,0:T(8,128)(2,1)S(1)}, f32[8192,3072]{1,0:T(8,128)}) custom-call(s32[2]{0:T(128)S(1)} %pad_add_fusion.kc_ref, s32[1024]{0:T(1024)S(1)} %get-tuple-element.62.list_ref, s32[1]{0:T(128)} %bitcast.6.cnt_ref, s32[1024]{0:T(1024)S(1)} %bitcast.29, ...), custom_call_target="tpu_custom_call" | custom-call | flops 40000000 | bytes 60000000 | tf_op jit(solution)/shard_map/look/pallas_call | solution.py:367
  52.1 1.3 select_add_fusion.4
  53.6 1.4 select_add_fusion.3
  56.0 2.0 collective-permute-start.32
  58.0 1.4 collective-permute-start.33
  59.4 13.7 %collective-permute-done.32 = f32[1,32,1536]{2,1,0:T(8,128)S(1)} collective-permute-done((f32[1,32,1536]{2,1,0:T(8,128)S(1)}, f32[1,32,1536]{2,1,0:T(8,128)S(1)}, u32[]{:S(2)}, u32[]{:S(2)}) %collective-permute-start.32) | collective-permute-done | bytes 196640 | tf_op jit(solution)/shard_map/ppermute | solution.py:242
  73.5 1.2 collective-permute-done.33
  75.7 7.8 %collective-permute-done.13 = bf16[4,32,1536]{2,1,0:T(8,128)(2,1)S(1)} collective-permute-done((bf16[4,32,1536]{2,1,0:T(8,128)(2,1)S(1)}, bf16[4,32,1536]{2,1,0:T(8,128)(2,1)S(1)}, u32[]{:S(2)}, u32[]{:S(2)}) %collective-permute-start.13) | collective-permute-done | bytes 393248 | tf_op jit(solution)/shard_map/ppermute | solution.py:242
  84.2 1.3 collective-permute-start.5
  86.3 1.5 collective-permute-start.9
  87.8 2.0 broadcast_select_fusion
  89.8 12.0 %collective-permute-done.5 = bf16[4,32,1536]{2,1,0:T(8,128)(2,1)S(1)} collective-permute-done((bf16[4,32,1536]{2,1,0:T(8,128)(2,1)S(1)}, bf16[4,32,1536]{2,1,0:T(8,128)(2,1)S(1)}, u32[]{:S(2)}, u32[]{:S(2)}) %collective-permute-start.5) | collective-permute-done | bytes 393248 | tf_op jit(solution)/shard_map/ppermute | solution.py:242
  101.8 1.2 collective-permute-done.9
  105.2 1.2 collective-permute-start.19
  106.4 1.4 collective-permute-start.21
  108.2 2.8 %fusion.12 = (f32[3072]{0:T(1024)S(1)}, f32[4,32]{1,0:T(4,128)S(1)}, f32[4,32,3072]{2,1,0:T(8,128)S(1)}) fusion(bf16[4,32,3072]{2,1,0:T(8,128)(2,1)S(1)} %get-tuple-element.117, f32[4,32]{1,0:T(4,128)S(1)} %add_rsqrt_fusion, f32[3072]{0:T(1024)S(1)} %convert_element_type.60, f32[4,32,3072]{2,1,0:T(8,128)S(1)} %collective-permute-done.34, ...), kind=kLoop, calls=%fused_computation.24 | loop fusion | flops 7467904 | bytes 8676353 | tf_op jit(solution)/shard_map/reduce_sum | solution.py:444
  111.0 1.2 collective-permute-done.49
  113.3 2.3 %collective-permute-done.10.refs_0_ = bf16[4,32,1536]{2,1,0:T(8,128)(2,1)S(1)} collective-permute-done((bf16[4,32,1536]{2,1,0:T(8,128)(2,1)S(1)}, bf16[4,32,1536]{2,1,0:T(8,128)(2,1)S(1)}, u32[]{:S(2)}, u32[]{:S(2)}) %collective-permute-start.10) | collective-permute-done | bytes 393248 | tf_op jit(solution)/shard_map/ppermute | solution.py:242
  116.5 1.2 collective-permute-start.16
  117.7 7.5 %collective-permute-done.50 = f32[3072]{0:T(1024)S(1)} collective-permute-done((f32[3072]{0:T(1024)S(1)}, f32[3072]{0:T(1024)S(1)}, u32[]{:S(2)}, u32[]{:S(2)}) %collective-permute-start.50) | collective-permute-done | bytes 12320 | tf_op jit(solution)/shard_map/ppermute | solution.py:242
  125.2 1.2 collective-permute-start.51
  127.8 4.0 %collective-permute-done.51 = f32[3072]{0:T(1024)S(1)} collective-permute-done((f32[3072]{0:T(1024)S(1)}, f32[3072]{0:T(1024)S(1)}, u32[]{:S(2)}, u32[]{:S(2)}) %collective-permute-start.51) | collective-permute-done | bytes 12320 | tf_op jit(solution)/shard_map/ppermute | solution.py:242
  135.2 1.4 collective-permute-start.38
  136.5 1.2 collective-permute-start.41
  140.8 5.6 %collective-permute-done.37.refs_4_ = bf16[2,32,3072]{2,1,0:T(8,128)(2,1)S(1)} collective-permute-done((bf16[2,32,3072]{2,1,0:T(8,128)(2,1)S(1)}, bf16[2,32,3072]{2,1,0:T(8,128)(2,1)S(1)}, u32[]{:S(2)}, u32[]{:S(2)}) %collective-permute-start.37) | collective-permute-done | bytes 393248 | tf_op jit(solution)/shard_map/ppermute | solution.py:242
  147.2 7.3 %collective-permute-done.38.refs_5_ = bf16[2,32,3072]{2,1,0:T(8,128)(2,1)} collective-permute-done((bf16[2,32,3072]{2,1,0:T(8,128)(2,1)S(1)}, bf16[2,32,3072]{2,1,0:T(8,128)(2,1)}, u32[]{:S(2)}, u32[]{:S(2)}) %collective-permute-start.38) | collective-permute-done | bytes 393248 | tf_op jit(solution)/shard_map/ppermute | solution.py:242
  156.0 1.2 collective-permute-start.46
  157.8 9.4 %collective-permute-done.45.refs_12_ = bf16[2,32,3072]{2,1,0:T(8,128)(2,1)} collective-permute-done((bf16[2,32,3072]{2,1,0:T(8,128)(2,1)}, bf16[2,32,3072]{2,1,0:T(8,128)(2,1)}, u32[]{:S(2)}, u32[]{:S(2)}) %collective-permute-start.45) | collective-permute-done | bytes 393248 | tf_op jit(solution)/shard_map/ppermute | solution.py:242
  167.7 6.6 %shard_map.103.de_in = f32[8192,3072]{1,0:T(8,128)} custom-call(f32[8192,3072]{1,0:T(8,128)} %get-tuple-element.79.de_in), custom_call_target="tpu_custom_call", output_to_operand_aliasing={{}: (0, {})} | custom-call | flops 10000000 | bytes 20000000 | tf_op jit(solution)/shard_map/pallas_call | solution.py:378
  174.4 10.1 %shard_map.104.refs_4_ = f32[8192,3072]{1,0:T(8,128)} custom-call(f32[8192,3072]{1,0:T(8,128)} %shard_map.103.de_in), custom_call_target="tpu_custom_call", output_to_operand_aliasing={{}: (0, {})} | custom-call | flops 10000000 | bytes 20000000 | tf_op jit(solution)/shard_map/pallas_call | solution.py:378
  184.4 3.6 %shard_map.105 = (bf16[3072,256]{1,0:T(8,128)(2,1)S(1)}, bf16[4,256,640]{2,1,0:T(8,128)(2,1)}, f32[8192,3072]{1,0:T(8,128)}) custom-call(s32[2]{0:T(128)S(1)} %pad_add_fusion.kc_ref, bf16[1,3072]{1,0:T(2,128)(2,1)S(1)} %reshape.91.g_ref, bf16[3072,640]{1,0:T(8,128)(2,1)S(1)} %copy-done.1, ...), custom_call_target="tpu_custom_call", output_to_operand_aliasing={{2}: (7, {})} | custom-call | flops 8000000 | bytes 12000000 | tf_op jit(solution)/shard_map/pallas_call | solution.py:408
  188.7 3.6 %shard_map.106 = (bf16[3072,256]{1,0:T(8,128)(2,1)S(1)}, bf16[4,256,640]{2,1,0:T(8,128)(2,1)}, f32[8192,3072]{1,0:T(8,128)}) custom-call(s32[2]{0:T(128)S(1)} %pad_add_fusion.kc_ref, bf16[1,3072]{1,0:T(2,128)(2,1)S(1)} %reshape.91.g_ref, bf16[3072,640]{1,0:T(8,128)(2,1)S(1)} %copy-done.1, ...), custom_call_target="tpu_custom_call", output_to_operand_aliasing={{1}: (7, {}), {2}: (8, {})} | custom-call | flops 8000000 | bytes 12000000 | tf_op jit(solution)/shard_map/pallas_call | solution.py:408
  192.4 3.8 %shard_map.107 = (bf16[3072,256]{1,0:T(8,128)(2,1)S(1)}, bf16[4,256,640]{2,1,0:T(8,128)(2,1)}, f32[8192,3072]{1,0:T(8,128)}) custom-call(s32[2]{0:T(128)S(1)} %pad_add_fusion.kc_ref, bf16[1,3072]{1,0:T(2,128)(2,1)S(1)} %reshape.91.g_ref, bf16[3072,640]{1,0:T(8,128)(2,1)S(1)} %copy-done.1, ...), custom_call_target="tpu_custom_call", output_to_operand_aliasing={{1}: (7, {}), {2}: (8, {})} | custom-call | flops 8000000 | bytes 12000000 | tf_op jit(solution)/shard_map/pallas_call | solution.py:408
  196.3 3.6 %shard_map.108 = (bf16[3072,256]{1,0:T(8,128)(2,1)S(1)}, bf16[4,256,640]{2,1,0:T(8,128)(2,1)}, f32[8192,3072]{1,0:T(8,128)}) custom-call(s32[2]{0:T(128)S(1)} %pad_add_fusion.kc_ref, bf16[1,3072]{1,0:T(2,128)(2,1)S(1)} %reshape.91.g_ref, bf16[3072,640]{1,0:T(8,128)(2,1)S(1)} %copy-done.1, ...), custom_call_target="tpu_custom_call", output_to_operand_aliasing={{1}: (7, {}), {2}: (8, {})} | custom-call | flops 8000000 | bytes 12000000 | tf_op jit(solution)/shard_map/pallas_call | solution.py:408
  200.0 7.2 %dw.1 = f32[3072,640]{1,0:T(8,128)} custom-call(s32[1]{0:T(128)} %bitcast.1.c_ref, bf16[4,256,640]{2,1,0:T(8,128)(2,1)S(1)} %copy-done.2, bf16[3072,256]{1,0:T(8,128)(2,1)S(1)} %get-tuple-element.107.refs_0_, bf16[3072,256]{1,0:T(8,128)(2,1)S(1)} %get-tuple-element.108.refs_1_, bf16[3072,256]{1,0:T(8,128)(2,1)S(1)} %get-tuple-element.109.refs_2_, ...), custom_call_target="tpu_custom_call" | custom-call | flops 30000000 | bytes 40000000 | tf_op jit(solution)/shard_map/dw/pallas_call | solution.py:423
  207.3 6.2 %put.1 = f32[8192,3072]{1,0:T(8,128)} custom-call(s32[1024]{0:T(1024)S(1)} %get-tuple-element.87.rows_ref, s32[1]{0:T(128)} %bitcast.5.cnt_ref, s32[1,1024]{1,0:T(1,128)S(1)} %bitcast.30, bf16[2,32,3072]{2,1,0:T(8,128)(2,1)S(1)} %copy-done.10, bf16[2,32,3072]{2,1,0:T(8,128)(2,1)S(1)} %copy-done.8, ...), custom_call_target="tpu_custom_call", output_to_operand_aliasing={{}: (19, {})} | custom-call | tf_op jit(solution)/shard_map/put/pallas_call | solution.py:450
  (218 shorter events, 26.6 us)
Async XLA Ops:
  4.2 20.6 %collective-permute-start = (bf16[4,32,1536]{2,1,0:T(8,128)(2,1)}, bf16[4,32,1536]{2,1,0:T(8,128)(2,1)S(1)}, u32[]{:S(2)}, u32[]{:S(2)}) collective-permute-start(bf16[4,32,1536]{2,1,0:T(8,128)(2,1)} %get-tuple-element.58), channel_id=1, source_target_pairs={{0,2},{1,3},{2,0},{3,1},{4,6},{5,7},{6,4},{7,5}} | collective-permute-start | bytes 1179656 | tf_op jit(solution)/shard_map/ppermute | solution.py:242
  11.0 14.2 %collective-permute-start.1 = (bf16[4,32,1536]{2,1,0:T(8,128)(2,1)}, bf16[4,32,1536]{2,1,0:T(8,128)(2,1)S(1)}, u32[]{:S(2)}, u32[]{:S(2)}) collective-permute-start(bf16[4,32,1536]{2,1,0:T(8,128)(2,1)} %get-tuple-element.59), channel_id=1, source_target_pairs={{0,2},{1,3},{2,0},{3,1},{4,6},{5,7},{6,4},{7,5}} | collective-permute-start | bytes 1179656 | tf_op jit(solution)/shard_map/ppermute | solution.py:242
  11.2 14.1 %collective-permute-start.2 = (bf16[4,32,1536]{2,1,0:T(8,128)(2,1)S(1)}, bf16[4,32,1536]{2,1,0:T(8,128)(2,1)S(1)}, u32[]{:S(2)}, u32[]{:S(2)}) collective-permute-start(bf16[4,32,1536]{2,1,0:T(8,128)(2,1)S(1)} %copy-done.47), channel_id=1, source_target_pairs={{0,4},{1,5},{2,6},{3,7},{4,0},{5,1},{6,2},{7,3}} | collective-permute-start | bytes 1179656 | tf_op jit(solution)/shard_map/ppermute | solution.py:242
  13.1 17.1 %collective-permute-start.3 = (bf16[4,32,1536]{2,1,0:T(8,128)(2,1)}, bf16[4,32,1536]{2,1,0:T(8,128)(2,1)S(1)}, u32[]{:S(2)}, u32[]{:S(2)}) collective-permute-start(bf16[4,32,1536]{2,1,0:T(8,128)(2,1)} %get-tuple-element.61), channel_id=1, source_target_pairs={{0,4},{1,5},{2,6},{3,7},{4,0},{5,1},{6,2},{7,3}} | collective-permute-start | bytes 1179656 | tf_op jit(solution)/shard_map/ppermute | solution.py:242
  31.3 20.3 %collective-permute-start.28 = (f32[4,32,1536]{2,1,0:T(8,128)}, f32[4,32,1536]{2,1,0:T(8,128)}, u32[]{:S(2)}, u32[]{:S(2)}) collective-permute-start(f32[4,32,1536]{2,1,0:T(8,128)} %fusion.14), channel_id=1, source_target_pairs={{0,1},{1,0},{2,3},{3,2},{4,5},{5,4},{6,7},{7,6}} | collective-permute-start | bytes 2359304 | tf_op jit(solution)/shard_map/ppermute | solution.py:242
  32.4 21.1 %collective-permute-start.30 = (f32[4,32,1536]{2,1,0:T(8,128)}, f32[4,32,1536]{2,1,0:T(8,128)}, u32[]{:S(2)}, u32[]{:S(2)}) collective-permute-start(f32[4,32,1536]{2,1,0:T(8,128)} %fusion.15), channel_id=1, source_target_pairs={{0,1},{1,0},{2,3},{3,2},{4,5},{5,4},{6,7},{7,6}} | collective-permute-start | bytes 2359304 | tf_op jit(solution)/shard_map/ppermute | solution.py:242
  33.0 22.1 %collective-permute-start.26 = (bf16[4,32,3072]{2,1,0:T(8,128)(2,1)}, bf16[4,32,3072]{2,1,0:T(8,128)(2,1)}, u32[]{:S(2)}, u32[]{:S(2)}) collective-permute-start(bf16[4,32,3072]{2,1,0:T(8,128)(2,1)} %get-tuple-element.91), channel_id=1, source_target_pairs={{0,2},{1,3},{2,0},{3,1},{4,6},{5,7},{6,4},{7,5}} | collective-permute-start | bytes 2359304 | tf_op jit(solution)/shard_map/ppermute | solution.py:242
  34.5 21.5 %collective-permute-start.27 = (bf16[4,32,3072]{2,1,0:T(8,128)(2,1)}, bf16[4,32,3072]{2,1,0:T(8,128)(2,1)}, u32[]{:S(2)}, u32[]{:S(2)}) collective-permute-start(bf16[4,32,3072]{2,1,0:T(8,128)(2,1)} %get-tuple-element.92), channel_id=1, source_target_pairs={{0,4},{1,5},{2,6},{3,7},{4,0},{5,1},{6,2},{7,3}} | collective-permute-start | bytes 2359304 | tf_op jit(solution)/shard_map/ppermute | solution.py:242
  51.6 23.9 %collective-permute-start.4 = (bf16[3,4,64,1536]{3,2,1,0:T(8,128)(2,1)S(1)}, bf16[3,4,64,1536]{3,2,1,0:T(8,128)(2,1)S(1)}, u32[]{:S(2)}, u32[]{:S(2)}) collective-permute-start(bf16[3,4,64,1536]{3,2,1,0:T(8,128)(2,1)S(1)} %get-tuple-element.67), channel_id=1, source_target_pairs={{0,1},{1,0},{2,3},{3,2},{4,5},{5,4},{6,7},{7,6}} | collective-permute-start | bytes 7077896 | tf_op jit(solution)/shard_map/ppermute | solution.py:242
  51.7 6.4 %collective-permute-start.7 = (bf16[1,4,64,1536]{3,2,1,0:T(8,128)(2,1)S(1)}, bf16[1,4,64,1536]{3,2,1,0:T(8,128)(2,1)S(1)}, u32[]{:S(2)}, u32[]{:S(2)}) collective-permute-start(bf16[1,4,64,1536]{3,2,1,0:T(8,128)(2,1)S(1)} %get-tuple-element.71), channel_id=1, source_target_pairs={{0,1},{1,0},{2,3},{3,2},{4,5},{5,4},{6,7},{7,6}} | collective-permute-start | bytes 2359304 | tf_op jit(solution)/shard_map/ppermute | solution.py:242
  53.6 21.8 %collective-permute-start.29 = (f32[3,32,1536]{2,1,0:T(8,128)S(1)}, f32[3,32,1536]{2,1,0:T(8,128)S(1)}, u32[]{:S(2)}, u32[]{:S(2)}) collective-permute-start(f32[3,32,1536]{2,1,0:T(8,128)S(1)} %slice.143), channel_id=1, source_target_pairs={{0,4},{1,5},{2,6},{3,7},{4,0},{5,1},{6,2},{7,3}} | collective-permute-start | bytes 1769480 | tf_op jit(solution)/shard_map/ppermute | solution.py:242
  55.0 20.3 %collective-permute-start.31 = (f32[3,32,1536]{2,1,0:T(8,128)S(1)}, f32[3,32,1536]{2,1,0:T(8,128)S(1)}, u32[]{:S(2)}, u32[]{:S(2)}) collective-permute-start(f32[3,32,1536]{2,1,0:T(8,128)S(1)} %slice.144), channel_id=1, source_target_pairs={{0,2},{1,3},{2,0},{3,1},{4,6},{5,7},{6,4},{7,5}} | collective-permute-start | bytes 1769480 | tf_op jit(solution)/shard_map/ppermute | solution.py:242
  56.0 17.2 %collective-permute-start.32 = (f32[1,32,1536]{2,1,0:T(8,128)S(1)}, f32[1,32,1536]{2,1,0:T(8,128)S(1)}, u32[]{:S(2)}, u32[]{:S(2)}) collective-permute-start(f32[1,32,1536]{2,1,0:T(8,128)S(1)} %slice.145), channel_id=1, source_target_pairs={{0,4},{1,5},{2,6},{3,7},{4,0},{5,1},{6,2},{7,3}} | collective-permute-start | bytes 589832 | tf_op jit(solution)/shard_map/ppermute | solution.py:242
  58.0 16.6 %collective-permute-start.33 = (f32[1,32,1536]{2,1,0:T(8,128)S(1)}, f32[1,32,1536]{2,1,0:T(8,128)S(1)}, u32[]{:S(2)}, u32[]{:S(2)}) collective-permute-start(f32[1,32,1536]{2,1,0:T(8,128)S(1)} %slice.146), channel_id=1, source_target_pairs={{0,2},{1,3},{2,0},{3,1},{4,6},{5,7},{6,4},{7,5}} | collective-permute-start | bytes 589832 | tf_op jit(solution)/shard_map/ppermute | solution.py:242
  73.2 10.3 %collective-permute-start.13 = (bf16[4,32,1536]{2,1,0:T(8,128)(2,1)S(1)}, bf16[4,32,1536]{2,1,0:T(8,128)(2,1)S(1)}, u32[]{:S(2)}, u32[]{:S(2)}) collective-permute-start(bf16[4,32,1536]{2,1,0:T(8,128)(2,1)S(1)} %get-tuple-element.132), channel_id=1, source_target_pairs={{0,4},{1,5},{2,6},{3,7},{4,0},{5,1},{6,2},{7,3}} | collective-permute-start | bytes 1179656 | tf_op jit(solution)/shard_map/ppermute | solution.py:242
  74.6 11.6 %collective-permute-start.8 = (bf16[4,32,1536]{2,1,0:T(8,128)(2,1)S(1)}, bf16[4,32,1536]{2,1,0:T(8,128)(2,1)S(1)}, u32[]{:S(2)}, u32[]{:S(2)}) collective-permute-start(bf16[4,32,1536]{2,1,0:T(8,128)(2,1)S(1)} %get-tuple-element.131), channel_id=1, source_target_pairs={{0,2},{1,3},{2,0},{3,1},{4,6},{5,7},{6,4},{7,5}} | collective-permute-start | bytes 1179656 | tf_op jit(solution)/shard_map/ppermute | solution.py:242
  83.5 18.3 %collective-permute-start.14 = (bf16[4,32,1536]{2,1,0:T(8,128)(2,1)S(1)}, bf16[4,32,1536]{2,1,0:T(8,128)(2,1)S(1)}, u32[]{:S(2)}, u32[]{:S(2)}) collective-permute-start(bf16[4,32,1536]{2,1,0:T(8,128)(2,1)S(1)} %add_add_fusion), channel_id=1, source_target_pairs={{0,2},{1,3},{2,0},{3,1},{4,6},{5,7},{6,4},{7,5}} | collective-permute-start | bytes 1179656 | tf_op jit(solution)/shard_map/ppermute | solution.py:242
  84.2 17.6 %collective-permute-start.5 = (bf16[4,32,1536]{2,1,0:T(8,128)(2,1)S(1)}, bf16[4,32,1536]{2,1,0:T(8,128)(2,1)S(1)}, u32[]{:S(2)}, u32[]{:S(2)}) collective-permute-start(bf16[4,32,1536]{2,1,0:T(8,128)(2,1)S(1)} %slice_add_fusion.3), channel_id=1, source_target_pairs={{0,2},{1,3},{2,0},{3,1},{4,6},{5,7},{6,4},{7,5}} | collective-permute-start | bytes 1179656 | tf_op jit(solution)/shard_map/ppermute | solution.py:242
  85.6 16.2 %collective-permute-start.6 = (bf16[4,32,1536]{2,1,0:T(8,128)(2,1)S(1)}, bf16[4,32,1536]{2,1,0:T(8,128)(2,1)S(1)}, u32[]{:S(2)}, u32[]{:S(2)}) collective-permute-start(bf16[4,32,1536]{2,1,0:T(8,128)(2,1)S(1)} %slice_add_fusion.2), channel_id=1, source_target_pairs={{0,4},{1,5},{2,6},{3,7},{4,0},{5,1},{6,2},{7,3}} | collective-permute-start | bytes 1179656 | tf_op jit(solution)/shard_map/ppermute | solution.py:242
  86.3 16.7 %collective-permute-start.9 = (bf16[4,32,1536]{2,1,0:T(8,128)(2,1)S(1)}, bf16[4,32,1536]{2,1,0:T(8,128)(2,1)S(1)}, u32[]{:S(2)}, u32[]{:S(2)}) collective-permute-start(bf16[4,32,1536]{2,1,0:T(8,128)(2,1)S(1)} %add_add_fusion.2), channel_id=1, source_target_pairs={{0,4},{1,5},{2,6},{3,7},{4,0},{5,1},{6,2},{7,3}} | collective-permute-start | bytes 1179656 | tf_op jit(solution)/shard_map/ppermute | solution.py:242
  89.8 18.3 %collective-permute-start.34 = (f32[4,32,3072]{2,1,0:T(8,128)S(1)}, f32[4,32,3072]{2,1,0:T(8,128)S(1)}, u32[]{:S(2)}, u32[]{:S(2)}) collective-permute-start(f32[4,32,3072]{2,1,0:T(8,128)S(1)} %broadcast_select_fusion), channel_id=1, source_target_pairs={{0,1},{1,0},{2,3},{3,2},{4,5},{5,4},{6,7},{7,6}} | collective-permute-start | bytes 4718600 | tf_op jit(solution)/shard_map/ppermute | solution.py:242
  103.7 12.0 %collective-permute-start.10 = (bf16[4,32,1536]{2,1,0:T(8,128)(2,1)S(1)}, bf16[4,32,1536]{2,1,0:T(8,128)(2,1)S(1)}, u32[]{:S(2)}, u32[]{:S(2)}) collective-permute-start(bf16[4,32,1536]{2,1,0:T(8,128)(2,1)S(1)} %get-tuple-element.120.refs_0_), channel_id=1, source_target_pairs={{0,4},{1,5},{2,6},{3,7},{4,0},{5,1},{6,2},{7,3}} | collective-permute-start | bytes 1179656 | tf_op jit(solution)/shard_map/ppermute | solution.py:242
  104.5 12.0 %collective-permute-start.15 = (bf16[4,32,1536]{2,1,0:T(8,128)(2,1)S(1)}, bf16[4,32,1536]{2,1,0:T(8,128)(2,1)S(1)}, u32[]{:S(2)}, u32[]{:S(2)}) collective-permute-start(bf16[4,32,1536]{2,1,0:T(8,128)(2,1)S(1)} %get-tuple-element.119.refs_2_), channel_id=1, source_target_pairs={{0,2},{1,3},{2,0},{3,1},{4,6},{5,7},{6,4},{7,5}} | collective-permute-start | bytes 1179656 | tf_op jit(solution)/shard_map/ppermute | solution.py:242
  105.2 21.3 %collective-permute-start.19 = (bf16[4,32,1536]{2,1,0:T(8,128)(2,1)S(1)}, bf16[4,32,1536]{2,1,0:T(8,128)(2,1)S(1)}, u32[]{:S(2)}, u32[]{:S(2)}) collective-permute-start(bf16[4,32,1536]{2,1,0:T(8,128)(2,1)S(1)} %get-tuple-element.119.refs_2_), channel_id=1, source_target_pairs={{0,4},{1,5},{2,6},{3,7},{4,0},{5,1},{6,2},{7,3}} | collective-permute-start | bytes 1179656 | tf_op jit(solution)/shard_map/ppermute | solution.py:242
  106.4 20.1 %collective-permute-start.21 = (bf16[4,32,1536]{2,1,0:T(8,128)(2,1)S(1)}, bf16[4,32,1536]{2,1,0:T(8,128)(2,1)S(1)}, u32[]{:S(2)}, u32[]{:S(2)}) collective-permute-start(bf16[4,32,1536]{2,1,0:T(8,128)(2,1)S(1)} %get-tuple-element.120.refs_0_), channel_id=1, source_target_pairs={{0,2},{1,3},{2,0},{3,1},{4,6},{5,7},{6,4},{7,5}} | collective-permute-start | bytes 1179656 | tf_op jit(solution)/shard_map/ppermute | solution.py:242
  112.1 13.1 %collective-permute-start.50 = (f32[3072]{0:T(1024)S(1)}, f32[3072]{0:T(1024)S(1)}, u32[]{:S(2)}, u32[]{:S(2)}) collective-permute-start(f32[3072]{0:T(1024)S(1)} %add.148), channel_id=1, source_target_pairs={{0,2},{1,3},{2,0},{3,1},{4,6},{5,7},{6,4},{7,5}} | collective-permute-start | bytes 36872 | tf_op jit(solution)/shard_map/ppermute | solution.py:242
  115.7 16.7 %collective-permute-start.11 = (bf16[4,32,1536]{2,1,0:T(8,128)(2,1)S(1)}, bf16[4,32,1536]{2,1,0:T(8,128)(2,1)S(1)}, u32[]{:S(2)}, u32[]{:S(2)}) collective-permute-start(bf16[4,32,1536]{2,1,0:T(8,128)(2,1)S(1)} %collective-permute-done.10.refs_0_), channel_id=1, source_target_pairs={{0,2},{1,3},{2,0},{3,1},{4,6},{5,7},{6,4},{7,5}} | collective-permute-start | bytes 1179656 | tf_op jit(solution)/shard_map/ppermute | solution.py:242
  116.5 15.9 %collective-permute-start.16 = (bf16[4,32,1536]{2,1,0:T(8,128)(2,1)S(1)}, bf16[4,32,1536]{2,1,0:T(8,128)(2,1)S(1)}, u32[]{:S(2)}, u32[]{:S(2)}) collective-permute-start(bf16[4,32,1536]{2,1,0:T(8,128)(2,1)S(1)} %collective-permute-done.15.refs_2_), channel_id=1, source_target_pairs={{0,4},{1,5},{2,6},{3,7},{4,0},{5,1},{6,2},{7,3}} | collective-permute-start | bytes 1179656 | tf_op jit(solution)/shard_map/ppermute | solution.py:242
  125.2 6.6 %collective-permute-start.51 = (f32[3072]{0:T(1024)S(1)}, f32[3072]{0:T(1024)S(1)}, u32[]{:S(2)}, u32[]{:S(2)}) collective-permute-start(f32[3072]{0:T(1024)S(1)} %add.149), channel_id=1, source_target_pairs={{0,4},{1,5},{2,6},{3,7},{4,0},{5,1},{6,2},{7,3}} | collective-permute-start | bytes 36872 | tf_op jit(solution)/shard_map/ppermute | solution.py:242
  126.5 6.5 %collective-permute-start.18 = (bf16[4,32,1536]{2,1,0:T(8,128)(2,1)S(1)}, bf16[4,32,1536]{2,1,0:T(8,128)(2,1)S(1)}, u32[]{:S(2)}, u32[]{:S(2)}) collective-permute-start(bf16[4,32,1536]{2,1,0:T(8,128)(2,1)S(1)} %collective-permute-done.10.refs_0_), channel_id=1, source_target_pairs={{0,1},{1,0},{2,3},{3,2},{4,5},{5,4},{6,7},{7,6}} | collective-permute-start | bytes 1179656 | tf_op jit(solution)/shard_map/ppermute | solution.py:242
  126.5 7.2 %collective-permute-start.20 = (bf16[4,32,1536]{2,1,0:T(8,128)(2,1)S(1)}, bf16[4,32,1536]{2,1,0:T(8,128)(2,1)S(1)}, u32[]{:S(2)}, u32[]{:S(2)}) collective-permute-start(bf16[4,32,1536]{2,1,0:T(8,128)(2,1)S(1)} %collective-permute-done.19.refs_2_), channel_id=1, source_target_pairs={{0,1},{1,0},{2,3},{3,2},{4,5},{5,4},{6,7},{7,6}} | collective-permute-start | bytes 1179656 | tf_op jit(solution)/shard_map/ppermute | solution.py:242
  131.8 3.3 %collective-permute-start.22 = (bf16[4,32,1536]{2,1,0:T(8,128)(2,1)S(1)}, bf16[4,32,1536]{2,1,0:T(8,128)(2,1)S(1)}, u32[]{:S(2)}, u32[]{:S(2)}) collective-permute-start(bf16[4,32,1536]{2,1,0:T(8,128)(2,1)S(1)} %collective-permute-done.21.refs_0_), channel_id=1, source_target_pairs={{0,1},{1,0},{2,3},{3,2},{4,5},{5,4},{6,7},{7,6}} | collective-permute-start | bytes 1179656 | tf_op jit(solution)/shard_map/ppermute | solution.py:242
  132.4 4.1 %collective-permute-start.23 = (bf16[4,32,1536]{2,1,0:T(8,128)(2,1)S(1)}, bf16[4,32,1536]{2,1,0:T(8,128)(2,1)S(1)}, u32[]{:S(2)}, u32[]{:S(2)}) collective-permute-start(bf16[4,32,1536]{2,1,0:T(8,128)(2,1)S(1)} %collective-permute-done.15.refs_2_), channel_id=1, source_target_pairs={{0,1},{1,0},{2,3},{3,2},{4,5},{5,4},{6,7},{7,6}} | collective-permute-start | bytes 1179656 | tf_op jit(solution)/shard_map/ppermute | solution.py:242
  132.4 5.3 %collective-permute-start.35 = (bf16[2,32,3072]{2,1,0:T(8,128)(2,1)S(1)}, bf16[2,32,3072]{2,1,0:T(8,128)(2,1)S(1)}, u32[]{:S(2)}, u32[]{:S(2)}) collective-permute-start(bf16[2,32,3072]{2,1,0:T(8,128)(2,1)S(1)} %get-tuple-element.134.refs_0_), channel_id=1, source_target_pairs={{0,1},{1,0},{2,3},{3,2},{4,5},{5,4},{6,7},{7,6}} | collective-permute-start | bytes 1179656 | tf_op jit(solution)/shard_map/ppermute | solution.py:242
  133.7 5.6 %collective-permute-start.36 = (bf16[2,32,3072]{2,1,0:T(8,128)(2,1)S(1)}, bf16[2,32,3072]{2,1,0:T(8,128)(2,1)S(1)}, u32[]{:S(2)}, u32[]{:S(2)}) collective-permute-start(bf16[2,32,3072]{2,1,0:T(8,128)(2,1)S(1)} %get-tuple-element.133.refs_1_), channel_id=1, source_target_pairs={{0,1},{1,0},{2,3},{3,2},{4,5},{5,4},{6,7},{7,6}} | collective-permute-start | bytes 1179656 | tf_op jit(solution)/shard_map/ppermute | solution.py:242
  134.5 12.0 %collective-permute-start.37 = (bf16[2,32,3072]{2,1,0:T(8,128)(2,1)S(1)}, bf16[2,32,3072]{2,1,0:T(8,128)(2,1)S(1)}, u32[]{:S(2)}, u32[]{:S(2)}) collective-permute-start(bf16[2,32,3072]{2,1,0:T(8,128)(2,1)S(1)} %get-tuple-element.134.refs_0_), channel_id=1, source_target_pairs={{0,2},{1,3},{2,0},{3,1},{4,6},{5,7},{6,4},{7,5}} | collective-permute-start | bytes 1179656 | tf_op jit(solution)/shard_map/ppermute | solution.py:242
  135.2 19.4 %collective-permute-start.38 = (bf16[2,32,3072]{2,1,0:T(8,128)(2,1)S(1)}, bf16[2,32,3072]{2,1,0:T(8,128)(2,1)}, u32[]{:S(2)}, u32[]{:S(2)}) collective-permute-start(bf16[2,32,3072]{2,1,0:T(8,128)(2,1)S(1)} %get-tuple-element.133.refs_1_), channel_id=1, source_target_pairs={{0,2},{1,3},{2,0},{3,1},{4,6},{5,7},{6,4},{7,5}} | collective-permute-start | bytes 1179656 | tf_op jit(solution)/shard_map/ppermute | solution.py:242
  136.5 18.8 %collective-permute-start.41 = (bf16[2,32,3072]{2,1,0:T(8,128)(2,1)S(1)}, bf16[2,32,3072]{2,1,0:T(8,128)(2,1)}, u32[]{:S(2)}, u32[]{:S(2)}) collective-permute-start(bf16[2,32,3072]{2,1,0:T(8,128)(2,1)S(1)} %get-tuple-element.134.refs_0_), channel_id=1, source_target_pairs={{0,4},{1,5},{2,6},{3,7},{4,0},{5,1},{6,2},{7,3}} | collective-permute-start | bytes 1179656 | tf_op jit(solution)/shard_map/ppermute | solution.py:242
  138.5 17.6 %collective-permute-start.42 = (bf16[2,32,3072]{2,1,0:T(8,128)(2,1)S(1)}, bf16[2,32,3072]{2,1,0:T(8,128)(2,1)}, u32[]{:S(2)}, u32[]{:S(2)}) collective-permute-start(bf16[2,32,3072]{2,1,0:T(8,128)(2,1)S(1)} %get-tuple-element.133.refs_1_), channel_id=1, source_target_pairs={{0,4},{1,5},{2,6},{3,7},{4,0},{5,1},{6,2},{7,3}} | collective-permute-start | bytes 1179656 | tf_op jit(solution)/shard_map/ppermute | solution.py:242
  140.1 17.1 %collective-permute-start.12 = (bf16[4,32,1536]{2,1,0:T(8,128)(2,1)S(1)}, bf16[4,32,1536]{2,1,0:T(8,128)(2,1)S(1)}, u32[]{:S(2)}, u32[]{:S(2)}) collective-permute-start(bf16[4,32,1536]{2,1,0:T(8,128)(2,1)S(1)} %collective-permute-done.11.refs_0_), channel_id=1, source_target_pairs={{0,1},{1,0},{2,3},{3,2},{4,5},{5,4},{6,7},{7,6}} | collective-permute-start | bytes 1179656 | tf_op jit(solution)/shard_map/ppermute | solution.py:242
  146.5 10.7 %collective-permute-start.17 = (bf16[4,32,1536]{2,1,0:T(8,128)(2,1)S(1)}, bf16[4,32,1536]{2,1,0:T(8,128)(2,1)S(1)}, u32[]{:S(2)}, u32[]{:S(2)}) collective-permute-start(bf16[4,32,1536]{2,1,0:T(8,128)(2,1)S(1)} %collective-permute-done.16.refs_2_), channel_id=1, source_target_pairs={{0,1},{1,0},{2,3},{3,2},{4,5},{5,4},{6,7},{7,6}} | collective-permute-start | bytes 1179656 | tf_op jit(solution)/shard_map/ppermute | solution.py:242
  155.3 11.8 %collective-permute-start.45 = (bf16[2,32,3072]{2,1,0:T(8,128)(2,1)}, bf16[2,32,3072]{2,1,0:T(8,128)(2,1)}, u32[]{:S(2)}, u32[]{:S(2)}) collective-permute-start(bf16[2,32,3072]{2,1,0:T(8,128)(2,1)} %collective-permute-done.41.refs_8_), channel_id=1, source_target_pairs={{0,2},{1,3},{2,0},{3,1},{4,6},{5,7},{6,4},{7,5}} | collective-permute-start | bytes 1179656 | tf_op jit(solution)/shard_map/ppermute | solution.py:242
  156.0 11.5 %collective-permute-start.46 = (bf16[2,32,3072]{2,1,0:T(8,128)(2,1)}, bf16[2,32,3072]{2,1,0:T(8,128)(2,1)}, u32[]{:S(2)}, u32[]{:S(2)}) collective-permute-start(bf16[2,32,3072]{2,1,0:T(8,128)(2,1)} %collective-permute-done.38.refs_5_), channel_id=1, source_target_pairs={{0,4},{1,5},{2,6},{3,7},{4,0},{5,1},{6,2},{7,3}} | collective-permute-start | bytes 1179656 | tf_op jit(solution)/shard_map/ppermute | solution.py:242
  157.2 50.0 %collective-permute-start.40 = (bf16[2,32,3072]{2,1,0:T(8,128)(2,1)}, bf16[2,32,3072]{2,1,0:T(8,128)(2,1)}, u32[]{:S(2)}, u32[]{:S(2)}) collective-permute-start(bf16[2,32,3072]{2,1,0:T(8,128)(2,1)} %collective-permute-done.38.refs_5_), channel_id=1, source_target_pairs={{0,1},{1,0},{2,3},{3,2},{4,5},{5,4},{6,7},{7,6}} | collective-permute-start | bytes 1179656 | tf_op jit(solution)/shard_map/ppermute | solution.py:242
  157.2 50.0 %collective-permute-start.43 = (bf16[2,32,3072]{2,1,0:T(8,128)(2,1)}, bf16[2,32,3072]{2,1,0:T(8,128)(2,1)}, u32[]{:S(2)}, u32[]{:S(2)}) collective-permute-start(bf16[2,32,3072]{2,1,0:T(8,128)(2,1)} %collective-permute-done.41.refs_8_), channel_id=1, source_target_pairs={{0,1},{1,0},{2,3},{3,2},{4,5},{5,4},{6,7},{7,6}} | collective-permute-start | bytes 1179656 | tf_op jit(solution)/shard_map/ppermute | solution.py:242
  157.7 49.5 %collective-permute-start.44 = (bf16[2,32,3072]{2,1,0:T(8,128)(2,1)}, bf16[2,32,3072]{2,1,0:T(8,128)(2,1)}, u32[]{:S(2)}, u32[]{:S(2)}) collective-permute-start(bf16[2,32,3072]{2,1,0:T(8,128)(2,1)} %collective-permute-done.42.refs_9_), channel_id=1, source_target_pairs={{0,1},{1,0},{2,3},{3,2},{4,5},{5,4},{6,7},{7,6}} | collective-permute-start | bytes 1179656 | tf_op jit(solution)/shard_map/ppermute | solution.py:242
  167.2 40.1 %collective-permute-start.47 = (bf16[2,32,3072]{2,1,0:T(8,128)(2,1)}, bf16[2,32,3072]{2,1,0:T(8,128)(2,1)}, u32[]{:S(2)}, u32[]{:S(2)}) collective-permute-start(bf16[2,32,3072]{2,1,0:T(8,128)(2,1)} %collective-permute-done.45.refs_12_), channel_id=1, source_target_pairs={{0,1},{1,0},{2,3},{3,2},{4,5},{5,4},{6,7},{7,6}} | collective-permute-start | bytes 1179656 | tf_op jit(solution)/shard_map/ppermute | solution.py:242
  167.6 39.7 %collective-permute-start.48 = (bf16[2,32,3072]{2,1,0:T(8,128)(2,1)}, bf16[2,32,3072]{2,1,0:T(8,128)(2,1)}, u32[]{:S(2)}, u32[]{:S(2)}) collective-permute-start(bf16[2,32,3072]{2,1,0:T(8,128)(2,1)} %collective-permute-done.46.refs_13_), channel_id=1, source_target_pairs={{0,1},{1,0},{2,3},{3,2},{4,5},{5,4},{6,7},{7,6}} | collective-permute-start | bytes 1179656 | tf_op jit(solution)/shard_map/ppermute | solution.py:242
  (52 other events, 432.3 us)

commit v7 on v6

--- a/solution.py
+++ b/solution.py
@@ -13,9 +13,8 @@
 SMEM = pl.BlockSpec(memory_space=pltpu.SMEM)
 HBM = pl.BlockSpec(memory_space=pltpu.HBM)
 ZR = 128
-CUT = 3
 BLK = 256
-LOOKUP_EARLY, LOOKUP_SHARE, ZERO_A, ZERO_B, NORM_SHARE = 8, 22, 34, 52, 3
+ZERO_FIRST, LOOKUP_EARLY, LOOKUP_SHARE, ZERO_A, ZERO_B, NORM_SHARE = 6, 14, 24, 36, 52, 3
 
 
 def zero_fill(de, z, sem, first, last):
@@ -34,8 +33,8 @@
     return start, wait
 
 
-def zero_kernel(first, last, de_in, de, z, sem):
-    del de_in
+def zero_kernel(first, last, *refs):
+    de, z, sem = refs[-3:]
     start, wait = zero_fill(de, z, sem, first, last)
     start()
     wait()
@@ -82,13 +81,14 @@
                 outs[2 * i + h][:, :, cols] = v[:, h * tl:(h + 1) * tl]
 
 
-def lookup_kernel(kc_ref, list_ref, cnt_ref, loc_ref, tgt_ref, emb, mine_ref, far_ref, near_ref, de, buf, sem, z, zsem):
+def lookup_kernel(kc_ref, list_ref, cnt_ref, loc_ref, tgt_ref, emb, de_in, mine_ref, far_ref, near_ref, de, buf, sem, z, zsem):
+    del de_in
     k, c = kc_ref[0], kc_ref[1]
     _, d = emb.shape
     nj, mb, tc, hd = mine_ref.shape
     n = nj * mb * tc
     step = 64
-    start, wait = zero_fill(de, z, zsem, 0, LOOKUP_EARLY)
+    start, wait = zero_fill(de, z, zsem, ZERO_FIRST, LOOKUP_EARLY)
     late_start, late_wait = zero_fill(de, z, zsem, LOOKUP_EARLY, LOOKUP_SHARE)
     start()
 
@@ -257,6 +257,18 @@
 
         def half_shape(nj):
             return jax.ShapeDtypeStruct((nj, mb, tc, hd), jnp.bfloat16)
+
+        def zeros(first, last, *de):
+            return pl.pallas_call(
+                functools.partial(zero_kernel, first, last),
+                out_shape=de_shape,
+                in_specs=[ANY] * len(de),
+                out_specs=ANY,
+                scratch_shapes=zero_scratch,
+                input_output_aliases={0: 0} if de else {},
+                cost_estimate=pl.CostEstimate(flops=10_000_000, bytes_accessed=20_000_000, transcendentals=0),
+                compiler_params=pltpu.CompilerParams(vmem_limit_bytes=4 * 2**20),
+            )(*de)
 
         def pdn(js):
             out = pl.pallas_call(
@@ -327,6 +339,7 @@
         part = {}
         part.update(pdn((1, 2)))
         part.update(pdn((0,)))
+        de = zeros(0, ZERO_FIRST)
         d0, d1 = ([swap(diag[q][h], bit) for q in range(2)] for h, bit in ((0, 2), (1, 4)))
         ex, ey = swap(part[1][0], 2), swap(part[2][1], 4)
         tgt = jnp.where(own, 2 * (jnp.arange(n) % tc) + (loc & 1), -1).astype(jnp.int32)
@@ -359,45 +372,32 @@
         def relay(mine, far, bit):
             left, right = f32(mine[..., :hd]) + f32(far[0]), f32(mine[..., hd:]) + f32(far[1])
             got = swap(pick(right, left), 1)
-            v = pick(left, right) + got
-            return swap(v[:CUT], bit), v[CUT:]
-
-        (fy, ly), (fx, lx) = relay(part[2][0], d0, 4), relay(part[1][1], d1, 2)
+            return swap(pick(left, right) + got, bit)
+
+        fy, fx = relay(part[2][0], d0, 4), relay(part[1][1], d1, 2)
 
         mine, far, near, de = pl.pallas_call(
             lookup_kernel,
             out_shape=(half_shape(4), half_shape(1), half_shape(3), de_shape),
-            in_specs=[SMEM, SMEM, SMEM, SMEM, VMEM, ANY],
+            in_specs=[SMEM, SMEM, SMEM, SMEM, VMEM, ANY, ANY],
+            input_output_aliases={6: 3},
             out_specs=(VMEM, VMEM, VMEM, ANY),
             scratch_shapes=[pltpu.VMEM((2 * n, d), jnp.bfloat16), pltpu.SemaphoreType.DMA] + zero_scratch,
             cost_estimate=pl.CostEstimate(flops=40_000_000, bytes_accessed=60_000_000, transcendentals=0),
             compiler_params=pltpu.CompilerParams(vmem_limit_bytes=32 * 2**20),
             name="look",
-        )(kc, owned, n_owned, loc, tgt.reshape(n, 1), emb)
-        for first, last in ((LOOKUP_SHARE, ZERO_A), (ZERO_A, ZERO_B)):
-            de = pl.pallas_call(
-                functools.partial(zero_kernel, first, last),
-                out_shape=de_shape,
-                in_specs=[ANY],
-                out_specs=ANY,
-                scratch_shapes=zero_scratch,
-                input_output_aliases={0: 0},
-                cost_estimate=pl.CostEstimate(flops=10_000_000, bytes_accessed=20_000_000, transcendentals=0),
-                compiler_params=pltpu.CompilerParams(vmem_limit_bytes=4 * 2**20),
-            )(de)
+        )(kc, owned, n_owned, loc, tgt.reshape(n, 1), emb, de)
+        de = zeros(LOOKUP_SHARE, ZERO_A, de)
+        de = zeros(ZERO_A, ZERO_B, de)
         far, near = swap(far, 1), swap(near, 1)
         xpairs = {j: (mine[j], far[0] if j == 3 else near[j]) for j in range(4)}
 
-        ly, lx = swap(ly, 4), swap(lx, 2)
-
         def widen(v):
             return to_rows(v, jnp.zeros_like(v))
 
-        ex, ey, fy, fx, ly, lx = lax.optimization_barrier((ex, ey, fy, fx, ly, lx))
-        v0 = f32(part[0][0]) + f32(ex) + widen(jnp.concatenate([fy, ly], axis=0))
-        v1 = f32(part[0][1]) + f32(ey) + widen(jnp.concatenate([fx, lx], axis=0))
-        keep, give = pick(v0, v1), pick(v1, v0)
-        dn = keep + swap(give, 1)
+        v0 = f32(part[0][0]) + f32(ex) + widen(fy)
+        v1 = f32(part[0][1]) + f32(ey) + widen(fx)
+        dn = pick(v0, v1) + swap(pick(v1, v0), 1)
         x0, x1 = reduce_to_home(xpairs, jnp.bfloat16)
         xo = gather_all((x0, x1))
         x = to_rows(jnp.where(k == 0, x0, x1), jnp.where(k == 0, xo[1][0], xo[1][1]))

time: 214 us -> 215 us (level)
  local copies, waits for them, and re-layouts: 9.52 us -> 15 us
  waiting for transfers between devices: 79.9 us -> 76.4 us
  starting transfers between devices: 34.7 us -> 32.4 us
    unnamed x99 -> x89, local copies, waits for them, and re-layouts: 8.49 us -> 14 us
    ppermute x52 -> x50, waiting for transfers between devices: 79.9 us -> 76.4 us  [swap(): return lax.ppermute(v, 'tp', [(i, i ^ bit) for i in range(groups)])]
    pallas_call x2 -> x3, Pallas kernels: 16.7 us -> 19.5 us  [zeros(): pl.pallas_call(functools.partial(zero_kernel, first, last), out_shape=de_...]
    ppermute x52 -> x50, starting transfers between devices: 34.7 us -> 32.4 us  [swap(): return lax.ppermute(v, 'tp', [(i, i ^ bit) for i in range(groups)])]
  transfers between devices with their start and end apart: 52 -> 50, of which waited for: 17 -> 16; matrix products, arithmetic and copies ran while one was open for 8% -> 9% of each run, Pallas kernels for 28% -> 29%
where the time goes in v7:
time: 215 us
  waiting for transfers between devices  76.4 us (36%)
  Pallas kernels  71.2 us (33%)
  starting transfers between devices  32.4 us (15%)
  other arithmetic  17.8 us (8%)
  local copies, waits for them, and re-layouts  15 us (7%)
    ppermute x50, waiting for transfers between devices, swap(): return lax.ppermute(v, 'tp', [(i, i ^ bit) for i in range(groups)])  76.4 us
    ppermute x50, starting transfers between devices, swap(): return lax.ppermute(v, 'tp', [(i, i ^ bit) for i in range(groups)])  32.4 us
    pallas_call x3, Pallas kernels, zeros(): pl.pallas_call(functools.partial(zero_kernel, first, last), out_shape=de_...  19.5 us
    pallas_call x4, Pallas kernels, local(): pl.pallas_call(functools.partial(norm_kernel, j), out_shape=(jax.ShapeDty...  14.8 us
    unnamed x89, local copies, waits for them, and re-layouts  14 us
    pallas_call x1, Pallas kernels, local(): pl.pallas_call(lookup_kernel, out_shape=(half_shape(4), half_shape(1), ha...  11.8 us
    pallas_call x1, Pallas kernels, local(): pl.pallas_call(dw_kernel, out_shape=jax.ShapeDtypeStruct((d, f), jnp.floa...  7.25 us
    pallas_call x2, Pallas kernels, local(): pl.pallas_call(functools.partial(pdn_first_kernel, 3, q * hd), out_shape=...  7.09 us
  transfers between devices with their start and end apart: 50, of which 16 were waited for; matrix products, arithmetic and copies ran while one was open for 9% of the time, Pallas kernels for 29%

profile of v7, /device:TPU:0, one launch (start us, length us, event | category | flops | bytes accessed | tf_op | source)
XLA Modules:
  0.0 214.6 jit_solution(15523768181686620971)
XLA Ops:
  0.6 3.5 %shard_map.101 = (bf16[4,32,1536]{2,1,0:T(8,128)(2,1)}, bf16[4,32,1536]{2,1,0:T(8,128)(2,1)}) custom-call(s32[1]{0:T(128)} %bitcast.1.c_ref, bf16[4,256,640]{2,1,0:T(8,128)(2,1)} %du_ref.5, bf16[3072,640]{1,0:T(8,128)(2,1)} %w_ref.11), custom_call_target="tpu_custom_call" | custom-call | flops 3000000 | bytes 4000000 | tf_op jit(solution)/shard_map/pallas_call | solution.py:325
  4.2 3.3 %collective-permute-start = (bf16[4,32,1536]{2,1,0:T(8,128)(2,1)}, bf16[4,32,1536]{2,1,0:T(8,128)(2,1)}, u32[]{:S(2)}, u32[]{:S(2)}) collective-permute-start(bf16[4,32,1536]{2,1,0:T(8,128)(2,1)} %get-tuple-element.52), channel_id=1, source_target_pairs={{0,2},{1,3},{2,0},{3,1},{4,6},{5,7},{6,4},{7,5}} | collective-permute-start | bytes 1179656 | tf_op jit(solution)/shard_map/ppermute | solution.py:242
  7.5 3.6 %shard_map.102 = (bf16[4,32,1536]{2,1,0:T(8,128)(2,1)}, bf16[4,32,1536]{2,1,0:T(8,128)(2,1)}) custom-call(s32[1]{0:T(128)} %bitcast.1.c_ref, bf16[4,256,640]{2,1,0:T(8,128)(2,1)} %du_ref.5, bf16[3072,640]{1,0:T(8,128)(2,1)} %w_ref.11), custom_call_target="tpu_custom_call" | custom-call | flops 3000000 | bytes 4000000 | tf_op jit(solution)/shard_map/pallas_call | solution.py:325
  11.3 2.2 %collective-permute-start.2 = (bf16[4,32,1536]{2,1,0:T(8,128)(2,1)}, bf16[4,32,1536]{2,1,0:T(8,128)(2,1)}, u32[]{:S(2)}, u32[]{:S(2)}) collective-permute-start(bf16[4,32,1536]{2,1,0:T(8,128)(2,1)} %get-tuple-element.54), channel_id=1, source_target_pairs={{0,4},{1,5},{2,6},{3,7},{4,0},{5,1},{6,2},{7,3}} | collective-permute-start | bytes 1179656 | tf_op jit(solution)/shard_map/ppermute | solution.py:242
  13.5 1.3 copy-done.3
  14.8 3.3 %shard_map.111 = (bf16[4,32,3072]{2,1,0:T(8,128)(2,1)}, bf16[4,32,3072]{2,1,0:T(8,128)(2,1)S(1)}, bf16[4,32,3072]{2,1,0:T(8,128)(2,1)S(1)}, bf16[4,32,3072]{2,1,0:T(8,128)(2,1)S(1)}) custom-call(s32[1]{0:T(128)} %bitcast.1.c_ref, bf16[4,256,640]{2,1,0:T(8,128)(2,1)S(1)} %copy-done.3, bf16[3072,640]{1,0:T(8,128)(2,1)S(1)} %copy-done), custom_call_target="tpu_custom_call" | custom-call | flops 10000000 | bytes 8000000 | tf_op jit(solution)/shard_map/pallas_call | solution.py:274
  20.8 1.7 collective-permute-start.26
  24.5 2.9 %select_reduce_fusion.2 = (s32[1024]{0:T(1024)S(1)}, s32[1024]{0:T(1024)S(1)}, s32[1024]{0:T(1024)S(1)}) fusion(s32[1024]{0:T(1024)S(1)} %get-tuple-element.111, s32[1024]{0:T(1024)S(1)} %select_reduce_fusion.4, pred[1024]{0:T(1024)(128)(4,1)S(1)} %get-tuple-element.109, s32[1024]{0:T(1024)S(1)} %select_reduce_fusion.5, s32[1024]{0:T(1024)S(1)} %select_reduce_fusion.1, ...), kind=kLoop, calls=%fused_computation.3 | loop fusion | flops 11531264 | bytes 30720 | tf_op jit(solution)/shard_map/reduce_sum | solution.py:363
  27.6 2.1 copy-done.1
  29.7 1.3 copy-done.4
  31.0 1.4 shard_map.110
  32.4 3.8 %shard_map.103.de_in = f32[8192,3072]{1,0:T(8,128)} custom-call(), custom_call_target="tpu_custom_call" | custom-call | flops 10000000 | bytes 20000000 | tf_op jit(solution)/shard_map/pallas_call | solution.py:262
  36.9 1.5 collective-permute-start.29
  38.7 11.8 %look.1 = (bf16[4,4,64,1536]{3,2,1,0:T(8,128)(2,1)S(1)}, bf16[1,4,64,1536]{3,2,1,0:T(8,128)(2,1)S(1)}, bf16[3,4,64,1536]{3,2,1,0:T(8,128)(2,1)S(1)}, f32[8192,3072]{1,0:T(8,128)}) custom-call(s32[2]{0:T(128)S(1)} %pad_add_fusion.kc_ref, s32[1024]{0:T(1024)S(1)} %get-tuple-element.56.list_ref, s32[1]{0:T(128)} %bitcast.6.cnt_ref, ...), custom_call_target="tpu_custom_call", output_to_operand_aliasing={{3}: (6, {})} | custom-call | flops 40000000 | bytes 60000000 | tf_op jit(solution)/shard_map/look/pallas_call | solution.py:379
  51.6 1.3 fusion.14
  53.0 1.3 fusion.15
  54.3 2.1 collective-permute-done.7
  57.5 1.3 select_add_fusion.4
  59.7 1.4 select_add_fusion.3
  61.1 2.0 collective-permute-start.28
  63.4 6.1 %collective-permute-done.13 = bf16[4,32,1536]{2,1,0:T(8,128)(2,1)S(1)} collective-permute-done((bf16[4,32,1536]{2,1,0:T(8,128)(2,1)S(1)}, bf16[4,32,1536]{2,1,0:T(8,128)(2,1)S(1)}, u32[]{:S(2)}, u32[]{:S(2)}) %collective-permute-start.13) | collective-permute-done | bytes 393248 | tf_op jit(solution)/shard_map/ppermute | solution.py:242
  70.4 1.3 collective-permute-start.14
  72.6 2.0 collective-permute-start.6
  74.7 11.7 %collective-permute-done.28 = f32[4,32,1536]{2,1,0:T(8,128)S(1)} collective-permute-done((f32[4,32,1536]{2,1,0:T(8,128)S(1)}, f32[4,32,1536]{2,1,0:T(8,128)S(1)}, u32[]{:S(2)}, u32[]{:S(2)}) %collective-permute-start.28) | collective-permute-done | bytes 786464 | tf_op jit(solution)/shard_map/ppermute | solution.py:242
  86.4 3.6 %collective-permute-done.31 = f32[4,32,1536]{2,1,0:T(8,128)S(1)} collective-permute-done((f32[4,32,1536]{2,1,0:T(8,128)S(1)}, f32[4,32,1536]{2,1,0:T(8,128)S(1)}, u32[]{:S(2)}, u32[]{:S(2)}) %collective-permute-start.31) | collective-permute-done | bytes 786464 | tf_op jit(solution)/shard_map/ppermute | solution.py:242
  89.9 2.1 broadcast_select_fusion
  92.1 12.2 %collective-permute-done.5 = bf16[4,32,1536]{2,1,0:T(8,128)(2,1)S(1)} collective-permute-done((bf16[4,32,1536]{2,1,0:T(8,128)(2,1)S(1)}, bf16[4,32,1536]{2,1,0:T(8,128)(2,1)S(1)}, u32[]{:S(2)}, u32[]{:S(2)}) %collective-permute-start.5) | collective-permute-done | bytes 393248 | tf_op jit(solution)/shard_map/ppermute | solution.py:242
  105.0 1.2 collective-permute-start.10
  107.8 1.2 collective-permute-start.21
  109.5 2.8 %fusion.12 = (f32[3072]{0:T(1024)S(1)}, f32[4,32]{1,0:T(4,128)S(1)}, f32[4,32,3072]{2,1,0:T(8,128)S(1)}) fusion(bf16[4,32,3072]{2,1,0:T(8,128)(2,1)S(1)} %get-tuple-element.105, f32[4,32]{1,0:T(4,128)S(1)} %add_rsqrt_fusion, f32[3072]{0:T(1024)S(1)} %convert_element_type.60, f32[4,32,3072]{2,1,0:T(8,128)S(1)} %collective-permute-done.32, ...), kind=kLoop, calls=%fused_computation.24 | loop fusion | flops 7467904 | bytes 8676353 | tf_op jit(solution)/shard_map/reduce_sum | solution.py:444
  112.4 1.2 collective-permute-done.47
  114.9 2.1 collective-permute-done.10.refs_0_
  119.1 7.9 %collective-permute-done.48 = f32[3072]{0:T(1024)S(1)} collective-permute-done((f32[3072]{0:T(1024)S(1)}, f32[3072]{0:T(1024)S(1)}, u32[]{:S(2)}, u32[]{:S(2)}) %collective-permute-start.48) | collective-permute-done | bytes 12320 | tf_op jit(solution)/shard_map/ppermute | solution.py:242
  129.1 4.1 %collective-permute-done.49 = f32[3072]{0:T(1024)S(1)} collective-permute-done((f32[3072]{0:T(1024)S(1)}, f32[3072]{0:T(1024)S(1)}, u32[]{:S(2)}, u32[]{:S(2)}) %collective-permute-start.49) | collective-permute-done | bytes 12320 | tf_op jit(solution)/shard_map/ppermute | solution.py:242
  133.2 1.0 collective-permute-done.11.refs_0_
  137.0 1.2 collective-permute-start.36
  139.8 1.2 collective-permute-start.40
  142.6 5.6 %collective-permute-done.35.refs_4_ = bf16[2,32,3072]{2,1,0:T(8,128)(2,1)S(1)} collective-permute-done((bf16[2,32,3072]{2,1,0:T(8,128)(2,1)S(1)}, bf16[2,32,3072]{2,1,0:T(8,128)(2,1)S(1)}, u32[]{:S(2)}, u32[]{:S(2)}) %collective-permute-start.35) | collective-permute-done | bytes 393248 | tf_op jit(solution)/shard_map/ppermute | solution.py:242
  149.0 7.3 %collective-permute-done.36.refs_5_ = bf16[2,32,3072]{2,1,0:T(8,128)(2,1)} collective-permute-done((bf16[2,32,3072]{2,1,0:T(8,128)(2,1)S(1)}, bf16[2,32,3072]{2,1,0:T(8,128)(2,1)}, u32[]{:S(2)}, u32[]{:S(2)}) %collective-permute-start.36) | collective-permute-done | bytes 393248 | tf_op jit(solution)/shard_map/ppermute | solution.py:242
  159.2 9.7 %collective-permute-done.43.refs_12_ = bf16[2,32,3072]{2,1,0:T(8,128)(2,1)} collective-permute-done((bf16[2,32,3072]{2,1,0:T(8,128)(2,1)}, bf16[2,32,3072]{2,1,0:T(8,128)(2,1)}, u32[]{:S(2)}, u32[]{:S(2)}) %collective-permute-start.43) | collective-permute-done | bytes 393248 | tf_op jit(solution)/shard_map/ppermute | solution.py:242
  169.4 6.6 %shard_map.104.refs_0_ = f32[8192,3072]{1,0:T(8,128)} custom-call(f32[8192,3072]{1,0:T(8,128)} %get-tuple-element.73.refs_0_), custom_call_target="tpu_custom_call", output_to_operand_aliasing={{}: (0, {})} | custom-call | flops 10000000 | bytes 20000000 | tf_op jit(solution)/shard_map/pallas_call | solution.py:262
  176.1 9.1 %shard_map.105.refs_4_ = f32[8192,3072]{1,0:T(8,128)} custom-call(f32[8192,3072]{1,0:T(8,128)} %shard_map.104.refs_0_), custom_call_target="tpu_custom_call", output_to_operand_aliasing={{}: (0, {})} | custom-call | flops 10000000 | bytes 20000000 | tf_op jit(solution)/shard_map/pallas_call | solution.py:262
  185.2 3.6 %shard_map.106 = (bf16[3072,256]{1,0:T(8,128)(2,1)S(1)}, bf16[4,256,640]{2,1,0:T(8,128)(2,1)}, f32[8192,3072]{1,0:T(8,128)}) custom-call(s32[2]{0:T(128)S(1)} %pad_add_fusion.kc_ref, bf16[1,3072]{1,0:T(2,128)(2,1)S(1)} %reshape.91.g_ref, bf16[3072,640]{1,0:T(8,128)(2,1)S(1)} %copy-done.2, ...), custom_call_target="tpu_custom_call", output_to_operand_aliasing={{2}: (7, {})} | custom-call | flops 8000000 | bytes 12000000 | tf_op jit(solution)/shard_map/pallas_call | solution.py:408
  189.5 3.6 %shard_map.107 = (bf16[3072,256]{1,0:T(8,128)(2,1)S(1)}, bf16[4,256,640]{2,1,0:T(8,128)(2,1)}, f32[8192,3072]{1,0:T(8,128)}) custom-call(s32[2]{0:T(128)S(1)} %pad_add_fusion.kc_ref, bf16[1,3072]{1,0:T(2,128)(2,1)S(1)} %reshape.91.g_ref, bf16[3072,640]{1,0:T(8,128)(2,1)S(1)} %copy-done.2, ...), custom_call_target="tpu_custom_call", output_to_operand_aliasing={{1}: (7, {}), {2}: (8, {})} | custom-call | flops 8000000 | bytes 12000000 | tf_op jit(solution)/shard_map/pallas_call | solution.py:408
  193.2 3.9 %shard_map.108 = (bf16[3072,256]{1,0:T(8,128)(2,1)S(1)}, bf16[4,256,640]{2,1,0:T(8,128)(2,1)}, f32[8192,3072]{1,0:T(8,128)}) custom-call(s32[2]{0:T(128)S(1)} %pad_add_fusion.kc_ref, bf16[1,3072]{1,0:T(2,128)(2,1)S(1)} %reshape.91.g_ref, bf16[3072,640]{1,0:T(8,128)(2,1)S(1)} %copy-done.2, ...), custom_call_target="tpu_custom_call", output_to_operand_aliasing={{1}: (7, {}), {2}: (8, {})} | custom-call | flops 8000000 | bytes 12000000 | tf_op jit(solution)/shard_map/pallas_call | solution.py:408
  197.1 3.6 %shard_map.109 = (bf16[3072,256]{1,0:T(8,128)(2,1)S(1)}, bf16[4,256,640]{2,1,0:T(8,128)(2,1)}, f32[8192,3072]{1,0:T(8,128)}) custom-call(s32[2]{0:T(128)S(1)} %pad_add_fusion.kc_ref, bf16[1,3072]{1,0:T(2,128)(2,1)S(1)} %reshape.91.g_ref, bf16[3072,640]{1,0:T(8,128)(2,1)S(1)} %copy-done.2, ...), custom_call_target="tpu_custom_call", output_to_operand_aliasing={{1}: (7, {}), {2}: (8, {})} | custom-call | flops 8000000 | bytes 12000000 | tf_op jit(solution)/shard_map/pallas_call | solution.py:408
  200.8 7.3 %dw.1 = f32[3072,640]{1,0:T(8,128)} custom-call(s32[1]{0:T(128)} %bitcast.1.c_ref, bf16[4,256,640]{2,1,0:T(8,128)(2,1)S(1)} %copy-done.5, bf16[3072,256]{1,0:T(8,128)(2,1)S(1)} %get-tuple-element.95.refs_0_, bf16[3072,256]{1,0:T(8,128)(2,1)S(1)} %get-tuple-element.96.refs_1_, bf16[3072,256]{1,0:T(8,128)(2,1)S(1)} %get-tuple-element.97.refs_2_, ...), custom_call_target="tpu_custom_call" | custom-call | flops 30000000 | bytes 40000000 | tf_op jit(solution)/shard_map/dw/pallas_call | solution.py:423
  208.2 6.2 %put.1 = f32[8192,3072]{1,0:T(8,128)} custom-call(s32[1024]{0:T(1024)S(1)} %get-tuple-element.81.rows_ref, s32[1]{0:T(128)} %bitcast.5.cnt_ref, s32[1,1024]{1,0:T(1,128)S(1)} %bitcast.30, bf16[2,32,3072]{2,1,0:T(8,128)(2,1)S(1)} %copy-done.13, bf16[2,32,3072]{2,1,0:T(8,128)(2,1)S(1)} %copy-done.11, ...), custom_call_target="tpu_custom_call", output_to_operand_aliasing={{}: (19, {})} | custom-call | tf_op jit(solution)/shard_map/put/pallas_call | solution.py:450
  (199 shorter events, 30.3 us)
Async XLA Ops:
  4.2 32.7 %collective-permute-start = (bf16[4,32,1536]{2,1,0:T(8,128)(2,1)}, bf16[4,32,1536]{2,1,0:T(8,128)(2,1)}, u32[]{:S(2)}, u32[]{:S(2)}) collective-permute-start(bf16[4,32,1536]{2,1,0:T(8,128)(2,1)} %get-tuple-element.52), channel_id=1, source_target_pairs={{0,2},{1,3},{2,0},{3,1},{4,6},{5,7},{6,4},{7,5}} | collective-permute-start | bytes 1179656 | tf_op jit(solution)/shard_map/ppermute | solution.py:242
  11.1 27.4 %collective-permute-start.1 = (bf16[4,32,1536]{2,1,0:T(8,128)(2,1)}, bf16[4,32,1536]{2,1,0:T(8,128)(2,1)}, u32[]{:S(2)}, u32[]{:S(2)}) collective-permute-start(bf16[4,32,1536]{2,1,0:T(8,128)(2,1)} %get-tuple-element.53), channel_id=1, source_target_pairs={{0,2},{1,3},{2,0},{3,1},{4,6},{5,7},{6,4},{7,5}} | collective-permute-start | bytes 1179656 | tf_op jit(solution)/shard_map/ppermute | solution.py:242
  11.3 27.2 %collective-permute-start.2 = (bf16[4,32,1536]{2,1,0:T(8,128)(2,1)}, bf16[4,32,1536]{2,1,0:T(8,128)(2,1)}, u32[]{:S(2)}, u32[]{:S(2)}) collective-permute-start(bf16[4,32,1536]{2,1,0:T(8,128)(2,1)} %get-tuple-element.54), channel_id=1, source_target_pairs={{0,4},{1,5},{2,6},{3,7},{4,0},{5,1},{6,2},{7,3}} | collective-permute-start | bytes 1179656 | tf_op jit(solution)/shard_map/ppermute | solution.py:242
  13.4 25.0 %collective-permute-start.3 = (bf16[4,32,1536]{2,1,0:T(8,128)(2,1)}, bf16[4,32,1536]{2,1,0:T(8,128)(2,1)}, u32[]{:S(2)}, u32[]{:S(2)}) collective-permute-start(bf16[4,32,1536]{2,1,0:T(8,128)(2,1)} %get-tuple-element.55), channel_id=1, source_target_pairs={{0,4},{1,5},{2,6},{3,7},{4,0},{5,1},{6,2},{7,3}} | collective-permute-start | bytes 1179656 | tf_op jit(solution)/shard_map/ppermute | solution.py:242
  20.8 51.0 %collective-permute-start.26 = (bf16[4,32,3072]{2,1,0:T(8,128)(2,1)}, bf16[4,32,3072]{2,1,0:T(8,128)(2,1)}, u32[]{:S(2)}, u32[]{:S(2)}) collective-permute-start(bf16[4,32,3072]{2,1,0:T(8,128)(2,1)} %get-tuple-element.85), channel_id=1, source_target_pairs={{0,2},{1,3},{2,0},{3,1},{4,6},{5,7},{6,4},{7,5}} | collective-permute-start | bytes 2359304 | tf_op jit(solution)/shard_map/ppermute | solution.py:242
  36.9 35.7 %collective-permute-start.29 = (bf16[4,32,3072]{2,1,0:T(8,128)(2,1)S(1)}, bf16[4,32,3072]{2,1,0:T(8,128)(2,1)}, u32[]{:S(2)}, u32[]{:S(2)}) collective-permute-start(bf16[4,32,3072]{2,1,0:T(8,128)(2,1)S(1)} %copy-done.39), channel_id=1, source_target_pairs={{0,4},{1,5},{2,6},{3,7},{4,0},{5,1},{6,2},{7,3}} | collective-permute-start | bytes 2359304 | tf_op jit(solution)/shard_map/ppermute | solution.py:242
  50.7 10.4 %collective-permute-start.4 = (bf16[3,4,64,1536]{3,2,1,0:T(8,128)(2,1)S(1)}, bf16[3,4,64,1536]{3,2,1,0:T(8,128)(2,1)S(1)}, u32[]{:S(2)}, u32[]{:S(2)}) collective-permute-start(bf16[3,4,64,1536]{3,2,1,0:T(8,128)(2,1)S(1)} %get-tuple-element.61), channel_id=1, source_target_pairs={{0,1},{1,0},{2,3},{3,2},{4,5},{5,4},{6,7},{7,6}} | collective-permute-start | bytes 7077896 | tf_op jit(solution)/shard_map/ppermute | solution.py:242
  50.8 5.6 %collective-permute-start.7 = (bf16[1,4,64,1536]{3,2,1,0:T(8,128)(2,1)S(1)}, bf16[1,4,64,1536]{3,2,1,0:T(8,128)(2,1)S(1)}, u32[]{:S(2)}, u32[]{:S(2)}) collective-permute-start(bf16[1,4,64,1536]{3,2,1,0:T(8,128)(2,1)S(1)} %get-tuple-element.65), channel_id=1, source_target_pairs={{0,1},{1,0},{2,3},{3,2},{4,5},{5,4},{6,7},{7,6}} | collective-permute-start | bytes 2359304 | tf_op jit(solution)/shard_map/ppermute | solution.py:242
  52.9 4.6 %collective-permute-start.27 = (f32[4,32,1536]{2,1,0:T(8,128)S(1)}, f32[4,32,1536]{2,1,0:T(8,128)S(1)}, u32[]{:S(2)}, u32[]{:S(2)}) collective-permute-start(f32[4,32,1536]{2,1,0:T(8,128)S(1)} %fusion.14), channel_id=1, source_target_pairs={{0,1},{1,0},{2,3},{3,2},{4,5},{5,4},{6,7},{7,6}} | collective-permute-start | bytes 2359304 | tf_op jit(solution)/shard_map/ppermute | solution.py:242
  57.5 12.0 %collective-permute-start.13 = (bf16[4,32,1536]{2,1,0:T(8,128)(2,1)S(1)}, bf16[4,32,1536]{2,1,0:T(8,128)(2,1)S(1)}, u32[]{:S(2)}, u32[]{:S(2)}) collective-permute-start(bf16[4,32,1536]{2,1,0:T(8,128)(2,1)S(1)} %get-tuple-element.120), channel_id=1, source_target_pairs={{0,4},{1,5},{2,6},{3,7},{4,0},{5,1},{6,2},{7,3}} | collective-permute-start | bytes 1179656 | tf_op jit(solution)/shard_map/ppermute | solution.py:242
  58.9 11.5 %collective-permute-start.8 = (bf16[4,32,1536]{2,1,0:T(8,128)(2,1)S(1)}, bf16[4,32,1536]{2,1,0:T(8,128)(2,1)S(1)}, u32[]{:S(2)}, u32[]{:S(2)}) collective-permute-start(bf16[4,32,1536]{2,1,0:T(8,128)(2,1)S(1)} %get-tuple-element.119), channel_id=1, source_target_pairs={{0,2},{1,3},{2,0},{3,1},{4,6},{5,7},{6,4},{7,5}} | collective-permute-start | bytes 1179656 | tf_op jit(solution)/shard_map/ppermute | solution.py:242
  61.1 25.3 %collective-permute-start.28 = (f32[4,32,1536]{2,1,0:T(8,128)S(1)}, f32[4,32,1536]{2,1,0:T(8,128)S(1)}, u32[]{:S(2)}, u32[]{:S(2)}) collective-permute-start(f32[4,32,1536]{2,1,0:T(8,128)S(1)} %select_add_fusion.4), channel_id=1, source_target_pairs={{0,4},{1,5},{2,6},{3,7},{4,0},{5,1},{6,2},{7,3}} | collective-permute-start | bytes 2359304 | tf_op jit(solution)/shard_map/ppermute | solution.py:242
  69.5 20.4 %collective-permute-start.31 = (f32[4,32,1536]{2,1,0:T(8,128)S(1)}, f32[4,32,1536]{2,1,0:T(8,128)S(1)}, u32[]{:S(2)}, u32[]{:S(2)}) collective-permute-start(f32[4,32,1536]{2,1,0:T(8,128)S(1)} %select_add_fusion.3), channel_id=1, source_target_pairs={{0,2},{1,3},{2,0},{3,1},{4,6},{5,7},{6,4},{7,5}} | collective-permute-start | bytes 2359304 | tf_op jit(solution)/shard_map/ppermute | solution.py:242
  70.4 33.8 %collective-permute-start.14 = (bf16[4,32,1536]{2,1,0:T(8,128)(2,1)S(1)}, bf16[4,32,1536]{2,1,0:T(8,128)(2,1)S(1)}, u32[]{:S(2)}, u32[]{:S(2)}) collective-permute-start(bf16[4,32,1536]{2,1,0:T(8,128)(2,1)S(1)} %add_add_fusion), channel_id=1, source_target_pairs={{0,2},{1,3},{2,0},{3,1},{4,6},{5,7},{6,4},{7,5}} | collective-permute-start | bytes 1179656 | tf_op jit(solution)/shard_map/ppermute | solution.py:242
  71.8 32.4 %collective-permute-start.5 = (bf16[4,32,1536]{2,1,0:T(8,128)(2,1)S(1)}, bf16[4,32,1536]{2,1,0:T(8,128)(2,1)S(1)}, u32[]{:S(2)}, u32[]{:S(2)}) collective-permute-start(bf16[4,32,1536]{2,1,0:T(8,128)(2,1)S(1)} %slice_add_fusion.3), channel_id=1, source_target_pairs={{0,2},{1,3},{2,0},{3,1},{4,6},{5,7},{6,4},{7,5}} | collective-permute-start | bytes 1179656 | tf_op jit(solution)/shard_map/ppermute | solution.py:242
  72.6 31.6 %collective-permute-start.6 = (bf16[4,32,1536]{2,1,0:T(8,128)(2,1)S(1)}, bf16[4,32,1536]{2,1,0:T(8,128)(2,1)S(1)}, u32[]{:S(2)}, u32[]{:S(2)}) collective-permute-start(bf16[4,32,1536]{2,1,0:T(8,128)(2,1)S(1)} %slice_add_fusion.2), channel_id=1, source_target_pairs={{0,4},{1,5},{2,6},{3,7},{4,0},{5,1},{6,2},{7,3}} | collective-permute-start | bytes 1179656 | tf_op jit(solution)/shard_map/ppermute | solution.py:242
  86.4 17.9 %collective-permute-start.9 = (bf16[4,32,1536]{2,1,0:T(8,128)(2,1)S(1)}, bf16[4,32,1536]{2,1,0:T(8,128)(2,1)S(1)}, u32[]{:S(2)}, u32[]{:S(2)}) collective-permute-start(bf16[4,32,1536]{2,1,0:T(8,128)(2,1)S(1)} %add_add_fusion.2), channel_id=1, source_target_pairs={{0,4},{1,5},{2,6},{3,7},{4,0},{5,1},{6,2},{7,3}} | collective-permute-start | bytes 1179656 | tf_op jit(solution)/shard_map/ppermute | solution.py:242
  92.0 17.5 %collective-permute-start.32 = (f32[4,32,3072]{2,1,0:T(8,128)S(1)}, f32[4,32,3072]{2,1,0:T(8,128)S(1)}, u32[]{:S(2)}, u32[]{:S(2)}) collective-permute-start(f32[4,32,3072]{2,1,0:T(8,128)S(1)} %broadcast_select_fusion), channel_id=1, source_target_pairs={{0,1},{1,0},{2,3},{3,2},{4,5},{5,4},{6,7},{7,6}} | collective-permute-start | bytes 4718600 | tf_op jit(solution)/shard_map/ppermute | solution.py:242
  104.5 2.6 %collective-permute-start.24 = (bf16[4,32,1536]{2,1,0:T(8,128)(2,1)S(1)}, bf16[4,32,1536]{2,1,0:T(8,128)(2,1)S(1)}, u32[]{:S(2)}, u32[]{:S(2)}) collective-permute-start(bf16[4,32,1536]{2,1,0:T(8,128)(2,1)S(1)} %get-tuple-element.108.refs_0_), channel_id=1, source_target_pairs={{0,1},{1,0},{2,3},{3,2},{4,5},{5,4},{6,7},{7,6}} | collective-permute-start | bytes 1179656 | tf_op jit(solution)/shard_map/ppermute | solution.py:242
  104.5 3.3 %collective-permute-start.25 = (bf16[4,32,1536]{2,1,0:T(8,128)(2,1)S(1)}, bf16[4,32,1536]{2,1,0:T(8,128)(2,1)S(1)}, u32[]{:S(2)}, u32[]{:S(2)}) collective-permute-start(bf16[4,32,1536]{2,1,0:T(8,128)(2,1)S(1)} %get-tuple-element.107.refs_2_), channel_id=1, source_target_pairs={{0,1},{1,0},{2,3},{3,2},{4,5},{5,4},{6,7},{7,6}} | collective-permute-start | bytes 1179656 | tf_op jit(solution)/shard_map/ppermute | solution.py:242
  105.0 12.0 %collective-permute-start.10 = (bf16[4,32,1536]{2,1,0:T(8,128)(2,1)S(1)}, bf16[4,32,1536]{2,1,0:T(8,128)(2,1)S(1)}, u32[]{:S(2)}, u32[]{:S(2)}) collective-permute-start(bf16[4,32,1536]{2,1,0:T(8,128)(2,1)S(1)} %get-tuple-element.108.refs_0_), channel_id=1, source_target_pairs={{0,4},{1,5},{2,6},{3,7},{4,0},{5,1},{6,2},{7,3}} | collective-permute-start | bytes 1179656 | tf_op jit(solution)/shard_map/ppermute | solution.py:242
  106.3 12.0 %collective-permute-start.15 = (bf16[4,32,1536]{2,1,0:T(8,128)(2,1)S(1)}, bf16[4,32,1536]{2,1,0:T(8,128)(2,1)S(1)}, u32[]{:S(2)}, u32[]{:S(2)}) collective-permute-start(bf16[4,32,1536]{2,1,0:T(8,128)(2,1)S(1)} %get-tuple-element.107.refs_2_), channel_id=1, source_target_pairs={{0,2},{1,3},{2,0},{3,1},{4,6},{5,7},{6,4},{7,5}} | collective-permute-start | bytes 1179656 | tf_op jit(solution)/shard_map/ppermute | solution.py:242
  107.1 20.7 %collective-permute-start.19 = (bf16[4,32,1536]{2,1,0:T(8,128)(2,1)S(1)}, bf16[4,32,1536]{2,1,0:T(8,128)(2,1)S(1)}, u32[]{:S(2)}, u32[]{:S(2)}) collective-permute-start(bf16[4,32,1536]{2,1,0:T(8,128)(2,1)S(1)} %get-tuple-element.107.refs_2_), channel_id=1, source_target_pairs={{0,4},{1,5},{2,6},{3,7},{4,0},{5,1},{6,2},{7,3}} | collective-permute-start | bytes 1179656 | tf_op jit(solution)/shard_map/ppermute | solution.py:242
  107.8 20.0 %collective-permute-start.21 = (bf16[4,32,1536]{2,1,0:T(8,128)(2,1)S(1)}, bf16[4,32,1536]{2,1,0:T(8,128)(2,1)S(1)}, u32[]{:S(2)}, u32[]{:S(2)}) collective-permute-start(bf16[4,32,1536]{2,1,0:T(8,128)(2,1)S(1)} %get-tuple-element.108.refs_0_), channel_id=1, source_target_pairs={{0,2},{1,3},{2,0},{3,1},{4,6},{5,7},{6,4},{7,5}} | collective-permute-start | bytes 1179656 | tf_op jit(solution)/shard_map/ppermute | solution.py:242
  113.5 13.4 %collective-permute-start.48 = (f32[3072]{0:T(1024)S(1)}, f32[3072]{0:T(1024)S(1)}, u32[]{:S(2)}, u32[]{:S(2)}) collective-permute-start(f32[3072]{0:T(1024)S(1)} %add.148), channel_id=1, source_target_pairs={{0,2},{1,3},{2,0},{3,1},{4,6},{5,7},{6,4},{7,5}} | collective-permute-start | bytes 36872 | tf_op jit(solution)/shard_map/ppermute | solution.py:242
  117.0 17.1 %collective-permute-start.11 = (bf16[4,32,1536]{2,1,0:T(8,128)(2,1)S(1)}, bf16[4,32,1536]{2,1,0:T(8,128)(2,1)S(1)}, u32[]{:S(2)}, u32[]{:S(2)}) collective-permute-start(bf16[4,32,1536]{2,1,0:T(8,128)(2,1)S(1)} %collective-permute-done.10.refs_0_), channel_id=1, source_target_pairs={{0,2},{1,3},{2,0},{3,1},{4,6},{5,7},{6,4},{7,5}} | collective-permute-start | bytes 1179656 | tf_op jit(solution)/shard_map/ppermute | solution.py:242
  118.3 15.9 %collective-permute-start.16 = (bf16[4,32,1536]{2,1,0:T(8,128)(2,1)S(1)}, bf16[4,32,1536]{2,1,0:T(8,128)(2,1)S(1)}, u32[]{:S(2)}, u32[]{:S(2)}) collective-permute-start(bf16[4,32,1536]{2,1,0:T(8,128)(2,1)S(1)} %collective-permute-done.15.refs_2_), channel_id=1, source_target_pairs={{0,4},{1,5},{2,6},{3,7},{4,0},{5,1},{6,2},{7,3}} | collective-permute-start | bytes 1179656 | tf_op jit(solution)/shard_map/ppermute | solution.py:242
  126.9 6.2 %collective-permute-start.49 = (f32[3072]{0:T(1024)S(1)}, f32[3072]{0:T(1024)S(1)}, u32[]{:S(2)}, u32[]{:S(2)}) collective-permute-start(f32[3072]{0:T(1024)S(1)} %add.149), channel_id=1, source_target_pairs={{0,4},{1,5},{2,6},{3,7},{4,0},{5,1},{6,2},{7,3}} | collective-permute-start | bytes 36872 | tf_op jit(solution)/shard_map/ppermute | solution.py:242
  127.8 6.9 %collective-permute-start.18 = (bf16[4,32,1536]{2,1,0:T(8,128)(2,1)S(1)}, bf16[4,32,1536]{2,1,0:T(8,128)(2,1)S(1)}, u32[]{:S(2)}, u32[]{:S(2)}) collective-permute-start(bf16[4,32,1536]{2,1,0:T(8,128)(2,1)S(1)} %collective-permute-done.10.refs_0_), channel_id=1, source_target_pairs={{0,1},{1,0},{2,3},{3,2},{4,5},{5,4},{6,7},{7,6}} | collective-permute-start | bytes 1179656 | tf_op jit(solution)/shard_map/ppermute | solution.py:242
  127.9 7.6 %collective-permute-start.20 = (bf16[4,32,1536]{2,1,0:T(8,128)(2,1)S(1)}, bf16[4,32,1536]{2,1,0:T(8,128)(2,1)S(1)}, u32[]{:S(2)}, u32[]{:S(2)}) collective-permute-start(bf16[4,32,1536]{2,1,0:T(8,128)(2,1)S(1)} %collective-permute-done.19.refs_2_), channel_id=1, source_target_pairs={{0,1},{1,0},{2,3},{3,2},{4,5},{5,4},{6,7},{7,6}} | collective-permute-start | bytes 1179656 | tf_op jit(solution)/shard_map/ppermute | solution.py:242
  133.2 3.8 %collective-permute-start.22 = (bf16[4,32,1536]{2,1,0:T(8,128)(2,1)S(1)}, bf16[4,32,1536]{2,1,0:T(8,128)(2,1)S(1)}, u32[]{:S(2)}, u32[]{:S(2)}) collective-permute-start(bf16[4,32,1536]{2,1,0:T(8,128)(2,1)S(1)} %collective-permute-done.21.refs_0_), channel_id=1, source_target_pairs={{0,1},{1,0},{2,3},{3,2},{4,5},{5,4},{6,7},{7,6}} | collective-permute-start | bytes 1179656 | tf_op jit(solution)/shard_map/ppermute | solution.py:242
  134.2 4.1 %collective-permute-start.23 = (bf16[4,32,1536]{2,1,0:T(8,128)(2,1)S(1)}, bf16[4,32,1536]{2,1,0:T(8,128)(2,1)S(1)}, u32[]{:S(2)}, u32[]{:S(2)}) collective-permute-start(bf16[4,32,1536]{2,1,0:T(8,128)(2,1)S(1)} %collective-permute-done.15.refs_2_), channel_id=1, source_target_pairs={{0,1},{1,0},{2,3},{3,2},{4,5},{5,4},{6,7},{7,6}} | collective-permute-start | bytes 1179656 | tf_op jit(solution)/shard_map/ppermute | solution.py:242
  134.2 4.9 %collective-permute-start.33 = (bf16[2,32,3072]{2,1,0:T(8,128)(2,1)S(1)}, bf16[2,32,3072]{2,1,0:T(8,128)(2,1)S(1)}, u32[]{:S(2)}, u32[]{:S(2)}) collective-permute-start(bf16[2,32,3072]{2,1,0:T(8,128)(2,1)S(1)} %get-tuple-element.122.refs_0_), channel_id=1, source_target_pairs={{0,1},{1,0},{2,3},{3,2},{4,5},{5,4},{6,7},{7,6}} | collective-permute-start | bytes 1179656 | tf_op jit(solution)/shard_map/ppermute | solution.py:242
  135.4 5.6 %collective-permute-start.34 = (bf16[2,32,3072]{2,1,0:T(8,128)(2,1)S(1)}, bf16[2,32,3072]{2,1,0:T(8,128)(2,1)S(1)}, u32[]{:S(2)}, u32[]{:S(2)}) collective-permute-start(bf16[2,32,3072]{2,1,0:T(8,128)(2,1)S(1)} %get-tuple-element.121.refs_1_), channel_id=1, source_target_pairs={{0,1},{1,0},{2,3},{3,2},{4,5},{5,4},{6,7},{7,6}} | collective-permute-start | bytes 1179656 | tf_op jit(solution)/shard_map/ppermute | solution.py:242
  136.2 12.0 %collective-permute-start.35 = (bf16[2,32,3072]{2,1,0:T(8,128)(2,1)S(1)}, bf16[2,32,3072]{2,1,0:T(8,128)(2,1)S(1)}, u32[]{:S(2)}, u32[]{:S(2)}) collective-permute-start(bf16[2,32,3072]{2,1,0:T(8,128)(2,1)S(1)} %get-tuple-element.122.refs_0_), channel_id=1, source_target_pairs={{0,2},{1,3},{2,0},{3,1},{4,6},{5,7},{6,4},{7,5}} | collective-permute-start | bytes 1179656 | tf_op jit(solution)/shard_map/ppermute | solution.py:242
  137.0 19.3 %collective-permute-start.36 = (bf16[2,32,3072]{2,1,0:T(8,128)(2,1)S(1)}, bf16[2,32,3072]{2,1,0:T(8,128)(2,1)}, u32[]{:S(2)}, u32[]{:S(2)}) collective-permute-start(bf16[2,32,3072]{2,1,0:T(8,128)(2,1)S(1)} %get-tuple-element.121.refs_1_), channel_id=1, source_target_pairs={{0,2},{1,3},{2,0},{3,1},{4,6},{5,7},{6,4},{7,5}} | collective-permute-start | bytes 1179656 | tf_op jit(solution)/shard_map/ppermute | solution.py:242
  138.3 18.8 %collective-permute-start.39 = (bf16[2,32,3072]{2,1,0:T(8,128)(2,1)S(1)}, bf16[2,32,3072]{2,1,0:T(8,128)(2,1)}, u32[]{:S(2)}, u32[]{:S(2)}) collective-permute-start(bf16[2,32,3072]{2,1,0:T(8,128)(2,1)S(1)} %get-tuple-element.122.refs_0_), channel_id=1, source_target_pairs={{0,4},{1,5},{2,6},{3,7},{4,0},{5,1},{6,2},{7,3}} | collective-permute-start | bytes 1179656 | tf_op jit(solution)/shard_map/ppermute | solution.py:242
  139.8 18.0 %collective-permute-start.40 = (bf16[2,32,3072]{2,1,0:T(8,128)(2,1)S(1)}, bf16[2,32,3072]{2,1,0:T(8,128)(2,1)}, u32[]{:S(2)}, u32[]{:S(2)}) collective-permute-start(bf16[2,32,3072]{2,1,0:T(8,128)(2,1)S(1)} %get-tuple-element.121.refs_1_), channel_id=1, source_target_pairs={{0,4},{1,5},{2,6},{3,7},{4,0},{5,1},{6,2},{7,3}} | collective-permute-start | bytes 1179656 | tf_op jit(solution)/shard_map/ppermute | solution.py:242
  141.8 16.8 %collective-permute-start.12 = (bf16[4,32,1536]{2,1,0:T(8,128)(2,1)S(1)}, bf16[4,32,1536]{2,1,0:T(8,128)(2,1)S(1)}, u32[]{:S(2)}, u32[]{:S(2)}) collective-permute-start(bf16[4,32,1536]{2,1,0:T(8,128)(2,1)S(1)} %collective-permute-done.11.refs_0_), channel_id=1, source_target_pairs={{0,1},{1,0},{2,3},{3,2},{4,5},{5,4},{6,7},{7,6}} | collective-permute-start | bytes 1179656 | tf_op jit(solution)/shard_map/ppermute | solution.py:242
  148.2 10.4 %collective-permute-start.17 = (bf16[4,32,1536]{2,1,0:T(8,128)(2,1)S(1)}, bf16[4,32,1536]{2,1,0:T(8,128)(2,1)S(1)}, u32[]{:S(2)}, u32[]{:S(2)}) collective-permute-start(bf16[4,32,1536]{2,1,0:T(8,128)(2,1)S(1)} %collective-permute-done.16.refs_2_), channel_id=1, source_target_pairs={{0,1},{1,0},{2,3},{3,2},{4,5},{5,4},{6,7},{7,6}} | collective-permute-start | bytes 1179656 | tf_op jit(solution)/shard_map/ppermute | solution.py:242
  156.3 2.9 %collective-permute-start.37 = (bf16[2,32,3072]{2,1,0:T(8,128)(2,1)S(1)}, bf16[2,32,3072]{2,1,0:T(8,128)(2,1)S(1)}, u32[]{:S(2)}, u32[]{:S(2)}) collective-permute-start(bf16[2,32,3072]{2,1,0:T(8,128)(2,1)S(1)} %collective-permute-done.35.refs_4_), channel_id=1, source_target_pairs={{0,1},{1,0},{2,3},{3,2},{4,5},{5,4},{6,7},{7,6}} | collective-permute-start | bytes 1179656 | tf_op jit(solution)/shard_map/ppermute | solution.py:242
  157.0 11.8 %collective-permute-start.43 = (bf16[2,32,3072]{2,1,0:T(8,128)(2,1)}, bf16[2,32,3072]{2,1,0:T(8,128)(2,1)}, u32[]{:S(2)}, u32[]{:S(2)}) collective-permute-start(bf16[2,32,3072]{2,1,0:T(8,128)(2,1)} %collective-permute-done.39.refs_8_), channel_id=1, source_target_pairs={{0,2},{1,3},{2,0},{3,1},{4,6},{5,7},{6,4},{7,5}} | collective-permute-start | bytes 1179656 | tf_op jit(solution)/shard_map/ppermute | solution.py:242
  157.8 11.6 %collective-permute-start.44 = (bf16[2,32,3072]{2,1,0:T(8,128)(2,1)}, bf16[2,32,3072]{2,1,0:T(8,128)(2,1)}, u32[]{:S(2)}, u32[]{:S(2)}) collective-permute-start(bf16[2,32,3072]{2,1,0:T(8,128)(2,1)} %collective-permute-done.36.refs_5_), channel_id=1, source_target_pairs={{0,4},{1,5},{2,6},{3,7},{4,0},{5,1},{6,2},{7,3}} | collective-permute-start | bytes 1179656 | tf_op jit(solution)/shard_map/ppermute | solution.py:242
  158.6 49.5 %collective-permute-start.38 = (bf16[2,32,3072]{2,1,0:T(8,128)(2,1)}, bf16[2,32,3072]{2,1,0:T(8,128)(2,1)}, u32[]{:S(2)}, u32[]{:S(2)}) collective-permute-start(bf16[2,32,3072]{2,1,0:T(8,128)(2,1)} %collective-permute-done.36.refs_5_), channel_id=1, source_target_pairs={{0,1},{1,0},{2,3},{3,2},{4,5},{5,4},{6,7},{7,6}} | collective-permute-start | bytes 1179656 | tf_op jit(solution)/shard_map/ppermute | solution.py:242
  158.6 49.5 %collective-permute-start.41 = (bf16[2,32,3072]{2,1,0:T(8,128)(2,1)}, bf16[2,32,3072]{2,1,0:T(8,128)(2,1)}, u32[]{:S(2)}, u32[]{:S(2)}) collective-permute-start(bf16[2,32,3072]{2,1,0:T(8,128)(2,1)} %collective-permute-done.39.refs_8_), channel_id=1, source_target_pairs={{0,1},{1,0},{2,3},{3,2},{4,5},{5,4},{6,7},{7,6}} | collective-permute-start | bytes 1179656 | tf_op jit(solution)/shard_map/ppermute | solution.py:242
  159.1 49.0 %collective-permute-start.42 = (bf16[2,32,3072]{2,1,0:T(8,128)(2,1)}, bf16[2,32,3072]{2,1,0:T(8,128)(2,1)}, u32[]{:S(2)}, u32[]{:S(2)}) collective-permute-start(bf16[2,32,3072]{2,1,0:T(8,128)(2,1)} %collective-permute-done.40.refs_9_), channel_id=1, source_target_pairs={{0,1},{1,0},{2,3},{3,2},{4,5},{5,4},{6,7},{7,6}} | collective-permute-start | bytes 1179656 | tf_op jit(solution)/shard_map/ppermute | solution.py:242
  168.9 39.2 %collective-permute-start.45 = (bf16[2,32,3072]{2,1,0:T(8,128)(2,1)}, bf16[2,32,3072]{2,1,0:T(8,128)(2,1)}, u32[]{:S(2)}, u32[]{:S(2)}) collective-permute-start(bf16[2,32,3072]{2,1,0:T(8,128)(2,1)} %collective-permute-done.43.refs_12_), channel_id=1, source_target_pairs={{0,1},{1,0},{2,3},{3,2},{4,5},{5,4},{6,7},{7,6}} | collective-permute-start | bytes 1179656 | tf_op jit(solution)/shard_map/ppermute | solution.py:242
  169.4 38.7 %collective-permute-start.46 = (bf16[2,32,3072]{2,1,0:T(8,128)(2,1)}, bf16[2,32,3072]{2,1,0:T(8,128)(2,1)}, u32[]{:S(2)}, u32[]{:S(2)}) collective-permute-start(bf16[2,32,3072]{2,1,0:T(8,128)(2,1)} %collective-permute-done.44.refs_13_), channel_id=1, source_target_pairs={{0,1},{1,0},{2,3},{3,2},{4,5},{5,4},{6,7},{7,6}} | collective-permute-start | bytes 1179656 | tf_op jit(solution)/shard_map/ppermute | solution.py:242
  (46 other events, 340.5 us)

commit v8 on v7

--- a/solution.py
+++ b/solution.py
@@ -14,7 +14,7 @@
 HBM = pl.BlockSpec(memory_space=pltpu.HBM)
 ZR = 128
 BLK = 256
-ZERO_FIRST, LOOKUP_EARLY, LOOKUP_SHARE, ZERO_A, ZERO_B, NORM_SHARE = 6, 14, 24, 36, 52, 3
+ZERO_FIRST, LOOKUP_EARLY, LOOKUP_SHARE, ZERO_A, ZERO_B, NORM_SHARE = 2, 10, 22, 33, 48, 4
 
 
 def zero_fill(de, z, sem, first, last):
@@ -384,7 +384,7 @@
             out_specs=(VMEM, VMEM, VMEM, ANY),
             scratch_shapes=[pltpu.VMEM((2 * n, d), jnp.bfloat16), pltpu.SemaphoreType.DMA] + zero_scratch,
             cost_estimate=pl.CostEstimate(flops=40_000_000, bytes_accessed=60_000_000, transcendentals=0),
-            compiler_params=pltpu.CompilerParams(vmem_limit_bytes=32 * 2**20),
+            compiler_params=pltpu.CompilerParams(vmem_limit_bytes=22 * 2**20),
             name="look",
         )(kc, owned, n_owned, loc, tgt.reshape(n, 1), emb, de)
         de = zeros(LOOKUP_SHARE, ZERO_A, de)
@@ -417,7 +417,7 @@
                 ] + zero_scratch,
                 input_output_aliases={7 + i: 3 - len(more) + i for i in range(len(more))},
                 cost_estimate=pl.CostEstimate(flops=8_000_000, bytes_accessed=12_000_000, transcendentals=0),
-                compiler_params=pltpu.CompilerParams(vmem_limit_bytes=24 * 2**20),
+                compiler_params=pltpu.CompilerParams(vmem_limit_bytes=14 * 2**20),
             )(kc, g.reshape(1, d), w, *(xo[2 * j + q][h] for h in range(2) for q in range(2)), *more)
             ns.append(nj)
         dw = pl.pallas_call(
@@ -431,7 +431,7 @@
                 pltpu.SemaphoreType.DMA((2,)),
             ],
             cost_estimate=pl.CostEstimate(flops=30_000_000, bytes_accessed=40_000_000, transcendentals=0),
-            compiler_params=pltpu.CompilerParams(vmem_limit_bytes=24 * 2**20),
+            compiler_params=pltpu.CompilerParams(vmem_limit_bytes=16 * 2**20),
             name="dw",
         )(c.reshape(1), du, *ns)
 

time: 215 us -> 213 us (level)
    pallas_call x3, Pallas kernels: 19.5 us -> 16.5 us  [zeros(): pl.pallas_call(functools.partial(zero_kernel, first, last), out_shape=de_...]
    unnamed x89 -> x73, local copies, waits for them, and re-layouts: 14 us -> 14 us
  transfers between devices with their start and end apart: 50 -> 50, of which waited for: 16 -> 16; matrix products, arithmetic and copies ran while one was open for 9% -> 9% of each run, Pallas kernels for 29% -> 28%
where the time goes in v8:
time: 213 us
  waiting for transfers between devices  76.5 us (36%)
  Pallas kernels  69.4 us (33%)
  starting transfers between devices  32.4 us (15%)
  other arithmetic  17.8 us (8%)
  local copies, waits for them, and re-layouts  14.9 us (7%)
    ppermute x50, waiting for transfers between devices, swap(): return lax.ppermute(v, 'tp', [(i, i ^ bit) for i in range(groups)])  76.5 us
    ppermute x50, starting transfers between devices, swap(): return lax.ppermute(v, 'tp', [(i, i ^ bit) for i in range(groups)])  32.4 us
    pallas_call x3, Pallas kernels, zeros(): pl.pallas_call(functools.partial(zero_kernel, first, last), out_shape=de_...  16.5 us
    pallas_call x4, Pallas kernels, local(): pl.pallas_call(functools.partial(norm_kernel, j), out_shape=(jax.ShapeDty...  14.9 us
    unnamed x73, local copies, waits for them, and re-layouts  14 us
    pallas_call x1, Pallas kernels, local(): pl.pallas_call(lookup_kernel, out_shape=(half_shape(4), half_shape(1), ha...  12.7 us
    pallas_call x1, Pallas kernels, local(): pl.pallas_call(dw_kernel, out_shape=jax.ShapeDtypeStruct((d, f), jnp.floa...  7.25 us
    pallas_call x2, Pallas kernels, local(): pl.pallas_call(functools.partial(pdn_first_kernel, 3, q * hd), out_shape=...  7.12 us
  transfers between devices with their start and end apart: 50, of which 16 were waited for; matrix products, arithmetic and copies ran while one was open for 9% of the time, Pallas kernels for 28%

profile of v8, /device:TPU:0, one launch (start us, length us, event | category | flops | bytes accessed | tf_op | source)
XLA Modules:
  0.0 212.5 jit_solution(10077209695277691449)
XLA Ops:
  0.6 3.6 %shard_map.101 = (bf16[4,32,1536]{2,1,0:T(8,128)(2,1)}, bf16[4,32,1536]{2,1,0:T(8,128)(2,1)}) custom-call(s32[1]{0:T(128)} %bitcast.1.c_ref, bf16[4,256,640]{2,1,0:T(8,128)(2,1)} %du_ref.5, bf16[3072,640]{1,0:T(8,128)(2,1)} %w_ref.11), custom_call_target="tpu_custom_call" | custom-call | flops 3000000 | bytes 4000000 | tf_op jit(solution)/shard_map/pallas_call | solution.py:325
  4.2 3.3 %collective-permute-start = (bf16[4,32,1536]{2,1,0:T(8,128)(2,1)}, bf16[4,32,1536]{2,1,0:T(8,128)(2,1)}, u32[]{:S(2)}, u32[]{:S(2)}) collective-permute-start(bf16[4,32,1536]{2,1,0:T(8,128)(2,1)} %get-tuple-element.52), channel_id=1, source_target_pairs={{0,2},{1,3},{2,0},{3,1},{4,6},{5,7},{6,4},{7,5}} | collective-permute-start | bytes 1179656 | tf_op jit(solution)/shard_map/ppermute | solution.py:242
  7.6 3.5 %shard_map.102 = (bf16[4,32,1536]{2,1,0:T(8,128)(2,1)}, bf16[4,32,1536]{2,1,0:T(8,128)(2,1)}) custom-call(s32[1]{0:T(128)} %bitcast.1.c_ref, bf16[4,256,640]{2,1,0:T(8,128)(2,1)} %du_ref.5, bf16[3072,640]{1,0:T(8,128)(2,1)} %w_ref.11), custom_call_target="tpu_custom_call" | custom-call | flops 3000000 | bytes 4000000 | tf_op jit(solution)/shard_map/pallas_call | solution.py:325
  11.3 2.2 %collective-permute-start.2 = (bf16[4,32,1536]{2,1,0:T(8,128)(2,1)}, bf16[4,32,1536]{2,1,0:T(8,128)(2,1)}, u32[]{:S(2)}, u32[]{:S(2)}) collective-permute-start(bf16[4,32,1536]{2,1,0:T(8,128)(2,1)} %get-tuple-element.54), channel_id=1, source_target_pairs={{0,4},{1,5},{2,6},{3,7},{4,0},{5,1},{6,2},{7,3}} | collective-permute-start | bytes 1179656 | tf_op jit(solution)/shard_map/ppermute | solution.py:242
  13.5 1.3 copy-done.3
  14.8 3.3 %shard_map.111 = (bf16[4,32,3072]{2,1,0:T(8,128)(2,1)}, bf16[4,32,3072]{2,1,0:T(8,128)(2,1)S(1)}, bf16[4,32,3072]{2,1,0:T(8,128)(2,1)S(1)}, bf16[4,32,3072]{2,1,0:T(8,128)(2,1)S(1)}) custom-call(s32[1]{0:T(128)} %bitcast.1.c_ref, bf16[4,256,640]{2,1,0:T(8,128)(2,1)S(1)} %copy-done.3, bf16[3072,640]{1,0:T(8,128)(2,1)S(1)} %copy-done), custom_call_target="tpu_custom_call" | custom-call | flops 10000000 | bytes 8000000 | tf_op jit(solution)/shard_map/pallas_call | solution.py:274
  20.8 1.7 collective-permute-start.26
  24.5 2.9 %select_reduce_fusion.2 = (s32[1024]{0:T(1024)S(1)}, s32[1024]{0:T(1024)S(1)}, s32[1024]{0:T(1024)S(1)}) fusion(s32[1024]{0:T(1024)S(1)} %get-tuple-element.111, s32[1024]{0:T(1024)S(1)} %select_reduce_fusion.4, pred[1024]{0:T(1024)(128)(4,1)S(1)} %get-tuple-element.109, s32[1024]{0:T(1024)S(1)} %select_reduce_fusion.5, s32[1024]{0:T(1024)S(1)} %select_reduce_fusion.1, ...), kind=kLoop, calls=%fused_computation.3 | loop fusion | flops 11531264 | bytes 30720 | tf_op jit(solution)/shard_map/reduce_sum | solution.py:363
  27.6 2.1 copy-done.1
  29.7 1.3 copy-done.4
  31.0 1.4 shard_map.110
  32.4 1.8 shard_map.103.de_in
  34.9 1.5 collective-permute-start.29
  36.7 12.7 %look.1 = (bf16[4,4,64,1536]{3,2,1,0:T(8,128)(2,1)S(1)}, bf16[1,4,64,1536]{3,2,1,0:T(8,128)(2,1)S(1)}, bf16[3,4,64,1536]{3,2,1,0:T(8,128)(2,1)S(1)}, f32[8192,3072]{1,0:T(8,128)}) custom-call(s32[2]{0:T(128)S(1)} %pad_add_fusion.kc_ref, s32[1024]{0:T(1024)S(1)} %get-tuple-element.56.list_ref, s32[1]{0:T(128)} %bitcast.6.cnt_ref, ...), custom_call_target="tpu_custom_call", output_to_operand_aliasing={{3}: (6, {})} | custom-call | flops 40000000 | bytes 60000000 | tf_op jit(solution)/shard_map/look/pallas_call | solution.py:379
  50.5 1.3 fusion.14
  51.8 1.3 fusion.15
  53.2 2.1 collective-permute-done.7
  56.4 1.3 select_add_fusion.4
  58.6 1.4 select_add_fusion.3
  60.0 2.0 collective-permute-start.28
  62.2 6.2 %collective-permute-done.13 = bf16[4,32,1536]{2,1,0:T(8,128)(2,1)S(1)} collective-permute-done((bf16[4,32,1536]{2,1,0:T(8,128)(2,1)S(1)}, bf16[4,32,1536]{2,1,0:T(8,128)(2,1)S(1)}, u32[]{:S(2)}, u32[]{:S(2)}) %collective-permute-start.13) | collective-permute-done | bytes 393248 | tf_op jit(solution)/shard_map/ppermute | solution.py:242
  69.3 1.2 collective-permute-start.14
  71.5 2.0 collective-permute-start.6
  73.6 11.7 %collective-permute-done.28 = f32[4,32,1536]{2,1,0:T(8,128)S(1)} collective-permute-done((f32[4,32,1536]{2,1,0:T(8,128)S(1)}, f32[4,32,1536]{2,1,0:T(8,128)S(1)}, u32[]{:S(2)}, u32[]{:S(2)}) %collective-permute-start.28) | collective-permute-done | bytes 786464 | tf_op jit(solution)/shard_map/ppermute | solution.py:242
  85.2 3.6 %collective-permute-done.31 = f32[4,32,1536]{2,1,0:T(8,128)S(1)} collective-permute-done((f32[4,32,1536]{2,1,0:T(8,128)S(1)}, f32[4,32,1536]{2,1,0:T(8,128)S(1)}, u32[]{:S(2)}, u32[]{:S(2)}) %collective-permute-start.31) | collective-permute-done | bytes 786464 | tf_op jit(solution)/shard_map/ppermute | solution.py:242
  88.8 2.1 broadcast_select_fusion
  90.9 12.2 %collective-permute-done.5 = bf16[4,32,1536]{2,1,0:T(8,128)(2,1)S(1)} collective-permute-done((bf16[4,32,1536]{2,1,0:T(8,128)(2,1)S(1)}, bf16[4,32,1536]{2,1,0:T(8,128)(2,1)S(1)}, u32[]{:S(2)}, u32[]{:S(2)}) %collective-permute-start.5) | collective-permute-done | bytes 393248 | tf_op jit(solution)/shard_map/ppermute | solution.py:242
  103.9 1.2 collective-permute-start.10
  106.7 1.2 collective-permute-start.21
  108.4 2.8 %fusion.12 = (f32[3072]{0:T(1024)S(1)}, f32[4,32]{1,0:T(4,128)S(1)}, f32[4,32,3072]{2,1,0:T(8,128)S(1)}) fusion(bf16[4,32,3072]{2,1,0:T(8,128)(2,1)S(1)} %get-tuple-element.105, f32[4,32]{1,0:T(4,128)S(1)} %add_rsqrt_fusion, f32[3072]{0:T(1024)S(1)} %convert_element_type.60, f32[4,32,3072]{2,1,0:T(8,128)S(1)} %collective-permute-done.32, ...), kind=kLoop, calls=%fused_computation.24 | loop fusion | flops 7467904 | bytes 8676353 | tf_op jit(solution)/shard_map/reduce_sum | solution.py:444
  111.3 1.2 collective-permute-done.47
  113.8 2.1 collective-permute-done.10.refs_0_
  117.9 7.9 %collective-permute-done.48 = f32[3072]{0:T(1024)S(1)} collective-permute-done((f32[3072]{0:T(1024)S(1)}, f32[3072]{0:T(1024)S(1)}, u32[]{:S(2)}, u32[]{:S(2)}) %collective-permute-start.48) | collective-permute-done | bytes 12320 | tf_op jit(solution)/shard_map/ppermute | solution.py:242
  127.2 4.8 %collective-permute-done.49 = f32[3072]{0:T(1024)S(1)} collective-permute-done((f32[3072]{0:T(1024)S(1)}, f32[3072]{0:T(1024)S(1)}, u32[]{:S(2)}, u32[]{:S(2)}) %collective-permute-start.49) | collective-permute-done | bytes 12320 | tf_op jit(solution)/shard_map/ppermute | solution.py:242
  132.1 1.0 collective-permute-done.11.refs_0_
  135.9 1.2 collective-permute-start.36
  138.7 1.2 collective-permute-start.40
  140.7 6.4 %collective-permute-done.35.refs_4_ = bf16[2,32,3072]{2,1,0:T(8,128)(2,1)S(1)} collective-permute-done((bf16[2,32,3072]{2,1,0:T(8,128)(2,1)S(1)}, bf16[2,32,3072]{2,1,0:T(8,128)(2,1)S(1)}, u32[]{:S(2)}, u32[]{:S(2)}) %collective-permute-start.35) | collective-permute-done | bytes 393248 | tf_op jit(solution)/shard_map/ppermute | solution.py:242
  147.1 8.1 %collective-permute-done.36.refs_5_ = bf16[2,32,3072]{2,1,0:T(8,128)(2,1)} collective-permute-done((bf16[2,32,3072]{2,1,0:T(8,128)(2,1)S(1)}, bf16[2,32,3072]{2,1,0:T(8,128)(2,1)}, u32[]{:S(2)}, u32[]{:S(2)}) %collective-permute-start.36) | collective-permute-done | bytes 393248 | tf_op jit(solution)/shard_map/ppermute | solution.py:242
  160.3 7.4 %collective-permute-done.43.refs_12_ = bf16[2,32,3072]{2,1,0:T(8,128)(2,1)} collective-permute-done((bf16[2,32,3072]{2,1,0:T(8,128)(2,1)}, bf16[2,32,3072]{2,1,0:T(8,128)(2,1)}, u32[]{:S(2)}, u32[]{:S(2)}) %collective-permute-start.43) | collective-permute-done | bytes 393248 | tf_op jit(solution)/shard_map/ppermute | solution.py:242
  168.3 6.1 %shard_map.104.refs_0_ = f32[8192,3072]{1,0:T(8,128)} custom-call(f32[8192,3072]{1,0:T(8,128)} %get-tuple-element.73.refs_0_), custom_call_target="tpu_custom_call", output_to_operand_aliasing={{}: (0, {})} | custom-call | flops 10000000 | bytes 20000000 | tf_op jit(solution)/shard_map/pallas_call | solution.py:262
  174.4 8.6 %shard_map.105.refs_4_ = f32[8192,3072]{1,0:T(8,128)} custom-call(f32[8192,3072]{1,0:T(8,128)} %shard_map.104.refs_0_), custom_call_target="tpu_custom_call", output_to_operand_aliasing={{}: (0, {})} | custom-call | flops 10000000 | bytes 20000000 | tf_op jit(solution)/shard_map/pallas_call | solution.py:262
  183.1 3.7 %shard_map.106 = (bf16[3072,256]{1,0:T(8,128)(2,1)S(1)}, bf16[4,256,640]{2,1,0:T(8,128)(2,1)}, f32[8192,3072]{1,0:T(8,128)}) custom-call(s32[2]{0:T(128)S(1)} %pad_add_fusion.kc_ref, bf16[1,3072]{1,0:T(2,128)(2,1)S(1)} %reshape.91.g_ref, bf16[3072,640]{1,0:T(8,128)(2,1)S(1)} %copy-done.2, ...), custom_call_target="tpu_custom_call", output_to_operand_aliasing={{2}: (7, {})} | custom-call | flops 8000000 | bytes 12000000 | tf_op jit(solution)/shard_map/pallas_call | solution.py:408
  187.4 3.7 %shard_map.107 = (bf16[3072,256]{1,0:T(8,128)(2,1)S(1)}, bf16[4,256,640]{2,1,0:T(8,128)(2,1)}, f32[8192,3072]{1,0:T(8,128)}) custom-call(s32[2]{0:T(128)S(1)} %pad_add_fusion.kc_ref, bf16[1,3072]{1,0:T(2,128)(2,1)S(1)} %reshape.91.g_ref, bf16[3072,640]{1,0:T(8,128)(2,1)S(1)} %copy-done.2, ...), custom_call_target="tpu_custom_call", output_to_operand_aliasing={{1}: (7, {}), {2}: (8, {})} | custom-call | flops 8000000 | bytes 12000000 | tf_op jit(solution)/shard_map/pallas_call | solution.py:408
  191.1 3.9 %shard_map.108 = (bf16[3072,256]{1,0:T(8,128)(2,1)S(1)}, bf16[4,256,640]{2,1,0:T(8,128)(2,1)}, f32[8192,3072]{1,0:T(8,128)}) custom-call(s32[2]{0:T(128)S(1)} %pad_add_fusion.kc_ref, bf16[1,3072]{1,0:T(2,128)(2,1)S(1)} %reshape.91.g_ref, bf16[3072,640]{1,0:T(8,128)(2,1)S(1)} %copy-done.2, ...), custom_call_target="tpu_custom_call", output_to_operand_aliasing={{1}: (7, {}), {2}: (8, {})} | custom-call | flops 8000000 | bytes 12000000 | tf_op jit(solution)/shard_map/pallas_call | solution.py:408
  195.0 3.7 %shard_map.109 = (bf16[3072,256]{1,0:T(8,128)(2,1)S(1)}, bf16[4,256,640]{2,1,0:T(8,128)(2,1)}, f32[8192,3072]{1,0:T(8,128)}) custom-call(s32[2]{0:T(128)S(1)} %pad_add_fusion.kc_ref, bf16[1,3072]{1,0:T(2,128)(2,1)S(1)} %reshape.91.g_ref, bf16[3072,640]{1,0:T(8,128)(2,1)S(1)} %copy-done.2, ...), custom_call_target="tpu_custom_call", output_to_operand_aliasing={{1}: (7, {}), {2}: (8, {})} | custom-call | flops 8000000 | bytes 12000000 | tf_op jit(solution)/shard_map/pallas_call | solution.py:408
  198.8 7.2 %dw.1 = f32[3072,640]{1,0:T(8,128)} custom-call(s32[1]{0:T(128)} %bitcast.1.c_ref, bf16[4,256,640]{2,1,0:T(8,128)(2,1)S(1)} %copy-done.5, bf16[3072,256]{1,0:T(8,128)(2,1)S(1)} %get-tuple-element.95.refs_0_, bf16[3072,256]{1,0:T(8,128)(2,1)S(1)} %get-tuple-element.96.refs_1_, bf16[3072,256]{1,0:T(8,128)(2,1)S(1)} %get-tuple-element.97.refs_2_, ...), custom_call_target="tpu_custom_call" | custom-call | flops 30000000 | bytes 40000000 | tf_op jit(solution)/shard_map/dw/pallas_call | solution.py:423
  206.2 6.2 %put.1 = f32[8192,3072]{1,0:T(8,128)} custom-call(s32[1024]{0:T(1024)S(1)} %get-tuple-element.81.rows_ref, s32[1]{0:T(128)} %bitcast.5.cnt_ref, s32[1,1024]{1,0:T(1,128)S(1)} %bitcast.30, bf16[2,32,3072]{2,1,0:T(8,128)(2,1)S(1)} %copy-done.13, bf16[2,32,3072]{2,1,0:T(8,128)(2,1)S(1)} %copy-done.11, ...), custom_call_target="tpu_custom_call", output_to_operand_aliasing={{}: (19, {})} | custom-call | tf_op jit(solution)/shard_map/put/pallas_call | solution.py:450
  (183 shorter events, 30.2 us)
Async XLA Ops:
  4.2 30.6 %collective-permute-start = (bf16[4,32,1536]{2,1,0:T(8,128)(2,1)}, bf16[4,32,1536]{2,1,0:T(8,128)(2,1)}, u32[]{:S(2)}, u32[]{:S(2)}) collective-permute-start(bf16[4,32,1536]{2,1,0:T(8,128)(2,1)} %get-tuple-element.52), channel_id=1, source_target_pairs={{0,2},{1,3},{2,0},{3,1},{4,6},{5,7},{6,4},{7,5}} | collective-permute-start | bytes 1179656 | tf_op jit(solution)/shard_map/ppermute | solution.py:242
  11.1 25.3 %collective-permute-start.1 = (bf16[4,32,1536]{2,1,0:T(8,128)(2,1)}, bf16[4,32,1536]{2,1,0:T(8,128)(2,1)}, u32[]{:S(2)}, u32[]{:S(2)}) collective-permute-start(bf16[4,32,1536]{2,1,0:T(8,128)(2,1)} %get-tuple-element.53), channel_id=1, source_target_pairs={{0,2},{1,3},{2,0},{3,1},{4,6},{5,7},{6,4},{7,5}} | collective-permute-start | bytes 1179656 | tf_op jit(solution)/shard_map/ppermute | solution.py:242
  11.3 25.1 %collective-permute-start.2 = (bf16[4,32,1536]{2,1,0:T(8,128)(2,1)}, bf16[4,32,1536]{2,1,0:T(8,128)(2,1)}, u32[]{:S(2)}, u32[]{:S(2)}) collective-permute-start(bf16[4,32,1536]{2,1,0:T(8,128)(2,1)} %get-tuple-element.54), channel_id=1, source_target_pairs={{0,4},{1,5},{2,6},{3,7},{4,0},{5,1},{6,2},{7,3}} | collective-permute-start | bytes 1179656 | tf_op jit(solution)/shard_map/ppermute | solution.py:242
  13.5 23.0 %collective-permute-start.3 = (bf16[4,32,1536]{2,1,0:T(8,128)(2,1)}, bf16[4,32,1536]{2,1,0:T(8,128)(2,1)}, u32[]{:S(2)}, u32[]{:S(2)}) collective-permute-start(bf16[4,32,1536]{2,1,0:T(8,128)(2,1)} %get-tuple-element.55), channel_id=1, source_target_pairs={{0,4},{1,5},{2,6},{3,7},{4,0},{5,1},{6,2},{7,3}} | collective-permute-start | bytes 1179656 | tf_op jit(solution)/shard_map/ppermute | solution.py:242
  20.8 49.9 %collective-permute-start.26 = (bf16[4,32,3072]{2,1,0:T(8,128)(2,1)}, bf16[4,32,3072]{2,1,0:T(8,128)(2,1)}, u32[]{:S(2)}, u32[]{:S(2)}) collective-permute-start(bf16[4,32,3072]{2,1,0:T(8,128)(2,1)} %get-tuple-element.85), channel_id=1, source_target_pairs={{0,2},{1,3},{2,0},{3,1},{4,6},{5,7},{6,4},{7,5}} | collective-permute-start | bytes 2359304 | tf_op jit(solution)/shard_map/ppermute | solution.py:242
  34.9 36.6 %collective-permute-start.29 = (bf16[4,32,3072]{2,1,0:T(8,128)(2,1)S(1)}, bf16[4,32,3072]{2,1,0:T(8,128)(2,1)}, u32[]{:S(2)}, u32[]{:S(2)}) collective-permute-start(bf16[4,32,3072]{2,1,0:T(8,128)(2,1)S(1)} %copy-done.31), channel_id=1, source_target_pairs={{0,4},{1,5},{2,6},{3,7},{4,0},{5,1},{6,2},{7,3}} | collective-permute-start | bytes 2359304 | tf_op jit(solution)/shard_map/ppermute | solution.py:242
  49.6 10.4 %collective-permute-start.4 = (bf16[3,4,64,1536]{3,2,1,0:T(8,128)(2,1)S(1)}, bf16[3,4,64,1536]{3,2,1,0:T(8,128)(2,1)S(1)}, u32[]{:S(2)}, u32[]{:S(2)}) collective-permute-start(bf16[3,4,64,1536]{3,2,1,0:T(8,128)(2,1)S(1)} %get-tuple-element.61), channel_id=1, source_target_pairs={{0,1},{1,0},{2,3},{3,2},{4,5},{5,4},{6,7},{7,6}} | collective-permute-start | bytes 7077896 | tf_op jit(solution)/shard_map/ppermute | solution.py:242
  49.6 5.6 %collective-permute-start.7 = (bf16[1,4,64,1536]{3,2,1,0:T(8,128)(2,1)S(1)}, bf16[1,4,64,1536]{3,2,1,0:T(8,128)(2,1)S(1)}, u32[]{:S(2)}, u32[]{:S(2)}) collective-permute-start(bf16[1,4,64,1536]{3,2,1,0:T(8,128)(2,1)S(1)} %get-tuple-element.65), channel_id=1, source_target_pairs={{0,1},{1,0},{2,3},{3,2},{4,5},{5,4},{6,7},{7,6}} | collective-permute-start | bytes 2359304 | tf_op jit(solution)/shard_map/ppermute | solution.py:242
  51.8 4.6 %collective-permute-start.27 = (f32[4,32,1536]{2,1,0:T(8,128)S(1)}, f32[4,32,1536]{2,1,0:T(8,128)S(1)}, u32[]{:S(2)}, u32[]{:S(2)}) collective-permute-start(f32[4,32,1536]{2,1,0:T(8,128)S(1)} %fusion.14), channel_id=1, source_target_pairs={{0,1},{1,0},{2,3},{3,2},{4,5},{5,4},{6,7},{7,6}} | collective-permute-start | bytes 2359304 | tf_op jit(solution)/shard_map/ppermute | solution.py:242
  56.4 12.0 %collective-permute-start.13 = (bf16[4,32,1536]{2,1,0:T(8,128)(2,1)S(1)}, bf16[4,32,1536]{2,1,0:T(8,128)(2,1)S(1)}, u32[]{:S(2)}, u32[]{:S(2)}) collective-permute-start(bf16[4,32,1536]{2,1,0:T(8,128)(2,1)S(1)} %get-tuple-element.120), channel_id=1, source_target_pairs={{0,4},{1,5},{2,6},{3,7},{4,0},{5,1},{6,2},{7,3}} | collective-permute-start | bytes 1179656 | tf_op jit(solution)/shard_map/ppermute | solution.py:242
  57.8 11.5 %collective-permute-start.8 = (bf16[4,32,1536]{2,1,0:T(8,128)(2,1)S(1)}, bf16[4,32,1536]{2,1,0:T(8,128)(2,1)S(1)}, u32[]{:S(2)}, u32[]{:S(2)}) collective-permute-start(bf16[4,32,1536]{2,1,0:T(8,128)(2,1)S(1)} %get-tuple-element.119), channel_id=1, source_target_pairs={{0,2},{1,3},{2,0},{3,1},{4,6},{5,7},{6,4},{7,5}} | collective-permute-start | bytes 1179656 | tf_op jit(solution)/shard_map/ppermute | solution.py:242
  60.0 25.3 %collective-permute-start.28 = (f32[4,32,1536]{2,1,0:T(8,128)S(1)}, f32[4,32,1536]{2,1,0:T(8,128)S(1)}, u32[]{:S(2)}, u32[]{:S(2)}) collective-permute-start(f32[4,32,1536]{2,1,0:T(8,128)S(1)} %select_add_fusion.4), channel_id=1, source_target_pairs={{0,4},{1,5},{2,6},{3,7},{4,0},{5,1},{6,2},{7,3}} | collective-permute-start | bytes 2359304 | tf_op jit(solution)/shard_map/ppermute | solution.py:242
  68.4 20.4 %collective-permute-start.31 = (f32[4,32,1536]{2,1,0:T(8,128)S(1)}, f32[4,32,1536]{2,1,0:T(8,128)S(1)}, u32[]{:S(2)}, u32[]{:S(2)}) collective-permute-start(f32[4,32,1536]{2,1,0:T(8,128)S(1)} %select_add_fusion.3), channel_id=1, source_target_pairs={{0,2},{1,3},{2,0},{3,1},{4,6},{5,7},{6,4},{7,5}} | collective-permute-start | bytes 2359304 | tf_op jit(solution)/shard_map/ppermute | solution.py:242
  69.3 33.8 %collective-permute-start.14 = (bf16[4,32,1536]{2,1,0:T(8,128)(2,1)S(1)}, bf16[4,32,1536]{2,1,0:T(8,128)(2,1)S(1)}, u32[]{:S(2)}, u32[]{:S(2)}) collective-permute-start(bf16[4,32,1536]{2,1,0:T(8,128)(2,1)S(1)} %add_add_fusion), channel_id=1, source_target_pairs={{0,2},{1,3},{2,0},{3,1},{4,6},{5,7},{6,4},{7,5}} | collective-permute-start | bytes 1179656 | tf_op jit(solution)/shard_map/ppermute | solution.py:242
  70.7 32.4 %collective-permute-start.5 = (bf16[4,32,1536]{2,1,0:T(8,128)(2,1)S(1)}, bf16[4,32,1536]{2,1,0:T(8,128)(2,1)S(1)}, u32[]{:S(2)}, u32[]{:S(2)}) collective-permute-start(bf16[4,32,1536]{2,1,0:T(8,128)(2,1)S(1)} %slice_add_fusion.3), channel_id=1, source_target_pairs={{0,2},{1,3},{2,0},{3,1},{4,6},{5,7},{6,4},{7,5}} | collective-permute-start | bytes 1179656 | tf_op jit(solution)/shard_map/ppermute | solution.py:242
  71.5 31.6 %collective-permute-start.6 = (bf16[4,32,1536]{2,1,0:T(8,128)(2,1)S(1)}, bf16[4,32,1536]{2,1,0:T(8,128)(2,1)S(1)}, u32[]{:S(2)}, u32[]{:S(2)}) collective-permute-start(bf16[4,32,1536]{2,1,0:T(8,128)(2,1)S(1)} %slice_add_fusion.2), channel_id=1, source_target_pairs={{0,4},{1,5},{2,6},{3,7},{4,0},{5,1},{6,2},{7,3}} | collective-permute-start | bytes 1179656 | tf_op jit(solution)/shard_map/ppermute | solution.py:242
  85.2 17.9 %collective-permute-start.9 = (bf16[4,32,1536]{2,1,0:T(8,128)(2,1)S(1)}, bf16[4,32,1536]{2,1,0:T(8,128)(2,1)S(1)}, u32[]{:S(2)}, u32[]{:S(2)}) collective-permute-start(bf16[4,32,1536]{2,1,0:T(8,128)(2,1)S(1)} %add_add_fusion.2), channel_id=1, source_target_pairs={{0,4},{1,5},{2,6},{3,7},{4,0},{5,1},{6,2},{7,3}} | collective-permute-start | bytes 1179656 | tf_op jit(solution)/shard_map/ppermute | solution.py:242
  90.9 17.5 %collective-permute-start.32 = (f32[4,32,3072]{2,1,0:T(8,128)S(1)}, f32[4,32,3072]{2,1,0:T(8,128)S(1)}, u32[]{:S(2)}, u32[]{:S(2)}) collective-permute-start(f32[4,32,3072]{2,1,0:T(8,128)S(1)} %broadcast_select_fusion), channel_id=1, source_target_pairs={{0,1},{1,0},{2,3},{3,2},{4,5},{5,4},{6,7},{7,6}} | collective-permute-start | bytes 4718600 | tf_op jit(solution)/shard_map/ppermute | solution.py:242
  103.3 2.6 %collective-permute-start.24 = (bf16[4,32,1536]{2,1,0:T(8,128)(2,1)S(1)}, bf16[4,32,1536]{2,1,0:T(8,128)(2,1)S(1)}, u32[]{:S(2)}, u32[]{:S(2)}) collective-permute-start(bf16[4,32,1536]{2,1,0:T(8,128)(2,1)S(1)} %get-tuple-element.108.refs_0_), channel_id=1, source_target_pairs={{0,1},{1,0},{2,3},{3,2},{4,5},{5,4},{6,7},{7,6}} | collective-permute-start | bytes 1179656 | tf_op jit(solution)/shard_map/ppermute | solution.py:242
  103.4 3.3 %collective-permute-start.25 = (bf16[4,32,1536]{2,1,0:T(8,128)(2,1)S(1)}, bf16[4,32,1536]{2,1,0:T(8,128)(2,1)S(1)}, u32[]{:S(2)}, u32[]{:S(2)}) collective-permute-start(bf16[4,32,1536]{2,1,0:T(8,128)(2,1)S(1)} %get-tuple-element.107.refs_2_), channel_id=1, source_target_pairs={{0,1},{1,0},{2,3},{3,2},{4,5},{5,4},{6,7},{7,6}} | collective-permute-start | bytes 1179656 | tf_op jit(solution)/shard_map/ppermute | solution.py:242
  103.9 12.0 %collective-permute-start.10 = (bf16[4,32,1536]{2,1,0:T(8,128)(2,1)S(1)}, bf16[4,32,1536]{2,1,0:T(8,128)(2,1)S(1)}, u32[]{:S(2)}, u32[]{:S(2)}) collective-permute-start(bf16[4,32,1536]{2,1,0:T(8,128)(2,1)S(1)} %get-tuple-element.108.refs_0_), channel_id=1, source_target_pairs={{0,4},{1,5},{2,6},{3,7},{4,0},{5,1},{6,2},{7,3}} | collective-permute-start | bytes 1179656 | tf_op jit(solution)/shard_map/ppermute | solution.py:242
  105.1 12.0 %collective-permute-start.15 = (bf16[4,32,1536]{2,1,0:T(8,128)(2,1)S(1)}, bf16[4,32,1536]{2,1,0:T(8,128)(2,1)S(1)}, u32[]{:S(2)}, u32[]{:S(2)}) collective-permute-start(bf16[4,32,1536]{2,1,0:T(8,128)(2,1)S(1)} %get-tuple-element.107.refs_2_), channel_id=1, source_target_pairs={{0,2},{1,3},{2,0},{3,1},{4,6},{5,7},{6,4},{7,5}} | collective-permute-start | bytes 1179656 | tf_op jit(solution)/shard_map/ppermute | solution.py:242
  105.9 20.7 %collective-permute-start.19 = (bf16[4,32,1536]{2,1,0:T(8,128)(2,1)S(1)}, bf16[4,32,1536]{2,1,0:T(8,128)(2,1)S(1)}, u32[]{:S(2)}, u32[]{:S(2)}) collective-permute-start(bf16[4,32,1536]{2,1,0:T(8,128)(2,1)S(1)} %get-tuple-element.107.refs_2_), channel_id=1, source_target_pairs={{0,4},{1,5},{2,6},{3,7},{4,0},{5,1},{6,2},{7,3}} | collective-permute-start | bytes 1179656 | tf_op jit(solution)/shard_map/ppermute | solution.py:242
  106.7 20.0 %collective-permute-start.21 = (bf16[4,32,1536]{2,1,0:T(8,128)(2,1)S(1)}, bf16[4,32,1536]{2,1,0:T(8,128)(2,1)S(1)}, u32[]{:S(2)}, u32[]{:S(2)}) collective-permute-start(bf16[4,32,1536]{2,1,0:T(8,128)(2,1)S(1)} %get-tuple-element.108.refs_0_), channel_id=1, source_target_pairs={{0,2},{1,3},{2,0},{3,1},{4,6},{5,7},{6,4},{7,5}} | collective-permute-start | bytes 1179656 | tf_op jit(solution)/shard_map/ppermute | solution.py:242
  112.4 13.4 %collective-permute-start.48 = (f32[3072]{0:T(1024)S(1)}, f32[3072]{0:T(1024)S(1)}, u32[]{:S(2)}, u32[]{:S(2)}) collective-permute-start(f32[3072]{0:T(1024)S(1)} %add.148), channel_id=1, source_target_pairs={{0,2},{1,3},{2,0},{3,1},{4,6},{5,7},{6,4},{7,5}} | collective-permute-start | bytes 36872 | tf_op jit(solution)/shard_map/ppermute | solution.py:242
  115.9 17.2 %collective-permute-start.11 = (bf16[4,32,1536]{2,1,0:T(8,128)(2,1)S(1)}, bf16[4,32,1536]{2,1,0:T(8,128)(2,1)S(1)}, u32[]{:S(2)}, u32[]{:S(2)}) collective-permute-start(bf16[4,32,1536]{2,1,0:T(8,128)(2,1)S(1)} %collective-permute-done.10.refs_0_), channel_id=1, source_target_pairs={{0,2},{1,3},{2,0},{3,1},{4,6},{5,7},{6,4},{7,5}} | collective-permute-start | bytes 1179656 | tf_op jit(solution)/shard_map/ppermute | solution.py:242
  117.1 15.9 %collective-permute-start.16 = (bf16[4,32,1536]{2,1,0:T(8,128)(2,1)S(1)}, bf16[4,32,1536]{2,1,0:T(8,128)(2,1)S(1)}, u32[]{:S(2)}, u32[]{:S(2)}) collective-permute-start(bf16[4,32,1536]{2,1,0:T(8,128)(2,1)S(1)} %collective-permute-done.15.refs_2_), channel_id=1, source_target_pairs={{0,4},{1,5},{2,6},{3,7},{4,0},{5,1},{6,2},{7,3}} | collective-permute-start | bytes 1179656 | tf_op jit(solution)/shard_map/ppermute | solution.py:242
  125.8 6.2 %collective-permute-start.49 = (f32[3072]{0:T(1024)S(1)}, f32[3072]{0:T(1024)S(1)}, u32[]{:S(2)}, u32[]{:S(2)}) collective-permute-start(f32[3072]{0:T(1024)S(1)} %add.149), channel_id=1, source_target_pairs={{0,4},{1,5},{2,6},{3,7},{4,0},{5,1},{6,2},{7,3}} | collective-permute-start | bytes 36872 | tf_op jit(solution)/shard_map/ppermute | solution.py:242
  126.7 6.9 %collective-permute-start.18 = (bf16[4,32,1536]{2,1,0:T(8,128)(2,1)S(1)}, bf16[4,32,1536]{2,1,0:T(8,128)(2,1)S(1)}, u32[]{:S(2)}, u32[]{:S(2)}) collective-permute-start(bf16[4,32,1536]{2,1,0:T(8,128)(2,1)S(1)} %collective-permute-done.10.refs_0_), channel_id=1, source_target_pairs={{0,1},{1,0},{2,3},{3,2},{4,5},{5,4},{6,7},{7,6}} | collective-permute-start | bytes 1179656 | tf_op jit(solution)/shard_map/ppermute | solution.py:242
  126.7 7.6 %collective-permute-start.20 = (bf16[4,32,1536]{2,1,0:T(8,128)(2,1)S(1)}, bf16[4,32,1536]{2,1,0:T(8,128)(2,1)S(1)}, u32[]{:S(2)}, u32[]{:S(2)}) collective-permute-start(bf16[4,32,1536]{2,1,0:T(8,128)(2,1)S(1)} %collective-permute-done.19.refs_2_), channel_id=1, source_target_pairs={{0,1},{1,0},{2,3},{3,2},{4,5},{5,4},{6,7},{7,6}} | collective-permute-start | bytes 1179656 | tf_op jit(solution)/shard_map/ppermute | solution.py:242
  132.1 3.8 %collective-permute-start.22 = (bf16[4,32,1536]{2,1,0:T(8,128)(2,1)S(1)}, bf16[4,32,1536]{2,1,0:T(8,128)(2,1)S(1)}, u32[]{:S(2)}, u32[]{:S(2)}) collective-permute-start(bf16[4,32,1536]{2,1,0:T(8,128)(2,1)S(1)} %collective-permute-done.21.refs_0_), channel_id=1, source_target_pairs={{0,1},{1,0},{2,3},{3,2},{4,5},{5,4},{6,7},{7,6}} | collective-permute-start | bytes 1179656 | tf_op jit(solution)/shard_map/ppermute | solution.py:242
  133.0 4.1 %collective-permute-start.23 = (bf16[4,32,1536]{2,1,0:T(8,128)(2,1)S(1)}, bf16[4,32,1536]{2,1,0:T(8,128)(2,1)S(1)}, u32[]{:S(2)}, u32[]{:S(2)}) collective-permute-start(bf16[4,32,1536]{2,1,0:T(8,128)(2,1)S(1)} %collective-permute-done.15.refs_2_), channel_id=1, source_target_pairs={{0,1},{1,0},{2,3},{3,2},{4,5},{5,4},{6,7},{7,6}} | collective-permute-start | bytes 1179656 | tf_op jit(solution)/shard_map/ppermute | solution.py:242
  133.0 4.9 %collective-permute-start.33 = (bf16[2,32,3072]{2,1,0:T(8,128)(2,1)S(1)}, bf16[2,32,3072]{2,1,0:T(8,128)(2,1)S(1)}, u32[]{:S(2)}, u32[]{:S(2)}) collective-permute-start(bf16[2,32,3072]{2,1,0:T(8,128)(2,1)S(1)} %get-tuple-element.122.refs_0_), channel_id=1, source_target_pairs={{0,1},{1,0},{2,3},{3,2},{4,5},{5,4},{6,7},{7,6}} | collective-permute-start | bytes 1179656 | tf_op jit(solution)/shard_map/ppermute | solution.py:242
  134.3 5.6 %collective-permute-start.34 = (bf16[2,32,3072]{2,1,0:T(8,128)(2,1)S(1)}, bf16[2,32,3072]{2,1,0:T(8,128)(2,1)S(1)}, u32[]{:S(2)}, u32[]{:S(2)}) collective-permute-start(bf16[2,32,3072]{2,1,0:T(8,128)(2,1)S(1)} %get-tuple-element.121.refs_1_), channel_id=1, source_target_pairs={{0,1},{1,0},{2,3},{3,2},{4,5},{5,4},{6,7},{7,6}} | collective-permute-start | bytes 1179656 | tf_op jit(solution)/shard_map/ppermute | solution.py:242
  135.1 12.0 %collective-permute-start.35 = (bf16[2,32,3072]{2,1,0:T(8,128)(2,1)S(1)}, bf16[2,32,3072]{2,1,0:T(8,128)(2,1)S(1)}, u32[]{:S(2)}, u32[]{:S(2)}) collective-permute-start(bf16[2,32,3072]{2,1,0:T(8,128)(2,1)S(1)} %get-tuple-element.122.refs_0_), channel_id=1, source_target_pairs={{0,2},{1,3},{2,0},{3,1},{4,6},{5,7},{6,4},{7,5}} | collective-permute-start | bytes 1179656 | tf_op jit(solution)/shard_map/ppermute | solution.py:242
  135.9 19.3 %collective-permute-start.36 = (bf16[2,32,3072]{2,1,0:T(8,128)(2,1)S(1)}, bf16[2,32,3072]{2,1,0:T(8,128)(2,1)}, u32[]{:S(2)}, u32[]{:S(2)}) collective-permute-start(bf16[2,32,3072]{2,1,0:T(8,128)(2,1)S(1)} %get-tuple-element.121.refs_1_), channel_id=1, source_target_pairs={{0,2},{1,3},{2,0},{3,1},{4,6},{5,7},{6,4},{7,5}} | collective-permute-start | bytes 1179656 | tf_op jit(solution)/shard_map/ppermute | solution.py:242
  137.1 18.8 %collective-permute-start.39 = (bf16[2,32,3072]{2,1,0:T(8,128)(2,1)S(1)}, bf16[2,32,3072]{2,1,0:T(8,128)(2,1)}, u32[]{:S(2)}, u32[]{:S(2)}) collective-permute-start(bf16[2,32,3072]{2,1,0:T(8,128)(2,1)S(1)} %get-tuple-element.122.refs_0_), channel_id=1, source_target_pairs={{0,4},{1,5},{2,6},{3,7},{4,0},{5,1},{6,2},{7,3}} | collective-permute-start | bytes 1179656 | tf_op jit(solution)/shard_map/ppermute | solution.py:242
  138.7 18.0 %collective-permute-start.40 = (bf16[2,32,3072]{2,1,0:T(8,128)(2,1)S(1)}, bf16[2,32,3072]{2,1,0:T(8,128)(2,1)}, u32[]{:S(2)}, u32[]{:S(2)}) collective-permute-start(bf16[2,32,3072]{2,1,0:T(8,128)(2,1)S(1)} %get-tuple-element.121.refs_1_), channel_id=1, source_target_pairs={{0,4},{1,5},{2,6},{3,7},{4,0},{5,1},{6,2},{7,3}} | collective-permute-start | bytes 1179656 | tf_op jit(solution)/shard_map/ppermute | solution.py:242
  140.7 16.8 %collective-permute-start.12 = (bf16[4,32,1536]{2,1,0:T(8,128)(2,1)S(1)}, bf16[4,32,1536]{2,1,0:T(8,128)(2,1)S(1)}, u32[]{:S(2)}, u32[]{:S(2)}) collective-permute-start(bf16[4,32,1536]{2,1,0:T(8,128)(2,1)S(1)} %collective-permute-done.11.refs_0_), channel_id=1, source_target_pairs={{0,1},{1,0},{2,3},{3,2},{4,5},{5,4},{6,7},{7,6}} | collective-permute-start | bytes 1179656 | tf_op jit(solution)/shard_map/ppermute | solution.py:242
  147.1 11.2 %collective-permute-start.17 = (bf16[4,32,1536]{2,1,0:T(8,128)(2,1)S(1)}, bf16[4,32,1536]{2,1,0:T(8,128)(2,1)S(1)}, u32[]{:S(2)}, u32[]{:S(2)}) collective-permute-start(bf16[4,32,1536]{2,1,0:T(8,128)(2,1)S(1)} %collective-permute-done.16.refs_2_), channel_id=1, source_target_pairs={{0,1},{1,0},{2,3},{3,2},{4,5},{5,4},{6,7},{7,6}} | collective-permute-start | bytes 1179656 | tf_op jit(solution)/shard_map/ppermute | solution.py:242
  155.1 4.4 %collective-permute-start.37 = (bf16[2,32,3072]{2,1,0:T(8,128)(2,1)S(1)}, bf16[2,32,3072]{2,1,0:T(8,128)(2,1)S(1)}, u32[]{:S(2)}, u32[]{:S(2)}) collective-permute-start(bf16[2,32,3072]{2,1,0:T(8,128)(2,1)S(1)} %collective-permute-done.35.refs_4_), channel_id=1, source_target_pairs={{0,1},{1,0},{2,3},{3,2},{4,5},{5,4},{6,7},{7,6}} | collective-permute-start | bytes 1179656 | tf_op jit(solution)/shard_map/ppermute | solution.py:242
  155.9 11.8 %collective-permute-start.43 = (bf16[2,32,3072]{2,1,0:T(8,128)(2,1)}, bf16[2,32,3072]{2,1,0:T(8,128)(2,1)}, u32[]{:S(2)}, u32[]{:S(2)}) collective-permute-start(bf16[2,32,3072]{2,1,0:T(8,128)(2,1)} %collective-permute-done.39.refs_8_), channel_id=1, source_target_pairs={{0,2},{1,3},{2,0},{3,1},{4,6},{5,7},{6,4},{7,5}} | collective-permute-start | bytes 1179656 | tf_op jit(solution)/shard_map/ppermute | solution.py:242
  156.7 11.6 %collective-permute-start.44 = (bf16[2,32,3072]{2,1,0:T(8,128)(2,1)}, bf16[2,32,3072]{2,1,0:T(8,128)(2,1)}, u32[]{:S(2)}, u32[]{:S(2)}) collective-permute-start(bf16[2,32,3072]{2,1,0:T(8,128)(2,1)} %collective-permute-done.36.refs_5_), channel_id=1, source_target_pairs={{0,4},{1,5},{2,6},{3,7},{4,0},{5,1},{6,2},{7,3}} | collective-permute-start | bytes 1179656 | tf_op jit(solution)/shard_map/ppermute | solution.py:242
  158.2 47.8 %collective-permute-start.38 = (bf16[2,32,3072]{2,1,0:T(8,128)(2,1)}, bf16[2,32,3072]{2,1,0:T(8,128)(2,1)}, u32[]{:S(2)}, u32[]{:S(2)}) collective-permute-start(bf16[2,32,3072]{2,1,0:T(8,128)(2,1)} %collective-permute-done.36.refs_5_), channel_id=1, source_target_pairs={{0,1},{1,0},{2,3},{3,2},{4,5},{5,4},{6,7},{7,6}} | collective-permute-start | bytes 1179656 | tf_op jit(solution)/shard_map/ppermute | solution.py:242
  159.1 47.0 %collective-permute-start.41 = (bf16[2,32,3072]{2,1,0:T(8,128)(2,1)}, bf16[2,32,3072]{2,1,0:T(8,128)(2,1)}, u32[]{:S(2)}, u32[]{:S(2)}) collective-permute-start(bf16[2,32,3072]{2,1,0:T(8,128)(2,1)} %collective-permute-done.39.refs_8_), channel_id=1, source_target_pairs={{0,1},{1,0},{2,3},{3,2},{4,5},{5,4},{6,7},{7,6}} | collective-permute-start | bytes 1179656 | tf_op jit(solution)/shard_map/ppermute | solution.py:242
  160.3 45.8 %collective-permute-start.42 = (bf16[2,32,3072]{2,1,0:T(8,128)(2,1)}, bf16[2,32,3072]{2,1,0:T(8,128)(2,1)}, u32[]{:S(2)}, u32[]{:S(2)}) collective-permute-start(bf16[2,32,3072]{2,1,0:T(8,128)(2,1)} %collective-permute-done.40.refs_9_), channel_id=1, source_target_pairs={{0,1},{1,0},{2,3},{3,2},{4,5},{5,4},{6,7},{7,6}} | collective-permute-start | bytes 1179656 | tf_op jit(solution)/shard_map/ppermute | solution.py:242
  167.7 38.3 %collective-permute-start.45 = (bf16[2,32,3072]{2,1,0:T(8,128)(2,1)}, bf16[2,32,3072]{2,1,0:T(8,128)(2,1)}, u32[]{:S(2)}, u32[]{:S(2)}) collective-permute-start(bf16[2,32,3072]{2,1,0:T(8,128)(2,1)} %collective-permute-done.43.refs_12_), channel_id=1, source_target_pairs={{0,1},{1,0},{2,3},{3,2},{4,5},{5,4},{6,7},{7,6}} | collective-permute-start | bytes 1179656 | tf_op jit(solution)/shard_map/ppermute | solution.py:242
  168.3 37.8 %collective-permute-start.46 = (bf16[2,32,3072]{2,1,0:T(8,128)(2,1)}, bf16[2,32,3072]{2,1,0:T(8,128)(2,1)}, u32[]{:S(2)}, u32[]{:S(2)}) collective-permute-start(bf16[2,32,3072]{2,1,0:T(8,128)(2,1)} %collective-permute-done.44.refs_13_), channel_id=1, source_target_pairs={{0,1},{1,0},{2,3},{3,2},{4,5},{5,4},{6,7},{7,6}} | collective-permute-start | bytes 1179656 | tf_op jit(solution)/shard_map/ppermute | solution.py:242
  (38 other events, 217.8 us)

commit v9 on v5

--- a/solution.py
+++ b/solution.py
@@ -14,7 +14,7 @@
 HBM = pl.BlockSpec(memory_space=pltpu.HBM)
 ZR = 128
 BLK = 256
-LOOKUP_EARLY, LOOKUP_SHARE, ZERO_A, ZERO_B, NORM_SHARE = 8, 22, 33, 48, 3
+LOOKUP_EARLY, LOOKUP_SHARE, ZERO_A, ZERO_B, NORM_SHARE = 8, 22, 34, 52, 3
 
 
 def zero_fill(de, z, sem, first, last):
@@ -50,12 +50,14 @@
     rows_in = pltpu.make_async_copy(du_hbm.at[:, pl.ds(z, tc), :], du_ref, sem)
     rows_in.start()
     loads = [pltpu.make_async_copy(w_hbm.at[pl.ds(n * wc, wc)], w_ref.at[pl.ds(n * wc, wc)], wsem.at[n]) for n in range(steps)]
-    for cp in loads:
+    for cp in loads[:3]:
         cp.start()
     rows_in.wait()
     rows = du_ref[...].reshape(mb * tc, du_ref.shape[2])
     for n in range(steps):
         loads[n].wait()
+        if n + 3 < steps:
+            loads[n + 3].start()
         cols = slice(n * wc, (n + 1) * wc)
         v = lax.dot_general(rows, w_ref[cols, :], (((1,), (1,)), ((), ())), preferred_element_type=jnp.float32)
         v = v.astype(jnp.bfloat16).reshape(mb, tc, wc)
@@ -200,33 +202,39 @@
     wait()
 
 
-def scatter_kernel(me_ref, rows_ref, cnt_ref, slot_ref, *refs):
-    blocks, (de, buf, stage, out_sem) = refs[:16], refs[-4:]
-    mb, t, d = buf.shape
-    hb, tl = blocks[0].shape[:2]
-    for i, b in enumerate(blocks):
-        at = pl.ds(pl.multiple_of(jnp.bitwise_xor(me_ref[0], i // 2) * tl, tl), tl)
-        for m in range(hb):
-            buf[(i % 2) * hb + m, at, :] = b[m]
+def scatter_kernel(rows_ref, cnt_ref, slot_ref, *refs):
+    blocks, (de, stage, out_sem) = refs[:16], refs[-3:]
+    hb, tl, d = blocks[0].shape
+    kb = hb * tl
     cnt = cnt_ref[0]
     cc = 512
 
-    def copy(q, r):
-        return pltpu.make_async_copy(stage.at[pl.ds(q, 1)], de.at[pl.ds(r, 1)], out_sem)
+    def copy(q, r, size=1):
+        return pltpu.make_async_copy(stage.at[pl.ds(q, size)], de.at[pl.ds(r, size)], out_sem)
 
     @pl.loop(0, (cnt + BLK - 1) // BLK)
     def _(b):
         base = b * BLK
-        ids = lax.broadcasted_iota(jnp.int32, (BLK, mb * t), 0) + base
+        ids = lax.broadcasted_iota(jnp.int32, (BLK, len(blocks) * kb), 0) + base
         oh = (ids == slot_ref[...]).astype(jnp.bfloat16)
         for i in range(d // cc):
-            acc = jnp.zeros((BLK, cc), jnp.float32)
-            for m in range(mb):
-                acc += jnp.dot(oh[:, m * t:(m + 1) * t], buf[m, :, i * cc:(i + 1) * cc], preferred_element_type=jnp.float32)
-            stage[:, i * cc:(i + 1) * cc] = acc
+            cols = slice(i * cc, (i + 1) * cc)
+            right = jnp.concatenate([v[:, :, cols].reshape(kb, cc) for v in blocks], axis=0)
+            stage[:, cols] = jnp.dot(oh, right, preferred_element_type=jnp.float32)
         n = jnp.minimum(cnt - base, BLK)
-        pl.loop(0, n)(lambda q: copy(q, rows_ref[base + q]).start())
-        pl.loop(0, n)(lambda q: copy(q, rows_ref[base + q]).wait())
+        full = n // 8
+
+        @pl.loop(0, full)
+        def _(i):
+            for u in range(8):
+                copy(i * 8 + u, rows_ref[base + i * 8 + u]).start()
+
+        pl.loop(full * 8, n)(lambda q: copy(q, rows_ref[base + q]).start())
+        for bit in range(9):
+
+            @pl.when((n >> bit) & 1 == 1)
+            def _():
+                copy(0, 0, 1 << bit).wait()
 
 
 def solution(mesh):
@@ -245,7 +253,6 @@
         tc = t // 4
         k, c = r & 1, r >> 1
         gf = g.astype(jnp.float32)
-        me = r.reshape(1)
         kc = jnp.stack([k, c]).astype(jnp.int32)
         de_shape = jax.ShapeDtypeStruct((vl, d), jnp.float32)
         zero_scratch = [pltpu.VMEM((ZR, d), jnp.float32), pltpu.SemaphoreType.DMA]
@@ -325,13 +332,22 @@
         tgt = jnp.where(own, 2 * (jnp.arange(n) % tc) + (loc & 1), -1).astype(jnp.int32)
         i0 = lax.broadcasted_iota(jnp.int32, (n, n), 0)
         i1 = lax.broadcasted_iota(jnp.int32, (n, n), 1)
-        same = flat[:, None] == flat[None, :]
-        first = jnp.min(jnp.where(same, i0, n), axis=0)
-        lead = own & (first == jnp.arange(n))
+
+        def by_piece(v):
+            v = v.reshape(mb, 2, 2, 2, tl)
+            for ax, bit in ((1, 4), (2, 2), (3, 1)):
+                v = jnp.where((r & bit) > 0, jnp.flip(v, ax), v)
+            return v.reshape(2, mb // 2, groups, tl).transpose(2, 0, 1, 3).reshape(-1)
+
+        flat_p = by_piece(ids)
+        loc_p = flat_p - r * vl
+        own_p = (loc_p >= 0) & (loc_p < vl)
+        first = jnp.min(jnp.where(flat_p[:, None] == flat_p[None, :], i0, n), axis=0)
+        lead = own_p & (first == jnp.arange(n))
         pos = jnp.sum(jnp.where(lead[:, None] & (i0 < i1), 1, 0), axis=0)
         pos_of_first = jnp.sum(jnp.where((i0 == first[None, :]), pos[:, None], 0), axis=0)
-        slot = jnp.where(own, pos_of_first, -1).astype(jnp.int32)
-        rows = jnp.sum(jnp.where(lead[:, None] & (pos[:, None] == i1), loc[:, None], 0), axis=0).astype(jnp.int32)
+        slot = jnp.where(own_p, pos_of_first, -1).astype(jnp.int32)
+        rows = jnp.sum(jnp.where(lead[:, None] & (pos[:, None] == i1), loc_p[:, None], 0), axis=0).astype(jnp.int32)
         cnt = jnp.sum(lead.astype(jnp.int32)).reshape(1)
         n_owned = jnp.sum(own.astype(jnp.int32)).reshape(1)
         own_pos = jnp.sum(jnp.where(own[:, None] & (i0 < i1), 1, 0), axis=0)
@@ -429,17 +445,16 @@
         de = pl.pallas_call(
             scatter_kernel,
             out_shape=de_shape,
-            in_specs=[SMEM, SMEM, SMEM, VMEM] + [VMEM] * 16 + [ANY],
+            in_specs=[SMEM, SMEM, VMEM] + [VMEM] * 16 + [ANY],
             out_specs=ANY,
             scratch_shapes=[
-                pltpu.VMEM((mb, t, d), jnp.bfloat16),
                 pltpu.VMEM((BLK, d), jnp.float32),
                 pltpu.SemaphoreType.DMA,
             ],
-            input_output_aliases={20: 0},
+            input_output_aliases={19: 0},
             compiler_params=pltpu.CompilerParams(vmem_limit_bytes=28 * 2**20),
             name="put",
-        )(me, rows, cnt, slot.reshape(1, n), *dxs, de)
+        )(rows, cnt, slot.reshape(1, n), *dxs, de)
         return u, x, de, dw, dg
 
     return jax.shard_map(

time: 211 us -> 210 us (level)
  transfers between devices with their start and end apart: 48 -> 48, of which waited for: 23 -> 22; matrix products, arithmetic and copies ran while one was open for 7% -> 7% of each run, Pallas kernels for 27% -> 27%
where the time goes in v9:
time: 210 us; the launch traced here: 209 us
  waiting for transfers between devices  80 us (38%)
  Pallas kernels  68.6 us (33%)
  starting transfers between devices  28.4 us (14%)
  local copies, waits for them, and re-layouts  15.7 us (7%)
  other arithmetic  14.7 us (7%)
    ppermute x48, waiting for transfers between devices, swap(): return lax.ppermute(v, 'tp', [(i, i ^ bit) for i in range(groups)])  80 us
    ppermute x48, starting transfers between devices, swap(): return lax.ppermute(v, 'tp', [(i, i ^ bit) for i in range(groups)])  28.4 us
    pallas_call x2, Pallas kernels, local(): pl.pallas_call(functools.partial(zero_kernel, first, last), out_shape=de_...  16.7 us
    unnamed x85, local copies, waits for them, and re-layouts  14.8 us
    pallas_call x4, Pallas kernels, local(): pl.pallas_call(functools.partial(norm_kernel, j), out_shape=(jax.ShapeDty...  14.7 us
    pallas_call x1, Pallas kernels, local(): pl.pallas_call(lookup_kernel, out_shape=(half_shape(4), half_shape(1), ha...  13.6 us
    pallas_call x1, Pallas kernels, local(): pl.pallas_call(dw_kernel, out_shape=(jax.ShapeDtypeStruct((d, f), jnp.flo...  7.23 us
    pallas_call x1, Pallas kernels, local(): pl.pallas_call(scatter_kernel, out_shape=de_shape, in_specs=[SMEM, SMEM,...  6.1 us
  transfers between devices with their start and end apart: 48, of which 22 were waited for; matrix products, arithmetic and copies ran while one was open for 7% of the time, Pallas kernels for 27%

profile of v9, /device:TPU:0, one launch (start us, length us, event | category | flops | bytes accessed | tf_op | source)
XLA Modules:
  0.0 209.1 jit_solution(16852841834360591172)
XLA Ops:
  0.6 5.3 %pa.1 = (bf16[4,32,3072]{2,1,0:T(8,128)(2,1)}, bf16[4,32,3072]{2,1,0:T(8,128)(2,1)}) custom-call(s32[1]{0:T(128)} %bitcast.1.c_ref, bf16[4,256,640]{2,1,0:T(8,128)(2,1)} %du_ref.5, bf16[3072,640]{1,0:T(8,128)(2,1)} %w_ref.11), custom_call_target="tpu_custom_call" | custom-call | flops 5000000 | bytes 8000000 | tf_op jit(solution)/shard_map/pa/pallas_call | solution.py:313
  5.9 3.3 %collective-permute-start = (bf16[4,32,3072]{2,1,0:T(8,128)(2,1)}, bf16[4,32,3072]{2,1,0:T(8,128)(2,1)}, u32[]{:S(2)}, u32[]{:S(2)}) collective-permute-start(bf16[4,32,3072]{2,1,0:T(8,128)(2,1)} %get-tuple-element.50), channel_id=1, source_target_pairs={{0,2},{1,3},{2,0},{3,1},{4,6},{5,7},{6,4},{7,5}} | collective-permute-start | bytes 2359304 | tf_op jit(solution)/shard_map/ppermute | solution.py:244
  9.2 1.5 collective-permute-start.1
  10.8 1.3 copy-done.3
  12.1 3.6 %shard_map.108 = (bf16[4,32,3072]{2,1,0:T(8,128)(2,1)}, bf16[4,32,3072]{2,1,0:T(8,128)(2,1)S(1)}, bf16[4,32,3072]{2,1,0:T(8,128)(2,1)S(1)}, bf16[4,32,3072]{2,1,0:T(8,128)(2,1)}) custom-call(s32[1]{0:T(128)} %bitcast.1.c_ref, bf16[4,256,640]{2,1,0:T(8,128)(2,1)S(1)} %copy-done.3, bf16[3072,640]{1,0:T(8,128)(2,1)S(1)} %copy-done), custom_call_target="tpu_custom_call" | custom-call | flops 10000000 | bytes 8000000 | tf_op jit(solution)/shard_map/pallas_call | solution.py:264
  16.6 0.9 copy-done.12
  19.7 2.1 %copy-done.1 = bf16[3072,640]{1,0:T(8,128)(2,1)S(1)} copy-done((bf16[3072,640]{1,0:T(8,128)(2,1)S(1)}, bf16[3072,640]{1,0:T(8,128)(2,1)}, u32[]{:S(2)}) %copy-start.1) | copy-done | bytes 3932184
  21.8 1.3 copy-done.4
  23.2 1.4 shard_map.107
  25.8 2.9 %select_reduce_fusion.2 = (s32[1024]{0:T(1024)S(1)}, s32[1024]{0:T(1024)S(1)}, s32[1024]{0:T(1024)S(1)}) fusion(s32[1024]{0:T(1024)S(1)} %get-tuple-element.107, s32[1024]{0:T(1024)S(1)} %select_reduce_fusion.4, pred[1024]{0:T(1024)(128)(4,1)S(1)} %get-tuple-element.105, s32[1024]{0:T(1024)S(1)} %select_reduce_fusion.5, s32[1024]{0:T(1024)S(1)} %select_reduce_fusion.1, ...), kind=kLoop, calls=%fused_computation.3 | loop fusion | flops 11531264 | bytes 30720 | tf_op jit(solution)/shard_map/reduce_sum | solution.py:350
  28.7 1.3 collective-permute-done.1
  30.2 13.6 %look.1 = (bf16[4,4,64,1536]{3,2,1,0:T(8,128)(2,1)S(1)}, bf16[1,4,64,1536]{3,2,1,0:T(8,128)(2,1)S(1)}, bf16[3,4,64,1536]{3,2,1,0:T(8,128)(2,1)S(1)}, f32[8192,3072]{1,0:T(8,128)}) custom-call(s32[2]{0:T(128)S(1)} %pad_add_fusion.kc_ref, s32[1024]{0:T(1024)S(1)} %get-tuple-element.52.list_ref, s32[1]{0:T(128)} %bitcast.6.cnt_ref, s32[1024]{0:T(1024)S(1)} %bitcast.29, ...), custom_call_target="tpu_custom_call" | custom-call | flops 40000000 | bytes 60000000 | tf_op jit(solution)/shard_map/look/pallas_call | solution.py:364
  45.0 1.3 convert_add_fusion.1
  46.4 1.0 copy-done.11
  47.4 1.3 convert_add_fusion
  49.0 1.9 collective-permute-done.25
  52.7 1.5 collective-permute-start.26
  54.3 7.7 %collective-permute-done.6 = bf16[4,32,1536]{2,1,0:T(8,128)(2,1)S(1)} collective-permute-done((bf16[4,32,1536]{2,1,0:T(8,128)(2,1)S(1)}, bf16[4,32,1536]{2,1,0:T(8,128)(2,1)S(1)}, u32[]{:S(2)}, u32[]{:S(2)}) %collective-permute-start.6) | collective-permute-done | bytes 393248 | tf_op jit(solution)/shard_map/ppermute | solution.py:244
  62.8 1.2 collective-permute-done.11
  64.7 1.5 collective-permute-start.4
  66.2 1.1 collective-permute-start.3
  67.2 13.6 %collective-permute-done.26 = f32[4,32,1536]{2,1,0:T(8,128)S(1)} collective-permute-done((f32[4,32,1536]{2,1,0:T(8,128)S(1)}, f32[4,32,1536]{2,1,0:T(8,128)S(1)}, u32[]{:S(2)}, u32[]{:S(2)}) %collective-permute-start.26) | collective-permute-done | bytes 786464 | tf_op jit(solution)/shard_map/ppermute | solution.py:244
  80.8 1.1 collective-permute-start.12
  82.5 1.8 broadcast_select_fusion
  84.3 12.6 %collective-permute-done.4 = bf16[4,32,1536]{2,1,0:T(8,128)(2,1)S(1)} collective-permute-done((bf16[4,32,1536]{2,1,0:T(8,128)(2,1)S(1)}, bf16[4,32,1536]{2,1,0:T(8,128)(2,1)S(1)}, u32[]{:S(2)}, u32[]{:S(2)}) %collective-permute-start.4) | collective-permute-done | bytes 393248 | tf_op jit(solution)/shard_map/ppermute | solution.py:244
  99.0 1.3 collective-permute-start.13
  100.9 1.5 collective-permute-start.17
  102.8 2.5 %fusion.12 = (f32[3072]{0:T(1024)S(1)}, f32[4,32]{1,0:T(4,128)S(1)}, f32[4,32,3072]{2,1,0:T(8,128)S(1)}) fusion(bf16[4,32,3072]{2,1,0:T(8,128)(2,1)S(1)} %get-tuple-element.101, f32[4,32]{1,0:T(4,128)S(1)} %add_rsqrt_fusion, f32[3072]{0:T(1024)S(1)} %convert_element_type.48, f32[4,32,3072]{2,1,0:T(8,128)S(1)} %collective-permute-done.30, ...), kind=kLoop, calls=%fused_computation.24 | loop fusion | flops 7467904 | bytes 8676353 | tf_op jit(solution)/shard_map/reduce_sum | solution.py:439
  105.4 1.2 collective-permute-done.45
  107.8 2.5 %collective-permute-done.19.refs_0_ = bf16[4,32,1536]{2,1,0:T(8,128)(2,1)S(1)} collective-permute-done((bf16[4,32,1536]{2,1,0:T(8,128)(2,1)S(1)}, bf16[4,32,1536]{2,1,0:T(8,128)(2,1)S(1)}, u32[]{:S(2)}, u32[]{:S(2)}) %collective-permute-start.19) | collective-permute-done | bytes 393248 | tf_op jit(solution)/shard_map/ppermute | solution.py:244
  110.3 7.6 %collective-permute-done.13.refs_2_ = bf16[4,32,1536]{2,1,0:T(8,128)(2,1)S(1)} collective-permute-done((bf16[4,32,1536]{2,1,0:T(8,128)(2,1)S(1)}, bf16[4,32,1536]{2,1,0:T(8,128)(2,1)S(1)}, u32[]{:S(2)}, u32[]{:S(2)}) %collective-permute-start.13) | collective-permute-done | bytes 393248 | tf_op jit(solution)/shard_map/ppermute | solution.py:244
  120.0 1.7 collective-permute-done.47
  123.7 1.5 collective-permute-start.37
  126.0 1.3 collective-permute-start.34
  128.8 5.0 %collective-permute-done.9.refs_0_ = bf16[4,32,1536]{2,1,0:T(8,128)(2,1)S(1)} collective-permute-done((bf16[4,32,1536]{2,1,0:T(8,128)(2,1)S(1)}, bf16[4,32,1536]{2,1,0:T(8,128)(2,1)S(1)}, u32[]{:S(2)}, u32[]{:S(2)}) %collective-permute-start.9) | collective-permute-done | bytes 393248 | tf_op jit(solution)/shard_map/ppermute | solution.py:244
  135.2 8.5 %collective-permute-done.37.refs_8_ = bf16[2,32,3072]{2,1,0:T(8,128)(2,1)} collective-permute-done((bf16[2,32,3072]{2,1,0:T(8,128)(2,1)S(1)}, bf16[2,32,3072]{2,1,0:T(8,128)(2,1)}, u32[]{:S(2)}, u32[]{:S(2)}) %collective-permute-start.37) | collective-permute-done | bytes 393248 | tf_op jit(solution)/shard_map/ppermute | solution.py:244
  145.0 3.9 %collective-permute-done.33.refs_4_ = bf16[2,32,3072]{2,1,0:T(8,128)(2,1)S(1)} collective-permute-done((bf16[2,32,3072]{2,1,0:T(8,128)(2,1)S(1)}, bf16[2,32,3072]{2,1,0:T(8,128)(2,1)S(1)}, u32[]{:S(2)}, u32[]{:S(2)}) %collective-permute-start.33) | collective-permute-done | bytes 393248 | tf_op jit(solution)/shard_map/ppermute | solution.py:244
  150.1 1.3 collective-permute-start.41
  154.9 6.6 %collective-permute-done.41.refs_12_ = bf16[2,32,3072]{2,1,0:T(8,128)(2,1)} collective-permute-done((bf16[2,32,3072]{2,1,0:T(8,128)(2,1)}, bf16[2,32,3072]{2,1,0:T(8,128)(2,1)}, u32[]{:S(2)}, u32[]{:S(2)}) %collective-permute-start.41) | collective-permute-done | bytes 393248 | tf_op jit(solution)/shard_map/ppermute | solution.py:244
  161.5 1.1 collective-permute-done.42.refs_13_
  163.2 6.6 %shard_map.101.de_in = f32[8192,3072]{1,0:T(8,128)} custom-call(f32[8192,3072]{1,0:T(8,128)} %get-tuple-element.69.de_in), custom_call_target="tpu_custom_call", output_to_operand_aliasing={{}: (0, {})} | custom-call | flops 10000000 | bytes 20000000 | tf_op jit(solution)/shard_map/pallas_call | solution.py:375
  169.8 10.1 %shard_map.102.refs_4_ = f32[8192,3072]{1,0:T(8,128)} custom-call(f32[8192,3072]{1,0:T(8,128)} %shard_map.101.de_in), custom_call_target="tpu_custom_call", output_to_operand_aliasing={{}: (0, {})} | custom-call | flops 10000000 | bytes 20000000 | tf_op jit(solution)/shard_map/pallas_call | solution.py:375
  179.9 3.6 %shard_map.103 = (bf16[3072,256]{1,0:T(8,128)(2,1)S(1)}, bf16[4,256,640]{2,1,0:T(8,128)(2,1)}, f32[8192,3072]{1,0:T(8,128)}) custom-call(s32[2]{0:T(128)S(1)} %pad_add_fusion.kc_ref, bf16[1,3072]{1,0:T(2,128)(2,1)S(1)} %reshape.90.g_ref, bf16[3072,640]{1,0:T(8,128)(2,1)S(1)} %copy-done.2, ...), custom_call_target="tpu_custom_call", output_to_operand_aliasing={{2}: (7, {})} | custom-call | flops 8000000 | bytes 12000000 | tf_op jit(solution)/shard_map/pallas_call | solution.py:402
  184.2 3.6 %shard_map.104 = (bf16[3072,256]{1,0:T(8,128)(2,1)S(1)}, bf16[4,256,640]{2,1,0:T(8,128)(2,1)}, f32[8192,3072]{1,0:T(8,128)}) custom-call(s32[2]{0:T(128)S(1)} %pad_add_fusion.kc_ref, bf16[1,3072]{1,0:T(2,128)(2,1)S(1)} %reshape.90.g_ref, bf16[3072,640]{1,0:T(8,128)(2,1)S(1)} %copy-done.2, ...), custom_call_target="tpu_custom_call", output_to_operand_aliasing={{1}: (7, {}), {2}: (8, {})} | custom-call | flops 8000000 | bytes 12000000 | tf_op jit(solution)/shard_map/pallas_call | solution.py:402
  187.9 3.8 %shard_map.105 = (bf16[3072,256]{1,0:T(8,128)(2,1)S(1)}, bf16[4,256,640]{2,1,0:T(8,128)(2,1)}, f32[8192,3072]{1,0:T(8,128)}) custom-call(s32[2]{0:T(128)S(1)} %pad_add_fusion.kc_ref, bf16[1,3072]{1,0:T(2,128)(2,1)S(1)} %reshape.90.g_ref, bf16[3072,640]{1,0:T(8,128)(2,1)S(1)} %copy-done.2, ...), custom_call_target="tpu_custom_call", output_to_operand_aliasing={{1}: (7, {}), {2}: (8, {})} | custom-call | flops 8000000 | bytes 12000000 | tf_op jit(solution)/shard_map/pallas_call | solution.py:402
  191.8 3.6 %shard_map.106 = (bf16[3072,256]{1,0:T(8,128)(2,1)S(1)}, bf16[4,256,640]{2,1,0:T(8,128)(2,1)}, f32[8192,3072]{1,0:T(8,128)}) custom-call(s32[2]{0:T(128)S(1)} %pad_add_fusion.kc_ref, bf16[1,3072]{1,0:T(2,128)(2,1)S(1)} %reshape.90.g_ref, bf16[3072,640]{1,0:T(8,128)(2,1)S(1)} %copy-done.2, ...), custom_call_target="tpu_custom_call", output_to_operand_aliasing={{1}: (7, {}), {2}: (8, {})} | custom-call | flops 8000000 | bytes 12000000 | tf_op jit(solution)/shard_map/pallas_call | solution.py:402
  195.5 7.2 %dw.1 = (f32[3072,640]{1,0:T(8,128)}, f32[8192,3072]{1,0:T(8,128)}) custom-call(s32[1]{0:T(128)} %bitcast.1.c_ref, bf16[4,256,640]{2,1,0:T(8,128)(2,1)S(1)} %copy-done.5, bf16[3072,256]{1,0:T(8,128)(2,1)S(1)} %get-tuple-element.88.refs_0_, bf16[3072,256]{1,0:T(8,128)(2,1)S(1)} %get-tuple-element.89.refs_1_, ...), custom_call_target="tpu_custom_call", output_to_operand_aliasing={{1}: (6, {})} | custom-call | flops 30000000 | bytes 40000000 | tf_op jit(solution)/shard_map/dw/pallas_call | solution.py:417
  202.8 6.1 %put.1 = f32[8192,3072]{1,0:T(8,128)} custom-call(s32[1024]{0:T(1024)S(1)} %get-tuple-element.77.rows_ref, s32[1]{0:T(128)} %bitcast.5.cnt_ref, s32[1,1024]{1,0:T(1,128)S(1)} %bitcast.30, bf16[2,32,3072]{2,1,0:T(8,128)(2,1)S(1)} %copy-done.9, bf16[2,32,3072]{2,1,0:T(8,128)(2,1)S(1)} %copy-done.7, ...), custom_call_target="tpu_custom_call", output_to_operand_aliasing={{}: (19, {})} | custom-call | tf_op jit(solution)/shard_map/put/pallas_call | solution.py:445
  (191 shorter events, 29.0 us)
Async XLA Ops:
  5.9 22.8 %collective-permute-start = (bf16[4,32,3072]{2,1,0:T(8,128)(2,1)}, bf16[4,32,3072]{2,1,0:T(8,128)(2,1)}, u32[]{:S(2)}, u32[]{:S(2)}) collective-permute-start(bf16[4,32,3072]{2,1,0:T(8,128)(2,1)} %get-tuple-element.50), channel_id=1, source_target_pairs={{0,2},{1,3},{2,0},{3,1},{4,6},{5,7},{6,4},{7,5}} | collective-permute-start | bytes 2359304 | tf_op jit(solution)/shard_map/ppermute | solution.py:244
  9.2 20.7 %collective-permute-start.1 = (bf16[4,32,3072]{2,1,0:T(8,128)(2,1)}, bf16[4,32,3072]{2,1,0:T(8,128)(2,1)}, u32[]{:S(2)}, u32[]{:S(2)}) collective-permute-start(bf16[4,32,3072]{2,1,0:T(8,128)(2,1)} %get-tuple-element.51), channel_id=1, source_target_pairs={{0,4},{1,5},{2,6},{3,7},{4,0},{5,1},{6,2},{7,3}} | collective-permute-start | bytes 2359304 | tf_op jit(solution)/shard_map/ppermute | solution.py:244
  17.5 47.2 %collective-permute-start.24 = (bf16[4,32,3072]{2,1,0:T(8,128)(2,1)}, bf16[4,32,3072]{2,1,0:T(8,128)(2,1)S(1)}, u32[]{:S(2)}, u32[]{:S(2)}) collective-permute-start(bf16[4,32,3072]{2,1,0:T(8,128)(2,1)} %get-tuple-element.81), channel_id=1, source_target_pairs={{0,2},{1,3},{2,0},{3,1},{4,6},{5,7},{6,4},{7,5}} | collective-permute-start | bytes 2359304 | tf_op jit(solution)/shard_map/ppermute | solution.py:244
  18.0 48.1 %collective-permute-start.27 = (bf16[4,32,3072]{2,1,0:T(8,128)(2,1)}, bf16[4,32,3072]{2,1,0:T(8,128)(2,1)}, u32[]{:S(2)}, u32[]{:S(2)}) collective-permute-start(bf16[4,32,3072]{2,1,0:T(8,128)(2,1)} %get-tuple-element.85), channel_id=1, source_target_pairs={{0,4},{1,5},{2,6},{3,7},{4,0},{5,1},{6,2},{7,3}} | collective-permute-start | bytes 2359304 | tf_op jit(solution)/shard_map/ppermute | solution.py:244
  44.1 4.8 %collective-permute-start.5 = (bf16[1,4,64,1536]{3,2,1,0:T(8,128)(2,1)S(1)}, bf16[1,4,64,1536]{3,2,1,0:T(8,128)(2,1)S(1)}, u32[]{:S(2)}, u32[]{:S(2)}) collective-permute-start(bf16[1,4,64,1536]{3,2,1,0:T(8,128)(2,1)S(1)} %get-tuple-element.61), channel_id=1, source_target_pairs={{0,1},{1,0},{2,3},{3,2},{4,5},{5,4},{6,7},{7,6}} | collective-permute-start | bytes 2359304 | tf_op jit(solution)/shard_map/ppermute | solution.py:244
  44.1 8.6 %collective-permute-start.2 = (bf16[3,4,64,1536]{3,2,1,0:T(8,128)(2,1)S(1)}, bf16[3,4,64,1536]{3,2,1,0:T(8,128)(2,1)S(1)}, u32[]{:S(2)}, u32[]{:S(2)}) collective-permute-start(bf16[3,4,64,1536]{3,2,1,0:T(8,128)(2,1)S(1)} %get-tuple-element.57), channel_id=1, source_target_pairs={{0,1},{1,0},{2,3},{3,2},{4,5},{5,4},{6,7},{7,6}} | collective-permute-start | bytes 7077896 | tf_op jit(solution)/shard_map/ppermute | solution.py:244
  46.4 4.5 %collective-permute-start.25 = (f32[4,32,1536]{2,1,0:T(8,128)S(1)}, f32[4,32,1536]{2,1,0:T(8,128)S(1)}, u32[]{:S(2)}, u32[]{:S(2)}) collective-permute-start(f32[4,32,1536]{2,1,0:T(8,128)S(1)} %slice_select_fusion.1), channel_id=1, source_target_pairs={{0,1},{1,0},{2,3},{3,2},{4,5},{5,4},{6,7},{7,6}} | collective-permute-start | bytes 2359304 | tf_op jit(solution)/shard_map/ppermute | solution.py:244
  48.9 3.1 %collective-permute-start.28 = (f32[4,32,1536]{2,1,0:T(8,128)S(1)}, f32[4,32,1536]{2,1,0:T(8,128)S(1)}, u32[]{:S(2)}, u32[]{:S(2)}) collective-permute-start(f32[4,32,1536]{2,1,0:T(8,128)S(1)} %slice_select_fusion), channel_id=1, source_target_pairs={{0,1},{1,0},{2,3},{3,2},{4,5},{5,4},{6,7},{7,6}} | collective-permute-start | bytes 2359304 | tf_op jit(solution)/shard_map/ppermute | solution.py:244
  50.9 11.2 %collective-permute-start.6 = (bf16[4,32,1536]{2,1,0:T(8,128)(2,1)S(1)}, bf16[4,32,1536]{2,1,0:T(8,128)(2,1)S(1)}, u32[]{:S(2)}, u32[]{:S(2)}) collective-permute-start(bf16[4,32,1536]{2,1,0:T(8,128)(2,1)S(1)} %get-tuple-element.115), channel_id=1, source_target_pairs={{0,2},{1,3},{2,0},{3,1},{4,6},{5,7},{6,4},{7,5}} | collective-permute-start | bytes 1179656 | tf_op jit(solution)/shard_map/ppermute | solution.py:244
  52.0 12.0 %collective-permute-start.11 = (bf16[4,32,1536]{2,1,0:T(8,128)(2,1)S(1)}, bf16[4,32,1536]{2,1,0:T(8,128)(2,1)S(1)}, u32[]{:S(2)}, u32[]{:S(2)}) collective-permute-start(bf16[4,32,1536]{2,1,0:T(8,128)(2,1)S(1)} %get-tuple-element.116), channel_id=1, source_target_pairs={{0,4},{1,5},{2,6},{3,7},{4,0},{5,1},{6,2},{7,3}} | collective-permute-start | bytes 1179656 | tf_op jit(solution)/shard_map/ppermute | solution.py:244
  52.7 28.1 %collective-permute-start.26 = (f32[4,32,1536]{2,1,0:T(8,128)S(1)}, f32[4,32,1536]{2,1,0:T(8,128)S(1)}, u32[]{:S(2)}, u32[]{:S(2)}) collective-permute-start(f32[4,32,1536]{2,1,0:T(8,128)S(1)} %select_add_fusion.4), channel_id=1, source_target_pairs={{0,4},{1,5},{2,6},{3,7},{4,0},{5,1},{6,2},{7,3}} | collective-permute-start | bytes 2359304 | tf_op jit(solution)/shard_map/ppermute | solution.py:244
  62.0 20.4 %collective-permute-start.29 = (f32[4,32,1536]{2,1,0:T(8,128)S(1)}, f32[4,32,1536]{2,1,0:T(8,128)S(1)}, u32[]{:S(2)}, u32[]{:S(2)}) collective-permute-start(f32[4,32,1536]{2,1,0:T(8,128)S(1)} %select_add_fusion.3), channel_id=1, source_target_pairs={{0,2},{1,3},{2,0},{3,1},{4,6},{5,7},{6,4},{7,5}} | collective-permute-start | bytes 2359304 | tf_op jit(solution)/shard_map/ppermute | solution.py:244
  64.0 32.9 %collective-permute-start.7 = (bf16[4,32,1536]{2,1,0:T(8,128)(2,1)S(1)}, bf16[4,32,1536]{2,1,0:T(8,128)(2,1)S(1)}, u32[]{:S(2)}, u32[]{:S(2)}) collective-permute-start(bf16[4,32,1536]{2,1,0:T(8,128)(2,1)S(1)} %add_add_fusion.2), channel_id=1, source_target_pairs={{0,4},{1,5},{2,6},{3,7},{4,0},{5,1},{6,2},{7,3}} | collective-permute-start | bytes 1179656 | tf_op jit(solution)/shard_map/ppermute | solution.py:244
  64.7 32.2 %collective-permute-start.4 = (bf16[4,32,1536]{2,1,0:T(8,128)(2,1)S(1)}, bf16[4,32,1536]{2,1,0:T(8,128)(2,1)S(1)}, u32[]{:S(2)}, u32[]{:S(2)}) collective-permute-start(bf16[4,32,1536]{2,1,0:T(8,128)(2,1)S(1)} %slice_add_fusion.2), channel_id=1, source_target_pairs={{0,4},{1,5},{2,6},{3,7},{4,0},{5,1},{6,2},{7,3}} | collective-permute-start | bytes 1179656 | tf_op jit(solution)/shard_map/ppermute | solution.py:244
  66.2 30.7 %collective-permute-start.3 = (bf16[4,32,1536]{2,1,0:T(8,128)(2,1)S(1)}, bf16[4,32,1536]{2,1,0:T(8,128)(2,1)S(1)}, u32[]{:S(2)}, u32[]{:S(2)}) collective-permute-start(bf16[4,32,1536]{2,1,0:T(8,128)(2,1)S(1)} %slice_add_fusion.3), channel_id=1, source_target_pairs={{0,2},{1,3},{2,0},{3,1},{4,6},{5,7},{6,4},{7,5}} | collective-permute-start | bytes 1179656 | tf_op jit(solution)/shard_map/ppermute | solution.py:244
  80.8 16.8 %collective-permute-start.12 = (bf16[4,32,1536]{2,1,0:T(8,128)(2,1)S(1)}, bf16[4,32,1536]{2,1,0:T(8,128)(2,1)S(1)}, u32[]{:S(2)}, u32[]{:S(2)}) collective-permute-start(bf16[4,32,1536]{2,1,0:T(8,128)(2,1)S(1)} %add_add_fusion), channel_id=1, source_target_pairs={{0,2},{1,3},{2,0},{3,1},{4,6},{5,7},{6,4},{7,5}} | collective-permute-start | bytes 1179656 | tf_op jit(solution)/shard_map/ppermute | solution.py:244
  84.2 18.5 %collective-permute-start.30 = (f32[4,32,3072]{2,1,0:T(8,128)S(1)}, f32[4,32,3072]{2,1,0:T(8,128)S(1)}, u32[]{:S(2)}, u32[]{:S(2)}) collective-permute-start(f32[4,32,3072]{2,1,0:T(8,128)S(1)} %broadcast_select_fusion), channel_id=1, source_target_pairs={{0,1},{1,0},{2,3},{3,2},{4,5},{5,4},{6,7},{7,6}} | collective-permute-start | bytes 4718600 | tf_op jit(solution)/shard_map/ppermute | solution.py:244
  97.8 2.6 %collective-permute-start.22 = (bf16[4,32,1536]{2,1,0:T(8,128)(2,1)S(1)}, bf16[4,32,1536]{2,1,0:T(8,128)(2,1)S(1)}, u32[]{:S(2)}, u32[]{:S(2)}) collective-permute-start(bf16[4,32,1536]{2,1,0:T(8,128)(2,1)S(1)} %get-tuple-element.104.refs_0_), channel_id=1, source_target_pairs={{0,1},{1,0},{2,3},{3,2},{4,5},{5,4},{6,7},{7,6}} | collective-permute-start | bytes 1179656 | tf_op jit(solution)/shard_map/ppermute | solution.py:244
  97.8 3.1 %collective-permute-start.23 = (bf16[4,32,1536]{2,1,0:T(8,128)(2,1)S(1)}, bf16[4,32,1536]{2,1,0:T(8,128)(2,1)S(1)}, u32[]{:S(2)}, u32[]{:S(2)}) collective-permute-start(bf16[4,32,1536]{2,1,0:T(8,128)(2,1)S(1)} %get-tuple-element.103.refs_2_), channel_id=1, source_target_pairs={{0,1},{1,0},{2,3},{3,2},{4,5},{5,4},{6,7},{7,6}} | collective-permute-start | bytes 1179656 | tf_op jit(solution)/shard_map/ppermute | solution.py:244
  98.3 12.0 %collective-permute-start.19 = (bf16[4,32,1536]{2,1,0:T(8,128)(2,1)S(1)}, bf16[4,32,1536]{2,1,0:T(8,128)(2,1)S(1)}, u32[]{:S(2)}, u32[]{:S(2)}) collective-permute-start(bf16[4,32,1536]{2,1,0:T(8,128)(2,1)S(1)} %get-tuple-element.104.refs_0_), channel_id=1, source_target_pairs={{0,2},{1,3},{2,0},{3,1},{4,6},{5,7},{6,4},{7,5}} | collective-permute-start | bytes 1179656 | tf_op jit(solution)/shard_map/ppermute | solution.py:244
  99.0 18.9 %collective-permute-start.13 = (bf16[4,32,1536]{2,1,0:T(8,128)(2,1)S(1)}, bf16[4,32,1536]{2,1,0:T(8,128)(2,1)S(1)}, u32[]{:S(2)}, u32[]{:S(2)}) collective-permute-start(bf16[4,32,1536]{2,1,0:T(8,128)(2,1)S(1)} %get-tuple-element.103.refs_2_), channel_id=1, source_target_pairs={{0,2},{1,3},{2,0},{3,1},{4,6},{5,7},{6,4},{7,5}} | collective-permute-start | bytes 1179656 | tf_op jit(solution)/shard_map/ppermute | solution.py:244
  100.3 18.4 %collective-permute-start.8 = (bf16[4,32,1536]{2,1,0:T(8,128)(2,1)S(1)}, bf16[4,32,1536]{2,1,0:T(8,128)(2,1)S(1)}, u32[]{:S(2)}, u32[]{:S(2)}) collective-permute-start(bf16[4,32,1536]{2,1,0:T(8,128)(2,1)S(1)} %get-tuple-element.104.refs_0_), channel_id=1, source_target_pairs={{0,4},{1,5},{2,6},{3,7},{4,0},{5,1},{6,2},{7,3}} | collective-permute-start | bytes 1179656 | tf_op jit(solution)/shard_map/ppermute | solution.py:244
  100.9 18.3 %collective-permute-start.17 = (bf16[4,32,1536]{2,1,0:T(8,128)(2,1)S(1)}, bf16[4,32,1536]{2,1,0:T(8,128)(2,1)S(1)}, u32[]{:S(2)}, u32[]{:S(2)}) collective-permute-start(bf16[4,32,1536]{2,1,0:T(8,128)(2,1)S(1)} %get-tuple-element.103.refs_2_), channel_id=1, source_target_pairs={{0,4},{1,5},{2,6},{3,7},{4,0},{5,1},{6,2},{7,3}} | collective-permute-start | bytes 1179656 | tf_op jit(solution)/shard_map/ppermute | solution.py:244
  105.3 1.2 collective-permute-start.45
  106.5 11.5 %collective-permute-start.46 = (f32[3072]{0:T(1024)S(1)}, f32[3072]{0:T(1024)S(1)}, u32[]{:S(2)}, u32[]{:S(2)}) collective-permute-start(f32[3072]{0:T(1024)S(1)} %add.140), channel_id=1, source_target_pairs={{0,2},{1,3},{2,0},{3,1},{4,6},{5,7},{6,4},{7,5}} | collective-permute-start | bytes 36872 | tf_op jit(solution)/shard_map/ppermute | solution.py:244
  110.3 12.9 %collective-permute-start.20 = (bf16[4,32,1536]{2,1,0:T(8,128)(2,1)S(1)}, bf16[4,32,1536]{2,1,0:T(8,128)(2,1)S(1)}, u32[]{:S(2)}, u32[]{:S(2)}) collective-permute-start(bf16[4,32,1536]{2,1,0:T(8,128)(2,1)S(1)} %collective-permute-done.19.refs_0_), channel_id=1, source_target_pairs={{0,1},{1,0},{2,3},{3,2},{4,5},{5,4},{6,7},{7,6}} | collective-permute-start | bytes 1179656 | tf_op jit(solution)/shard_map/ppermute | solution.py:244
  117.9 5.8 %collective-permute-start.21 = (bf16[4,32,1536]{2,1,0:T(8,128)(2,1)S(1)}, bf16[4,32,1536]{2,1,0:T(8,128)(2,1)S(1)}, u32[]{:S(2)}, u32[]{:S(2)}) collective-permute-start(bf16[4,32,1536]{2,1,0:T(8,128)(2,1)S(1)} %collective-permute-done.13.refs_2_), channel_id=1, source_target_pairs={{0,1},{1,0},{2,3},{3,2},{4,5},{5,4},{6,7},{7,6}} | collective-permute-start | bytes 1179656 | tf_op jit(solution)/shard_map/ppermute | solution.py:244
  118.1 3.7 %collective-permute-start.47 = (f32[3072]{0:T(1024)S(1)}, f32[3072]{0:T(1024)S(1)}, u32[]{:S(2)}, u32[]{:S(2)}) collective-permute-start(f32[3072]{0:T(1024)S(1)} %add.141), channel_id=1, source_target_pairs={{0,4},{1,5},{2,6},{3,7},{4,0},{5,1},{6,2},{7,3}} | collective-permute-start | bytes 36872 | tf_op jit(solution)/shard_map/ppermute | solution.py:244
  118.7 6.5 %collective-permute-start.16 = (bf16[4,32,1536]{2,1,0:T(8,128)(2,1)S(1)}, bf16[4,32,1536]{2,1,0:T(8,128)(2,1)S(1)}, u32[]{:S(2)}, u32[]{:S(2)}) collective-permute-start(bf16[4,32,1536]{2,1,0:T(8,128)(2,1)S(1)} %collective-permute-done.8.refs_0_), channel_id=1, source_target_pairs={{0,1},{1,0},{2,3},{3,2},{4,5},{5,4},{6,7},{7,6}} | collective-permute-start | bytes 1179656 | tf_op jit(solution)/shard_map/ppermute | solution.py:244
  119.3 8.0 %collective-permute-start.18 = (bf16[4,32,1536]{2,1,0:T(8,128)(2,1)S(1)}, bf16[4,32,1536]{2,1,0:T(8,128)(2,1)S(1)}, u32[]{:S(2)}, u32[]{:S(2)}) collective-permute-start(bf16[4,32,1536]{2,1,0:T(8,128)(2,1)S(1)} %collective-permute-done.17.refs_2_), channel_id=1, source_target_pairs={{0,1},{1,0},{2,3},{3,2},{4,5},{5,4},{6,7},{7,6}} | collective-permute-start | bytes 1179656 | tf_op jit(solution)/shard_map/ppermute | solution.py:244
  121.8 12.0 %collective-permute-start.9 = (bf16[4,32,1536]{2,1,0:T(8,128)(2,1)S(1)}, bf16[4,32,1536]{2,1,0:T(8,128)(2,1)S(1)}, u32[]{:S(2)}, u32[]{:S(2)}) collective-permute-start(bf16[4,32,1536]{2,1,0:T(8,128)(2,1)S(1)} %collective-permute-done.8.refs_0_), channel_id=1, source_target_pairs={{0,2},{1,3},{2,0},{3,1},{4,6},{5,7},{6,4},{7,5}} | collective-permute-start | bytes 1179656 | tf_op jit(solution)/shard_map/ppermute | solution.py:244
  123.2 12.0 %collective-permute-start.14 = (bf16[4,32,1536]{2,1,0:T(8,128)(2,1)S(1)}, bf16[4,32,1536]{2,1,0:T(8,128)(2,1)S(1)}, u32[]{:S(2)}, u32[]{:S(2)}) collective-permute-start(bf16[4,32,1536]{2,1,0:T(8,128)(2,1)S(1)} %collective-permute-done.13.refs_2_), channel_id=1, source_target_pairs={{0,4},{1,5},{2,6},{3,7},{4,0},{5,1},{6,2},{7,3}} | collective-permute-start | bytes 1179656 | tf_op jit(solution)/shard_map/ppermute | solution.py:244
  123.7 20.0 %collective-permute-start.37 = (bf16[2,32,3072]{2,1,0:T(8,128)(2,1)S(1)}, bf16[2,32,3072]{2,1,0:T(8,128)(2,1)}, u32[]{:S(2)}, u32[]{:S(2)}) collective-permute-start(bf16[2,32,3072]{2,1,0:T(8,128)(2,1)S(1)} %get-tuple-element.118.refs_0_), channel_id=1, source_target_pairs={{0,4},{1,5},{2,6},{3,7},{4,0},{5,1},{6,2},{7,3}} | collective-permute-start | bytes 1179656 | tf_op jit(solution)/shard_map/ppermute | solution.py:244
  126.0 17.8 %collective-permute-start.34 = (bf16[2,32,3072]{2,1,0:T(8,128)(2,1)S(1)}, bf16[2,32,3072]{2,1,0:T(8,128)(2,1)}, u32[]{:S(2)}, u32[]{:S(2)}) collective-permute-start(bf16[2,32,3072]{2,1,0:T(8,128)(2,1)S(1)} %get-tuple-element.117.refs_1_), channel_id=1, source_target_pairs={{0,2},{1,3},{2,0},{3,1},{4,6},{5,7},{6,4},{7,5}} | collective-permute-start | bytes 1179656 | tf_op jit(solution)/shard_map/ppermute | solution.py:244
  128.1 20.8 %collective-permute-start.33 = (bf16[2,32,3072]{2,1,0:T(8,128)(2,1)S(1)}, bf16[2,32,3072]{2,1,0:T(8,128)(2,1)S(1)}, u32[]{:S(2)}, u32[]{:S(2)}) collective-permute-start(bf16[2,32,3072]{2,1,0:T(8,128)(2,1)S(1)} %get-tuple-element.118.refs_0_), channel_id=1, source_target_pairs={{0,2},{1,3},{2,0},{3,1},{4,6},{5,7},{6,4},{7,5}} | collective-permute-start | bytes 1179656 | tf_op jit(solution)/shard_map/ppermute | solution.py:244
  133.8 16.4 %collective-permute-start.38 = (bf16[2,32,3072]{2,1,0:T(8,128)(2,1)S(1)}, bf16[2,32,3072]{2,1,0:T(8,128)(2,1)}, u32[]{:S(2)}, u32[]{:S(2)}) collective-permute-start(bf16[2,32,3072]{2,1,0:T(8,128)(2,1)S(1)} %get-tuple-element.117.refs_1_), channel_id=1, source_target_pairs={{0,4},{1,5},{2,6},{3,7},{4,0},{5,1},{6,2},{7,3}} | collective-permute-start | bytes 1179656 | tf_op jit(solution)/shard_map/ppermute | solution.py:244
  135.2 16.3 %collective-permute-start.31 = (bf16[2,32,3072]{2,1,0:T(8,128)(2,1)S(1)}, bf16[2,32,3072]{2,1,0:T(8,128)(2,1)S(1)}, u32[]{:S(2)}, u32[]{:S(2)}) collective-permute-start(bf16[2,32,3072]{2,1,0:T(8,128)(2,1)S(1)} %get-tuple-element.118.refs_0_), channel_id=1, source_target_pairs={{0,1},{1,0},{2,3},{3,2},{4,5},{5,4},{6,7},{7,6}} | collective-permute-start | bytes 1179656 | tf_op jit(solution)/shard_map/ppermute | solution.py:244
  143.7 9.1 %collective-permute-start.32 = (bf16[2,32,3072]{2,1,0:T(8,128)(2,1)S(1)}, bf16[2,32,3072]{2,1,0:T(8,128)(2,1)S(1)}, u32[]{:S(2)}, u32[]{:S(2)}) collective-permute-start(bf16[2,32,3072]{2,1,0:T(8,128)(2,1)S(1)} %get-tuple-element.117.refs_1_), channel_id=1, source_target_pairs={{0,1},{1,0},{2,3},{3,2},{4,5},{5,4},{6,7},{7,6}} | collective-permute-start | bytes 1179656 | tf_op jit(solution)/shard_map/ppermute | solution.py:244
  143.7 10.6 %collective-permute-start.10 = (bf16[4,32,1536]{2,1,0:T(8,128)(2,1)S(1)}, bf16[4,32,1536]{2,1,0:T(8,128)(2,1)S(1)}, u32[]{:S(2)}, u32[]{:S(2)}) collective-permute-start(bf16[4,32,1536]{2,1,0:T(8,128)(2,1)S(1)} %collective-permute-done.9.refs_0_), channel_id=1, source_target_pairs={{0,1},{1,0},{2,3},{3,2},{4,5},{5,4},{6,7},{7,6}} | collective-permute-start | bytes 1179656 | tf_op jit(solution)/shard_map/ppermute | solution.py:244
  148.9 6.0 %collective-permute-start.15 = (bf16[4,32,1536]{2,1,0:T(8,128)(2,1)S(1)}, bf16[4,32,1536]{2,1,0:T(8,128)(2,1)S(1)}, u32[]{:S(2)}, u32[]{:S(2)}) collective-permute-start(bf16[4,32,1536]{2,1,0:T(8,128)(2,1)S(1)} %collective-permute-done.14.refs_2_), channel_id=1, source_target_pairs={{0,1},{1,0},{2,3},{3,2},{4,5},{5,4},{6,7},{7,6}} | collective-permute-start | bytes 1179656 | tf_op jit(solution)/shard_map/ppermute | solution.py:244
  150.1 11.4 %collective-permute-start.41 = (bf16[2,32,3072]{2,1,0:T(8,128)(2,1)}, bf16[2,32,3072]{2,1,0:T(8,128)(2,1)}, u32[]{:S(2)}, u32[]{:S(2)}) collective-permute-start(bf16[2,32,3072]{2,1,0:T(8,128)(2,1)} %collective-permute-done.37.refs_8_), channel_id=1, source_target_pairs={{0,2},{1,3},{2,0},{3,1},{4,6},{5,7},{6,4},{7,5}} | collective-permute-start | bytes 1179656 | tf_op jit(solution)/shard_map/ppermute | solution.py:244
  152.2 10.4 %collective-permute-start.42 = (bf16[2,32,3072]{2,1,0:T(8,128)(2,1)}, bf16[2,32,3072]{2,1,0:T(8,128)(2,1)}, u32[]{:S(2)}, u32[]{:S(2)}) collective-permute-start(bf16[2,32,3072]{2,1,0:T(8,128)(2,1)} %collective-permute-done.34.refs_5_), channel_id=1, source_target_pairs={{0,4},{1,5},{2,6},{3,7},{4,0},{5,1},{6,2},{7,3}} | collective-permute-start | bytes 1179656 | tf_op jit(solution)/shard_map/ppermute | solution.py:244
  153.6 9.1 %collective-permute-start.35 = (bf16[2,32,3072]{2,1,0:T(8,128)(2,1)S(1)}, bf16[2,32,3072]{2,1,0:T(8,128)(2,1)S(1)}, u32[]{:S(2)}, u32[]{:S(2)}) collective-permute-start(bf16[2,32,3072]{2,1,0:T(8,128)(2,1)S(1)} %collective-permute-done.33.refs_4_), channel_id=1, source_target_pairs={{0,1},{1,0},{2,3},{3,2},{4,5},{5,4},{6,7},{7,6}} | collective-permute-start | bytes 1179656 | tf_op jit(solution)/shard_map/ppermute | solution.py:244
  154.3 48.4 %collective-permute-start.36 = (bf16[2,32,3072]{2,1,0:T(8,128)(2,1)}, bf16[2,32,3072]{2,1,0:T(8,128)(2,1)}, u32[]{:S(2)}, u32[]{:S(2)}) collective-permute-start(bf16[2,32,3072]{2,1,0:T(8,128)(2,1)} %collective-permute-done.34.refs_5_), channel_id=1, source_target_pairs={{0,1},{1,0},{2,3},{3,2},{4,5},{5,4},{6,7},{7,6}} | collective-permute-start | bytes 1179656 | tf_op jit(solution)/shard_map/ppermute | solution.py:244
  154.9 47.9 %collective-permute-start.39 = (bf16[2,32,3072]{2,1,0:T(8,128)(2,1)}, bf16[2,32,3072]{2,1,0:T(8,128)(2,1)}, u32[]{:S(2)}, u32[]{:S(2)}) collective-permute-start(bf16[2,32,3072]{2,1,0:T(8,128)(2,1)} %collective-permute-done.37.refs_8_), channel_id=1, source_target_pairs={{0,1},{1,0},{2,3},{3,2},{4,5},{5,4},{6,7},{7,6}} | collective-permute-start | bytes 1179656 | tf_op jit(solution)/shard_map/ppermute | solution.py:244
  161.5 41.2 %collective-permute-start.40 = (bf16[2,32,3072]{2,1,0:T(8,128)(2,1)}, bf16[2,32,3072]{2,1,0:T(8,128)(2,1)}, u32[]{:S(2)}, u32[]{:S(2)}) collective-permute-start(bf16[2,32,3072]{2,1,0:T(8,128)(2,1)} %collective-permute-done.38.refs_9_), channel_id=1, source_target_pairs={{0,1},{1,0},{2,3},{3,2},{4,5},{5,4},{6,7},{7,6}} | collective-permute-start | bytes 1179656 | tf_op jit(solution)/shard_map/ppermute | solution.py:244
  162.7 40.1 %collective-permute-start.43 = (bf16[2,32,3072]{2,1,0:T(8,128)(2,1)}, bf16[2,32,3072]{2,1,0:T(8,128)(2,1)}, u32[]{:S(2)}, u32[]{:S(2)}) collective-permute-start(bf16[2,32,3072]{2,1,0:T(8,128)(2,1)} %collective-permute-done.41.refs_12_), channel_id=1, source_target_pairs={{0,1},{1,0},{2,3},{3,2},{4,5},{5,4},{6,7},{7,6}} | collective-permute-start | bytes 1179656 | tf_op jit(solution)/shard_map/ppermute | solution.py:244
  162.7 40.1 %collective-permute-start.44 = (bf16[2,32,3072]{2,1,0:T(8,128)(2,1)}, bf16[2,32,3072]{2,1,0:T(8,128)(2,1)}, u32[]{:S(2)}, u32[]{:S(2)}) collective-permute-start(bf16[2,32,3072]{2,1,0:T(8,128)(2,1)} %collective-permute-done.42.refs_13_), channel_id=1, source_target_pairs={{0,1},{1,0},{2,3},{3,2},{4,5},{5,4},{6,7},{7,6}} | collective-permute-start | bytes 1179656 | tf_op jit(solution)/shard_map/ppermute | solution.py:244
  (42 other events, 269.9 us)
